TPU v7x, 32 devices: a whole 2x2x4 slice. The times are simulated.
32 devices in a mesh: groups: 2 (over x), depth: 2 (over core), row: 8 (over z, y).
Axes of the slice: x: 2, y: 2, z: 4, core: 2. Of those that a mesh axis runs over, the one named last changes fastest.
Arguments:
- planes: float32 [4, 4, 512, 512], P('groups', None, 'row'), parts along dimension 0, may hold values from -6 to 6
- slowness: float32 [2, 512, 512], P('depth', 'row'), may hold values from 0.6 to 1.4
- ref_slowness: float32 [2], replicated, may hold values from 0.8 to 1.2
- freq_index: int32 [2], replicated, may hold values from 10 to 51
Outputs:
- image: float32 [4, 512, 512], P(('groups', 'depth'), 'row'), parts along dimension 0
- leaving: float32 [4, 4, 512, 512], P(('groups', 'depth'), None, 'row'), parts along dimension 0
There are 2 independent parts, one for each index of `groups`. A program takes and returns all parts, laid end to end along the dimension named above; an argument that names none is the same for every part. Nothing has to cross between parts.
All inputs are finite; a program needn't handle non-finite values.
Results may differ from a plain program's by a relative error of at most 0.0003.
Values sent between devices are 32-bit elements; how exact they have to be, the bound alone decides.
No kernel may reach another device: no remote copies, remote signals or barrier semaphores. Data moves between devices by JAX's collectives and lax.ppermute only.
A program may use at most 64 MiB of HBM per device.

v0:
```python
import functools

import jax
import jax.numpy as jnp
import numpy as np
from jax import lax
from jax.experimental import pallas as pl
from jax.experimental.pallas import tpu as pltpu
from jax.sharding import PartitionSpec as P

omega_step = 0.05
depth_step = 1.0
lanes = 128


def pair(table):
    high = table.astype(jnp.bfloat16)
    low = (table - high.astype(np.float64)).astype(jnp.bfloat16)
    return np.stack([high, low])


def real_form(points):
    product = np.outer(np.arange(points), np.arange(points)) % points
    angle = 2.0 * np.pi / points * product
    c, s = np.cos(angle), np.sin(angle)
    return pair(np.block([[c, -s], [s, c]])), pair(np.block([[c, s], [-s, c]]))


def twiddles(length, radix):
    points = length // radix
    angle = 2.0 * np.pi / length * np.outer(np.arange(radix), np.arange(points))
    return np.stack([np.cos(angle), -np.sin(angle)], axis=1).astype(np.float32)


def split(x):
    high = x.astype(jnp.bfloat16)
    return high, (x - high.astype(jnp.float32)).astype(jnp.bfloat16)


def dot(a, b):
    return jnp.dot(a, b, preferred_element_type=jnp.float32)


def times_table(x, table):
    high, low = split(x)
    return dot(high, table[0]) + dot(low, table[0]) + dot(high, table[1])


def table_times(table, x):
    high, low = split(x)
    return dot(table[0], high) + dot(table[0], low) + dot(table[1], high)


def scaled(value, factor):
    if value is None or factor == 0.0:
        return None
    if factor == 1.0:
        return value
    return -value if factor == -1.0 else value * factor


def plus(a, b):
    if a is None:
        return b
    return a if b is None else a + b


def small_transform(parts, sign):
    radix = len(parts)
    if radix == 1:
        return parts
    if radix % 2 == 0:
        half = radix // 2
        even = small_transform(parts[0::2], sign)
        odd = small_transform(parts[1::2], sign)
        first, second = [], []
        for r in range(half):
            angle = sign * 2.0 * np.pi * r / radix
            c, s = float(np.round(np.cos(angle), 15)), float(np.round(np.sin(angle), 15))
            ore, oim = odd[r]
            tre = plus(scaled(ore, c), scaled(oim, -s))
            tim = plus(scaled(oim, c), scaled(ore, s))
            ere, eim = even[r]
            first.append((ere + tre, eim + tim))
            second.append((ere - tre, eim - tim))
        return first + second
    raise ValueError("radix")


def turn(part, factor, conjugate):
    re, im = part
    fre, fim = factor
    if conjugate:
        return re * fre + im * fim, im * fre - re * fim
    return re * fre - im * fim, im * fre + re * fim


def rows_of(parts):
    return jnp.concatenate([jnp.concatenate(part, axis=1) for part in parts], axis=0)


def row_forward(cells, tw, table, points):
    stacked = []
    for parts in cells:
        for r, part in enumerate(small_transform(parts, -1.0)):
            factor = (tw[r, 0:1], tw[r, 1:2])
            stacked.append(part if r == 0 else turn(part, factor, False))
    return times_table(rows_of(stacked), table)


def row_inverse(ref, tw, table, radix, planes):
    rows, points = ref.shape[2], ref.shape[3]
    count = planes * radix
    stacked = jnp.concatenate(
        [ref[:, 0].reshape(count * rows, points), ref[:, 1].reshape(count * rows, points)], axis=1
    )
    out = times_table(stacked, table)
    cells = []
    for p in range(planes):
        parts = []
        for r in range(radix):
            at = (p * radix + r) * rows
            part = (out[at : at + rows, :points], out[at : at + rows, points:])
            parts.append(part if r == 0 else turn(part, (tw[r, 0:1], tw[r, 1:2]), True))
        cells.append(small_transform(parts, 1.0))
    return cells


def store_blocks(out_ref, value, count, rows, points):
    out_ref[:, 0] = value[:, :points].reshape(count, rows, points)
    out_ref[:, 1] = value[:, points:].reshape(count, rows, points)


def first_kernel(radix, freq_ref, planes_ref, tw, table, out_ref):
    rows, points = out_ref.shape[2], out_ref.shape[3]
    cells = []
    for p in range(2):
        cells.append(
            [
                (
                    planes_ref[0, 2 * p, :, m * points : (m + 1) * points],
                    planes_ref[0, 2 * p + 1, :, m * points : (m + 1) * points],
                )
                for m in range(radix)
            ]
        )
    value = row_forward(cells, tw, table, points)
    store_blocks(out_ref, value, 2 * radix, rows, points)


def column_kernel(radix, in_ref, hre, him, tw, forward, inverse, out_ref):
    count, _, rows, width = in_ref.shape
    points = count * rows // radix
    per = points // rows

    def block(m, part):
        return in_ref[m * per : (m + 1) * per, part].reshape(points, width)

    parts = small_transform([(block(m, 0), block(m, 1)) for m in range(radix)], -1.0)
    columns = []
    for r, part in enumerate(parts):
        if r > 0:
            factor = (tw[:, 2 * r : 2 * r + 1], tw[:, 2 * r + 1 : 2 * r + 2])
            part = turn(part, factor, False)
        columns.append(jnp.concatenate(part, axis=0))
    spectrum = table_times(forward, jnp.concatenate(columns, axis=1))
    columns = []
    for r in range(radix):
        at = slice(r * width, (r + 1) * width)
        part = turn((spectrum[:points, at], spectrum[points:, at]), (hre[r], him[r]), False)
        columns.append(jnp.concatenate(part, axis=0))
    back = table_times(inverse, jnp.concatenate(columns, axis=1))
    parts = []
    for r in range(radix):
        at = slice(r * width, (r + 1) * width)
        part = (back[:points, at], back[points:, at])
        if r > 0:
            factor = (tw[:, 2 * r : 2 * r + 1], tw[:, 2 * r + 1 : 2 * r + 2])
            part = turn(part, factor, True)
        parts.append(part)
    for m, (re, im) in enumerate(small_transform(parts, 1.0)):
        out_ref[m * per : (m + 1) * per, 0] = re.reshape(per, rows, width)
        out_ref[m * per : (m + 1) * per, 1] = im.reshape(per, rows, width)


def screened(cells, cos_ref, sin_ref, points):
    turned = ([], [])
    for m in range(len(cells[0])):
        at = slice(m * points, (m + 1) * points)
        factor = (cos_ref[:, at], sin_ref[:, at])
        turned[0].append(turn(cells[0][m], factor, True))
        turned[1].append(turn(cells[1][m], factor, False))
    return turned


def middle_kernel(radix, in_ref, cos_ref, sin_ref, tw, inverse, forward, out_ref, image_ref):
    rows, points = in_ref.shape[2], in_ref.shape[3]
    cells = screened(row_inverse(in_ref, tw, inverse, radix, 2), cos_ref, sin_ref, points)
    for m in range(radix):
        (sre, sim), (rre, rim) = cells[0][m], cells[1][m]
        image_ref[:, m * points : (m + 1) * points] = sre * rre + sim * rim
    value = row_forward(cells, tw, forward, points)
    store_blocks(out_ref, value, 2 * radix, rows, points)


def last_kernel(radix, in_ref, cos_ref, sin_ref, tw, inverse, leaving_ref, image_ref):
    points = in_ref.shape[3]
    cells = screened(row_inverse(in_ref, tw, inverse, radix, 2), cos_ref, sin_ref, points)
    for m in range(radix):
        at = slice(m * points, (m + 1) * points)
        (sre, sim), (rre, rim) = cells[0][m], cells[1][m]
        leaving_ref[0, 0, :, at] = sre
        leaving_ref[0, 1, :, at] = sim
        leaving_ref[0, 2, :, at] = rre
        leaving_ref[0, 3, :, at] = rim
        image_ref[:, at] = sre * rre + sim * rim


def signed_wave(positions, length):
    signed = jnp.where(positions < length // 2, positions, positions - length)
    return 2.0 * jnp.pi / length * signed.astype(jnp.float32)


def call(kernel, out_shapes):
    return pl.pallas_call(kernel, out_shape=[jax.ShapeDtypeStruct(s, jnp.float32) for s in out_shapes])


def shards(planes, slowness, ref_slowness, freq_index):
    _, _, rows, length = planes.shape
    ranks = lax.axis_size("row")
    radix = ranks // 2
    points = length // radix
    col_radix = length // lanes
    row_index, core = lax.axis_index("row"), lax.axis_index("depth")

    row_forward_table, row_inverse_table = real_form(points)
    col_inverse_table, col_forward_table = real_form(lanes)
    row_tw = twiddles(length, radix)
    col_tw = twiddles(length, col_radix).transpose(2, 0, 1).reshape(lanes, 2 * col_radix)

    omega = omega_step * freq_index[core].astype(jnp.float32)
    other = lax.ppermute(slowness, "depth", [(0, 1), (1, 0)])
    own_first = core == 0
    screens = [
        jnp.where(own_first, slowness[0], other[0]),
        jnp.where(own_first, other[0], slowness[0]),
    ]

    blocks = (ranks, 2, rows, points)
    spectra = pl.pallas_call(
        functools.partial(first_kernel, radix),
        grid_spec=pltpu.PrefetchScalarGridSpec(
            num_scalar_prefetch=1,
            grid=(1,),
            in_specs=[
                pl.BlockSpec((1,) + planes.shape[1:], lambda i, f: (f[0], 0, 0, 0)),
                pl.BlockSpec(row_tw.shape, lambda i, f: (0, 0, 0)),
                pl.BlockSpec(row_forward_table.shape, lambda i, f: (0, 0, 0)),
            ],
            out_specs=pl.BlockSpec(blocks, lambda i, f: (0, 0, 0, 0)),
        ),
        out_shape=jax.ShapeDtypeStruct(blocks, jnp.float32),
    )(core.astype(jnp.int32).reshape(1), planes, row_tw, row_forward_table)

    residue = row_index % radix
    sign = jnp.where(row_index < radix, -1.0, 1.0)
    col_wave = signed_wave(
        (jnp.arange(lanes, dtype=jnp.int32)[None, :] * col_radix)
        + jnp.arange(col_radix, dtype=jnp.int32)[:, None],
        length,
    )
    row_wave = signed_wave(jnp.arange(points, dtype=jnp.int32) * radix + residue, length)
    plane_waves = col_wave[:, :, None] ** 2 + row_wave[None, None, :] ** 2
    scale = 1.0 / (length * length)

    def exchange(x):
        return lax.all_to_all(x, "row", split_axis=0, concat_axis=0, tiled=True)

    images = []
    for level in range(2):
        radicand = (omega * ref_slowness[level]) ** 2 - plane_waves
        vertical = jnp.sqrt(jnp.maximum(radicand, 0.0)) * depth_step
        damping = scale * jnp.exp(-jnp.sqrt(jnp.maximum(-radicand, 0.0)) * depth_step)
        hre, him = damping * jnp.cos(vertical), sign * damping * jnp.sin(vertical)
        theta = omega * (screens[level] - ref_slowness[level]) * depth_step
        cos_theta, sin_theta = jnp.cos(theta), jnp.sin(theta)
        columns = exchange(spectra)
        (columns,) = call(functools.partial(column_kernel, col_radix), [blocks])(
            columns, hre, him, col_tw, col_forward_table, col_inverse_table
        )
        cells = exchange(columns)
        if level == 0:
            spectra, image = call(functools.partial(middle_kernel, radix), [blocks, (rows, length)])(
                cells, cos_theta, sin_theta, row_tw, row_inverse_table, row_forward_table
            )
        else:
            leaving, image = call(
                functools.partial(last_kernel, radix), [(1,) + planes.shape[1:], (rows, length)]
            )(cells, cos_theta, sin_theta, row_tw, row_inverse_table)
        images.append(image)
    keep = jnp.where(own_first, images[0], images[1])
    send = jnp.where(own_first, images[1], images[0])
    image = keep + lax.ppermute(send, "depth", [(0, 1), (1, 0)])
    return image[None], leaving


def solution(mesh):
    in_specs = (P("groups", None, "row", None), P("depth", "row", None), P(), P())
    out_specs = (P(("groups", "depth"), "row", None), P(("groups", "depth"), None, "row", None))
    return jax.shard_map(shards, mesh=mesh, in_specs=in_specs, out_specs=out_specs, check_vma=False)
```

profile of v0, /device:TPU:0, one launch (start us, length us, event | category | flops | bytes accessed | tf_op | source)
XLA Modules:
  0.0 96.3 jit_solution(205039158852256695)
XLA Ops:
  0.6 2.3 %shard_map.113 = f32[8,2,64,128]{3,2,1,0:T(8,128)} custom-call(s32[1]{0:T(128)} %bitcast.freq_ref, f32[2,4,64,512]{3,2,1,0:T(8,128)} %planes_ref.1, f32[4,2,128]{2,1,0:T(2,128)} %constant.57.clone.tw, bf16[2,256,256]{2,1,0:T(8,128)(2,1)} %constant.58.clone.table.inverse.forward), custom_call_target="tpu_custom_call" | custom-call | tf_op jit(solution)/shard_map/pallas_call | solution.py:250
  2.9 7.3 %all-to-all-start = ((f32[8,2,64,128]{3,2,1,0:T(8,128)}), f32[8,2,64,128]{3,2,1,0:T(8,128)S(1)}, u32[]{:S(2)}, u32[]{:S(2)}) async-start(f32[8,2,64,128]{3,2,1,0:T(8,128)} %shard_map.113), calls=%async_computation | async-start | bytes 1048576 | tf_op jit(solution)/shard_map/all_to_all | solution.py:277
  10.2 0.7 copy-done.6
  10.9 0.6 dynamic_slice.3
  12.0 0.6 copy-done.5
  12.7 0.6 fusion.32
  14.7 3.3 %fusion.11 = (f32[4,128,128]{2,1,0:T(8,128)}, f32[4,128,128]{2,1,0:T(8,128)}, f32[4,128,128]{2,1,0:T(8,128)}, f32[4,128,128]{2,1,0:T(8,128)}) fusion(f32[]{:T(128)S(6)} %integer_pow.25, f32[]{:T(128)S(6)} %mul.96, f32[128]{0:T(128)S(1)} %fusion.31, f32[4,128]{1,0:T(4,128)S(1)} %fusion.28, f32[]{:T(128)S(6)} %integer_pow.22), kind=kLoop, calls=%fused_computation.13 | loop fusion | flops 1245184 | bytes 1051148 | tf_op jit(solution)/shard_map/mul | solution.py:284
  18.0 6.7 %all-to-all-done.in_ref = f32[8,2,64,128]{3,2,1,0:T(8,128)S(1)} async-done(((f32[8,2,64,128]{3,2,1,0:T(8,128)}), f32[8,2,64,128]{3,2,1,0:T(8,128)S(1)}, u32[]{:S(2)}, u32[]{:S(2)}) %all-to-all-start) | async-done | bytes 524320 | tf_op jit(solution)/shard_map/all_to_all | solution.py:277
  24.7 0.8 copy-done.1
  25.5 3.2 %shard_map.114 = f32[8,2,64,128]{3,2,1,0:T(8,128)} custom-call(f32[8,2,64,128]{3,2,1,0:T(8,128)} %copy-done.1, f32[4,128,128]{2,1,0:T(8,128)} %get-tuple-element.15.hre, f32[4,128,128]{2,1,0:T(8,128)} %get-tuple-element.16.him, f32[128,8]{1,0:T(8,128)} %constant.59.clone.tw, bf16[2,256,256]{2,1,0:T(8,128)(2,1)} %constant.60.clone.forward.inverse, ...), custom_call_target="tpu_custom_call" | custom-call | tf_op jit(solution)/shard_map/pallas_call | solution.py:288
  28.7 3.8 %all-to-all-start.1 = ((f32[8,2,64,128]{3,2,1,0:T(8,128)}), f32[8,2,64,128]{3,2,1,0:T(8,128)S(1)}, u32[]{:S(2)}, u32[]{:S(2)}) async-start(f32[8,2,64,128]{3,2,1,0:T(8,128)} %shard_map.114), calls=%async_computation.1 | async-start | bytes 1048576 | tf_op jit(solution)/shard_map/all_to_all | solution.py:277
  32.5 0.1 collective-permute-start
  32.6 1.3 %collective-permute-done = f32[1,64,512]{2,1,0:T(8,128)S(1)} collective-permute-done((f32[1,64,512]{2,1,0:T(8,128)S(1)}, f32[1,64,512]{2,1,0:T(8,128)S(1)}, u32[]{:S(2)}, u32[]{:S(2)}) %collective-permute-start) | collective-permute-done | bytes 131104 | tf_op jit(solution)/shard_map/ppermute | solution.py:242
  33.9 3.0 %sine_bitcast_fusion = (f32[64,512]{1,0:T(8,128)}, f32[64,512]{1,0:T(8,128)}, f32[64,512]{1,0:T(8,128)}, f32[64,512]{1,0:T(8,128)}) fusion(f32[]{:T(128)} %bitcast.5, f32[1,64,512]{2,1,0:T(8,128)S(1)} %collective-permute-done, f32[1,64,512]{2,1,0:T(8,128)S(1)} %copy-done.4, pred[]{:T(512)S(6)} %eq.5, f32[]{:T(128)} %bitcast.1, f32[]{:T(128)} %bitcast.2), kind=kLoop, calls=%fused_computation.29 | loop fusion | flops 196608 | bytes 786445 | tf_op jit(solution)/shard_map/sin | solution.py:286
  36.9 10.3 %all-to-all-done.1.in_ref = f32[8,2,64,128]{3,2,1,0:T(8,128)S(1)} async-done(((f32[8,2,64,128]{3,2,1,0:T(8,128)}), f32[8,2,64,128]{3,2,1,0:T(8,128)S(1)}, u32[]{:S(2)}, u32[]{:S(2)}) %all-to-all-start.1) | async-done | bytes 524320 | tf_op jit(solution)/shard_map/all_to_all | solution.py:277
  47.2 0.8 copy-done
  48.0 3.2 %shard_map.115 = (f32[8,2,64,128]{3,2,1,0:T(8,128)}, f32[64,512]{1,0:T(8,128)}) custom-call(f32[8,2,64,128]{3,2,1,0:T(8,128)} %copy-done, f32[64,512]{1,0:T(8,128)} %get-tuple-element.12.cos_ref, f32[64,512]{1,0:T(8,128)} %get-tuple-element.11.sin_ref, f32[4,2,128]{2,1,0:T(2,128)} %constant.57.clone.tw, bf16[2,256,256]{2,1,0:T(8,128)(2,1)} %constant.60.clone.forward.inverse, ...), custom_call_target="tpu_custom_call" | custom-call | tf_op jit(solution)/shard_map/pallas_call | solution.py:293
  51.2 18.4 %all_to_all.20.in_ref = f32[8,2,64,128]{3,2,1,0:T(8,128)} all-to-all(f32[8,2,64,128]{3,2,1,0:T(8,128)} %get-tuple-element.7), channel_id=1, replica_groups=mesh['groups'=2,'depth'=2,'row'=8] {'row'}, dimensions={0} | all-to-all | bytes 1048576 | tf_op jit(solution)/shard_map/all_to_all | solution.py:277
  69.6 3.2 %shard_map.116 = f32[8,2,64,128]{3,2,1,0:T(8,128)} custom-call(f32[8,2,64,128]{3,2,1,0:T(8,128)} %all_to_all.20.in_ref, f32[4,128,128]{2,1,0:T(8,128)} %get-tuple-element.17.hre, f32[4,128,128]{2,1,0:T(8,128)} %get-tuple-element.14.him, f32[128,8]{1,0:T(8,128)} %constant.59.clone.tw, bf16[2,256,256]{2,1,0:T(8,128)(2,1)} %constant.60.clone.forward.inverse, ...), custom_call_target="tpu_custom_call" | custom-call | tf_op jit(solution)/shard_map/pallas_call | solution.py:288
  72.8 17.9 %all_to_all.21.in_ref = f32[8,2,64,128]{3,2,1,0:T(8,128)} all-to-all(f32[8,2,64,128]{3,2,1,0:T(8,128)} %shard_map.116), channel_id=1, replica_groups=mesh['groups'=2,'depth'=2,'row'=8] {'row'}, dimensions={0} | all-to-all | bytes 1048576 | tf_op jit(solution)/shard_map/all_to_all | solution.py:277
  90.7 2.5 %shard_map.117 = (f32[1,4,64,512]{3,2,1,0:T(8,128)}, f32[64,512]{1,0:T(8,128)}) custom-call(f32[8,2,64,128]{3,2,1,0:T(8,128)} %all_to_all.21.in_ref, f32[64,512]{1,0:T(8,128)} %get-tuple-element.13.cos_ref, f32[64,512]{1,0:T(8,128)} %get-tuple-element.10.sin_ref, f32[4,2,128]{2,1,0:T(2,128)} %constant.57.clone.tw, ...), custom_call_target="tpu_custom_call" | custom-call | tf_op jit(solution)/shard_map/pallas_call | solution.py:297
  93.2 1.0 %broadcast_select_fusion = f32[64,512]{1,0:T(8,128)S(1)} fusion(f32[64,512]{1,0:T(8,128)} %get-tuple-element.8, f32[64,512]{1,0:T(8,128)S(1)} %copy-done.2, pred[]{:T(512)S(6)} %eq.5), kind=kLoop, calls=%fused_computation.35 | loop fusion | flops 32768 | bytes 393217 | tf_op jit(solution)/shard_map/jit(_where)/select_n | solution.py:302
  94.3 1.3 %collective-permute-done.1 = f32[64,512]{1,0:T(8,128)S(1)} collective-permute-done((f32[64,512]{1,0:T(8,128)S(1)}, f32[64,512]{1,0:T(8,128)S(1)}, u32[]{:S(2)}, u32[]{:S(2)}) %collective-permute-start.1) | collective-permute-done | bytes 131104 | tf_op jit(solution)/shard_map/ppermute | solution.py:303
  95.6 0.7 add_bitcast_fusion
  (14 shorter events, 0.1 us)
Async XLA Ops:
  2.9 21.8 %all-to-all-start = ((f32[8,2,64,128]{3,2,1,0:T(8,128)}), f32[8,2,64,128]{3,2,1,0:T(8,128)S(1)}, u32[]{:S(2)}, u32[]{:S(2)}) async-start(f32[8,2,64,128]{3,2,1,0:T(8,128)} %shard_map.113), calls=%async_computation | async-start | bytes 1048576 | tf_op jit(solution)/shard_map/all_to_all | solution.py:277
  10.2 0.7 copy-start.6
  12.0 0.7 copy-start.5
  24.7 0.8 copy-start.1
  28.7 3.8 %copy-start.4 = (f32[1,64,512]{2,1,0:T(8,128)S(1)}, f32[1,64,512]{2,1,0:T(8,128)}, u32[]{:S(2)}) copy-start(f32[1,64,512]{2,1,0:T(8,128)} %param.11) | copy-start | bytes 393220
  28.7 18.4 %all-to-all-start.1 = ((f32[8,2,64,128]{3,2,1,0:T(8,128)}), f32[8,2,64,128]{3,2,1,0:T(8,128)S(1)}, u32[]{:S(2)}, u32[]{:S(2)}) async-start(f32[8,2,64,128]{3,2,1,0:T(8,128)} %shard_map.114), calls=%async_computation.1 | async-start | bytes 1048576 | tf_op jit(solution)/shard_map/all_to_all | solution.py:277
  32.5 1.4 %collective-permute-start = (f32[1,64,512]{2,1,0:T(8,128)S(1)}, f32[1,64,512]{2,1,0:T(8,128)S(1)}, u32[]{:S(2)}, u32[]{:S(2)}) collective-permute-start(f32[1,64,512]{2,1,0:T(8,128)S(1)} %copy-done.4), channel_id=1, source_target_pairs={{0,8},{8,0},{1,9},{9,1},{2,10},{10,2},{3,11},{11,3},{4,12},{12,4},... | collective-permute-start | bytes 393224 | tf_op jit(solution)/shard_map/ppermute | solution.py:242
  47.2 0.8 copy-start
  90.7 2.5 %copy-start.2 = (f32[64,512]{1,0:T(8,128)S(1)}, f32[64,512]{1,0:T(8,128)}, u32[]{:S(2)}) copy-start(f32[64,512]{1,0:T(8,128)} %get-tuple-element.6) | copy-start | bytes 393220
  93.2 2.4 %copy-start.3 = (f32[64,512]{1,0:T(8,128)S(1)}, f32[64,512]{1,0:T(8,128)}, u32[]{:S(2)}) copy-start(f32[64,512]{1,0:T(8,128)} %get-tuple-element.8) | copy-start | bytes 393220
  94.2 1.4 %collective-permute-start.1 = (f32[64,512]{1,0:T(8,128)S(1)}, f32[64,512]{1,0:T(8,128)S(1)}, u32[]{:S(2)}, u32[]{:S(2)}) collective-permute-start(f32[64,512]{1,0:T(8,128)S(1)} %broadcast_select_fusion), channel_id=1, source_target_pairs={{0,8},{8,0},{1,9},{9,1},{2,10},{10,2},{3,11},{11,3},{4,12},{12,4},... | collective-permute-start | bytes 393224 | tf_op jit(solution)/shard_map/ppermute | solution.py:303
where the time goes:
time: 97 us; the launch traced here: 96.3 us
  blocking collectives  36.3 us (37%)
  waiting for transfers between devices  19.7 us (20%)
  Pallas kernels  14.5 us (15%)
  starting transfers between devices  11.2 us (12%)
  other arithmetic  7.97 us (8%)
  local copies, waits for them, and re-layouts  4.1 us (4%)
  between operations  2.59 us (3%)
    all_to_all x2, blocking collectives, exchange(): return lax.all_to_all(x, 'row', split_axis=0, concat_axis=0, tiled=True)  36.3 us
    all_to_all x2, waiting for transfers between devices, exchange(): return lax.all_to_all(x, 'row', split_axis=0, concat_axis=0, tiled=True)  17 us
    all_to_all x2, starting transfers between devices, exchange(): return lax.all_to_all(x, 'row', split_axis=0, concat_axis=0, tiled=True)  11.1 us
    pallas_call x2, Pallas kernels, shards(): call(functools.partial(column_kernel, col_radix), [blocks])  6.39 us
    mul x1, other arithmetic, shards(): hre, him = (damping * jnp.cos(vertical), sign * damping * jnp.sin(vertical))  3.31 us
    pallas_call x1, Pallas kernels, shards(): call(functools.partial(middle_kernel, radix), [blocks, (rows, length)])  3.24 us
    sin x1, other arithmetic, shards(): cos_theta, sin_theta = (jnp.cos(theta), jnp.sin(theta))  2.96 us
    unnamed x14, local copies, waits for them, and re-layouts  2.9 us
  transfers between devices with their start and end apart: 4, of which 4 were waited for; matrix products, arithmetic and copies ran while one was open for 8% of the time, Pallas kernels for 0%

commit v1 on v0

--- a/solution.py
+++ b/solution.py
@@ -131,27 +131,98 @@
     out_ref[:, 1] = value[:, points:].reshape(count, rows, points)
 
 
-def first_kernel(radix, freq_ref, planes_ref, tw, table, out_ref):
-    rows, points = out_ref.shape[2], out_ref.shape[3]
-    cells = []
-    for p in range(2):
-        cells.append(
-            [
-                (
-                    planes_ref[0, 2 * p, :, m * points : (m + 1) * points],
-                    planes_ref[0, 2 * p + 1, :, m * points : (m + 1) * points],
-                )
-                for m in range(radix)
-            ]
-        )
-    value = row_forward(cells, tw, table, points)
-    store_blocks(out_ref, value, 2 * radix, rows, points)
+def half_transform(parts, odd):
+    half = len(parts) // 2
+    folded = []
+    for m in range(half):
+        (are, aim), (bre, bim) = parts[m], parts[m + half]
+        if not odd:
+            folded.append((are + bre, aim + bim))
+            continue
+        re, im = are - bre, aim - bim
+        angle = -2.0 * np.pi * m / len(parts)
+        c, s = float(np.round(np.cos(angle), 15)), float(np.round(np.sin(angle), 15))
+        folded.append((plus(scaled(re, c), scaled(im, -s)), plus(scaled(im, c), scaled(re, s))))
+    return small_transform(folded, -1.0)
+
+
+def first_kernel(radix, planes_ref, tw, table, out_ref):
+    count, _, rows, points = out_ref.shape
+    for core in range(2):
+
+        @pl.when(lax.axis_index("depth") == core)
+        def _():
+            stacked = []
+            for p in range(planes_ref.shape[0] * 2):
+                f, c = p // 2, 2 * (p % 2)
+                parts = [
+                    tuple(planes_ref[f, c + i, :, m * points : (m + 1) * points] for i in range(2))
+                    for m in range(radix)
+                ]
+                for y, part in enumerate(half_transform(parts, core == 1)):
+                    r = 2 * y + core
+                    stacked.append(part if r == 0 else turn(part, (tw[r, 0:1], tw[r, 1:2]), False))
+            value = times_table(rows_of(stacked), table)
+            store_blocks(out_ref, value, count, rows, points)
+
+
+def residue_of():
+    per_plane = lax.axis_size("row") // 4
+    return lax.axis_index("depth") + 2 * lax.rem(lax.axis_index("row"), per_plane)
+
+
+def spread(held, out_refs):
+    own = residue_of()
+    for step, ref in enumerate(out_refs):
+        ref[...] = held[own ^ step]
+
+
+def collect(in_refs, held):
+    own = residue_of()
+    for step, ref in enumerate(in_refs):
+        held[own ^ step] = ref[...]
+
+
+def columns_to_quarters(col_radix, in_ref, hre, him, tw, forward, inverse, *rest):
+    out_refs, held = rest[:-1], rest[-1]
+    column_kernel(col_radix, in_ref, hre, him, tw, forward, inverse, held)
+    spread(held, out_refs)
+
+
+def quarters_to_columns(col_radix, radix, *refs):
+    in_refs, (hre, him, tw, forward, inverse, out_ref, held) = refs[:radix], refs[radix:]
+    collect(in_refs, held)
+    column_kernel(col_radix, held, hre, him, tw, forward, inverse, out_ref)
+
+
+def middle_kernel(radix, *refs):
+    in_refs, (cos_ref, sin_ref, tw, inverse, forward) = refs[:radix], refs[radix : radix + 5]
+    out_refs, (keep_ref, send_ref, held, field) = refs[radix + 5 : 2 * radix + 5], refs[2 * radix + 5 :]
+    rows, points = held.shape[2], held.shape[3]
+    collect(in_refs, held)
+    (cells,) = row_inverse(held, tw, inverse, radix, 1)
+    turned = []
+    for m in range(radix):
+        at = slice(m * points, (m + 1) * points)
+        part = turn(cells[m], (cos_ref[:, at], sin_ref[:, at]), False)
+        for half in range(2):
+            for i in range(2):
+                field[half, i, :, at] = part[i][half * rows // 2 : (half + 1) * rows // 2]
+        turned.append(part)
+    mine = lax.rem(lax.axis_index("row") // (lax.axis_size("row") // 4), 2)
+    keep_ref[...] = field[mine]
+    send_ref[...] = field[1 - mine]
+    value = row_forward([turned], tw, forward, points)
+    store_blocks(held, value, radix, rows, points)
+    spread(held, out_refs)
 
 
 def column_kernel(radix, in_ref, hre, him, tw, forward, inverse, out_ref):
     count, _, rows, width = in_ref.shape
     points = count * rows // radix
     per = points // rows
+    out_rows = out_ref.shape[2]
+    out_per = points // out_rows
 
     def block(m, part):
         return in_ref[m * per : (m + 1) * per, part].reshape(points, width)
@@ -179,8 +250,8 @@
             part = turn(part, factor, True)
         parts.append(part)
     for m, (re, im) in enumerate(small_transform(parts, 1.0)):
-        out_ref[m * per : (m + 1) * per, 0] = re.reshape(per, rows, width)
-        out_ref[m * per : (m + 1) * per, 1] = im.reshape(per, rows, width)
+        out_ref[m * out_per : (m + 1) * out_per, 0] = re.reshape(out_per, out_rows, width)
+        out_ref[m * out_per : (m + 1) * out_per, 1] = im.reshape(out_per, out_rows, width)
 
 
 def screened(cells, cos_ref, sin_ref, points):
@@ -193,19 +264,16 @@
     return turned
 
 
-def middle_kernel(radix, in_ref, cos_ref, sin_ref, tw, inverse, forward, out_ref, image_ref):
-    rows, points = in_ref.shape[2], in_ref.shape[3]
-    cells = screened(row_inverse(in_ref, tw, inverse, radix, 2), cos_ref, sin_ref, points)
-    for m in range(radix):
-        (sre, sim), (rre, rim) = cells[0][m], cells[1][m]
-        image_ref[:, m * points : (m + 1) * points] = sre * rre + sim * rim
-    value = row_forward(cells, tw, forward, points)
-    store_blocks(out_ref, value, 2 * radix, rows, points)
-
-
-def last_kernel(radix, in_ref, cos_ref, sin_ref, tw, inverse, leaving_ref, image_ref):
+def last_kernel(radix, in_ref, got_ref, cos_ref, sin_ref, tw, inverse, leaving_ref, image_ref, held):
     points = in_ref.shape[3]
-    cells = screened(row_inverse(in_ref, tw, inverse, radix, 2), cos_ref, sin_ref, points)
+    core = lax.axis_index("depth")
+    per_plane = radix // 2
+    for p in range(2):
+        for y in range(per_plane):
+            at = p * radix + 2 * y
+            held[at + core] = in_ref[core * radix + p * per_plane + y]
+            held[at + 1 - core] = got_ref[p * per_plane + y]
+    cells = screened(row_inverse(held, tw, inverse, radix, 2), cos_ref, sin_ref, points)
     for m in range(radix):
         at = slice(m * points, (m + 1) * points)
         (sre, sim), (rre, rim) = cells[0][m], cells[1][m]
@@ -221,49 +289,72 @@
     return 2.0 * jnp.pi / length * signed.astype(jnp.float32)
 
 
-def call(kernel, out_shapes):
-    return pl.pallas_call(kernel, out_shape=[jax.ShapeDtypeStruct(s, jnp.float32) for s in out_shapes])
+def call(kernel, out_shapes, scratch):
+    return pl.pallas_call(
+        kernel,
+        out_shape=[jax.ShapeDtypeStruct(s, jnp.float32) for s in out_shapes],
+        scratch_shapes=[pltpu.VMEM(s, jnp.float32) for s in scratch],
+    )
 
 
 def shards(planes, slowness, ref_slowness, freq_index):
     _, _, rows, length = planes.shape
     ranks = lax.axis_size("row")
     radix = ranks // 2
+    per_plane = radix // 2
     points = length // radix
     col_radix = length // lanes
     row_index, core = lax.axis_index("row"), lax.axis_index("depth")
+    own_first = core == 0
 
     row_forward_table, row_inverse_table = real_form(points)
     col_inverse_table, col_forward_table = real_form(lanes)
     row_tw = twiddles(length, radix)
     col_tw = twiddles(length, col_radix).transpose(2, 0, 1).reshape(lanes, 2 * col_radix)
-
-    omega = omega_step * freq_index[core].astype(jnp.float32)
-    other = lax.ppermute(slowness, "depth", [(0, 1), (1, 0)])
-    own_first = core == 0
-    screens = [
-        jnp.where(own_first, slowness[0], other[0]),
-        jnp.where(own_first, other[0], slowness[0]),
+    swap = [(0, 1), (1, 0)]
+    both = ("depth", "row")
+
+    def flat(c, r):
+        return c * ranks + r
+
+    def inner(arrays):
+        got = [arrays[0]] + [None] * (radix - 1)
+        for step in list(range(2, radix)) + [1]:
+            pairs = [
+                (flat(c, r), flat(c ^ (step & 1), r ^ (step >> 1))) for c in range(2) for r in range(ranks)
+            ]
+            got[step] = lax.ppermute(arrays[step], both, pairs)
+        return got
+
+    def exchange(x):
+        return lax.all_to_all(x, "row", split_axis=0, concat_axis=0, tiled=True)
+
+    def twin(x):
+        return lax.ppermute(x, "row", [(r, r ^ per_plane) for r in range(ranks)])
+
+    plane = row_index // per_plane
+    residue = residue_of()
+    sign = jnp.where(plane % 2 == 0, -1.0, 1.0)
+    omegas = omega_step * freq_index.astype(jnp.float32)
+    omega = omegas[plane // 2]
+
+    other = lax.ppermute(slowness, "depth", swap)
+    blocks = (ranks, 2, rows, points)
+    quarter = (2, 2 * rows, points)
+    half_field = (2, rows, length)
+    (spectra,) = call(functools.partial(first_kernel, radix), [blocks], [])(
+        planes, row_tw, row_forward_table
+    )
+    first_slow = jnp.where(own_first, slowness[0], other[0])
+    last_slow = jnp.where(own_first, other[0], slowness[0])
+    pairs = [
+        (flat(f, b), flat((b // 2) % 2, (2 * f + b % 2) * per_plane + b // 4))
+        for f in range(2)
+        for b in range(ranks)
     ]
-
-    blocks = (ranks, 2, rows, points)
-    spectra = pl.pallas_call(
-        functools.partial(first_kernel, radix),
-        grid_spec=pltpu.PrefetchScalarGridSpec(
-            num_scalar_prefetch=1,
-            grid=(1,),
-            in_specs=[
-                pl.BlockSpec((1,) + planes.shape[1:], lambda i, f: (f[0], 0, 0, 0)),
-                pl.BlockSpec(row_tw.shape, lambda i, f: (0, 0, 0)),
-                pl.BlockSpec(row_forward_table.shape, lambda i, f: (0, 0, 0)),
-            ],
-            out_specs=pl.BlockSpec(blocks, lambda i, f: (0, 0, 0, 0)),
-        ),
-        out_shape=jax.ShapeDtypeStruct(blocks, jnp.float32),
-    )(core.astype(jnp.int32).reshape(1), planes, row_tw, row_forward_table)
-
-    residue = row_index % radix
-    sign = jnp.where(row_index < radix, -1.0, 1.0)
+    near = lax.ppermute(first_slow, both, pairs)
+    far = twin(near)
+
     col_wave = signed_wave(
         (jnp.arange(lanes, dtype=jnp.int32)[None, :] * col_radix)
         + jnp.arange(col_radix, dtype=jnp.int32)[:, None],
@@ -272,36 +363,53 @@
     row_wave = signed_wave(jnp.arange(points, dtype=jnp.int32) * radix + residue, length)
     plane_waves = col_wave[:, :, None] ** 2 + row_wave[None, None, :] ** 2
     scale = 1.0 / (length * length)
-
-    def exchange(x):
-        return lax.all_to_all(x, "row", split_axis=0, concat_axis=0, tiled=True)
-
-    images = []
+    propagators = []
     for level in range(2):
         radicand = (omega * ref_slowness[level]) ** 2 - plane_waves
         vertical = jnp.sqrt(jnp.maximum(radicand, 0.0)) * depth_step
         damping = scale * jnp.exp(-jnp.sqrt(jnp.maximum(-radicand, 0.0)) * depth_step)
-        hre, him = damping * jnp.cos(vertical), sign * damping * jnp.sin(vertical)
-        theta = omega * (screens[level] - ref_slowness[level]) * depth_step
-        cos_theta, sin_theta = jnp.cos(theta), jnp.sin(theta)
-        columns = exchange(spectra)
-        (columns,) = call(functools.partial(column_kernel, col_radix), [blocks])(
-            columns, hre, him, col_tw, col_forward_table, col_inverse_table
-        )
-        cells = exchange(columns)
-        if level == 0:
-            spectra, image = call(functools.partial(middle_kernel, radix), [blocks, (rows, length)])(
-                cells, cos_theta, sin_theta, row_tw, row_inverse_table, row_forward_table
-            )
-        else:
-            leaving, image = call(
-                functools.partial(last_kernel, radix), [(1,) + planes.shape[1:], (rows, length)]
-            )(cells, cos_theta, sin_theta, row_tw, row_inverse_table)
-        images.append(image)
-    keep = jnp.where(own_first, images[0], images[1])
-    send = jnp.where(own_first, images[1], images[0])
-    image = keep + lax.ppermute(send, "depth", [(0, 1), (1, 0)])
-    return image[None], leaving
+        propagators.append((damping * jnp.cos(vertical), sign * damping * jnp.sin(vertical)))
+
+    columns = exchange(spectra)
+    quarters = call(
+        functools.partial(columns_to_quarters, col_radix), [quarter] * radix, [(radix,) + quarter]
+    )(columns, *propagators[0], col_tw, col_forward_table, col_inverse_table)
+    quarters = inner(quarters)
+
+    slow = jnp.where(plane % 2 == 0, jnp.concatenate([near, far]), jnp.concatenate([far, near]))
+    theta = omega * (slow - ref_slowness[0]) * depth_step
+    *quarters, keep, send = call(
+        functools.partial(middle_kernel, radix),
+        [quarter] * radix + [half_field] * 2,
+        [(radix,) + quarter, (2,) + half_field],
+    )(*quarters, jnp.cos(theta), sign * jnp.sin(theta), row_tw, row_inverse_table, row_forward_table)
+    quarters = inner(quarters)
+    got = twin(send)
+    (columns,) = call(
+        functools.partial(quarters_to_columns, col_radix, radix), [blocks], [(radix,) + quarter]
+    )(*quarters, *propagators[1], col_tw, col_forward_table, col_inverse_table)
+    cells = exchange(columns)
+
+    share = keep[0] * got[0] + keep[1] * got[1]
+    first_image = 0.0
+    for f in range(2):
+        pairs = [
+            (flat(c, (2 * f + h) * per_plane + y), flat(0, 2 * (c + 2 * y) + h))
+            for c in range(2)
+            for h in range(2)
+            for y in range(per_plane)
+        ]
+        first_image = first_image + lax.ppermute(share, both, pairs)
+
+    across = lax.ppermute(lax.dynamic_slice_in_dim(cells, (1 - core) * radix, radix), "depth", swap)
+    theta = omegas[core] * (last_slow - ref_slowness[1]) * depth_step
+    leaving, share = call(
+        functools.partial(last_kernel, radix),
+        [(1,) + planes.shape[1:], (rows, length)],
+        [(2 * radix,) + blocks[1:]],
+    )(cells, across, jnp.cos(theta), jnp.sin(theta), row_tw, row_inverse_table)
+    last_image = share + lax.ppermute(share, "depth", [(0, 1)])
+    return jnp.where(own_first, first_image, last_image)[None], leaving
 
 
 def solution(mesh):

time: 97 us -> 98.5 us (1.015)
  the two profiles are of different devices: /device:TPU:0 before, /device:TPU:7 now
where the time goes in v1:
time: 98.5 us; the launch traced here: 97.9 us
  starting transfers between devices  35.6 us (36%)
  waiting for transfers between devices  28.8 us (29%)
  Pallas kernels  15.1 us (15%)
  other arithmetic  10.4 us (11%)
  local copies, waits for them, and re-layouts  4.71 us (5%)
  between operations  3.33 us (3%)
    all_to_all x2, waiting for transfers between devices, exchange(): return lax.all_to_all(x, 'row', split_axis=0, concat_axis=0, tiled=True)  12.9 us
    ppermute x6, waiting for transfers between devices, inner(): got[step] = lax.ppermute(arrays[step], both, pairs)  9.9 us
    all_to_all x2, starting transfers between devices, exchange(): return lax.all_to_all(x, 'row', split_axis=0, concat_axis=0, tiled=True)  9.78 us
    ppermute x2, starting transfers between devices, shards(): first_image = first_image + lax.ppermute(share, both, pairs)  9.19 us
    ppermute x6, starting transfers between devices, inner(): got[step] = lax.ppermute(arrays[step], both, pairs)  6.4 us
    ppermute x1, starting transfers between devices, shards(): near = lax.ppermute(first_slow, both, pairs)  5.34 us
    pallas_call x1, Pallas kernels, shards(): call(functools.partial(middle_kernel, radix), [quarter] * radix + [half_f...  3.57 us
    unnamed x28, local copies, waits for them, and re-layouts  3.45 us
  transfers between devices with their start and end apart: 16, of which 8 were waited for; matrix products, arithmetic and copies ran while one was open for 10% of the time, Pallas kernels for 8%

profile of v1, /device:TPU:7, one launch (start us, length us, event | category | flops | bytes accessed | tf_op | source)
XLA Modules:
  0.0 97.9 jit_solution(11397840225674178278)
XLA Ops:
  1.4 2.5 %shard_map.113 = f32[8,2,64,128]{3,2,1,0:T(8,128)} custom-call(f32[2,4,64,512]{3,2,1,0:T(8,128)} %planes_ref.1, f32[4,2,128]{2,1,0:T(2,128)} %constant.79.clone.tw.refs_6_, bf16[2,256,256]{2,1,0:T(8,128)(2,1)} %constant.80.clone.table.inverse.refs_8_), custom_call_target="tpu_custom_call" | custom-call | tf_op jit(solution)/shard_map/pallas_call | solution.py:345
  3.8 5.9 %all-to-all-start = ((f32[8,2,64,128]{3,2,1,0:T(8,128)}), f32[8,2,64,128]{3,2,1,0:T(8,128)S(1)}, u32[]{:S(2)}, u32[]{:S(2)}) async-start(f32[8,2,64,128]{3,2,1,0:T(8,128)} %shard_map.113), calls=%async_computation | async-start | bytes 1048576 | tf_op jit(solution)/shard_map/all_to_all | solution.py:330
  11.7 2.5 %sine_bitcast_fusion = (f32[64,512]{1,0:T(8,128)}, f32[64,512]{1,0:T(8,128)S(1)}, f32[64,512]{1,0:T(8,128)}) fusion(f32[]{:T(128)} %bitcast.4, f32[1,64,512]{2,1,0:T(8,128)S(1)} %collective-permute-done.3, f32[1,64,512]{2,1,0:T(8,128)S(1)} %copy-done.10, pred[]{:T(512)S(6)} %eq.10, f32[]{:T(128)} %bitcast.5), kind=kLoop, calls=%fused_computation.37 | loop fusion | flops 131072 | bytes 655369 | tf_op jit(solution)/shard_map/sin | solution.py:410
  14.2 5.3 %collective-permute-start.4 = (f32[64,512]{1,0:T(8,128)S(1)}, f32[64,512]{1,0:T(8,128)S(1)}, u32[]{:S(2)}, u32[]{:S(2)}) collective-permute-start(f32[64,512]{1,0:T(8,128)S(1)} %get-tuple-element.27), channel_id=1, source_target_pairs={{0,0},{1,2},{2,8},{3,10},{4,1},{5,3},{6,9},{7,11},{8,4},{9,6},{10,... | collective-permute-start | bytes 393224 | tf_op jit(solution)/shard_map/ppermute | solution.py:355
  22.1 3.0 %collective-permute-done.4 = f32[64,512]{1,0:T(8,128)S(1)} collective-permute-done((f32[64,512]{1,0:T(8,128)S(1)}, f32[64,512]{1,0:T(8,128)S(1)}, u32[]{:S(2)}, u32[]{:S(2)}) %collective-permute-start.4) | collective-permute-done | bytes 131104 | tf_op jit(solution)/shard_map/ppermute | solution.py:355
  25.7 3.3 %fusion.11 = (f32[4,128,128]{2,1,0:T(8,128)}, f32[4,128,128]{2,1,0:T(8,128)}, f32[4,128,128]{2,1,0:T(8,128)}, f32[4,128,128]{2,1,0:T(8,128)}) fusion(f32[]{:T(128)S(6)} %integer_pow.25, f32[]{:T(128)S(6)} %mul.122, f32[128]{0:T(128)S(1)} %fusion.36, f32[4,128]{1,0:T(4,128)S(1)} %fusion.33, f32[]{:T(128)S(6)} %integer_pow.22), kind=kLoop, calls=%fused_computation.13 | loop fusion | flops 1245184 | bytes 1051148 | tf_op jit(solution)/shard_map/mul | solution.py:371
  29.8 3.2 %shard_map.114 = (f32[2,128,128]{2,1,0:T(8,128)}, f32[2,128,128]{2,1,0:T(8,128)}, f32[2,128,128]{2,1,0:T(8,128)}, f32[2,128,128]{2,1,0:T(8,128)}) custom-call(f32[8,2,64,128]{3,2,1,0:T(8,128)} %copy-done.1, f32[4,128,128]{2,1,0:T(8,128)} %get-tuple-element.32.hre, f32[4,128,128]{2,1,0:T(8,128)} %get-tuple-element.33.him, ...), custom_call_target="tpu_custom_call" | custom-call | tf_op jit(solution)/shard_map/pallas_call | solution.py:374
  33.0 2.6 %collective-permute-start = (f32[2,128,128]{2,1,0:T(8,128)}, f32[2,128,128]{2,1,0:T(8,128)S(1)}, u32[]{:S(2)}, u32[]{:S(2)}) collective-permute-start(f32[2,128,128]{2,1,0:T(8,128)} %get-tuple-element.15), channel_id=1, source_target_pairs={{0,8},{1,9},{2,10},{3,11},{4,12},{5,13},{6,14},{7,15},{8,0},{9,1},... | collective-permute-start | bytes 393224 | tf_op jit(solution)/shard_map/ppermute | solution.py:326
  35.6 1.7 %collective-permute-start.2 = (f32[2,128,128]{2,1,0:T(8,128)}, f32[2,128,128]{2,1,0:T(8,128)S(1)}, u32[]{:S(2)}, u32[]{:S(2)}) collective-permute-start(f32[2,128,128]{2,1,0:T(8,128)} %get-tuple-element.17), channel_id=1, source_target_pairs={{0,9},{1,8},{2,11},{3,10},{4,13},{5,12},{6,15},{7,14},{8,1},{9,0},... | collective-permute-start | bytes 393224 | tf_op jit(solution)/shard_map/ppermute | solution.py:326
  37.3 3.0 %sine_multiply_fusion = (f32[128,512]{1,0:T(8,128)}, f32[128,512]{1,0:T(8,128)}) fusion(f32[]{:T(128)S(6)} %select_n.82, f32[]{:T(128)} %bitcast.1, f32[64,512]{1,0:T(8,128)S(1)} %collective-permute-done.4, f32[64,512]{1,0:T(8,128)S(1)} %collective-permute-done.5, pred[]{:T(512)S(6)} %eq.11, f32[]{:T(128)} %bitcast), kind=kLoop, calls=%fused_computation.31 | loop fusion | flops 393216 | bytes 786445 | tf_op jit(solution)/shard_map/mul | solution.py:385
  40.8 3.0 %collective-permute-done.2.refs_3_ = f32[2,128,128]{2,1,0:T(8,128)S(1)} collective-permute-done((f32[2,128,128]{2,1,0:T(8,128)}, f32[2,128,128]{2,1,0:T(8,128)S(1)}, u32[]{:S(2)}, u32[]{:S(2)}) %collective-permute-start.2) | collective-permute-done | bytes 131104 | tf_op jit(solution)/shard_map/ppermute | solution.py:326
  44.5 3.6 %shard_map.115 = (f32[2,128,128]{2,1,0:T(8,128)}, f32[2,128,128]{2,1,0:T(8,128)}, f32[2,128,128]{2,1,0:T(8,128)}, f32[2,128,128]{2,1,0:T(8,128)}, f32[2,64,512]{2,1,0:T(8,128)}, /*index=5*/f32[2,64,512]{2,1,0:T(8,128)}) custom-call(f32[2,128,128]{2,1,0:T(8,128)} %get-tuple-element.14.refs_0_, f32[2,128,128]{2,1,0:T(8,128)} %copy-done.4, ...), custom_call_target="tpu_custom_call" | custom-call | tf_op jit(solution)/shard_map/pallas_call | solution.py:381
  48.5 1.7 %collective-permute-start.11 = (f32[2,128,128]{2,1,0:T(8,128)}, f32[2,128,128]{2,1,0:T(8,128)S(1)}, u32[]{:S(2)}, u32[]{:S(2)}) collective-permute-start(f32[2,128,128]{2,1,0:T(8,128)} %get-tuple-element.23), channel_id=1, source_target_pairs={{0,9},{1,8},{2,11},{3,10},{4,13},{5,12},{6,15},{7,14},{8,1},{9,0},... | collective-permute-start | bytes 393224 | tf_op jit(solution)/shard_map/ppermute | solution.py:326
  50.2 3.0 %collective-permute-done.10.refs_2_ = f32[2,128,128]{2,1,0:T(8,128)S(1)} collective-permute-done((f32[2,128,128]{2,1,0:T(8,128)}, f32[2,128,128]{2,1,0:T(8,128)S(1)}, u32[]{:S(2)}, u32[]{:S(2)}) %collective-permute-start.10) | collective-permute-done | bytes 131104 | tf_op jit(solution)/shard_map/ppermute | solution.py:326
  53.2 3.3 %collective-permute-done.11.refs_3_ = f32[2,128,128]{2,1,0:T(8,128)S(1)} collective-permute-done((f32[2,128,128]{2,1,0:T(8,128)}, f32[2,128,128]{2,1,0:T(8,128)S(1)}, u32[]{:S(2)}, u32[]{:S(2)}) %collective-permute-start.11) | collective-permute-done | bytes 131104 | tf_op jit(solution)/shard_map/ppermute | solution.py:326
  57.1 3.2 %shard_map.116 = f32[8,2,64,128]{3,2,1,0:T(8,128)} custom-call(f32[2,128,128]{2,1,0:T(8,128)} %get-tuple-element.20.refs_0_, f32[2,128,128]{2,1,0:T(8,128)} %copy-done.7, f32[2,128,128]{2,1,0:T(8,128)} %copy-done.8, f32[2,128,128]{2,1,0:T(8,128)} %copy-done.9, f32[4,128,128]{2,1,0:T(8,128)} %get-tuple-element.34.refs_4_, ...), custom_call_target="tpu_custom_call" | custom-call | tf_op jit(solution)/shard_map/pallas_call | solution.py:388
  60.4 3.9 %all-to-all-start.1 = ((f32[8,2,64,128]{3,2,1,0:T(8,128)}), f32[8,2,64,128]{3,2,1,0:T(8,128)S(1)}, u32[]{:S(2)}, u32[]{:S(2)}) async-start(f32[8,2,64,128]{3,2,1,0:T(8,128)} %shard_map.116), calls=%async_computation.1 | async-start | bytes 1048576 | tf_op jit(solution)/shard_map/all_to_all | solution.py:330
  64.3 1.2 %collective-permute-start.6 = (f32[2,64,512]{2,1,0:T(8,128)S(1)}, f32[2,64,512]{2,1,0:T(8,128)S(1)}, u32[]{:S(2)}, u32[]{:S(2)}) collective-permute-start(f32[2,64,512]{2,1,0:T(8,128)S(1)} %copy-done.12), channel_id=1, source_target_pairs={{0,2},{1,3},{2,0},{3,1},{4,6},{5,7},{6,4},{7,5},{8,10},{9,11},{10,... | collective-permute-start | bytes 786440 | tf_op jit(solution)/shard_map/ppermute | solution.py:333
  65.5 12.9 %all-to-all-done.1.in_ref = f32[8,2,64,128]{3,2,1,0:T(8,128)S(1)} async-done(((f32[8,2,64,128]{3,2,1,0:T(8,128)}), f32[8,2,64,128]{3,2,1,0:T(8,128)S(1)}, u32[]{:S(2)}, u32[]{:S(2)}) %all-to-all-start.1) | async-done | bytes 524320 | tf_op jit(solution)/shard_map/all_to_all | solution.py:330
  81.0 8.5 %collective-permute-start.7 = (f32[64,512]{1,0:T(8,128)S(1)}, f32[64,512]{1,0:T(8,128)S(1)}, u32[]{:S(2)}, u32[]{:S(2)}) collective-permute-start(f32[64,512]{1,0:T(8,128)S(1)} %fusion.29), channel_id=1, source_target_pairs={{0,0},{1,4},{2,1},{3,5},{8,2},{9,6},{10,3},{11,7},{16,16},{17,20},... | collective-permute-start | bytes 393224 | tf_op jit(solution)/shard_map/ppermute | solution.py:402
  90.3 2.6 %shard_map.117 = (f32[1,4,64,512]{3,2,1,0:T(8,128)}, f32[64,512]{1,0:T(8,128)}) custom-call(f32[8,2,64,128]{3,2,1,0:T(8,128)} %copy-done, f32[4,2,64,128]{3,2,1,0:T(8,128)} %copy-done.2, f32[64,512]{1,0:T(8,128)} %get-tuple-element.28.cos_ref, f32[64,512]{1,0:T(8,128)} %get-tuple-element.26.sin_ref, f32[4,2,128]{2,1,0:T(2,128)} %constant.79.clone.tw.refs_6_, ...), custom_call_target="tpu_custom_call" | custom-call | tf_op jit(solution)/shard_map/pallas_call | solution.py:406
  92.9 1.3 %collective-permute-start.13 = (f32[64,512]{1,0:T(8,128)}, f32[64,512]{1,0:T(8,128)S(1)}, u32[]{:S(2)}, u32[]{:S(2)}) collective-permute-start(f32[64,512]{1,0:T(8,128)} %get-tuple-element.24), channel_id=1, source_target_pairs={{0,8},{1,9},{2,10},{3,11},{4,12},{5,13},{6,14},{7,15},{16,24},{17,... | collective-permute-start | bytes 393224 | tf_op jit(solution)/shard_map/ppermute | solution.py:411
  94.2 2.1 %collective-permute-done.13 = f32[64,512]{1,0:T(8,128)S(1)} collective-permute-done((f32[64,512]{1,0:T(8,128)}, f32[64,512]{1,0:T(8,128)S(1)}, u32[]{:S(2)}, u32[]{:S(2)}) %collective-permute-start.13) | collective-permute-done | bytes 131104 | tf_op jit(solution)/shard_map/ppermute | solution.py:411
  96.3 1.6 %select_bitcast_fusion = f32[1,64,512]{2,1,0:T(8,128)} fusion(f32[64,512]{1,0:T(8,128)} %get-tuple-element.24, f32[64,512]{1,0:T(8,128)S(1)} %collective-permute-done.13, f32[64,512]{1,0:T(8,128)S(1)} %collective-permute-done.7, f32[64,512]{1,0:T(8,128)S(1)} %collective-permute-done.8, pred[]{:T(512)S(6)} %eq.10), kind=kLoop, calls=%fused_computation.36 | loop fusion | flops 98304 | bytes 655361 | tf_op jit(solution)/shard_map/broadcast_in_dim | solution.py:412
  (53 shorter events, 9.7 us)
Async XLA Ops:
  0.6 11.0 %collective-permute-start.3 = (f32[1,64,512]{2,1,0:T(8,128)}, f32[1,64,512]{2,1,0:T(8,128)S(1)}, u32[]{:S(2)}, u32[]{:S(2)}) collective-permute-start(f32[1,64,512]{2,1,0:T(8,128)} %param.11), channel_id=1, source_target_pairs={{0,8},{8,0},{1,9},{9,1},{2,10},{10,2},{3,11},{11,3},{4,12},{12,4},... | collective-permute-start | bytes 393224 | tf_op jit(solution)/shard_map/ppermute | solution.py:341
  3.8 5.9 %copy-start.13 = (s32[2]{0:T(128)S(1)}, s32[2]{0:T(128)}, u32[]{:S(2)}) copy-start(s32[2]{0:T(128)} %param.13) | copy-start | bytes 28
  3.8 7.8 %copy-start.10 = (f32[1,64,512]{2,1,0:T(8,128)S(1)}, f32[1,64,512]{2,1,0:T(8,128)}, u32[]{:S(2)}) copy-start(f32[1,64,512]{2,1,0:T(8,128)} %param.11) | copy-start | bytes 393220
  3.8 25.1 %all-to-all-start = ((f32[8,2,64,128]{3,2,1,0:T(8,128)}), f32[8,2,64,128]{3,2,1,0:T(8,128)S(1)}, u32[]{:S(2)}, u32[]{:S(2)}) async-start(f32[8,2,64,128]{3,2,1,0:T(8,128)} %shard_map.113), calls=%async_computation | async-start | bytes 1048576 | tf_op jit(solution)/shard_map/all_to_all | solution.py:330
  14.2 11.0 %collective-permute-start.4 = (f32[64,512]{1,0:T(8,128)S(1)}, f32[64,512]{1,0:T(8,128)S(1)}, u32[]{:S(2)}, u32[]{:S(2)}) collective-permute-start(f32[64,512]{1,0:T(8,128)S(1)} %get-tuple-element.27), channel_id=1, source_target_pairs={{0,0},{1,2},{2,8},{3,10},{4,1},{5,3},{6,9},{7,11},{8,4},{9,6},{10,... | collective-permute-start | bytes 393224 | tf_op jit(solution)/shard_map/ppermute | solution.py:355
  25.1 12.1 %collective-permute-start.5 = (f32[64,512]{1,0:T(8,128)S(1)}, f32[64,512]{1,0:T(8,128)S(1)}, u32[]{:S(2)}, u32[]{:S(2)}) collective-permute-start(f32[64,512]{1,0:T(8,128)S(1)} %collective-permute-done.4), channel_id=1, source_target_pairs={{0,2},{1,3},{2,0},{3,1},{4,6},{5,7},{6,4},{7,5},{8,10},{9,11},{10,... | collective-permute-start | bytes 393224 | tf_op jit(solution)/shard_map/ppermute | solution.py:333
  33.0 7.2 %collective-permute-start = (f32[2,128,128]{2,1,0:T(8,128)}, f32[2,128,128]{2,1,0:T(8,128)S(1)}, u32[]{:S(2)}, u32[]{:S(2)}) collective-permute-start(f32[2,128,128]{2,1,0:T(8,128)} %get-tuple-element.15), channel_id=1, source_target_pairs={{0,8},{1,9},{2,10},{3,11},{4,12},{5,13},{6,14},{7,15},{8,0},{9,1},... | collective-permute-start | bytes 393224 | tf_op jit(solution)/shard_map/ppermute | solution.py:326
  35.6 5.2 %collective-permute-start.1 = (f32[2,128,128]{2,1,0:T(8,128)}, f32[2,128,128]{2,1,0:T(8,128)S(1)}, u32[]{:S(2)}, u32[]{:S(2)}) collective-permute-start(f32[2,128,128]{2,1,0:T(8,128)} %get-tuple-element.16), channel_id=1, source_target_pairs={{0,1},{1,0},{2,3},{3,2},{4,5},{5,4},{6,7},{7,6},{8,9},{9,8},{10,11... | collective-permute-start | bytes 393224 | tf_op jit(solution)/shard_map/ppermute | solution.py:326
  35.6 8.2 %collective-permute-start.2 = (f32[2,128,128]{2,1,0:T(8,128)}, f32[2,128,128]{2,1,0:T(8,128)S(1)}, u32[]{:S(2)}, u32[]{:S(2)}) collective-permute-start(f32[2,128,128]{2,1,0:T(8,128)} %get-tuple-element.17), channel_id=1, source_target_pairs={{0,9},{1,8},{2,11},{3,10},{4,13},{5,12},{6,15},{7,14},{8,1},{9,0},... | collective-permute-start | bytes 393224 | tf_op jit(solution)/shard_map/ppermute | solution.py:326
  40.2 3.6 %copy-start.4 = (f32[2,128,128]{2,1,0:T(8,128)}, f32[2,128,128]{2,1,0:T(8,128)S(1)}, u32[]{:S(2)}) copy-start(f32[2,128,128]{2,1,0:T(8,128)S(1)} %collective-permute-done.refs_1_) | copy-start | bytes 393220
  40.8 3.0 %copy-start.5 = (f32[2,128,128]{2,1,0:T(8,128)}, f32[2,128,128]{2,1,0:T(8,128)S(1)}, u32[]{:S(2)}) copy-start(f32[2,128,128]{2,1,0:T(8,128)S(1)} %collective-permute-done.1.refs_2_) | copy-start | bytes 393220
  48.1 2.1 %collective-permute-start.9 = (f32[2,128,128]{2,1,0:T(8,128)}, f32[2,128,128]{2,1,0:T(8,128)S(1)}, u32[]{:S(2)}, u32[]{:S(2)}) collective-permute-start(f32[2,128,128]{2,1,0:T(8,128)} %get-tuple-element.21), channel_id=1, source_target_pairs={{0,8},{1,9},{2,10},{3,11},{4,12},{5,13},{6,14},{7,15},{8,0},{9,1},... | collective-permute-start | bytes 393224 | tf_op jit(solution)/shard_map/ppermute | solution.py:326
  48.3 4.9 %collective-permute-start.10 = (f32[2,128,128]{2,1,0:T(8,128)}, f32[2,128,128]{2,1,0:T(8,128)S(1)}, u32[]{:S(2)}, u32[]{:S(2)}) collective-permute-start(f32[2,128,128]{2,1,0:T(8,128)} %get-tuple-element.22), channel_id=1, source_target_pairs={{0,1},{1,0},{2,3},{3,2},{4,5},{5,4},{6,7},{7,6},{8,9},{9,8},{10,11... | collective-permute-start | bytes 393224 | tf_op jit(solution)/shard_map/ppermute | solution.py:326
  48.5 8.0 %collective-permute-start.11 = (f32[2,128,128]{2,1,0:T(8,128)}, f32[2,128,128]{2,1,0:T(8,128)S(1)}, u32[]{:S(2)}, u32[]{:S(2)}) collective-permute-start(f32[2,128,128]{2,1,0:T(8,128)} %get-tuple-element.23), channel_id=1, source_target_pairs={{0,9},{1,8},{2,11},{3,10},{4,13},{5,12},{6,15},{7,14},{8,1},{9,0},... | collective-permute-start | bytes 393224 | tf_op jit(solution)/shard_map/ppermute | solution.py:326
  50.2 6.3 %copy-start.7 = (f32[2,128,128]{2,1,0:T(8,128)}, f32[2,128,128]{2,1,0:T(8,128)S(1)}, u32[]{:S(2)}) copy-start(f32[2,128,128]{2,1,0:T(8,128)S(1)} %collective-permute-done.9.refs_1_) | copy-start | bytes 393220
  53.2 3.3 %copy-start.8 = (f32[2,128,128]{2,1,0:T(8,128)}, f32[2,128,128]{2,1,0:T(8,128)S(1)}, u32[]{:S(2)}) copy-start(f32[2,128,128]{2,1,0:T(8,128)S(1)} %collective-permute-done.10.refs_2_) | copy-start | bytes 393220
  60.4 3.9 %copy-start.12 = (f32[2,64,512]{2,1,0:T(8,128)S(1)}, f32[2,64,512]{2,1,0:T(8,128)}, u32[]{:S(2)}) copy-start(f32[2,64,512]{2,1,0:T(8,128)} %get-tuple-element.19) | copy-start | bytes 786436
  60.4 18.0 %all-to-all-start.1 = ((f32[8,2,64,128]{3,2,1,0:T(8,128)}), f32[8,2,64,128]{3,2,1,0:T(8,128)S(1)}, u32[]{:S(2)}, u32[]{:S(2)}) async-start(f32[8,2,64,128]{3,2,1,0:T(8,128)} %shard_map.116), calls=%async_computation.1 | async-start | bytes 1048576 | tf_op jit(solution)/shard_map/all_to_all | solution.py:330
  64.3 16.0 %collective-permute-start.6 = (f32[2,64,512]{2,1,0:T(8,128)S(1)}, f32[2,64,512]{2,1,0:T(8,128)S(1)}, u32[]{:S(2)}, u32[]{:S(2)}) collective-permute-start(f32[2,64,512]{2,1,0:T(8,128)S(1)} %copy-done.12), channel_id=1, source_target_pairs={{0,2},{1,3},{2,0},{3,1},{4,6},{5,7},{6,4},{7,5},{8,10},{9,11},{10,... | collective-permute-start | bytes 786440 | tf_op jit(solution)/shard_map/ppermute | solution.py:333
  65.5 14.8 %copy-start.3 = (f32[2,64,512]{2,1,0:T(8,128)S(1)}, f32[2,64,512]{2,1,0:T(8,128)}, u32[]{:S(2)}) copy-start(f32[2,64,512]{2,1,0:T(8,128)} %get-tuple-element.18) | copy-start | bytes 786436
  78.4 11.1 %collective-permute-start.12 = (f32[4,2,64,128]{3,2,1,0:T(8,128)S(1)}, f32[4,2,64,128]{3,2,1,0:T(8,128)S(1)}, u32[]{:S(2)}, u32[]{:S(2)}) collective-permute-start(f32[4,2,64,128]{3,2,1,0:T(8,128)S(1)} %constant_dynamic-slice_fusion), channel_id=1, source_target_pairs={{0,8},{8,0},{1,9},{9,1},{2,10},{10,2},{3,11},{11,3},{4,12},{12,4},... | collective-permute-start | bytes 786440 | tf_op jit(solution)/shard_map/ppermute | solution.py:404
  80.4 13.8 %collective-permute-start.8 = (f32[64,512]{1,0:T(8,128)S(1)}, f32[64,512]{1,0:T(8,128)S(1)}, u32[]{:S(2)}, u32[]{:S(2)}) collective-permute-start(f32[64,512]{1,0:T(8,128)S(1)} %fusion.29), channel_id=1, source_target_pairs={{4,0},{5,4},{6,1},{7,5},{12,2},{13,6},{14,3},{15,7},{20,16},{21,20... | collective-permute-start | bytes 393224 | tf_op jit(solution)/shard_map/ppermute | solution.py:402
  81.0 13.1 %collective-permute-start.7 = (f32[64,512]{1,0:T(8,128)S(1)}, f32[64,512]{1,0:T(8,128)S(1)}, u32[]{:S(2)}, u32[]{:S(2)}) collective-permute-start(f32[64,512]{1,0:T(8,128)S(1)} %fusion.29), channel_id=1, source_target_pairs={{0,0},{1,4},{2,1},{3,5},{8,2},{9,6},{10,3},{11,7},{16,16},{17,20},... | collective-permute-start | bytes 393224 | tf_op jit(solution)/shard_map/ppermute | solution.py:402
  92.9 3.4 %collective-permute-start.13 = (f32[64,512]{1,0:T(8,128)}, f32[64,512]{1,0:T(8,128)S(1)}, u32[]{:S(2)}, u32[]{:S(2)}) collective-permute-start(f32[64,512]{1,0:T(8,128)} %get-tuple-element.24), channel_id=1, source_target_pairs={{0,8},{1,9},{2,10},{3,11},{4,12},{5,13},{6,14},{7,15},{16,24},{17,... | collective-permute-start | bytes 393224 | tf_op jit(solution)/shard_map/ppermute | solution.py:411
  (6 other events, 5.4 us)

commit v2 on v1

--- a/solution.py
+++ b/solution.py
@@ -190,7 +190,9 @@
 
 
 def quarters_to_columns(col_radix, radix, *refs):
-    in_refs, (hre, him, tw, forward, inverse, out_ref, held) = refs[:radix], refs[radix:]
+    in_refs, refs = refs[:radix], refs[radix:]
+    keep_ref, got_ref, hre, him, tw, forward, inverse, out_ref, share_ref, held = refs
+    share_ref[...] = keep_ref[0] * got_ref[0] + keep_ref[1] * got_ref[1]
     collect(in_refs, held)
     column_kernel(col_radix, held, hre, him, tw, forward, inverse, out_ref)
 
@@ -264,7 +266,9 @@
     return turned
 
 
-def last_kernel(radix, in_ref, got_ref, cos_ref, sin_ref, tw, inverse, leaving_ref, image_ref, held):
+def last_kernel(
+    radix, in_ref, got_ref, first_ref, second_ref, cos_ref, sin_ref, tw, inverse, leaving_ref, image_ref, base_ref, held
+):
     points = in_ref.shape[3]
     core = lax.axis_index("depth")
     per_plane = radix // 2
@@ -282,6 +286,11 @@
         leaving_ref[0, 2, :, at] = rre
         leaving_ref[0, 3, :, at] = rim
         image_ref[:, at] = sre * rre + sim * rim
+    base_ref[...] = image_ref[...]
+
+    @pl.when(core == 0)
+    def _():
+        base_ref[...] = first_ref[...] + second_ref[...]
 
 
 def signed_wave(positions, length):
@@ -289,12 +298,15 @@
     return 2.0 * jnp.pi / length * signed.astype(jnp.float32)
 
 
-def call(kernel, out_shapes, scratch):
+def call(kernel, out_shapes, scratch, args, held_args=True):
+    vmem = pl.BlockSpec(memory_space=pltpu.VMEM)
     return pl.pallas_call(
         kernel,
-        out_shape=[jax.ShapeDtypeStruct(s, jnp.float32) for s in out_shapes],
+        in_specs=[vmem] * len(args),
+        out_specs=[vmem] * len(out_shapes),
+        out_shape=[pltpu.VMEM(s, jnp.float32) for s in out_shapes],
         scratch_shapes=[pltpu.VMEM(s, jnp.float32) for s in scratch],
-    )
+    )(*[pltpu.with_memory_space_constraint(a, pltpu.VMEM) if held_args else a for a in args])
 
 
 def shards(planes, slowness, ref_slowness, freq_index):
@@ -342,8 +354,12 @@
     blocks = (ranks, 2, rows, points)
     quarter = (2, 2 * rows, points)
     half_field = (2, rows, length)
-    (spectra,) = call(functools.partial(first_kernel, radix), [blocks], [])(
-        planes, row_tw, row_forward_table
+    (spectra,) = call(
+        functools.partial(first_kernel, radix),
+        [blocks],
+        [],
+        (planes, row_tw, row_forward_table),
+        held_args=False,
     )
     first_slow = jnp.where(own_first, slowness[0], other[0])
     last_slow = jnp.where(own_first, other[0], slowness[0])
@@ -353,8 +369,6 @@
         for b in range(ranks)
     ]
     near = lax.ppermute(first_slow, both, pairs)
-    far = twin(near)
-
     col_wave = signed_wave(
         (jnp.arange(lanes, dtype=jnp.int32)[None, :] * col_radix)
         + jnp.arange(col_radix, dtype=jnp.int32)[:, None],
@@ -370,10 +384,15 @@
         damping = scale * jnp.exp(-jnp.sqrt(jnp.maximum(-radicand, 0.0)) * depth_step)
         propagators.append((damping * jnp.cos(vertical), sign * damping * jnp.sin(vertical)))
 
+    near, propagators = lax.optimization_barrier((near, propagators))
+    far = twin(near)
     columns = exchange(spectra)
     quarters = call(
-        functools.partial(columns_to_quarters, col_radix), [quarter] * radix, [(radix,) + quarter]
-    )(columns, *propagators[0], col_tw, col_forward_table, col_inverse_table)
+        functools.partial(columns_to_quarters, col_radix),
+        [quarter] * radix,
+        [(radix,) + quarter],
+        (columns, *propagators[0], col_tw, col_forward_table, col_inverse_table),
+    )
     quarters = inner(quarters)
 
     slow = jnp.where(plane % 2 == 0, jnp.concatenate([near, far]), jnp.concatenate([far, near]))
@@ -382,16 +401,19 @@
         functools.partial(middle_kernel, radix),
         [quarter] * radix + [half_field] * 2,
         [(radix,) + quarter, (2,) + half_field],
-    )(*quarters, jnp.cos(theta), sign * jnp.sin(theta), row_tw, row_inverse_table, row_forward_table)
+        (*quarters, jnp.cos(theta), sign * jnp.sin(theta), row_tw, row_inverse_table, row_forward_table),
+    )
     quarters = inner(quarters)
     got = twin(send)
-    (columns,) = call(
-        functools.partial(quarters_to_columns, col_radix, radix), [blocks], [(radix,) + quarter]
-    )(*quarters, *propagators[1], col_tw, col_forward_table, col_inverse_table)
+    columns, share = call(
+        functools.partial(quarters_to_columns, col_radix, radix),
+        [blocks, (rows, length)],
+        [(radix,) + quarter],
+        (*quarters, keep, got, *propagators[1], col_tw, col_forward_table, col_inverse_table),
+    )
     cells = exchange(columns)
 
-    share = keep[0] * got[0] + keep[1] * got[1]
-    first_image = 0.0
+    shares = []
     for f in range(2):
         pairs = [
             (flat(c, (2 * f + h) * per_plane + y), flat(0, 2 * (c + 2 * y) + h))
@@ -399,17 +421,19 @@
             for h in range(2)
             for y in range(per_plane)
         ]
-        first_image = first_image + lax.ppermute(share, both, pairs)
-
+        shares.append(lax.ppermute(share, both, pairs))
+
+    cells, *shares = lax.optimization_barrier((cells, *shares))
     across = lax.ppermute(lax.dynamic_slice_in_dim(cells, (1 - core) * radix, radix), "depth", swap)
     theta = omegas[core] * (last_slow - ref_slowness[1]) * depth_step
-    leaving, share = call(
+    leaving, share, base = call(
         functools.partial(last_kernel, radix),
-        [(1,) + planes.shape[1:], (rows, length)],
+        [(1,) + planes.shape[1:], (rows, length), (rows, length)],
         [(2 * radix,) + blocks[1:]],
-    )(cells, across, jnp.cos(theta), jnp.sin(theta), row_tw, row_inverse_table)
-    last_image = share + lax.ppermute(share, "depth", [(0, 1)])
-    return jnp.where(own_first, first_image, last_image)[None], leaving
+        (cells, across, *shares, jnp.cos(theta), jnp.sin(theta), row_tw, row_inverse_table),
+    )
+    image = base + lax.ppermute(share, "depth", [(0, 1)])
+    return image[None], leaving
 
 
 def solution(mesh):

time: 98.5 us -> 83.7 us (0.85)
  the two profiles are of different devices: /device:TPU:7 before, /device:TPU:0 now
where the time goes in v2:
time: 83.7 us; the launch traced here: 83.3 us
  waiting for transfers between devices  31.9 us (38%)
  starting transfers between devices  29.6 us (35%)
  other arithmetic  7.92 us (9%)
  Pallas kernels  7.46 us (9%)
  between operations  3.33 us (4%)
  local copies, waits for them, and re-layouts  3.07 us (4%)
    ppermute x2, waiting for transfers between devices, shards(): shares.append(lax.ppermute(share, both, pairs))  18.7 us
    all_to_all x2, starting transfers between devices, exchange(): return lax.all_to_all(x, 'row', split_axis=0, concat_axis=0, tiled=True)  11.1 us
    ppermute x6, waiting for transfers between devices, inner(): got[step] = lax.ppermute(arrays[step], both, pairs)  10.7 us
    ppermute x2, starting transfers between devices, twin(): return lax.ppermute(x, 'row', [(r, r ^ per_plane) for r in range(ranks)])  7.58 us
    pallas_call x5, Pallas kernels, call(): pl.pallas_call(kernel, in_specs=[vmem] * len(args), out_specs=[vmem] * le...  7.46 us
    ppermute x6, starting transfers between devices, inner(): got[step] = lax.ppermute(arrays[step], both, pairs)  5.48 us
    mul x1, other arithmetic, shards(): sign * damping * jnp.sin(vertical)  3.22 us
    mul x1, other arithmetic, shards(): sign * jnp.sin(theta)  2.26 us
  transfers between devices with their start and end apart: 16, of which 8 were waited for; matrix products, arithmetic and copies ran while one was open for 11% of the time, Pallas kernels for 4%

profile of v2, /device:TPU:0, one launch (start us, length us, event | category | flops | bytes accessed | tf_op | source)
XLA Modules:
  0.0 83.3 jit_solution(7120773594651226774)
XLA Ops:
  1.2 2.5 %shard_map.113 = f32[8,2,64,128]{3,2,1,0:T(8,128)} custom-call(f32[2,4,64,512]{3,2,1,0:T(8,128)} %planes_ref.1, f32[4,2,128]{2,1,0:T(2,128)} %constant.79.clone.tw.refs_6_, bf16[2,256,256]{2,1,0:T(8,128)(2,1)} %constant.80.clone.table.inverse.refs_8_.refs_10_), custom_call_target="tpu_custom_call" | custom-call | tf_op jit(solution)/shard_map/pallas_call | solution.py:303
  3.7 7.0 %all-to-all-start = ((f32[8,2,64,128]{3,2,1,0:T(8,128)}), f32[8,2,64,128]{3,2,1,0:T(8,128)S(1)}, u32[]{:S(2)}, u32[]{:S(2)}) async-start(f32[8,2,64,128]{3,2,1,0:T(8,128)} %shard_map.113), calls=%async_computation | async-start | bytes 1048576 | tf_op jit(solution)/shard_map/all_to_all | solution.py:342
  14.5 1.7 %sine_bitcast_fusion = (f32[64,512]{1,0:T(8,128)S(1)}, f32[64,512]{1,0:T(8,128)S(1)}, f32[64,512]{1,0:T(8,128)S(1)}) fusion(f32[]{:T(128)} %bitcast.3, f32[1,64,512]{2,1,0:T(8,128)S(1)} %collective-permute-done, f32[1,64,512]{2,1,0:T(8,128)S(1)} %copy-done.5, pred[]{:T(512)S(6)} %eq.10, f32[]{:T(128)} %bitcast.4), kind=kLoop, calls=%fused_computation.33 | loop fusion | flops 131072 | bytes 655369 | tf_op jit(solution)/shard_map/sin | solution.py:433
  16.3 0.8 collective-permute-start.1
  17.1 3.2 %fusion.11 = (f32[4,128,128]{2,1,0:T(8,128)S(1)}, f32[4,128,128]{2,1,0:T(8,128)S(1)}, f32[4,128,128]{2,1,0:T(8,128)S(1)}, f32[4,128,128]{2,1,0:T(8,128)}) fusion(f32[]{:T(128)S(6)} %integer_pow.25, f32[]{:T(128)S(6)} %mul.114, f32[128]{0:T(128)S(1)} %fusion.34, f32[4,128]{1,0:T(4,128)S(1)} %fusion.31, f32[]{:T(128)S(6)} %integer_pow.22), kind=kLoop, calls=%fused_computation.13 | loop fusion | flops 1245184 | bytes 1051148 | tf_op jit(solution)/shard_map/mul | solution.py:385
  20.3 6.0 %collective-permute-start.5 = (f32[64,512]{1,0:T(8,128)S(1)}, f32[64,512]{1,0:T(8,128)S(1)}, u32[]{:S(2)}, u32[]{:S(2)}) collective-permute-start(f32[64,512]{1,0:T(8,128)S(1)} %collective-permute-done.1), channel_id=1, source_target_pairs={{0,2},{1,3},{2,0},{3,1},{4,6},{5,7},{6,4},{7,5},{8,10},{9,11},{10,... | collective-permute-start | bytes 393224 | tf_op jit(solution)/shard_map/ppermute | solution.py:345
  26.3 0.8 all-to-all-done.in_ref
  27.2 1.1 %shard_map.114 = (f32[2,128,128]{2,1,0:T(8,128)S(1)}, f32[2,128,128]{2,1,0:T(8,128)S(1)}, f32[2,128,128]{2,1,0:T(8,128)S(1)}, f32[2,128,128]{2,1,0:T(8,128)S(1)}) custom-call(f32[8,2,64,128]{3,2,1,0:T(8,128)S(1)} %all-to-all-done.in_ref, f32[4,128,128]{2,1,0:T(8,128)S(1)} %get-tuple-element.25.hre, f32[4,128,128]{2,1,0:T(8,128)S(1)} %get-tuple-element.26.him, ...), custom_call_target="tpu_custom_call" | custom-call | tf_op jit(solution)/shard_map/pallas_call | solution.py:303
  28.4 3.5 %collective-permute-start.3 = (f32[2,128,128]{2,1,0:T(8,128)S(1)}, f32[2,128,128]{2,1,0:T(8,128)S(1)}, u32[]{:S(2)}, u32[]{:S(2)}) collective-permute-start(f32[2,128,128]{2,1,0:T(8,128)S(1)} %get-tuple-element.29), channel_id=1, source_target_pairs={{0,1},{1,0},{2,3},{3,2},{4,5},{5,4},{6,7},{7,6},{8,9},{9,8},{10,11... | collective-permute-start | bytes 393224 | tf_op jit(solution)/shard_map/ppermute | solution.py:338
  31.9 2.3 %sine_multiply_fusion = (f32[128,512]{1,0:T(8,128)S(1)}, f32[128,512]{1,0:T(8,128)S(1)}) fusion(f32[]{:T(128)S(6)} %select_n.78, f32[]{:T(128)} %bitcast.2, f32[64,512]{1,0:T(8,128)S(1)} %collective-permute-done.1, f32[64,512]{1,0:T(8,128)S(1)} %collective-permute-done.5, pred[]{:T(512)S(6)} %eq.11, f32[]{:T(128)} %bitcast.1), kind=kLoop, calls=%fused_computation.31 | loop fusion | flops 393216 | bytes 786445 | tf_op jit(solution)/shard_map/mul | solution.py:404
  34.2 2.0 %collective-permute-done.3.refs_2_ = f32[2,128,128]{2,1,0:T(8,128)S(1)} collective-permute-done((f32[2,128,128]{2,1,0:T(8,128)S(1)}, f32[2,128,128]{2,1,0:T(8,128)S(1)}, u32[]{:S(2)}, u32[]{:S(2)}) %collective-permute-start.3) | collective-permute-done | bytes 131104 | tf_op jit(solution)/shard_map/ppermute | solution.py:338
  36.2 2.3 %collective-permute-done.4.refs_3_ = f32[2,128,128]{2,1,0:T(8,128)S(1)} collective-permute-done((f32[2,128,128]{2,1,0:T(8,128)S(1)}, f32[2,128,128]{2,1,0:T(8,128)S(1)}, u32[]{:S(2)}, u32[]{:S(2)}) %collective-permute-start.4) | collective-permute-done | bytes 131104 | tf_op jit(solution)/shard_map/ppermute | solution.py:338
  38.5 1.6 %shard_map.115 = (f32[2,128,128]{2,1,0:T(8,128)S(1)}, f32[2,128,128]{2,1,0:T(8,128)S(1)}, f32[2,128,128]{2,1,0:T(8,128)S(1)}, f32[2,128,128]{2,1,0:T(8,128)S(1)}...) custom-call(f32[2,128,128]{2,1,0:T(8,128)S(1)} %get-tuple-element.27.refs_0_, ...), custom_call_target="tpu_custom_call" | custom-call | tf_op jit(solution)/shard_map/pallas_call | solution.py:303
  40.1 1.5 %collective-permute-start.9 = (f32[2,64,512]{2,1,0:T(8,128)}, f32[2,64,512]{2,1,0:T(8,128)S(1)}, u32[]{:S(2)}, u32[]{:S(2)}) collective-permute-start(f32[2,64,512]{2,1,0:T(8,128)} %get-tuple-element.37), channel_id=1, source_target_pairs={{0,2},{1,3},{2,0},{3,1},{4,6},{5,7},{6,4},{7,5},{8,10},{9,11},{10,... | collective-permute-start | bytes 786440 | tf_op jit(solution)/shard_map/ppermute | solution.py:345
  41.6 1.5 %collective-permute-start.7 = (f32[2,128,128]{2,1,0:T(8,128)S(1)}, f32[2,128,128]{2,1,0:T(8,128)S(1)}, u32[]{:S(2)}, u32[]{:S(2)}) collective-permute-start(f32[2,128,128]{2,1,0:T(8,128)S(1)} %get-tuple-element.34), channel_id=1, source_target_pairs={{0,1},{1,0},{2,3},{3,2},{4,5},{5,4},{6,7},{7,6},{8,9},{9,8},{10,11... | collective-permute-start | bytes 393224 | tf_op jit(solution)/shard_map/ppermute | solution.py:338
  43.5 4.5 %collective-permute-done.7.refs_2_ = f32[2,128,128]{2,1,0:T(8,128)S(1)} collective-permute-done((f32[2,128,128]{2,1,0:T(8,128)S(1)}, f32[2,128,128]{2,1,0:T(8,128)S(1)}, u32[]{:S(2)}, u32[]{:S(2)}) %collective-permute-start.7) | collective-permute-done | bytes 131104 | tf_op jit(solution)/shard_map/ppermute | solution.py:338
  48.0 1.9 %collective-permute-done.8.refs_3_ = f32[2,128,128]{2,1,0:T(8,128)S(1)} collective-permute-done((f32[2,128,128]{2,1,0:T(8,128)S(1)}, f32[2,128,128]{2,1,0:T(8,128)S(1)}, u32[]{:S(2)}, u32[]{:S(2)}) %collective-permute-start.8) | collective-permute-done | bytes 131104 | tf_op jit(solution)/shard_map/ppermute | solution.py:338
  49.9 0.9 %copy-done.2 = f32[4,128,128]{2,1,0:T(8,128)S(1)} copy-done((f32[4,128,128]{2,1,0:T(8,128)S(1)}, f32[4,128,128]{2,1,0:T(8,128)}, u32[]{:S(2)}) %copy-start.2) | copy-done | bytes 262168
  50.8 1.9 %shard_map.116 = (f32[8,2,64,128]{3,2,1,0:T(8,128)}, f32[64,512]{1,0:T(8,128)S(1)}) custom-call(f32[2,128,128]{2,1,0:T(8,128)S(1)} %get-tuple-element.32.refs_0_, f32[2,128,128]{2,1,0:T(8,128)S(1)} %collective-permute-done.6.refs_1_, f32[2,128,128]{2,1,0:T(8,128)S(1)} %collective-permute-done.7.refs_2_, f32[2,128,128]{2,1,0:T(8,128)S(1)} %collective-permute-done.8.refs_3_, ...), custom_call_target="tpu_custom_call" | custom-call | tf_op jit(solution)/shard_map/pallas_call | solution.py:303
  52.7 4.2 %all-to-all-start.1 = ((f32[8,2,64,128]{3,2,1,0:T(8,128)}), f32[8,2,64,128]{3,2,1,0:T(8,128)S(1)}, u32[]{:S(2)}, u32[]{:S(2)}) async-start(f32[8,2,64,128]{3,2,1,0:T(8,128)} %get-tuple-element.40), calls=%async_computation.1 | async-start | bytes 1048576 | tf_op jit(solution)/shard_map/all_to_all | solution.py:342
  56.8 1.3 %collective-permute-start.11 = (f32[64,512]{1,0:T(8,128)S(1)}, f32[64,512]{1,0:T(8,128)S(1)}, u32[]{:S(2)}, u32[]{:S(2)}) collective-permute-start(f32[64,512]{1,0:T(8,128)S(1)} %get-tuple-element.41), channel_id=1, source_target_pairs={{4,0},{5,4},{6,1},{7,5},{12,2},{13,6},{14,3},{15,7},{20,16},{21,20... | collective-permute-start | bytes 393224 | tf_op jit(solution)/shard_map/ppermute | solution.py:424
  58.8 18.7 %collective-permute-done.11.second_ref = f32[64,512]{1,0:T(8,128)S(1)} collective-permute-done((f32[64,512]{1,0:T(8,128)S(1)}, f32[64,512]{1,0:T(8,128)S(1)}, u32[]{:S(2)}, u32[]{:S(2)}) %collective-permute-start.11) | collective-permute-done | bytes 131104 | tf_op jit(solution)/shard_map/ppermute | solution.py:424
  77.6 1.5 %collective-permute-done.12.got_ref = f32[4,2,64,128]{3,2,1,0:T(8,128)S(1)} collective-permute-done((f32[4,2,64,128]{3,2,1,0:T(8,128)S(1)}, f32[4,2,64,128]{3,2,1,0:T(8,128)S(1)}, u32[]{:S(2)}, u32[]{:S(2)}) %collective-permute-start.12) | collective-permute-done | bytes 262176 | tf_op jit(solution)/shard_map/ppermute | solution.py:427
  79.6 2.0 %collective-permute-start.13 = (f32[64,512]{1,0:T(8,128)S(1)}, f32[64,512]{1,0:T(8,128)S(1)}, u32[]{:S(2)}, u32[]{:S(2)}) collective-permute-start(f32[64,512]{1,0:T(8,128)S(1)} %get-tuple-element.46), channel_id=1, source_target_pairs={{0,8},{1,9},{2,10},{3,11},{4,12},{5,13},{6,14},{7,15},{16,24},{17,... | collective-permute-start | bytes 393224 | tf_op jit(solution)/shard_map/ppermute | solution.py:435
  (41 shorter events, 5.2 us)
Async XLA Ops:
  0.6 13.8 %collective-permute-start = (f32[1,64,512]{2,1,0:T(8,128)}, f32[1,64,512]{2,1,0:T(8,128)S(1)}, u32[]{:S(2)}, u32[]{:S(2)}) collective-permute-start(f32[1,64,512]{2,1,0:T(8,128)} %param.11), channel_id=1, source_target_pairs={{0,8},{8,0},{1,9},{9,1},{2,10},{10,2},{3,11},{11,3},{4,12},{12,4},... | collective-permute-start | bytes 393224 | tf_op jit(solution)/shard_map/ppermute | solution.py:353
  3.7 7.0 %copy-start.7 = (s32[2]{0:T(128)S(1)}, s32[2]{0:T(128)}, u32[]{:S(2)}) copy-start(s32[2]{0:T(128)} %param.13) | copy-start | bytes 28
  3.7 7.0 %copy-start.6 = (f32[2]{0:T(128)S(1)}, f32[2]{0:T(128)}, u32[]{:S(2)}) copy-start(f32[2]{0:T(128)} %param.12) | copy-start | bytes 28
  3.7 23.5 %all-to-all-start = ((f32[8,2,64,128]{3,2,1,0:T(8,128)}), f32[8,2,64,128]{3,2,1,0:T(8,128)S(1)}, u32[]{:S(2)}, u32[]{:S(2)}) async-start(f32[8,2,64,128]{3,2,1,0:T(8,128)} %shard_map.113), calls=%async_computation | async-start | bytes 1048576 | tf_op jit(solution)/shard_map/all_to_all | solution.py:342
  10.6 3.9 %copy-start.5 = (f32[1,64,512]{2,1,0:T(8,128)S(1)}, f32[1,64,512]{2,1,0:T(8,128)}, u32[]{:S(2)}) copy-start(f32[1,64,512]{2,1,0:T(8,128)} %param.11) | copy-start | bytes 393220
  16.2 10.9 %copy-start = (bf16[2,256,256]{2,1,0:T(8,128)(2,1)S(1)}, bf16[2,256,256]{2,1,0:T(8,128)(2,1)}, u32[]{:S(2)}) copy-start(bf16[2,256,256]{2,1,0:T(8,128)(2,1)} %constant.80.clone.table.inverse.refs_8_.refs_10_) | copy-start | bytes 786436
  16.2 10.9 %copy-start.1 = (bf16[2,256,256]{2,1,0:T(8,128)(2,1)S(1)}, bf16[2,256,256]{2,1,0:T(8,128)(2,1)}, u32[]{:S(2)}) copy-start(bf16[2,256,256]{2,1,0:T(8,128)(2,1)} %constant.82.clone.forward.refs_7_.refs_9_.inverse) | copy-start | bytes 786436
  16.3 10.9 %copy-start.3 = (f32[128,8]{1,0:T(8,128)S(1)}, f32[128,8]{1,0:T(8,128)}, u32[]{:S(2)}) copy-start(f32[128,8]{1,0:T(8,128)} %constant.81.clone.tw.refs_8_) | copy-start | bytes 12292
  16.3 4.0 %collective-permute-start.1 = (f32[64,512]{1,0:T(8,128)S(1)}, f32[64,512]{1,0:T(8,128)S(1)}, u32[]{:S(2)}, u32[]{:S(2)}) collective-permute-start(f32[64,512]{1,0:T(8,128)S(1)} %get-tuple-element.49), channel_id=1, source_target_pairs={{0,0},{1,2},{2,8},{3,10},{4,1},{5,3},{6,9},{7,11},{8,4},{9,6},{10,... | collective-permute-start | bytes 393224 | tf_op jit(solution)/shard_map/ppermute | solution.py:371
  20.3 11.6 %collective-permute-start.5 = (f32[64,512]{1,0:T(8,128)S(1)}, f32[64,512]{1,0:T(8,128)S(1)}, u32[]{:S(2)}, u32[]{:S(2)}) collective-permute-start(f32[64,512]{1,0:T(8,128)S(1)} %collective-permute-done.1), channel_id=1, source_target_pairs={{0,2},{1,3},{2,0},{3,1},{4,6},{5,7},{6,4},{7,5},{8,10},{9,11},{10,... | collective-permute-start | bytes 393224 | tf_op jit(solution)/shard_map/ppermute | solution.py:345
  28.3 5.9 %collective-permute-start.2 = (f32[2,128,128]{2,1,0:T(8,128)S(1)}, f32[2,128,128]{2,1,0:T(8,128)S(1)}, u32[]{:S(2)}, u32[]{:S(2)}) collective-permute-start(f32[2,128,128]{2,1,0:T(8,128)S(1)} %get-tuple-element.28), channel_id=1, source_target_pairs={{0,8},{1,9},{2,10},{3,11},{4,12},{5,13},{6,14},{7,15},{8,0},{9,1},... | collective-permute-start | bytes 393224 | tf_op jit(solution)/shard_map/ppermute | solution.py:338
  28.4 7.9 %collective-permute-start.3 = (f32[2,128,128]{2,1,0:T(8,128)S(1)}, f32[2,128,128]{2,1,0:T(8,128)S(1)}, u32[]{:S(2)}, u32[]{:S(2)}) collective-permute-start(f32[2,128,128]{2,1,0:T(8,128)S(1)} %get-tuple-element.29), channel_id=1, source_target_pairs={{0,1},{1,0},{2,3},{3,2},{4,5},{5,4},{6,7},{7,6},{8,9},{9,8},{10,11... | collective-permute-start | bytes 393224 | tf_op jit(solution)/shard_map/ppermute | solution.py:338
  31.9 6.6 %collective-permute-start.4 = (f32[2,128,128]{2,1,0:T(8,128)S(1)}, f32[2,128,128]{2,1,0:T(8,128)S(1)}, u32[]{:S(2)}, u32[]{:S(2)}) collective-permute-start(f32[2,128,128]{2,1,0:T(8,128)S(1)} %get-tuple-element.30), channel_id=1, source_target_pairs={{0,9},{1,8},{2,11},{3,10},{4,13},{5,12},{6,15},{7,14},{8,1},{9,0},... | collective-permute-start | bytes 393224 | tf_op jit(solution)/shard_map/ppermute | solution.py:338
  34.2 4.3 %copy-start.4 = (f32[4,2,128]{2,1,0:T(2,128)S(1)}, f32[4,2,128]{2,1,0:T(2,128)}, u32[]{:S(2)}) copy-start(f32[4,2,128]{2,1,0:T(2,128)} %constant.79.clone.tw.refs_6_) | copy-start | bytes 12292
  40.1 9.8 %collective-permute-start.9 = (f32[2,64,512]{2,1,0:T(8,128)}, f32[2,64,512]{2,1,0:T(8,128)S(1)}, u32[]{:S(2)}, u32[]{:S(2)}) collective-permute-start(f32[2,64,512]{2,1,0:T(8,128)} %get-tuple-element.37), channel_id=1, source_target_pairs={{0,2},{1,3},{2,0},{3,1},{4,6},{5,7},{6,4},{7,5},{8,10},{9,11},{10,... | collective-permute-start | bytes 786440 | tf_op jit(solution)/shard_map/ppermute | solution.py:345
  41.6 1.9 %collective-permute-start.6 = (f32[2,128,128]{2,1,0:T(8,128)S(1)}, f32[2,128,128]{2,1,0:T(8,128)S(1)}, u32[]{:S(2)}, u32[]{:S(2)}) collective-permute-start(f32[2,128,128]{2,1,0:T(8,128)S(1)} %get-tuple-element.33), channel_id=1, source_target_pairs={{0,8},{1,9},{2,10},{3,11},{4,12},{5,13},{6,14},{7,15},{8,0},{9,1},... | collective-permute-start | bytes 393224 | tf_op jit(solution)/shard_map/ppermute | solution.py:338
  41.6 6.4 %collective-permute-start.7 = (f32[2,128,128]{2,1,0:T(8,128)S(1)}, f32[2,128,128]{2,1,0:T(8,128)S(1)}, u32[]{:S(2)}, u32[]{:S(2)}) collective-permute-start(f32[2,128,128]{2,1,0:T(8,128)S(1)} %get-tuple-element.34), channel_id=1, source_target_pairs={{0,1},{1,0},{2,3},{3,2},{4,5},{5,4},{6,7},{7,6},{8,9},{9,8},{10,11... | collective-permute-start | bytes 393224 | tf_op jit(solution)/shard_map/ppermute | solution.py:338
  43.2 6.7 %collective-permute-start.8 = (f32[2,128,128]{2,1,0:T(8,128)S(1)}, f32[2,128,128]{2,1,0:T(8,128)S(1)}, u32[]{:S(2)}, u32[]{:S(2)}) collective-permute-start(f32[2,128,128]{2,1,0:T(8,128)S(1)} %get-tuple-element.35), channel_id=1, source_target_pairs={{0,9},{1,8},{2,11},{3,10},{4,13},{5,12},{6,15},{7,14},{8,1},{9,0},... | collective-permute-start | bytes 393224 | tf_op jit(solution)/shard_map/ppermute | solution.py:338
  49.9 1.0 %copy-start.2 = (f32[4,128,128]{2,1,0:T(8,128)S(1)}, f32[4,128,128]{2,1,0:T(8,128)}, u32[]{:S(2)}) copy-start(f32[4,128,128]{2,1,0:T(8,128)} %get-tuple-element.38.refs_6_) | copy-start | bytes 786436
  52.7 24.8 %all-to-all-start.1 = ((f32[8,2,64,128]{3,2,1,0:T(8,128)}), f32[8,2,64,128]{3,2,1,0:T(8,128)S(1)}, u32[]{:S(2)}, u32[]{:S(2)}) async-start(f32[8,2,64,128]{3,2,1,0:T(8,128)} %get-tuple-element.40), calls=%async_computation.1 | async-start | bytes 1048576 | tf_op jit(solution)/shard_map/all_to_all | solution.py:342
  56.8 20.6 %collective-permute-start.11 = (f32[64,512]{1,0:T(8,128)S(1)}, f32[64,512]{1,0:T(8,128)S(1)}, u32[]{:S(2)}, u32[]{:S(2)}) collective-permute-start(f32[64,512]{1,0:T(8,128)S(1)} %get-tuple-element.41), channel_id=1, source_target_pairs={{4,0},{5,4},{6,1},{7,5},{12,2},{13,6},{14,3},{15,7},{20,16},{21,20... | collective-permute-start | bytes 393224 | tf_op jit(solution)/shard_map/ppermute | solution.py:424
  58.1 19.4 %collective-permute-start.10 = (f32[64,512]{1,0:T(8,128)S(1)}, f32[64,512]{1,0:T(8,128)S(1)}, u32[]{:S(2)}, u32[]{:S(2)}) collective-permute-start(f32[64,512]{1,0:T(8,128)S(1)} %get-tuple-element.41), channel_id=1, source_target_pairs={{0,0},{1,4},{2,1},{3,5},{8,2},{9,6},{10,3},{11,7},{16,16},{17,20},... | collective-permute-start | bytes 393224 | tf_op jit(solution)/shard_map/ppermute | solution.py:424
  77.5 1.6 %collective-permute-start.12 = (f32[4,2,64,128]{3,2,1,0:T(8,128)S(1)}, f32[4,2,64,128]{3,2,1,0:T(8,128)S(1)}, u32[]{:S(2)}, u32[]{:S(2)}) collective-permute-start(f32[4,2,64,128]{3,2,1,0:T(8,128)S(1)} %constant_dynamic-slice_fusion), channel_id=1, source_target_pairs={{0,8},{8,0},{1,9},{9,1},{2,10},{10,2},{3,11},{11,3},{4,12},{12,4},... | collective-permute-start | bytes 786440 | tf_op jit(solution)/shard_map/ppermute | solution.py:427
  79.6 3.0 %collective-permute-start.13 = (f32[64,512]{1,0:T(8,128)S(1)}, f32[64,512]{1,0:T(8,128)S(1)}, u32[]{:S(2)}, u32[]{:S(2)}) collective-permute-start(f32[64,512]{1,0:T(8,128)S(1)} %get-tuple-element.46), channel_id=1, source_target_pairs={{0,8},{1,9},{2,10},{3,11},{4,12},{5,13},{6,14},{7,15},{16,24},{17,... | collective-permute-start | bytes 393224 | tf_op jit(solution)/shard_map/ppermute | solution.py:435

commit v3 on v2

--- a/solution.py
+++ b/solution.py
@@ -7,6 +7,7 @@
 from jax.experimental import pallas as pl
 from jax.experimental.pallas import tpu as pltpu
 from jax.sharding import PartitionSpec as P
+
 
 omega_step = 0.05
 depth_step = 1.0
@@ -99,7 +100,7 @@
     return jnp.concatenate([jnp.concatenate(part, axis=1) for part in parts], axis=0)
 
 
-def row_forward(cells, tw, table, points):
+def row_forward(cells, tw, table):
     stacked = []
     for parts in cells:
         for r, part in enumerate(small_transform(parts, -1.0)):
@@ -183,51 +184,77 @@
         held[own ^ step] = ref[...]
 
 
+def quarter_place(block, ranks):
+    per_plane = ranks // 4
+    step, place = block // per_plane, block % per_plane
+    return step // 2 + 2 * place, step % 2
+
+
+class Blocks:
+    def __init__(self, ref, ranks, rows):
+        self.ref, self.ranks, self.rows = ref, ranks, rows
+
+    def at(self, block, part):
+        return block, part
+
+
+class Quarters(Blocks):
+    def at(self, block, part):
+        quarter, half = quarter_place(block, self.ranks)
+        return quarter, part, slice(half * self.rows, (half + 1) * self.rows)
+
+
 def columns_to_quarters(col_radix, in_ref, hre, him, tw, forward, inverse, *rest):
     out_refs, held = rest[:-1], rest[-1]
-    column_kernel(col_radix, in_ref, hre, him, tw, forward, inverse, held)
+    ranks, rows = in_ref.shape[0], in_ref.shape[2]
+    source, target = Blocks(in_ref, ranks, rows), Quarters(held, ranks, rows)
+    column_kernel(col_radix, source, hre, him, tw, forward, inverse, target)
     spread(held, out_refs)
 
 
 def quarters_to_columns(col_radix, radix, *refs):
+    in_refs, (hre, him, tw, forward, inverse, out_ref, held) = refs[:radix], refs[radix:]
+    ranks, rows = out_ref.shape[0], out_ref.shape[2]
+    collect(in_refs, held)
+    source, target = Quarters(held, ranks, rows), Blocks(out_ref, ranks, rows)
+    column_kernel(col_radix, source, hre, him, tw, forward, inverse, target)
+
+
+def middle_kernel(radix, *refs):
     in_refs, refs = refs[:radix], refs[radix:]
-    keep_ref, got_ref, hre, him, tw, forward, inverse, out_ref, share_ref, held = refs
-    share_ref[...] = keep_ref[0] * got_ref[0] + keep_ref[1] * got_ref[1]
-    collect(in_refs, held)
-    column_kernel(col_radix, held, hre, him, tw, forward, inverse, out_ref)
-
-
-def middle_kernel(radix, *refs):
-    in_refs, (cos_ref, sin_ref, tw, inverse, forward) = refs[:radix], refs[radix : radix + 5]
-    out_refs, (keep_ref, send_ref, held, field) = refs[radix + 5 : 2 * radix + 5], refs[2 * radix + 5 :]
+    (near_cos, near_sin, far_cos, far_sin, tw, inverse, forward), refs = refs[:7], refs[7:]
+    out_refs, (keep_ref, send_ref, held, field, screen) = refs[:radix], refs[radix:]
     rows, points = held.shape[2], held.shape[3]
+    mine = lax.rem(lax.axis_index("row") // (lax.axis_size("row") // 4), 2)
+    for half, pair_refs in ((mine, (near_cos, near_sin)), (1 - mine, (far_cos, far_sin))):
+        for i, ref in enumerate(pair_refs):
+            screen[i, half] = ref[...]
     collect(in_refs, held)
     (cells,) = row_inverse(held, tw, inverse, radix, 1)
     turned = []
     for m in range(radix):
         at = slice(m * points, (m + 1) * points)
-        part = turn(cells[m], (cos_ref[:, at], sin_ref[:, at]), False)
+        factor = [screen[i, :, :, at].reshape(rows, points) for i in range(2)]
+        part = turn(cells[m], factor, False)
         for half in range(2):
             for i in range(2):
                 field[half, i, :, at] = part[i][half * rows // 2 : (half + 1) * rows // 2]
         turned.append(part)
-    mine = lax.rem(lax.axis_index("row") // (lax.axis_size("row") // 4), 2)
     keep_ref[...] = field[mine]
     send_ref[...] = field[1 - mine]
-    value = row_forward([turned], tw, forward, points)
+    value = row_forward([turned], tw, forward)
     store_blocks(held, value, radix, rows, points)
     spread(held, out_refs)
 
 
-def column_kernel(radix, in_ref, hre, him, tw, forward, inverse, out_ref):
-    count, _, rows, width = in_ref.shape
-    points = count * rows // radix
+def column_kernel(radix, source, hre, him, tw, forward, inverse, target):
+    points, width = hre.shape[1], hre.shape[2]
+    rows = source.rows
     per = points // rows
-    out_rows = out_ref.shape[2]
-    out_per = points // out_rows
 
     def block(m, part):
-        return in_ref[m * per : (m + 1) * per, part].reshape(points, width)
+        pieces = [source.ref[source.at(m * per + i, part)] for i in range(per)]
+        return jnp.concatenate(pieces, axis=0)
 
     parts = small_transform([(block(m, 0), block(m, 1)) for m in range(radix)], -1.0)
     columns = []
@@ -252,8 +279,10 @@
             part = turn(part, factor, True)
         parts.append(part)
     for m, (re, im) in enumerate(small_transform(parts, 1.0)):
-        out_ref[m * out_per : (m + 1) * out_per, 0] = re.reshape(out_per, out_rows, width)
-        out_ref[m * out_per : (m + 1) * out_per, 1] = im.reshape(out_per, out_rows, width)
+        for i in range(per):
+            at = slice(i * rows, (i + 1) * rows)
+            target.ref[target.at(m * per + i, 0)] = re[at]
+            target.ref[target.at(m * per + i, 1)] = im[at]
 
 
 def screened(cells, cos_ref, sin_ref, points):
@@ -267,7 +296,7 @@
 
 
 def last_kernel(
-    radix, in_ref, got_ref, first_ref, second_ref, cos_ref, sin_ref, tw, inverse, leaving_ref, image_ref, base_ref, held
+    radix, in_ref, got_ref, cos_ref, sin_ref, tw, inverse, leaving_ref, image_ref, base_ref, held
 ):
     points = in_ref.shape[3]
     core = lax.axis_index("depth")
@@ -286,11 +315,7 @@
         leaving_ref[0, 2, :, at] = rre
         leaving_ref[0, 3, :, at] = rim
         image_ref[:, at] = sre * rre + sim * rim
-    base_ref[...] = image_ref[...]
-
-    @pl.when(core == 0)
-    def _():
-        base_ref[...] = first_ref[...] + second_ref[...]
+    base_ref[...] = jnp.where(core == 0, 0.0, image_ref[...])
 
 
 def signed_wave(positions, length):
@@ -363,12 +388,7 @@
     )
     first_slow = jnp.where(own_first, slowness[0], other[0])
     last_slow = jnp.where(own_first, other[0], slowness[0])
-    pairs = [
-        (flat(f, b), flat((b // 2) % 2, (2 * f + b % 2) * per_plane + b // 4))
-        for f in range(2)
-        for b in range(ranks)
-    ]
-    near = lax.ppermute(first_slow, both, pairs)
+
     col_wave = signed_wave(
         (jnp.arange(lanes, dtype=jnp.int32)[None, :] * col_radix)
         + jnp.arange(col_radix, dtype=jnp.int32)[:, None],
@@ -377,62 +397,83 @@
     row_wave = signed_wave(jnp.arange(points, dtype=jnp.int32) * radix + residue, length)
     plane_waves = col_wave[:, :, None] ** 2 + row_wave[None, None, :] ** 2
     scale = 1.0 / (length * length)
-    propagators = []
-    for level in range(2):
-        radicand = (omega * ref_slowness[level]) ** 2 - plane_waves
+
+    def propagator(slow_ref):
+        radicand = (omega * slow_ref) ** 2 - plane_waves
         vertical = jnp.sqrt(jnp.maximum(radicand, 0.0)) * depth_step
         damping = scale * jnp.exp(-jnp.sqrt(jnp.maximum(-radicand, 0.0)) * depth_step)
-        propagators.append((damping * jnp.cos(vertical), sign * damping * jnp.sin(vertical)))
-
-    near, propagators = lax.optimization_barrier((near, propagators))
+        return damping * jnp.cos(vertical), sign * damping * jnp.sin(vertical)
+
+    def screen(slow, slow_ref, frequency, turned):
+        theta = frequency * (slow - slow_ref) * depth_step
+        return jnp.cos(theta), turned * jnp.sin(theta)
+
+    first_propagator = propagator(ref_slowness[0])
+    columns = exchange(spectra)
+    columns, first_slow = lax.optimization_barrier((columns, first_slow))
+    pairs = []
+    for f in range(2):
+        for b in range(ranks):
+            (quarter_at, half) = quarter_place(b, ranks)
+            pairs.append(
+                (flat(f, b), flat(quarter_at % 2, (2 * f + half) * per_plane + quarter_at // 2))
+            )
+    near = lax.ppermute(first_slow, both, pairs)
     far = twin(near)
-    columns = exchange(spectra)
     quarters = call(
         functools.partial(columns_to_quarters, col_radix),
         [quarter] * radix,
         [(radix,) + quarter],
-        (columns, *propagators[0], col_tw, col_forward_table, col_inverse_table),
+        (columns, *first_propagator, col_tw, col_forward_table, col_inverse_table),
     )
     quarters = inner(quarters)
 
-    slow = jnp.where(plane % 2 == 0, jnp.concatenate([near, far]), jnp.concatenate([far, near]))
-    theta = omega * (slow - ref_slowness[0]) * depth_step
+    screens = screen(near, ref_slowness[0], omega, sign) + screen(far, ref_slowness[0], omega, sign)
     *quarters, keep, send = call(
         functools.partial(middle_kernel, radix),
         [quarter] * radix + [half_field] * 2,
-        [(radix,) + quarter, (2,) + half_field],
-        (*quarters, jnp.cos(theta), sign * jnp.sin(theta), row_tw, row_inverse_table, row_forward_table),
+        [(radix,) + quarter, (2,) + half_field, (2,) + half_field],
+        (*quarters, *screens, row_tw, row_inverse_table, row_forward_table),
     )
     quarters = inner(quarters)
     got = twin(send)
-    columns, share = call(
+    keep, last_ref = lax.optimization_barrier((keep, ref_slowness[1]))
+    (columns,) = call(
         functools.partial(quarters_to_columns, col_radix, radix),
-        [blocks, (rows, length)],
+        [blocks],
         [(radix,) + quarter],
-        (*quarters, keep, got, *propagators[1], col_tw, col_forward_table, col_inverse_table),
-    )
+        (*quarters, *propagator(last_ref), col_tw, col_forward_table, col_inverse_table),
+    )
+    columns, last_slow = lax.optimization_barrier((columns, last_slow))
     cells = exchange(columns)
-
-    shares = []
+    share = keep[0] * got[0] + keep[1] * got[1]
+    last_screen = screen(last_slow, ref_slowness[1], omegas[core], 1.0)
+
+    cells, share = lax.optimization_barrier((cells, share))
+    across = lax.ppermute(
+        lax.dynamic_slice_in_dim(cells, (1 - core) * radix, radix), "depth", swap
+    )
+    image = 0.0
     for f in range(2):
-        pairs = [
-            (flat(c, (2 * f + h) * per_plane + y), flat(0, 2 * (c + 2 * y) + h))
-            for c in range(2)
-            for h in range(2)
-            for y in range(per_plane)
-        ]
-        shares.append(lax.ppermute(share, both, pairs))
-
-    cells, *shares = lax.optimization_barrier((cells, *shares))
-    across = lax.ppermute(lax.dynamic_slice_in_dim(cells, (1 - core) * radix, radix), "depth", swap)
-    theta = omegas[core] * (last_slow - ref_slowness[1]) * depth_step
+        pairs = []
+        for b in range(ranks):
+            (quarter_at, half) = quarter_place(b, ranks)
+            source = flat(quarter_at % 2, (2 * f + half) * per_plane + quarter_at // 2)
+            pairs.append((source, flat(0, b)))
+        image = image + lax.ppermute(share, both, pairs)
     leaving, share, base = call(
         functools.partial(last_kernel, radix),
         [(1,) + planes.shape[1:], (rows, length), (rows, length)],
         [(2 * radix,) + blocks[1:]],
-        (cells, across, *shares, jnp.cos(theta), jnp.sin(theta), row_tw, row_inverse_table),
-    )
-    image = base + lax.ppermute(share, "depth", [(0, 1)])
+        (
+            cells,
+            across,
+            *last_screen,
+            row_tw,
+            row_inverse_table,
+        ),
+    )
+    image = image + base + lax.ppermute(share, "depth", [(0, 1)])
     return image[None], leaving
 
 

time: 83.7 us -> 87.6 us (1.047)
  waiting for transfers between devices: 31.9 us -> 33.6 us
  local copies, waits for them, and re-layouts: 3.07 us -> 4.04 us
    ppermute x3, waiting for transfers between devices: 18.8 us -> 0.16 us  [the longest x1 0.16 us: shards(): image = image + base + lax.ppermute(share, 'depth', [(0, 1)])]
    ppermute x2, waiting for transfers between devices: 0.01 us -> 17.2 us  [twin(): return lax.ppermute(x, 'row', [(r, r ^ per_plane) for r in range(ranks)])]
    all_to_all x2, waiting for transfers between devices: 0.82 us -> 11.2 us  [exchange(): return lax.all_to_all(x, 'row', split_axis=0, concat_axis=0, tiled=True)]
    ppermute x6, waiting for transfers between devices: 10.7 us -> 5.08 us  [inner(): got[step] = lax.ppermute(arrays[step], both, pairs)]
    ppermute x3, starting transfers between devices: 3.99 us -> 8.77 us  [the longest x1 6.81 us: shards(): image = image + base + lax.ppermute(share, 'depth', [(0, 1)])]
    ppermute x2, starting transfers between devices: 7.58 us -> 3.97 us  [twin(): return lax.ppermute(x, 'row', [(r, r ^ per_plane) for r in range(ranks)])]
    ppermute x1, waiting for transfers between devices: 1.52 us -> 0.01 us  [shards(): lax.ppermute(lax.dynamic_slice_in_dim(cells, (1 - core) * radix, radix),...]
    unnamed x17 -> x15, local copies, waits for them, and re-layouts: 1.79 us -> 2.78 us
  transfers between devices with their start and end apart: 16 -> 16, of which waited for: 8 -> 6; matrix products, arithmetic and copies ran while one was open for 11% -> 11% of each run, Pallas kernels for 4% -> 5%
where the time goes in v3:
time: 87.6 us; the launch traced here: 87 us
  waiting for transfers between devices  33.6 us (38%)
  starting transfers between devices  30.3 us (35%)
  other arithmetic  8.49 us (10%)
  Pallas kernels  7.14 us (8%)
  local copies, waits for them, and re-layouts  4.04 us (5%)
  between operations  3.46 us (4%)
    ppermute x2, waiting for transfers between devices, twin(): return lax.ppermute(x, 'row', [(r, r ^ per_plane) for r in range(ranks)])  17.2 us
    all_to_all x2, starting transfers between devices, exchange(): return lax.all_to_all(x, 'row', split_axis=0, concat_axis=0, tiled=True)  11.2 us
    all_to_all x2, waiting for transfers between devices, exchange(): return lax.all_to_all(x, 'row', split_axis=0, concat_axis=0, tiled=True)  11.2 us
    pallas_call x5, Pallas kernels, call(): pl.pallas_call(kernel, in_specs=[vmem] * len(args), out_specs=[vmem] * le...  7.14 us
    ppermute x1, starting transfers between devices, shards(): image = image + base + lax.ppermute(share, 'depth', [(0, 1)])  6.81 us
    ppermute x6, waiting for transfers between devices, inner(): got[step] = lax.ppermute(arrays[step], both, pairs)  5.08 us
    ppermute x6, starting transfers between devices, inner(): got[step] = lax.ppermute(arrays[step], both, pairs)  4.9 us
    ppermute x2, starting transfers between devices, twin(): return lax.ppermute(x, 'row', [(r, r ^ per_plane) for r in range(ranks)])  3.97 us
  transfers between devices with their start and end apart: 16, of which 6 were waited for; matrix products, arithmetic and copies ran while one was open for 11% of the time, Pallas kernels for 5%

profile of v3, /device:TPU:0, one launch (start us, length us, event | category | flops | bytes accessed | tf_op | source)
XLA Modules:
  0.0 87.0 jit_solution(8568059644618401887)
XLA Ops:
  1.2 2.5 %shard_map.113 = f32[8,2,64,128]{3,2,1,0:T(8,128)} custom-call(f32[2,4,64,512]{3,2,1,0:T(8,128)} %planes_ref.1, f32[4,2,128]{2,1,0:T(2,128)} %constant.77.clone.tw.refs_8_, bf16[2,256,256]{2,1,0:T(8,128)(2,1)} %constant.78.clone.table.inverse.refs_10_.refs_8_), custom_call_target="tpu_custom_call" | custom-call | tf_op jit(solution)/shard_map/pallas_call | solution.py:328
  3.7 7.0 %all-to-all-start = ((f32[8,2,64,128]{3,2,1,0:T(8,128)}), f32[8,2,64,128]{3,2,1,0:T(8,128)S(1)}, u32[]{:S(2)}, u32[]{:S(2)}) async-start(f32[8,2,64,128]{3,2,1,0:T(8,128)} %shard_map.113), calls=%async_computation | async-start | bytes 1048576 | tf_op jit(solution)/shard_map/all_to_all | solution.py:367
  14.6 11.2 %all-to-all-done.in_ref = f32[8,2,64,128]{3,2,1,0:T(8,128)S(1)} async-done(((f32[8,2,64,128]{3,2,1,0:T(8,128)}), f32[8,2,64,128]{3,2,1,0:T(8,128)S(1)}, u32[]{:S(2)}, u32[]{:S(2)}) %all-to-all-start) | async-done | bytes 524320 | tf_op jit(solution)/shard_map/all_to_all | solution.py:367
  26.6 1.2 %fusion.22 = (f32[4,128,128]{2,1,0:T(8,128)S(1)}, f32[4,128,128]{2,1,0:T(8,128)S(1)}) fusion(f32[]{:T(128)S(6)} %mul.129, f32[128]{0:T(128)S(1)} %fusion.37, f32[4,128]{1,0:T(4,128)S(1)} %fusion.34, f32[]{:T(128)S(6)} %integer_pow.22), kind=kLoop, calls=%fused_computation.24 | loop fusion | flops 655360 | bytes 526856 | tf_op jit(solution)/shard_map/mul | solution.py:405
  27.8 1.1 %shard_map.114 = (f32[2,128,128]{2,1,0:T(8,128)S(1)}, f32[2,128,128]{2,1,0:T(8,128)S(1)}, f32[2,128,128]{2,1,0:T(8,128)S(1)}, f32[2,128,128]{2,1,0:T(8,128)S(1)}) custom-call(f32[8,2,64,128]{3,2,1,0:T(8,128)S(1)} %all-to-all-done.in_ref, f32[4,128,128]{2,1,0:T(8,128)S(1)} %get-tuple-element.55.hre, f32[4,128,128]{2,1,0:T(8,128)S(1)} %get-tuple-element.54.him, ...), custom_call_target="tpu_custom_call" | custom-call | tf_op jit(solution)/shard_map/pallas_call | solution.py:328
  28.9 1.5 %collective-permute-start.1 = (f32[2,128,128]{2,1,0:T(8,128)S(1)}, f32[2,128,128]{2,1,0:T(8,128)S(1)}, u32[]{:S(2)}, u32[]{:S(2)}) collective-permute-start(f32[2,128,128]{2,1,0:T(8,128)S(1)} %get-tuple-element.25), channel_id=1, source_target_pairs={{0,8},{1,9},{2,10},{3,11},{4,12},{5,13},{6,14},{7,15},{8,0},{9,1},... | collective-permute-start | bytes 393224 | tf_op jit(solution)/shard_map/ppermute | solution.py:363
  30.4 1.0 %collective-permute-start.2 = (f32[2,128,128]{2,1,0:T(8,128)S(1)}, f32[2,128,128]{2,1,0:T(8,128)S(1)}, u32[]{:S(2)}, u32[]{:S(2)}) collective-permute-start(f32[2,128,128]{2,1,0:T(8,128)S(1)} %get-tuple-element.26), channel_id=1, source_target_pairs={{0,1},{1,0},{2,3},{3,2},{4,5},{5,4},{6,7},{7,6},{8,9},{9,8},{10,11... | collective-permute-start | bytes 393224 | tf_op jit(solution)/shard_map/ppermute | solution.py:363
  31.9 1.9 %collective-permute-start.5 = (f32[64,512]{1,0:T(8,128)S(1)}, f32[64,512]{1,0:T(8,128)S(1)}, u32[]{:S(2)}, u32[]{:S(2)}) collective-permute-start(f32[64,512]{1,0:T(8,128)S(1)} %collective-permute-done.4), channel_id=1, source_target_pairs={{0,2},{1,3},{2,0},{3,1},{4,6},{5,7},{6,4},{7,5},{8,10},{9,11},{10,... | collective-permute-start | bytes 393224 | tf_op jit(solution)/shard_map/ppermute | solution.py:370
  33.8 1.8 %sine_multiply_fusion.1 = (f32[64,512]{1,0:T(8,128)S(1)}, f32[64,512]{1,0:T(8,128)S(1)}) fusion(f32[64,512]{1,0:T(8,128)S(1)} %collective-permute-done.4, f32[]{:T(128)S(6)} %select_n.70, f32[]{:T(128)} %bitcast.2, f32[]{:T(128)} %bitcast.1), kind=kLoop, calls=%fused_computation.37 | loop fusion | flops 98304 | bytes 393228 | tf_op jit(solution)/shard_map/mul | solution.py:409
  35.6 2.3 %collective-permute-done.5 = f32[64,512]{1,0:T(8,128)S(1)} collective-permute-done((f32[64,512]{1,0:T(8,128)S(1)}, f32[64,512]{1,0:T(8,128)S(1)}, u32[]{:S(2)}, u32[]{:S(2)}) %collective-permute-start.5) | collective-permute-done | bytes 131104 | tf_op jit(solution)/shard_map/ppermute | solution.py:370
  37.9 1.8 %sine_multiply_fusion = (f32[64,512]{1,0:T(8,128)S(1)}, f32[64,512]{1,0:T(8,128)S(1)}) fusion(f32[64,512]{1,0:T(8,128)S(1)} %collective-permute-done.5, f32[]{:T(128)S(6)} %select_n.70, f32[]{:T(128)} %bitcast.2, f32[]{:T(128)} %bitcast.1), kind=kLoop, calls=%fused_computation.35 | loop fusion | flops 98304 | bytes 393228 | tf_op jit(solution)/shard_map/mul | solution.py:409
  40.5 1.3 %shard_map.115 = (f32[2,128,128]{2,1,0:T(8,128)S(1)}, f32[2,128,128]{2,1,0:T(8,128)S(1)}, f32[2,128,128]{2,1,0:T(8,128)S(1)}, f32[2,128,128]{2,1,0:T(8,128)S(1)}...) custom-call(f32[2,128,128]{2,1,0:T(8,128)S(1)} %get-tuple-element.24.refs_0_, ...), custom_call_target="tpu_custom_call" | custom-call | tf_op jit(solution)/shard_map/pallas_call | solution.py:328
  43.2 1.4 %collective-permute-start.7 = (f32[2,128,128]{2,1,0:T(8,128)S(1)}, f32[2,128,128]{2,1,0:T(8,128)S(1)}, u32[]{:S(2)}, u32[]{:S(2)}) collective-permute-start(f32[2,128,128]{2,1,0:T(8,128)S(1)} %get-tuple-element.31), channel_id=1, source_target_pairs={{0,1},{1,0},{2,3},{3,2},{4,5},{5,4},{6,7},{7,6},{8,9},{9,8},{10,11... | collective-permute-start | bytes 393224 | tf_op jit(solution)/shard_map/ppermute | solution.py:363
  44.9 1.2 %fusion.11 = (f32[4,128,128]{2,1,0:T(8,128)S(1)}, f32[4,128,128]{2,1,0:T(8,128)S(1)}) fusion(f32[]{:T(128)S(6)} %integer_pow.25, f32[]{:T(128)S(6)} %mul.129, f32[128]{0:T(128)S(1)} %fusion.37, f32[4,128]{1,0:T(4,128)S(1)} %fusion.34), kind=kLoop, calls=%fused_computation.13 | loop fusion | flops 655360 | bytes 526856 | tf_op jit(solution)/shard_map/mul | solution.py:405
  46.1 3.4 %collective-permute-done.7.refs_2_ = f32[2,128,128]{2,1,0:T(8,128)S(1)} collective-permute-done((f32[2,128,128]{2,1,0:T(8,128)S(1)}, f32[2,128,128]{2,1,0:T(8,128)S(1)}, u32[]{:S(2)}, u32[]{:S(2)}) %collective-permute-start.7) | collective-permute-done | bytes 131104 | tf_op jit(solution)/shard_map/ppermute | solution.py:363
  49.6 1.6 %collective-permute-done.8.refs_3_ = f32[2,128,128]{2,1,0:T(8,128)S(1)} collective-permute-done((f32[2,128,128]{2,1,0:T(8,128)S(1)}, f32[2,128,128]{2,1,0:T(8,128)S(1)}, u32[]{:S(2)}, u32[]{:S(2)}) %collective-permute-start.8) | collective-permute-done | bytes 131104 | tf_op jit(solution)/shard_map/ppermute | solution.py:363
  51.2 1.8 %shard_map.116 = f32[8,2,64,128]{3,2,1,0:T(8,128)} custom-call(f32[2,128,128]{2,1,0:T(8,128)S(1)} %get-tuple-element.29.refs_0_, f32[2,128,128]{2,1,0:T(8,128)S(1)} %collective-permute-done.6.refs_1_, f32[2,128,128]{2,1,0:T(8,128)S(1)} %collective-permute-done.7.refs_2_, f32[2,128,128]{2,1,0:T(8,128)S(1)} %collective-permute-done.8.refs_3_, ...), custom_call_target="tpu_custom_call" | custom-call | tf_op jit(solution)/shard_map/pallas_call | solution.py:328
  53.0 4.3 %all-to-all-start.1 = ((f32[8,2,64,128]{3,2,1,0:T(8,128)}), f32[8,2,64,128]{3,2,1,0:T(8,128)S(1)}, u32[]{:S(2)}, u32[]{:S(2)}) async-start(f32[8,2,64,128]{3,2,1,0:T(8,128)} %shard_map.116), calls=%async_computation.1 | async-start | bytes 1048576 | tf_op jit(solution)/shard_map/all_to_all | solution.py:367
  57.3 2.0 %collective-permute-start.9 = (f32[2,64,512]{2,1,0:T(8,128)S(1)}, f32[2,64,512]{2,1,0:T(8,128)S(1)}, u32[]{:S(2)}, u32[]{:S(2)}) collective-permute-start(f32[2,64,512]{2,1,0:T(8,128)S(1)} %get-tuple-element.37), channel_id=1, source_target_pairs={{0,2},{1,3},{2,0},{3,1},{4,6},{5,7},{6,4},{7,5},{8,10},{9,11},{10,... | collective-permute-start | bytes 786440 | tf_op jit(solution)/shard_map/ppermute | solution.py:370
  59.3 14.9 %collective-permute-done.9 = f32[2,64,512]{2,1,0:T(8,128)S(1)} collective-permute-done((f32[2,64,512]{2,1,0:T(8,128)S(1)}, f32[2,64,512]{2,1,0:T(8,128)S(1)}, u32[]{:S(2)}, u32[]{:S(2)}) %collective-permute-start.9) | collective-permute-done | bytes 262176 | tf_op jit(solution)/shard_map/ppermute | solution.py:370
  74.4 1.7 %fusion.30 = (f32[64,512]{1,0:T(8,128)S(1)}, f32[64,512]{1,0:T(8,128)S(1)}) fusion(f32[64,512]{1,0:T(8,128)S(1)} %get-tuple-element.40, f32[]{:T(128)} %bitcast.3, f32[]{:T(128)} %bitcast.6), kind=kLoop, calls=%fused_computation.42 | loop fusion | flops 65536 | bytes 393224 | tf_op jit(solution)/shard_map/sin | solution.py:409
  76.1 1.3 %collective-permute-start.11 = (f32[64,512]{1,0:T(8,128)S(1)}, f32[64,512]{1,0:T(8,128)S(1)}, u32[]{:S(2)}, u32[]{:S(2)}) collective-permute-start(f32[64,512]{1,0:T(8,128)S(1)} %fusion.27), channel_id=1, source_target_pairs={{4,0},{5,1},{6,2},{7,3},{12,4},{13,5},{14,6},{15,7},{20,16},{21,17... | collective-permute-start | bytes 393224 | tf_op jit(solution)/shard_map/ppermute | solution.py:463
  78.6 6.8 %collective-permute-start.13 = (f32[64,512]{1,0:T(8,128)S(1)}, f32[64,512]{1,0:T(8,128)S(1)}, u32[]{:S(2)}, u32[]{:S(2)}) collective-permute-start(f32[64,512]{1,0:T(8,128)S(1)} %get-tuple-element.42), channel_id=1, source_target_pairs={{0,8},{1,9},{2,10},{3,11},{4,12},{5,13},{6,14},{7,15},{16,24},{17,... | collective-permute-start | bytes 393224 | tf_op jit(solution)/shard_map/ppermute | solution.py:476
  85.4 0.8 copy.12
  (43 shorter events, 7.8 us)
Async XLA Ops:
  0.6 13.9 %collective-permute-start = (f32[1,64,512]{2,1,0:T(8,128)}, f32[1,64,512]{2,1,0:T(8,128)S(1)}, u32[]{:S(2)}, u32[]{:S(2)}) collective-permute-start(f32[1,64,512]{2,1,0:T(8,128)} %param.11), channel_id=1, source_target_pairs={{0,8},{8,0},{1,9},{9,1},{2,10},{10,2},{3,11},{11,3},{4,12},{12,4},... | collective-permute-start | bytes 393224 | tf_op jit(solution)/shard_map/ppermute | solution.py:378
  3.7 10.9 %copy-start.4 = (f32[1,64,512]{2,1,0:T(8,128)S(1)}, f32[1,64,512]{2,1,0:T(8,128)}, u32[]{:S(2)}) copy-start(f32[1,64,512]{2,1,0:T(8,128)} %param.11) | copy-start | bytes 393220
  3.7 22.1 %all-to-all-start = ((f32[8,2,64,128]{3,2,1,0:T(8,128)}), f32[8,2,64,128]{3,2,1,0:T(8,128)S(1)}, u32[]{:S(2)}, u32[]{:S(2)}) async-start(f32[8,2,64,128]{3,2,1,0:T(8,128)} %shard_map.113), calls=%async_computation | async-start | bytes 1048576 | tf_op jit(solution)/shard_map/all_to_all | solution.py:367
  10.6 0.7 copy-start.6
  11.3 0.7 copy-start.5
  25.8 2.0 %copy-start = (bf16[2,256,256]{2,1,0:T(8,128)(2,1)S(1)}, bf16[2,256,256]{2,1,0:T(8,128)(2,1)}, u32[]{:S(2)}) copy-start(bf16[2,256,256]{2,1,0:T(8,128)(2,1)} %constant.80.clone.forward.refs_9_.refs_7_.inverse) | copy-start | bytes 786436
  25.8 2.0 %copy-start.1 = (bf16[2,256,256]{2,1,0:T(8,128)(2,1)S(1)}, bf16[2,256,256]{2,1,0:T(8,128)(2,1)}, u32[]{:S(2)}) copy-start(bf16[2,256,256]{2,1,0:T(8,128)(2,1)} %constant.78.clone.table.inverse.refs_10_.refs_8_) | copy-start | bytes 786436
  25.8 2.0 %copy-start.2 = (f32[128,8]{1,0:T(8,128)S(1)}, f32[128,8]{1,0:T(8,128)}, u32[]{:S(2)}) copy-start(f32[128,8]{1,0:T(8,128)} %constant.79.clone.tw.refs_6_) | copy-start | bytes 12292
  25.8 6.1 %collective-permute-start.4 = (f32[64,512]{1,0:T(8,128)S(1)}, f32[64,512]{1,0:T(8,128)S(1)}, u32[]{:S(2)}, u32[]{:S(2)}) collective-permute-start(f32[64,512]{1,0:T(8,128)S(1)} %get-tuple-element.28), channel_id=1, source_target_pairs={{0,0},{1,1},{2,2},{3,3},{4,8},{5,9},{6,10},{7,11},{8,4},{9,5},{10,... | collective-permute-start | bytes 393224 | tf_op jit(solution)/shard_map/ppermute | solution.py:421
  28.9 10.9 %collective-permute-start.1 = (f32[2,128,128]{2,1,0:T(8,128)S(1)}, f32[2,128,128]{2,1,0:T(8,128)S(1)}, u32[]{:S(2)}, u32[]{:S(2)}) collective-permute-start(f32[2,128,128]{2,1,0:T(8,128)S(1)} %get-tuple-element.25), channel_id=1, source_target_pairs={{0,8},{1,9},{2,10},{3,11},{4,12},{5,13},{6,14},{7,15},{8,0},{9,1},... | collective-permute-start | bytes 393224 | tf_op jit(solution)/shard_map/ppermute | solution.py:363
  30.4 9.3 %collective-permute-start.2 = (f32[2,128,128]{2,1,0:T(8,128)S(1)}, f32[2,128,128]{2,1,0:T(8,128)S(1)}, u32[]{:S(2)}, u32[]{:S(2)}) collective-permute-start(f32[2,128,128]{2,1,0:T(8,128)S(1)} %get-tuple-element.26), channel_id=1, source_target_pairs={{0,1},{1,0},{2,3},{3,2},{4,5},{5,4},{6,7},{7,6},{8,9},{9,8},{10,11... | collective-permute-start | bytes 393224 | tf_op jit(solution)/shard_map/ppermute | solution.py:363
  31.4 8.4 %collective-permute-start.3 = (f32[2,128,128]{2,1,0:T(8,128)S(1)}, f32[2,128,128]{2,1,0:T(8,128)S(1)}, u32[]{:S(2)}, u32[]{:S(2)}) collective-permute-start(f32[2,128,128]{2,1,0:T(8,128)S(1)} %get-tuple-element.27), channel_id=1, source_target_pairs={{0,9},{1,8},{2,11},{3,10},{4,13},{5,12},{6,15},{7,14},{8,1},{9,0},... | collective-permute-start | bytes 393224 | tf_op jit(solution)/shard_map/ppermute | solution.py:363
  31.9 6.1 %collective-permute-start.5 = (f32[64,512]{1,0:T(8,128)S(1)}, f32[64,512]{1,0:T(8,128)S(1)}, u32[]{:S(2)}, u32[]{:S(2)}) collective-permute-start(f32[64,512]{1,0:T(8,128)S(1)} %collective-permute-done.4), channel_id=1, source_target_pairs={{0,2},{1,3},{2,0},{3,1},{4,6},{5,7},{6,4},{7,5},{8,10},{9,11},{10,... | collective-permute-start | bytes 393224 | tf_op jit(solution)/shard_map/ppermute | solution.py:370
  39.8 0.7 copy-start.3
  43.0 3.1 %collective-permute-start.6 = (f32[2,128,128]{2,1,0:T(8,128)S(1)}, f32[2,128,128]{2,1,0:T(8,128)S(1)}, u32[]{:S(2)}, u32[]{:S(2)}) collective-permute-start(f32[2,128,128]{2,1,0:T(8,128)S(1)} %get-tuple-element.30), channel_id=1, source_target_pairs={{0,8},{1,9},{2,10},{3,11},{4,12},{5,13},{6,14},{7,15},{8,0},{9,1},... | collective-permute-start | bytes 393224 | tf_op jit(solution)/shard_map/ppermute | solution.py:363
  43.2 6.4 %collective-permute-start.7 = (f32[2,128,128]{2,1,0:T(8,128)S(1)}, f32[2,128,128]{2,1,0:T(8,128)S(1)}, u32[]{:S(2)}, u32[]{:S(2)}) collective-permute-start(f32[2,128,128]{2,1,0:T(8,128)S(1)} %get-tuple-element.31), channel_id=1, source_target_pairs={{0,1},{1,0},{2,3},{3,2},{4,5},{5,4},{6,7},{7,6},{8,9},{9,8},{10,11... | collective-permute-start | bytes 393224 | tf_op jit(solution)/shard_map/ppermute | solution.py:363
  44.5 6.6 %collective-permute-start.8 = (f32[2,128,128]{2,1,0:T(8,128)S(1)}, f32[2,128,128]{2,1,0:T(8,128)S(1)}, u32[]{:S(2)}, u32[]{:S(2)}) collective-permute-start(f32[2,128,128]{2,1,0:T(8,128)S(1)} %get-tuple-element.32), channel_id=1, source_target_pairs={{0,9},{1,8},{2,11},{3,10},{4,13},{5,12},{6,15},{7,14},{8,1},{9,0},... | collective-permute-start | bytes 393224 | tf_op jit(solution)/shard_map/ppermute | solution.py:363
  53.0 21.3 %all-to-all-start.1 = ((f32[8,2,64,128]{3,2,1,0:T(8,128)}), f32[8,2,64,128]{3,2,1,0:T(8,128)S(1)}, u32[]{:S(2)}, u32[]{:S(2)}) async-start(f32[8,2,64,128]{3,2,1,0:T(8,128)} %shard_map.116), calls=%async_computation.1 | async-start | bytes 1048576 | tf_op jit(solution)/shard_map/all_to_all | solution.py:367
  57.3 16.9 %collective-permute-start.9 = (f32[2,64,512]{2,1,0:T(8,128)S(1)}, f32[2,64,512]{2,1,0:T(8,128)S(1)}, u32[]{:S(2)}, u32[]{:S(2)}) collective-permute-start(f32[2,64,512]{2,1,0:T(8,128)S(1)} %get-tuple-element.37), channel_id=1, source_target_pairs={{0,2},{1,3},{2,0},{3,1},{4,6},{5,7},{6,4},{7,5},{8,10},{9,11},{10,... | collective-permute-start | bytes 786440 | tf_op jit(solution)/shard_map/ppermute | solution.py:370
  74.3 3.7 %collective-permute-start.12 = (f32[4,2,64,128]{3,2,1,0:T(8,128)S(1)}, f32[4,2,64,128]{3,2,1,0:T(8,128)S(1)}, u32[]{:S(2)}, u32[]{:S(2)}) collective-permute-start(f32[4,2,64,128]{3,2,1,0:T(8,128)S(1)} %constant_dynamic-slice_fusion), channel_id=1, source_target_pairs={{0,8},{8,0},{1,9},{9,1},{2,10},{10,2},{3,11},{11,3},{4,12},{12,4},... | collective-permute-start | bytes 786440 | tf_op jit(solution)/shard_map/ppermute | solution.py:453
  76.1 10.1 %collective-permute-start.11 = (f32[64,512]{1,0:T(8,128)S(1)}, f32[64,512]{1,0:T(8,128)S(1)}, u32[]{:S(2)}, u32[]{:S(2)}) collective-permute-start(f32[64,512]{1,0:T(8,128)S(1)} %fusion.27), channel_id=1, source_target_pairs={{4,0},{5,1},{6,2},{7,3},{12,4},{13,5},{14,6},{15,7},{20,16},{21,17... | collective-permute-start | bytes 393224 | tf_op jit(solution)/shard_map/ppermute | solution.py:463
  77.4 8.8 %collective-permute-start.10 = (f32[64,512]{1,0:T(8,128)S(1)}, f32[64,512]{1,0:T(8,128)S(1)}, u32[]{:S(2)}, u32[]{:S(2)}) collective-permute-start(f32[64,512]{1,0:T(8,128)S(1)} %fusion.27), channel_id=1, source_target_pairs={{0,0},{1,1},{2,2},{3,3},{8,4},{9,5},{10,6},{11,7},{16,16},{17,17},... | collective-permute-start | bytes 393224 | tf_op jit(solution)/shard_map/ppermute | solution.py:463
  78.6 7.8 %collective-permute-start.13 = (f32[64,512]{1,0:T(8,128)S(1)}, f32[64,512]{1,0:T(8,128)S(1)}, u32[]{:S(2)}, u32[]{:S(2)}) collective-permute-start(f32[64,512]{1,0:T(8,128)S(1)} %get-tuple-element.42), channel_id=1, source_target_pairs={{0,8},{1,9},{2,10},{3,11},{4,12},{5,13},{6,14},{7,15},{16,24},{17,... | collective-permute-start | bytes 393224 | tf_op jit(solution)/shard_map/ppermute | solution.py:476

commit v4 on v3

--- a/solution.py
+++ b/solution.py
@@ -12,6 +12,7 @@
 omega_step = 0.05
 depth_step = 1.0
 lanes = 128
+kernel_vmem = 24 << 20
 
 
 def pair(table):
@@ -132,44 +133,21 @@
     out_ref[:, 1] = value[:, points:].reshape(count, rows, points)
 
 
-def half_transform(parts, odd):
-    half = len(parts) // 2
-    folded = []
-    for m in range(half):
-        (are, aim), (bre, bim) = parts[m], parts[m + half]
-        if not odd:
-            folded.append((are + bre, aim + bim))
-            continue
-        re, im = are - bre, aim - bim
-        angle = -2.0 * np.pi * m / len(parts)
-        c, s = float(np.round(np.cos(angle), 15)), float(np.round(np.sin(angle), 15))
-        folded.append((plus(scaled(re, c), scaled(im, -s)), plus(scaled(im, c), scaled(re, s))))
-    return small_transform(folded, -1.0)
-
-
-def first_kernel(radix, planes_ref, tw, table, out_ref):
+def first_kernel(radix, core_ref, planes_ref, tw, table, out_ref):
     count, _, rows, points = out_ref.shape
-    for core in range(2):
-
-        @pl.when(lax.axis_index("depth") == core)
-        def _():
-            stacked = []
-            for p in range(planes_ref.shape[0] * 2):
-                f, c = p // 2, 2 * (p % 2)
-                parts = [
-                    tuple(planes_ref[f, c + i, :, m * points : (m + 1) * points] for i in range(2))
-                    for m in range(radix)
-                ]
-                for y, part in enumerate(half_transform(parts, core == 1)):
-                    r = 2 * y + core
-                    stacked.append(part if r == 0 else turn(part, (tw[r, 0:1], tw[r, 1:2]), False))
-            value = times_table(rows_of(stacked), table)
-            store_blocks(out_ref, value, count, rows, points)
+    parts = [
+        tuple(planes_ref[0, i, :, m * points : (m + 1) * points] for i in range(2)) for m in range(radix)
+    ]
+    value = row_forward([parts], tw, table)
+    store_blocks(out_ref, value, count, rows, points)
 
 
 def residue_of():
-    per_plane = lax.axis_size("row") // 4
-    return lax.axis_index("depth") + 2 * lax.rem(lax.axis_index("row"), per_plane)
+    return lax.rem(lax.axis_index("row"), lax.axis_size("row") // 2)
+
+
+def frequency_of():
+    return lax.axis_index("row") // (lax.axis_size("row") // 2)
 
 
 def spread(held, out_refs):
@@ -185,9 +163,7 @@
 
 
 def quarter_place(block, ranks):
-    per_plane = ranks // 4
-    step, place = block // per_plane, block % per_plane
-    return step // 2 + 2 * place, step % 2
+    return block % (ranks // 2), block // (ranks // 2)
 
 
 class Blocks:
@@ -222,11 +198,11 @@
 
 def middle_kernel(radix, *refs):
     in_refs, refs = refs[:radix], refs[radix:]
-    (near_cos, near_sin, far_cos, far_sin, tw, inverse, forward), refs = refs[:7], refs[7:]
+    (own_cos, own_sin, far_cos, far_sin, tw, inverse, forward), refs = refs[:7], refs[7:]
     out_refs, (keep_ref, send_ref, held, field, screen) = refs[:radix], refs[radix:]
     rows, points = held.shape[2], held.shape[3]
-    mine = lax.rem(lax.axis_index("row") // (lax.axis_size("row") // 4), 2)
-    for half, pair_refs in ((mine, (near_cos, near_sin)), (1 - mine, (far_cos, far_sin))):
+    mine = frequency_of()
+    for half, pair_refs in ((mine, (own_cos, own_sin)), (1 - mine, (far_cos, far_sin))):
         for i, ref in enumerate(pair_refs):
             screen[i, half] = ref[...]
     collect(in_refs, held)
@@ -240,8 +216,9 @@
             for i in range(2):
                 field[half, i, :, at] = part[i][half * rows // 2 : (half + 1) * rows // 2]
         turned.append(part)
-    keep_ref[...] = field[mine]
-    send_ref[...] = field[1 - mine]
+    kept = mine ^ lax.axis_index("depth")
+    keep_ref[...] = field[kept]
+    send_ref[...] = field[1 - kept]
     value = row_forward([turned], tw, forward)
     store_blocks(held, value, radix, rows, points)
     spread(held, out_refs)
@@ -285,37 +262,96 @@
             target.ref[target.at(m * per + i, 1)] = im[at]
 
 
-def screened(cells, cos_ref, sin_ref, points):
-    turned = ([], [])
-    for m in range(len(cells[0])):
-        at = slice(m * points, (m + 1) * points)
-        factor = (cos_ref[:, at], sin_ref[:, at])
-        turned[0].append(turn(cells[0][m], factor, True))
-        turned[1].append(turn(cells[1][m], factor, False))
-    return turned
-
-
-def last_kernel(
-    radix, in_ref, got_ref, cos_ref, sin_ref, tw, inverse, leaving_ref, image_ref, base_ref, held
-):
-    points = in_ref.shape[3]
-    core = lax.axis_index("depth")
-    per_plane = radix // 2
-    for p in range(2):
-        for y in range(per_plane):
-            at = p * radix + 2 * y
-            held[at + core] = in_ref[core * radix + p * per_plane + y]
-            held[at + 1 - core] = got_ref[p * per_plane + y]
-    cells = screened(row_inverse(held, tw, inverse, radix, 2), cos_ref, sin_ref, points)
+def middle_kernel(radix, *refs):
+    in_refs, refs = refs[:radix], refs[radix:]
+    (own_cos, own_sin, far_cos, far_sin, tw, inverse, forward), refs = refs[:7], refs[7:]
+    out_refs, (keep_ref, send_ref, held, field, screen) = refs[:radix], refs[radix:]
+    rows, points = held.shape[2], held.shape[3]
+    mine = frequency_of()
+    for half, pair_refs in ((mine, (own_cos, own_sin)), (1 - mine, (far_cos, far_sin))):
+        for i, ref in enumerate(pair_refs):
+            screen[i, half] = ref[...]
+    collect(in_refs, held)
+    (cells,) = row_inverse(held, tw, inverse, radix, 1)
+    turned = []
     for m in range(radix):
         at = slice(m * points, (m + 1) * points)
-        (sre, sim), (rre, rim) = cells[0][m], cells[1][m]
-        leaving_ref[0, 0, :, at] = sre
-        leaving_ref[0, 1, :, at] = sim
-        leaving_ref[0, 2, :, at] = rre
-        leaving_ref[0, 3, :, at] = rim
-        image_ref[:, at] = sre * rre + sim * rim
-    base_ref[...] = jnp.where(core == 0, 0.0, image_ref[...])
+        factor = [screen[i, :, :, at].reshape(rows, points) for i in range(2)]
+        part = turn(cells[m], factor, False)
+        for half in range(2):
+            for i in range(2):
+                field[half, i, :, at] = part[i][half * rows // 2 : (half + 1) * rows // 2]
+        turned.append(part)
+    kept = mine ^ lax.axis_index("depth")
+    keep_ref[...] = field[kept]
+    send_ref[...] = field[1 - kept]
+    value = row_forward([turned], tw, forward)
+    store_blocks(held, value, radix, rows, points)
+    spread(held, out_refs)
+
+
+def column_kernel(radix, source, hre, him, tw, forward, inverse, target):
+    points, width = hre.shape[1], hre.shape[2]
+    rows = source.rows
+    per = points // rows
+
+    def block(m, part):
+        pieces = [source.ref[source.at(m * per + i, part)] for i in range(per)]
+        return jnp.concatenate(pieces, axis=0)
+
+    parts = small_transform([(block(m, 0), block(m, 1)) for m in range(radix)], -1.0)
+    columns = []
+    for r, part in enumerate(parts):
+        if r > 0:
+            factor = (tw[:, 2 * r : 2 * r + 1], tw[:, 2 * r + 1 : 2 * r + 2])
+            part = turn(part, factor, False)
+        columns.append(jnp.concatenate(part, axis=0))
+    spectrum = table_times(forward, jnp.concatenate(columns, axis=1))
+    columns = []
+    for r in range(radix):
+        at = slice(r * width, (r + 1) * width)
+        part = turn((spectrum[:points, at], spectrum[points:, at]), (hre[r], him[r]), False)
+        columns.append(jnp.concatenate(part, axis=0))
+    back = table_times(inverse, jnp.concatenate(columns, axis=1))
+    parts = []
+    for r in range(radix):
+        at = slice(r * width, (r + 1) * width)
+        part = (back[:points, at], back[points:, at])
+        if r > 0:
+            factor = (tw[:, 2 * r : 2 * r + 1], tw[:, 2 * r + 1 : 2 * r + 2])
+            part = turn(part, factor, True)
+        parts.append(part)
+    for m, (re, im) in enumerate(small_transform(parts, 1.0)):
+        for i in range(per):
+            at = slice(i * rows, (i + 1) * rows)
+            target.ref[target.at(m * per + i, 0)] = re[at]
+            target.ref[target.at(m * per + i, 1)] = im[at]
+
+
+def last_kernel(radix, in_ref, *refs):
+    screens, (tw, inverse, out_ref) = refs[:4], refs[4:]
+    points = in_ref.shape[3]
+    for f, parts in enumerate(row_inverse(in_ref, tw, inverse, radix, 2)):
+        for m, part in enumerate(parts):
+            at = slice(m * points, (m + 1) * points)
+            factor = (screens[2 * f][:, at], screens[2 * f + 1][:, at])
+            re, im = turn(part, factor, False)
+            out_ref[f, 0, :, at] = re
+            out_ref[f, 1, :, at] = im
+
+
+def output_kernel(own_ref, got_ref, share_ref, more_ref, image_ref, leaving_ref):
+    for core, (source, receiver) in enumerate(((own_ref, got_ref), (got_ref, own_ref))):
+
+        @pl.when(lax.axis_index("depth") == core)
+        def _():
+            leaving_ref[0, 0:2] = source[core]
+            leaving_ref[0, 2:4] = receiver[core]
+            if core == 0:
+                image_ref[0] = share_ref[...] + more_ref[...]
+            else:
+                terms = [source[f, i] * receiver[f, i] for f in range(2) for i in range(2)]
+                image_ref[0] = (terms[0] + terms[1]) + (terms[2] + terms[3])
 
 
 def signed_wave(positions, length):
@@ -323,26 +359,26 @@
     return 2.0 * jnp.pi / length * signed.astype(jnp.float32)
 
 
-def call(kernel, out_shapes, scratch, args, held_args=True):
+def call(kernel, out_shapes, scratch, args, held=True):
     vmem = pl.BlockSpec(memory_space=pltpu.VMEM)
+    shape = pltpu.VMEM if held else jax.ShapeDtypeStruct
     return pl.pallas_call(
         kernel,
         in_specs=[vmem] * len(args),
         out_specs=[vmem] * len(out_shapes),
-        out_shape=[pltpu.VMEM(s, jnp.float32) for s in out_shapes],
+        out_shape=[shape(s, jnp.float32) for s in out_shapes],
         scratch_shapes=[pltpu.VMEM(s, jnp.float32) for s in scratch],
-    )(*[pltpu.with_memory_space_constraint(a, pltpu.VMEM) if held_args else a for a in args])
+        compiler_params=pltpu.CompilerParams(vmem_limit_bytes=kernel_vmem),
+    )(*[pltpu.with_memory_space_constraint(a, pltpu.VMEM) for a in args])
 
 
 def shards(planes, slowness, ref_slowness, freq_index):
-    _, _, rows, length = planes.shape
+    freqs, _, rows, length = planes.shape
     ranks = lax.axis_size("row")
     radix = ranks // 2
-    per_plane = radix // 2
     points = length // radix
     col_radix = length // lanes
-    row_index, core = lax.axis_index("row"), lax.axis_index("depth")
-    own_first = core == 0
+    core = lax.axis_index("depth")
 
     row_forward_table, row_inverse_table = real_form(points)
     col_inverse_table, col_forward_table = real_form(lanes)
@@ -355,39 +391,40 @@
         return c * ranks + r
 
     def inner(arrays):
-        got = [arrays[0]] + [None] * (radix - 1)
-        for step in list(range(2, radix)) + [1]:
-            pairs = [
-                (flat(c, r), flat(c ^ (step & 1), r ^ (step >> 1))) for c in range(2) for r in range(ranks)
-            ]
-            got[step] = lax.ppermute(arrays[step], both, pairs)
+        got = [arrays[0]]
+        for step in range(1, radix):
+            got.append(lax.ppermute(arrays[step], "row", [(r, r ^ step) for r in range(ranks)]))
         return got
 
     def exchange(x):
         return lax.all_to_all(x, "row", split_axis=0, concat_axis=0, tiled=True)
 
-    def twin(x):
-        return lax.ppermute(x, "row", [(r, r ^ per_plane) for r in range(ranks)])
-
-    plane = row_index // per_plane
     residue = residue_of()
-    sign = jnp.where(plane % 2 == 0, -1.0, 1.0)
+    sign = jnp.where(core == 0, -1.0, 1.0)
     omegas = omega_step * freq_index.astype(jnp.float32)
-    omega = omegas[plane // 2]
-
+    omega = omegas[frequency_of()]
+    tied_tw = row_tw + 0.0 * omega
+
+    far = lax.ppermute(slowness[0], both, [(flat(0, r), flat(0, r ^ radix)) for r in range(ranks)])
     other = lax.ppermute(slowness, "depth", swap)
     blocks = (ranks, 2, rows, points)
     quarter = (2, 2 * rows, points)
     half_field = (2, rows, length)
-    (spectra,) = call(
+    per_freq = (ranks // freqs,) + blocks[1:]
+    spectra = pl.pallas_call(
         functools.partial(first_kernel, radix),
-        [blocks],
-        [],
-        (planes, row_tw, row_forward_table),
-        held_args=False,
-    )
-    first_slow = jnp.where(own_first, slowness[0], other[0])
-    last_slow = jnp.where(own_first, other[0], slowness[0])
+        grid_spec=pltpu.PrefetchScalarGridSpec(
+            num_scalar_prefetch=1,
+            grid=(freqs,),
+            in_specs=[
+                pl.BlockSpec((1, 2, rows, length), lambda f, c: (f, c[0], 0, 0)),
+                pl.BlockSpec(row_tw.shape, lambda f, c: (0, 0, 0)),
+                pl.BlockSpec(row_forward_table.shape, lambda f, c: (0, 0, 0)),
+            ],
+            out_specs=pl.BlockSpec(per_freq, lambda f, c: (f, 0, 0, 0)),
+        ),
+        out_shape=jax.ShapeDtypeStruct(blocks, jnp.float32),
+    )(core.astype(jnp.int32).reshape(1), planes, row_tw, row_forward_table)
 
     col_wave = signed_wave(
         (jnp.arange(lanes, dtype=jnp.int32)[None, :] * col_radix)
@@ -398,83 +435,68 @@
     plane_waves = col_wave[:, :, None] ** 2 + row_wave[None, None, :] ** 2
     scale = 1.0 / (length * length)
 
-    def propagator(slow_ref):
-        radicand = (omega * slow_ref) ** 2 - plane_waves
+    squares = [(omega * ref_slowness[level]) ** 2 for level in range(2)]
+
+    def propagator(square):
+        radicand = square - plane_waves
         vertical = jnp.sqrt(jnp.maximum(radicand, 0.0)) * depth_step
         damping = scale * jnp.exp(-jnp.sqrt(jnp.maximum(-radicand, 0.0)) * depth_step)
         return damping * jnp.cos(vertical), sign * damping * jnp.sin(vertical)
 
-    def screen(slow, slow_ref, frequency, turned):
+    def screen(slow, slow_ref, frequency):
         theta = frequency * (slow - slow_ref) * depth_step
-        return jnp.cos(theta), turned * jnp.sin(theta)
-
-    first_propagator = propagator(ref_slowness[0])
+        return jnp.cos(theta), sign * jnp.sin(theta)
+
+    propagator_a = propagator(squares[0])
+    sent = lax.ppermute(far, "depth", [(0, 1)])
+    first_slow = jnp.where(core == 0, slowness[0], other[0])
+    screens_a = screen(first_slow, ref_slowness[0], omega)
+    screens_a += screen(jnp.where(core == 0, far, sent), ref_slowness[0], omega)
     columns = exchange(spectra)
-    columns, first_slow = lax.optimization_barrier((columns, first_slow))
-    pairs = []
-    for f in range(2):
-        for b in range(ranks):
-            (quarter_at, half) = quarter_place(b, ranks)
-            pairs.append(
-                (flat(f, b), flat(quarter_at % 2, (2 * f + half) * per_plane + quarter_at // 2))
-            )
-    near = lax.ppermute(first_slow, both, pairs)
-    far = twin(near)
     quarters = call(
         functools.partial(columns_to_quarters, col_radix),
         [quarter] * radix,
         [(radix,) + quarter],
-        (columns, *first_propagator, col_tw, col_forward_table, col_inverse_table),
-    )
+        (columns, *propagator_a, col_tw, col_forward_table, col_inverse_table),
+    )
+    first, square = lax.optimization_barrier((quarters[0], squares[1]))
+    quarters = [first, *quarters[1:]]
     quarters = inner(quarters)
-
-    screens = screen(near, ref_slowness[0], omega, sign) + screen(far, ref_slowness[0], omega, sign)
+    propagator_b = propagator(square)
     *quarters, keep, send = call(
         functools.partial(middle_kernel, radix),
         [quarter] * radix + [half_field] * 2,
         [(radix,) + quarter, (2,) + half_field, (2,) + half_field],
-        (*quarters, *screens, row_tw, row_inverse_table, row_forward_table),
+        (*quarters, *screens_a, tied_tw, row_inverse_table, row_forward_table),
     )
     quarters = inner(quarters)
-    got = twin(send)
-    keep, last_ref = lax.optimization_barrier((keep, ref_slowness[1]))
+    got = lax.ppermute(send, "depth", swap)
+    share = keep[0] * got[0] + keep[1] * got[1]
+    more = lax.ppermute(share, both, [(flat(1, r), flat(0, r ^ radix)) for r in range(ranks)])
     (columns,) = call(
         functools.partial(quarters_to_columns, col_radix, radix),
         [blocks],
         [(radix,) + quarter],
-        (*quarters, *propagator(last_ref), col_tw, col_forward_table, col_inverse_table),
-    )
-    columns, last_slow = lax.optimization_barrier((columns, last_slow))
+        (*quarters, *propagator_b, col_tw, col_forward_table, col_inverse_table),
+    )
     cells = exchange(columns)
-    share = keep[0] * got[0] + keep[1] * got[1]
-    last_screen = screen(last_slow, ref_slowness[1], omegas[core], 1.0)
-
-    cells, share = lax.optimization_barrier((cells, share))
-    across = lax.ppermute(
-        lax.dynamic_slice_in_dim(cells, (1 - core) * radix, radix), "depth", swap
-    )
-    image = 0.0
-    for f in range(2):
-        pairs = []
-        for b in range(ranks):
-            (quarter_at, half) = quarter_place(b, ranks)
-            source = flat(quarter_at % 2, (2 * f + half) * per_plane + quarter_at // 2)
-            pairs.append((source, flat(0, b)))
-        image = image + lax.ppermute(share, both, pairs)
-    leaving, share, base = call(
+    last_slow = jnp.where(core == 0, other[0], slowness[0])
+    screens_b = [x for f in range(2) for x in screen(last_slow, ref_slowness[1], omegas[f])]
+    (fields,) = call(
         functools.partial(last_kernel, radix),
-        [(1,) + planes.shape[1:], (rows, length), (rows, length)],
-        [(2 * radix,) + blocks[1:]],
-        (
-            cells,
-            across,
-            *last_screen,
-            row_tw,
-            row_inverse_table,
-        ),
-    )
-    image = image + base + lax.ppermute(share, "depth", [(0, 1)])
-    return image[None], leaving
+        [(freqs,) + half_field],
+        [],
+        (cells, *screens_b, tied_tw, row_inverse_table),
+    )
+    swapped = lax.ppermute(fields, "depth", swap)
+    image, leaving = call(
+        output_kernel,
+        [(1, rows, length), (1,) + planes.shape[1:]],
+        [],
+        (fields, swapped, share, more),
+        held=False,
+    )
+    return image, leaving
 
 
 def solution(mesh):

time: 87.6 us -> 80.3 us (0.917)
  waiting for transfers between devices: 33.6 us -> 28.4 us
  starting transfers between devices: 30.3 us -> 27.3 us
  local copies, waits for them, and re-layouts: 4.04 us -> 2.64 us
  other arithmetic: 8.49 us -> 9.8 us
    ppermute x13 -> x11, starting transfers between devices: 18.5 us -> 14.5 us  [the longest x6 7.11 us: inner(): lax.ppermute(arrays[step], 'row', [(r, r ^ step) for r in range(ranks)])]
    all_to_all x2, waiting for transfers between devices: 11.2 us -> 8.05 us  [exchange(): return lax.all_to_all(x, 'row', split_axis=0, concat_axis=0, tiled=True)]
    pallas_call x0 -> x1, Pallas kernels: none -> 2.35 us  [shards(): pl.pallas_call(functools.partial(first_kernel, radix), grid_spec=pltpu.Pr...]
    cos x0 -> x1, other arithmetic: none -> 2.22 us  [screen(): return (jnp.cos(theta), sign * jnp.sin(theta))]
    ppermute x13 -> x11, waiting for transfers between devices: 22.5 us -> 20.3 us  [the longest x6 7.85 us: inner(): lax.ppermute(arrays[step], 'row', [(r, r ^ step) for r in range(ranks)])]
    sin x1 -> x0, other arithmetic: 1.67 us -> none  [screen(): return (jnp.cos(theta), turned * jnp.sin(theta))]
    pallas_call x5, Pallas kernels: 7.14 us -> 5.51 us  [call(): pl.pallas_call(kernel, in_specs=[vmem] * len(args), out_specs=[vmem] * le...]
    all_to_all x2, starting transfers between devices: 11.2 us -> 12.7 us  [exchange(): return lax.all_to_all(x, 'row', split_axis=0, concat_axis=0, tiled=True)]
  transfers between devices with their start and end apart: 16 -> 14, of which waited for: 6 -> 9; matrix products, arithmetic and copies ran while one was open for 11% -> 14% of each run, Pallas kernels for 5% -> 2%
where the time goes in v4:
time: 80.3 us; the launch traced here: 79.8 us
  waiting for transfers between devices  28.4 us (35%)
  starting transfers between devices  27.3 us (34%)
  other arithmetic  9.8 us (12%)
  Pallas kernels  7.87 us (10%)
  between operations  3.85 us (5%)
  local copies, waits for them, and re-layouts  2.64 us (3%)
    all_to_all x2, starting transfers between devices, exchange(): return lax.all_to_all(x, 'row', split_axis=0, concat_axis=0, tiled=True)  12.7 us
    all_to_all x2, waiting for transfers between devices, exchange(): return lax.all_to_all(x, 'row', split_axis=0, concat_axis=0, tiled=True)  8.05 us
    ppermute x6, waiting for transfers between devices, inner(): lax.ppermute(arrays[step], 'row', [(r, r ^ step) for r in range(ranks)])  7.85 us
    ppermute x6, starting transfers between devices, inner(): lax.ppermute(arrays[step], 'row', [(r, r ^ step) for r in range(ranks)])  7.11 us
    ppermute x1, waiting for transfers between devices, shards(): lax.ppermute(share, both, [(flat(1, r), flat(0, r ^ radix)) for r in rang...  6.89 us
    ppermute x1, waiting for transfers between devices, shards(): lax.ppermute(slowness[0], both, [(flat(0, r), flat(0, r ^ radix)) for r i...  5.58 us
    pallas_call x5, Pallas kernels, call(): pl.pallas_call(kernel, in_specs=[vmem] * len(args), out_specs=[vmem] * le...  5.51 us
    mul x2, other arithmetic, screen(): return (jnp.cos(theta), sign * jnp.sin(theta))  5.12 us
  transfers between devices with their start and end apart: 14, of which 9 were waited for; matrix products, arithmetic and copies ran while one was open for 14% of the time, Pallas kernels for 2%

profile of v4, /device:TPU:0, one launch (start us, length us, event | category | flops | bytes accessed | tf_op | source)
XLA Modules:
  0.0 79.8 jit_solution(257829906328195762)
XLA Ops:
  0.6 2.4 %shard_map.113 = f32[8,2,64,128]{3,2,1,0:T(8,128)} custom-call(s32[1]{0:T(128)} %bitcast.core_ref, f32[2,4,64,512]{3,2,1,0:T(8,128)} %planes_ref.1, f32[4,2,128]{2,1,0:T(2,128)} %constant.60.clone.tw, bf16[2,256,256]{2,1,0:T(8,128)(2,1)} %constant.61.clone.table.inverse.refs_10_.refs_8_), custom_call_target="tpu_custom_call" | custom-call | tf_op jit(solution)/shard_map/pallas_call | solution.py:414
  3.0 7.4 %all-to-all-start = ((f32[8,2,64,128]{3,2,1,0:T(8,128)}), f32[8,2,64,128]{3,2,1,0:T(8,128)S(1)}, u32[]{:S(2)}, u32[]{:S(2)}) async-start(f32[8,2,64,128]{3,2,1,0:T(8,128)} %shard_map.113), calls=%async_computation | async-start | bytes 1048576 | tf_op jit(solution)/shard_map/all_to_all | solution.py:400
  10.5 4.8 %collective-permute-start.4 = (f32[64,512]{1,0:T(8,128)S(1)}, f32[64,512]{1,0:T(8,128)S(1)}, u32[]{:S(2)}, u32[]{:S(2)}) collective-permute-start(f32[64,512]{1,0:T(8,128)S(1)} %bitcast.31), channel_id=1, source_target_pairs={{0,4},{1,5},{2,6},{3,7},{4,0},{5,1},{6,2},{7,3},{16,20},{17,21},{1... | collective-permute-start | bytes 393224 | tf_op jit(solution)/shard_map/ppermute | solution.py:408
  20.9 1.2 %fusion.22 = (f32[4,128,128]{2,1,0:T(8,128)S(1)}, f32[4,128,128]{2,1,0:T(8,128)S(1)}) fusion(f32[]{:T(128)S(6)} %mul.139, f32[128]{0:T(128)S(1)} %fusion.38, f32[4,128]{1,0:T(4,128)S(1)} %fusion.35, f32[]{:T(128)S(6)} %integer_pow.22), kind=kLoop, calls=%fused_computation.24 | loop fusion | flops 655360 | bytes 526856 | tf_op jit(solution)/shard_map/mul | solution.py:444
  22.2 5.6 %collective-permute-done.4 = f32[64,512]{1,0:T(8,128)S(1)} collective-permute-done((f32[64,512]{1,0:T(8,128)S(1)}, f32[64,512]{1,0:T(8,128)S(1)}, u32[]{:S(2)}, u32[]{:S(2)}) %collective-permute-start.4) | collective-permute-done | bytes 131104 | tf_op jit(solution)/shard_map/ppermute | solution.py:408
  27.7 1.3 %collective-permute-start.5 = (f32[64,512]{1,0:T(8,128)S(1)}, f32[64,512]{1,0:T(8,128)S(1)}, u32[]{:S(2)}, u32[]{:S(2)}) collective-permute-start(f32[64,512]{1,0:T(8,128)S(1)} %collective-permute-done.4), channel_id=1, source_target_pairs={{0,8},{1,9},{2,10},{3,11},{4,12},{5,13},{6,14},{7,15},{16,24},{17,... | collective-permute-start | bytes 393224 | tf_op jit(solution)/shard_map/ppermute | solution.py:451
  29.1 3.5 %sine_multiply_fusion = (f32[64,512]{1,0:T(8,128)S(1)}, f32[64,512]{1,0:T(8,128)S(1)}, f32[64,512]{1,0:T(8,128)S(1)}, f32[64,512]{1,0:T(8,128)S(1)}) fusion(f32[]{:T(128)} %bitcast.7, f32[]{:T(128)S(6)} %select_n.48, f32[]{:T(128)} %bitcast.3, f32[1,64,512]{2,1,0:T(8,128)S(1)} %copy-done.3, f32[1,64,512]{2,1,0:T(8,128)S(1)} %collective-permute-done.3, ...), kind=kLoop, calls=%fused_computation.37 | loop fusion | flops 262144 | bytes 786453 | tf_op jit(solution)/shard_map/mul | solution.py:448
  33.7 1.5 %collective-permute-start = (f32[2,128,128]{2,1,0:T(8,128)S(1)}, f32[2,128,128]{2,1,0:T(8,128)S(1)}, u32[]{:S(2)}, u32[]{:S(2)}) collective-permute-start(f32[2,128,128]{2,1,0:T(8,128)S(1)} %get-tuple-element.16), channel_id=1, source_target_pairs={{0,1},{1,0},{2,3},{3,2},{4,5},{5,4},{6,7},{7,6},{8,9},{9,8},{10,11... | collective-permute-start | bytes 393224 | tf_op jit(solution)/shard_map/ppermute | solution.py:396
  35.2 2.0 %collective-permute-start.2 = (f32[2,128,128]{2,1,0:T(8,128)S(1)}, f32[2,128,128]{2,1,0:T(8,128)S(1)}, u32[]{:S(2)}, u32[]{:S(2)}) collective-permute-start(f32[2,128,128]{2,1,0:T(8,128)S(1)} %get-tuple-element.18), channel_id=1, source_target_pairs={{0,3},{1,2},{2,1},{3,0},{4,7},{5,6},{6,5},{7,4},{8,11},{9,10},{10,... | collective-permute-start | bytes 393224 | tf_op jit(solution)/shard_map/ppermute | solution.py:396
  37.2 1.7 %sine_multiply_fusion.2 = (f32[64,512]{1,0:T(8,128)S(1)}, f32[64,512]{1,0:T(8,128)S(1)}) fusion(f32[]{:T(128)S(6)} %select_n.48, f32[]{:T(128)} %bitcast.2, f32[64,512]{1,0:T(8,128)S(1)} %collective-permute-done.4, f32[64,512]{1,0:T(8,128)S(1)} %collective-permute-done.5, pred[]{:T(512)S(6)} %eq.2, f32[]{:T(128)} %bitcast.1), kind=kLoop, calls=%fused_computation.39 | loop fusion | flops 131072 | bytes 524301 | tf_op jit(solution)/shard_map/mul | solution.py:448
  39.5 2.0 %collective-permute-done.1.refs_2_ = f32[2,128,128]{2,1,0:T(8,128)S(1)} collective-permute-done((f32[2,128,128]{2,1,0:T(8,128)S(1)}, f32[2,128,128]{2,1,0:T(8,128)S(1)}, u32[]{:S(2)}, u32[]{:S(2)}) %collective-permute-start.1) | collective-permute-done | bytes 131104 | tf_op jit(solution)/shard_map/ppermute | solution.py:396
  41.6 2.0 %collective-permute-done.2.refs_3_ = f32[2,128,128]{2,1,0:T(8,128)S(1)} collective-permute-done((f32[2,128,128]{2,1,0:T(8,128)S(1)}, f32[2,128,128]{2,1,0:T(8,128)S(1)}, u32[]{:S(2)}, u32[]{:S(2)}) %collective-permute-start.2) | collective-permute-done | bytes 131104 | tf_op jit(solution)/shard_map/ppermute | solution.py:396
  43.5 1.3 %shard_map.115 = (f32[2,128,128]{2,1,0:T(8,128)S(1)}, f32[2,128,128]{2,1,0:T(8,128)S(1)}, f32[2,128,128]{2,1,0:T(8,128)S(1)}, f32[2,128,128]{2,1,0:T(8,128)S(1)}...) custom-call(f32[2,128,128]{2,1,0:T(8,128)S(1)} %get-tuple-element.15.refs_0_, ...), custom_call_target="tpu_custom_call" | custom-call | tf_op jit(solution)/shard_map/pallas_call | solution.py:365
  44.8 1.7 %collective-permute-start.6 = (f32[2,128,128]{2,1,0:T(8,128)S(1)}, f32[2,128,128]{2,1,0:T(8,128)S(1)}, u32[]{:S(2)}, u32[]{:S(2)}) collective-permute-start(f32[2,128,128]{2,1,0:T(8,128)S(1)} %get-tuple-element.20), channel_id=1, source_target_pairs={{0,1},{1,0},{2,3},{3,2},{4,5},{5,4},{6,7},{7,6},{8,9},{9,8},{10,11... | collective-permute-start | bytes 393224 | tf_op jit(solution)/shard_map/ppermute | solution.py:396
  46.8 1.5 %collective-permute-start.8 = (f32[2,128,128]{2,1,0:T(8,128)S(1)}, f32[2,128,128]{2,1,0:T(8,128)S(1)}, u32[]{:S(2)}, u32[]{:S(2)}) collective-permute-start(f32[2,128,128]{2,1,0:T(8,128)S(1)} %get-tuple-element.22), channel_id=1, source_target_pairs={{0,3},{1,2},{2,1},{3,0},{4,7},{5,6},{6,5},{7,4},{8,11},{9,10},{10,... | collective-permute-start | bytes 393224 | tf_op jit(solution)/shard_map/ppermute | solution.py:396
  48.4 1.2 %fusion.11 = (f32[4,128,128]{2,1,0:T(8,128)S(1)}, f32[4,128,128]{2,1,0:T(8,128)S(1)}) fusion(f32[]{:T(128)S(6)} %integer_pow.25, f32[]{:T(128)S(6)} %mul.139, f32[128]{0:T(128)S(1)} %fusion.38, f32[4,128]{1,0:T(4,128)S(1)} %fusion.35), kind=kLoop, calls=%fused_computation.13 | loop fusion | flops 655360 | bytes 526856 | tf_op jit(solution)/shard_map/mul | solution.py:444
  49.8 1.7 %collective-permute-done.7.refs_2_ = f32[2,128,128]{2,1,0:T(8,128)S(1)} collective-permute-done((f32[2,128,128]{2,1,0:T(8,128)S(1)}, f32[2,128,128]{2,1,0:T(8,128)S(1)}, u32[]{:S(2)}, u32[]{:S(2)}) %collective-permute-start.7) | collective-permute-done | bytes 131104 | tf_op jit(solution)/shard_map/ppermute | solution.py:396
  51.5 1.3 %collective-permute-done.8.refs_3_ = f32[2,128,128]{2,1,0:T(8,128)S(1)} collective-permute-done((f32[2,128,128]{2,1,0:T(8,128)S(1)}, f32[2,128,128]{2,1,0:T(8,128)S(1)}, u32[]{:S(2)}, u32[]{:S(2)}) %collective-permute-start.8) | collective-permute-done | bytes 131104 | tf_op jit(solution)/shard_map/ppermute | solution.py:396
  52.8 1.8 %shard_map.116 = f32[8,2,64,128]{3,2,1,0:T(8,128)} custom-call(f32[2,128,128]{2,1,0:T(8,128)S(1)} %get-tuple-element.19.refs_0_, f32[2,128,128]{2,1,0:T(8,128)S(1)} %collective-permute-done.6.refs_1_, f32[2,128,128]{2,1,0:T(8,128)S(1)} %collective-permute-done.7.refs_2_, f32[2,128,128]{2,1,0:T(8,128)S(1)} %collective-permute-done.8.refs_3_, ...), custom_call_target="tpu_custom_call" | custom-call | tf_op jit(solution)/shard_map/pallas_call | solution.py:365
  54.6 5.3 %all-to-all-start.1 = ((f32[8,2,64,128]{3,2,1,0:T(8,128)}), f32[8,2,64,128]{3,2,1,0:T(8,128)S(1)}, u32[]{:S(2)}, u32[]{:S(2)}) async-start(f32[8,2,64,128]{3,2,1,0:T(8,128)} %shard_map.116), calls=%async_computation.1 | async-start | bytes 1048576 | tf_op jit(solution)/shard_map/all_to_all | solution.py:400
  59.9 2.2 %multiply_cosine_fusion = (f32[64,512]{1,0:T(8,128)S(1)}, f32[64,512]{1,0:T(8,128)S(1)}, f32[64,512]{1,0:T(8,128)S(1)}) fusion(f32[64,512]{1,0:T(8,128)S(1)} %get-tuple-element.27, f32[]{:T(128)} %bitcast.7, f32[]{:T(128)} %bitcast.6, f32[]{:T(128)S(6)} %select_n.48), kind=kLoop, calls=%fused_computation.42 | loop fusion | flops 98304 | bytes 524300 | tf_op jit(solution)/shard_map/cos | solution.py:448
  62.1 8.0 %all-to-all-done.1.in_ref = f32[8,2,64,128]{3,2,1,0:T(8,128)S(1)} async-done(((f32[8,2,64,128]{3,2,1,0:T(8,128)}), f32[8,2,64,128]{3,2,1,0:T(8,128)S(1)}, u32[]{:S(2)}, u32[]{:S(2)}) %all-to-all-start.1) | async-done | bytes 524320 | tf_op jit(solution)/shard_map/all_to_all | solution.py:400
  70.7 1.3 %collective-permute-start.11 = (f32[64,512]{1,0:T(8,128)S(1)}, f32[64,512]{1,0:T(8,128)S(1)}, u32[]{:S(2)}, u32[]{:S(2)}) collective-permute-start(f32[64,512]{1,0:T(8,128)S(1)} %fusion.27.share_ref), channel_id=1, source_target_pairs={{8,4},{9,5},{10,6},{11,7},{12,0},{13,1},{14,2},{15,3},{24,20},{25,... | collective-permute-start | bytes 393224 | tf_op jit(solution)/shard_map/ppermute | solution.py:475
  72.0 6.9 %collective-permute-done.11.more_ref = f32[64,512]{1,0:T(8,128)S(1)} collective-permute-done((f32[64,512]{1,0:T(8,128)S(1)}, f32[64,512]{1,0:T(8,128)S(1)}, u32[]{:S(2)}, u32[]{:S(2)}) %collective-permute-start.11) | collective-permute-done | bytes 131104 | tf_op jit(solution)/shard_map/ppermute | solution.py:475
  (37 shorter events, 6.5 us)
Async XLA Ops:
  3.0 7.4 %copy-start.3 = (f32[1,64,512]{2,1,0:T(8,128)S(1)}, f32[1,64,512]{2,1,0:T(8,128)}, u32[]{:S(2)}) copy-start(f32[1,64,512]{2,1,0:T(8,128)} %param.11) | copy-start | bytes 393220
  3.0 29.6 %all-to-all-start = ((f32[8,2,64,128]{3,2,1,0:T(8,128)}), f32[8,2,64,128]{3,2,1,0:T(8,128)S(1)}, u32[]{:S(2)}, u32[]{:S(2)}) async-start(f32[8,2,64,128]{3,2,1,0:T(8,128)} %shard_map.113), calls=%async_computation | async-start | bytes 1048576 | tf_op jit(solution)/shard_map/all_to_all | solution.py:400
  10.4 18.6 %collective-permute-start.3 = (f32[1,64,512]{2,1,0:T(8,128)S(1)}, f32[1,64,512]{2,1,0:T(8,128)S(1)}, u32[]{:S(2)}, u32[]{:S(2)}) collective-permute-start(f32[1,64,512]{2,1,0:T(8,128)S(1)} %copy-done.3), channel_id=1, source_target_pairs={{0,8},{8,0},{1,9},{9,1},{2,10},{10,2},{3,11},{11,3},{4,12},{12,4},... | collective-permute-start | bytes 393224 | tf_op jit(solution)/shard_map/ppermute | solution.py:409
  10.5 17.2 %collective-permute-start.4 = (f32[64,512]{1,0:T(8,128)S(1)}, f32[64,512]{1,0:T(8,128)S(1)}, u32[]{:S(2)}, u32[]{:S(2)}) collective-permute-start(f32[64,512]{1,0:T(8,128)S(1)} %bitcast.31), channel_id=1, source_target_pairs={{0,4},{1,5},{2,6},{3,7},{4,0},{5,1},{6,2},{7,3},{16,20},{17,21},{1... | collective-permute-start | bytes 393224 | tf_op jit(solution)/shard_map/ppermute | solution.py:408
  15.3 0.7 copy-start.6
  16.0 0.7 copy-start.5
  20.9 1.2 %copy-start.4 = (f32[4,2,128]{2,1,0:T(2,128)S(1)}, f32[4,2,128]{2,1,0:T(2,128)}, u32[]{:S(2)}) copy-start(f32[4,2,128]{2,1,0:T(2,128)} %constant.60.clone.tw) | copy-start | bytes 12292
  27.7 9.5 %collective-permute-start.5 = (f32[64,512]{1,0:T(8,128)S(1)}, f32[64,512]{1,0:T(8,128)S(1)}, u32[]{:S(2)}, u32[]{:S(2)}) collective-permute-start(f32[64,512]{1,0:T(8,128)S(1)} %collective-permute-done.4), channel_id=1, source_target_pairs={{0,8},{1,9},{2,10},{3,11},{4,12},{5,13},{6,14},{7,15},{16,24},{17,... | collective-permute-start | bytes 393224 | tf_op jit(solution)/shard_map/ppermute | solution.py:451
  29.0 3.5 %copy-start = (bf16[2,256,256]{2,1,0:T(8,128)(2,1)S(1)}, bf16[2,256,256]{2,1,0:T(8,128)(2,1)}, u32[]{:S(2)}) copy-start(bf16[2,256,256]{2,1,0:T(8,128)(2,1)} %constant.63.clone.forward.refs_9_.refs_7_.refs_5_) | copy-start | bytes 786436
  29.0 3.5 %copy-start.1 = (bf16[2,256,256]{2,1,0:T(8,128)(2,1)S(1)}, bf16[2,256,256]{2,1,0:T(8,128)(2,1)}, u32[]{:S(2)}) copy-start(bf16[2,256,256]{2,1,0:T(8,128)(2,1)} %constant.61.clone.table.inverse.refs_10_.refs_8_) | copy-start | bytes 786436
  29.1 3.5 %copy-start.2 = (f32[128,8]{1,0:T(8,128)S(1)}, f32[128,8]{1,0:T(8,128)}, u32[]{:S(2)}) copy-start(f32[128,8]{1,0:T(8,128)} %constant.62.clone.tw.refs_6_) | copy-start | bytes 12292
  33.7 5.9 %collective-permute-start = (f32[2,128,128]{2,1,0:T(8,128)S(1)}, f32[2,128,128]{2,1,0:T(8,128)S(1)}, u32[]{:S(2)}, u32[]{:S(2)}) collective-permute-start(f32[2,128,128]{2,1,0:T(8,128)S(1)} %get-tuple-element.16), channel_id=1, source_target_pairs={{0,1},{1,0},{2,3},{3,2},{4,5},{5,4},{6,7},{7,6},{8,9},{9,8},{10,11... | collective-permute-start | bytes 393224 | tf_op jit(solution)/shard_map/ppermute | solution.py:396
  35.2 6.4 %collective-permute-start.1 = (f32[2,128,128]{2,1,0:T(8,128)S(1)}, f32[2,128,128]{2,1,0:T(8,128)S(1)}, u32[]{:S(2)}, u32[]{:S(2)}) collective-permute-start(f32[2,128,128]{2,1,0:T(8,128)S(1)} %get-tuple-element.17), channel_id=1, source_target_pairs={{0,2},{1,3},{2,0},{3,1},{4,6},{5,7},{6,4},{7,5},{8,10},{9,11},{10,... | collective-permute-start | bytes 393224 | tf_op jit(solution)/shard_map/ppermute | solution.py:396
  35.2 8.3 %collective-permute-start.2 = (f32[2,128,128]{2,1,0:T(8,128)S(1)}, f32[2,128,128]{2,1,0:T(8,128)S(1)}, u32[]{:S(2)}, u32[]{:S(2)}) collective-permute-start(f32[2,128,128]{2,1,0:T(8,128)S(1)} %get-tuple-element.18), channel_id=1, source_target_pairs={{0,3},{1,2},{2,1},{3,0},{4,7},{5,6},{6,5},{7,4},{8,11},{9,10},{10,... | collective-permute-start | bytes 393224 | tf_op jit(solution)/shard_map/ppermute | solution.py:396
  44.8 5.0 %collective-permute-start.6 = (f32[2,128,128]{2,1,0:T(8,128)S(1)}, f32[2,128,128]{2,1,0:T(8,128)S(1)}, u32[]{:S(2)}, u32[]{:S(2)}) collective-permute-start(f32[2,128,128]{2,1,0:T(8,128)S(1)} %get-tuple-element.20), channel_id=1, source_target_pairs={{0,1},{1,0},{2,3},{3,2},{4,5},{5,4},{6,7},{7,6},{8,9},{9,8},{10,11... | collective-permute-start | bytes 393224 | tf_op jit(solution)/shard_map/ppermute | solution.py:396
  46.5 5.0 %collective-permute-start.7 = (f32[2,128,128]{2,1,0:T(8,128)S(1)}, f32[2,128,128]{2,1,0:T(8,128)S(1)}, u32[]{:S(2)}, u32[]{:S(2)}) collective-permute-start(f32[2,128,128]{2,1,0:T(8,128)S(1)} %get-tuple-element.21), channel_id=1, source_target_pairs={{0,2},{1,3},{2,0},{3,1},{4,6},{5,7},{6,4},{7,5},{8,10},{9,11},{10,... | collective-permute-start | bytes 393224 | tf_op jit(solution)/shard_map/ppermute | solution.py:396
  46.8 5.9 %collective-permute-start.8 = (f32[2,128,128]{2,1,0:T(8,128)S(1)}, f32[2,128,128]{2,1,0:T(8,128)S(1)}, u32[]{:S(2)}, u32[]{:S(2)}) collective-permute-start(f32[2,128,128]{2,1,0:T(8,128)S(1)} %get-tuple-element.22), channel_id=1, source_target_pairs={{0,3},{1,2},{2,1},{3,0},{4,7},{5,6},{6,5},{7,4},{8,11},{9,10},{10,... | collective-permute-start | bytes 393224 | tf_op jit(solution)/shard_map/ppermute | solution.py:396
  54.6 15.6 %all-to-all-start.1 = ((f32[8,2,64,128]{3,2,1,0:T(8,128)}), f32[8,2,64,128]{3,2,1,0:T(8,128)S(1)}, u32[]{:S(2)}, u32[]{:S(2)}) async-start(f32[8,2,64,128]{3,2,1,0:T(8,128)} %shard_map.116), calls=%async_computation.1 | async-start | bytes 1048576 | tf_op jit(solution)/shard_map/all_to_all | solution.py:400
  59.9 10.8 %collective-permute-start.10 = (f32[2,64,512]{2,1,0:T(8,128)S(1)}, f32[2,64,512]{2,1,0:T(8,128)S(1)}, u32[]{:S(2)}, u32[]{:S(2)}) collective-permute-start(f32[2,64,512]{2,1,0:T(8,128)S(1)} %get-tuple-element.25), channel_id=1, source_target_pairs={{0,8},{8,0},{1,9},{9,1},{2,10},{10,2},{3,11},{11,3},{4,12},{12,4},... | collective-permute-start | bytes 786440 | tf_op jit(solution)/shard_map/ppermute | solution.py:473
  70.6 8.3 %collective-permute-start.9 = (f32[2,2,64,512]{3,2,1,0:T(8,128)S(1)}, f32[2,2,64,512]{3,2,1,0:T(8,128)S(1)}, u32[]{:S(2)}, u32[]{:S(2)}) collective-permute-start(f32[2,2,64,512]{3,2,1,0:T(8,128)S(1)} %shard_map.117.own_ref), channel_id=1, source_target_pairs={{0,8},{8,0},{1,9},{9,1},{2,10},{10,2},{3,11},{11,3},{4,12},{12,4},... | collective-permute-start | bytes 1572872 | tf_op jit(solution)/shard_map/ppermute | solution.py:491
  70.7 8.2 %collective-permute-start.11 = (f32[64,512]{1,0:T(8,128)S(1)}, f32[64,512]{1,0:T(8,128)S(1)}, u32[]{:S(2)}, u32[]{:S(2)}) collective-permute-start(f32[64,512]{1,0:T(8,128)S(1)} %fusion.27.share_ref), channel_id=1, source_target_pairs={{8,4},{9,5},{10,6},{11,7},{12,0},{13,1},{14,2},{15,3},{24,20},{25,... | collective-permute-start | bytes 393224 | tf_op jit(solution)/shard_map/ppermute | solution.py:475

commit v5 on v4

--- a/solution.py
+++ b/solution.py
@@ -359,17 +359,75 @@
     return 2.0 * jnp.pi / length * signed.astype(jnp.float32)
 
 
-def call(kernel, out_shapes, scratch, args, held=True):
+def cos_sin(x):
+    turns = jnp.floor(x * (2.0 / np.pi) + 0.5)
+    rest = ((x - turns * 1.5703125) - turns * 4.837512969970703e-04) - turns * 7.549789948768648e-08
+    square = rest * rest
+    sine = 2.75573192e-06 - 2.50521084e-08 * square
+    sine = -1.98412698e-04 + square * sine
+    sine = 8.33333333e-03 + square * sine
+    sine = -1.66666667e-01 + square * sine
+    sine = rest + rest * square * sine
+    cosine = -2.75573192e-07 + 2.08767570e-09 * square
+    cosine = 2.48015873e-05 + square * cosine
+    cosine = -1.38888889e-03 + square * cosine
+    cosine = 4.16666667e-02 + square * cosine
+    cosine = 1.0 - 0.5 * square + square * square * cosine
+    count = turns.astype(jnp.int32)
+    odd = (count & 1) == 1
+    new_cos, new_sin = jnp.where(odd, sine, cosine), jnp.where(odd, cosine, sine)
+    new_cos = jnp.where(((count + 1) & 2) == 2, -new_cos, new_cos)
+    new_sin = jnp.where((count & 2) == 2, -new_sin, new_sin)
+    return new_cos, new_sin
+
+
+def factor_kernel(radix, freq_ref, ref_ref, slow_ref, other_ref, far_ref, sent_ref, tw_ref, *outs):
+    (tw_out, hre_a, him_a, hre_b, him_b), outs = outs[:5], outs[5:]
+    tw_out[...] = tw_ref[...]
+    col_radix, points, width = hre_a.shape
+    length = col_radix * points
+    core = lax.axis_index("depth")
+    first = core == 0
+    sign = jnp.where(first, -1.0, 1.0)
+    omegas = [omega_step * freq_ref[f].astype(jnp.float32) for f in range(2)]
+    omega = jnp.where(frequency_of() == 0, omegas[0], omegas[1])
+    scale = 1.0 / (length * length)
+    row_at = lax.broadcasted_iota(jnp.int32, (1, width), 1) * radix + residue_of()
+    row_square = signed_wave(row_at, length) ** 2
+    for r in range(col_radix):
+        col_at = lax.broadcasted_iota(jnp.int32, (points, width), 0) * col_radix + r
+        plane_waves = signed_wave(col_at, length) ** 2 + row_square
+        for level, (hre, him) in enumerate(((hre_a, him_a), (hre_b, him_b))):
+            radicand = (omega * ref_ref[level]) ** 2 - plane_waves
+            vertical = jnp.sqrt(jnp.maximum(radicand, 0.0)) * depth_step
+            damping = scale * jnp.exp(-jnp.sqrt(jnp.maximum(-radicand, 0.0)) * depth_step)
+            cosine, sine = cos_sin(vertical)
+            hre[r], him[r] = damping * cosine, sign * damping * sine
+
+    def screen(slow, level, frequency, at):
+        cosine, sine = cos_sin(frequency * (slow - ref_ref[level]) * depth_step)
+        outs[at][...], outs[at + 1][...] = cosine, sign * sine
+
+    own, other = slow_ref[0], other_ref[0]
+    screen(jnp.where(first, own, other), 0, omega, 0)
+    screen(jnp.where(first, far_ref[...], sent_ref[...]), 0, omega, 2)
+    last = jnp.where(first, other, own)
+    for f in range(2):
+        screen(last, 1, omegas[f], 4 + 2 * f)
+
+
+def call(kernel, out_shapes, scratch, args, held=True, scalars=()):
     vmem = pl.BlockSpec(memory_space=pltpu.VMEM)
+    smem = pl.BlockSpec(memory_space=pltpu.SMEM)
     shape = pltpu.VMEM if held else jax.ShapeDtypeStruct
     return pl.pallas_call(
         kernel,
-        in_specs=[vmem] * len(args),
+        in_specs=[smem] * len(scalars) + [vmem] * len(args),
         out_specs=[vmem] * len(out_shapes),
         out_shape=[shape(s, jnp.float32) for s in out_shapes],
         scratch_shapes=[pltpu.VMEM(s, jnp.float32) for s in scratch],
         compiler_params=pltpu.CompilerParams(vmem_limit_bytes=kernel_vmem),
-    )(*[pltpu.with_memory_space_constraint(a, pltpu.VMEM) for a in args])
+    )(*scalars, *[pltpu.with_memory_space_constraint(a, pltpu.VMEM) for a in args])
 
 
 def shards(planes, slowness, ref_slowness, freq_index):
@@ -398,12 +456,6 @@
 
     def exchange(x):
         return lax.all_to_all(x, "row", split_axis=0, concat_axis=0, tiled=True)
-
-    residue = residue_of()
-    sign = jnp.where(core == 0, -1.0, 1.0)
-    omegas = omega_step * freq_index.astype(jnp.float32)
-    omega = omegas[frequency_of()]
-    tied_tw = row_tw + 0.0 * omega
 
     far = lax.ppermute(slowness[0], both, [(flat(0, r), flat(0, r ^ radix)) for r in range(ranks)])
     other = lax.ppermute(slowness, "depth", swap)
@@ -426,32 +478,18 @@
         out_shape=jax.ShapeDtypeStruct(blocks, jnp.float32),
     )(core.astype(jnp.int32).reshape(1), planes, row_tw, row_forward_table)
 
-    col_wave = signed_wave(
-        (jnp.arange(lanes, dtype=jnp.int32)[None, :] * col_radix)
-        + jnp.arange(col_radix, dtype=jnp.int32)[:, None],
-        length,
-    )
-    row_wave = signed_wave(jnp.arange(points, dtype=jnp.int32) * radix + residue, length)
-    plane_waves = col_wave[:, :, None] ** 2 + row_wave[None, None, :] ** 2
-    scale = 1.0 / (length * length)
-
-    squares = [(omega * ref_slowness[level]) ** 2 for level in range(2)]
-
-    def propagator(square):
-        radicand = square - plane_waves
-        vertical = jnp.sqrt(jnp.maximum(radicand, 0.0)) * depth_step
-        damping = scale * jnp.exp(-jnp.sqrt(jnp.maximum(-radicand, 0.0)) * depth_step)
-        return damping * jnp.cos(vertical), sign * damping * jnp.sin(vertical)
-
-    def screen(slow, slow_ref, frequency):
-        theta = frequency * (slow - slow_ref) * depth_step
-        return jnp.cos(theta), sign * jnp.sin(theta)
-
-    propagator_a = propagator(squares[0])
     sent = lax.ppermute(far, "depth", [(0, 1)])
-    first_slow = jnp.where(core == 0, slowness[0], other[0])
-    screens_a = screen(first_slow, ref_slowness[0], omega)
-    screens_a += screen(jnp.where(core == 0, far, sent), ref_slowness[0], omega)
+    plane = (rows, length)
+    factor = (col_radix, lanes, points)
+    held_tw, *factors = call(
+        functools.partial(factor_kernel, radix),
+        [row_tw.shape] + [factor] * 4 + [plane] * 8,
+        [],
+        (slowness, other, far, sent, row_tw),
+        scalars=(freq_index, ref_slowness),
+    )
+    propagator_a, propagator_b = factors[:2], factors[2:4]
+    screens_a, screens_b = factors[4:8], factors[8:12]
     columns = exchange(spectra)
     quarters = call(
         functools.partial(columns_to_quarters, col_radix),
@@ -459,15 +497,12 @@
         [(radix,) + quarter],
         (columns, *propagator_a, col_tw, col_forward_table, col_inverse_table),
     )
-    first, square = lax.optimization_barrier((quarters[0], squares[1]))
-    quarters = [first, *quarters[1:]]
     quarters = inner(quarters)
-    propagator_b = propagator(square)
     *quarters, keep, send = call(
         functools.partial(middle_kernel, radix),
         [quarter] * radix + [half_field] * 2,
         [(radix,) + quarter, (2,) + half_field, (2,) + half_field],
-        (*quarters, *screens_a, tied_tw, row_inverse_table, row_forward_table),
+        (*quarters, *screens_a, held_tw, row_inverse_table, row_forward_table),
     )
     quarters = inner(quarters)
     got = lax.ppermute(send, "depth", swap)
@@ -480,13 +515,11 @@
         (*quarters, *propagator_b, col_tw, col_forward_table, col_inverse_table),
     )
     cells = exchange(columns)
-    last_slow = jnp.where(core == 0, other[0], slowness[0])
-    screens_b = [x for f in range(2) for x in screen(last_slow, ref_slowness[1], omegas[f])]
     (fields,) = call(
         functools.partial(last_kernel, radix),
         [(freqs,) + half_field],
         [],
-        (cells, *screens_b, tied_tw, row_inverse_table),
+        (cells, *screens_b, held_tw, row_inverse_table),
     )
     swapped = lax.ppermute(fields, "depth", swap)
     image, leaving = call(

time: 80.3 us -> 82.3 us (1.025)
  waiting for transfers between devices: 28.4 us -> 44.4 us
  other arithmetic: 9.8 us -> 0.04 us
  between operations: 3.85 us -> 0.81 us
  Pallas kernels: 7.87 us -> 10.7 us
  local copies, waits for them, and re-layouts: 2.64 us -> 0.03 us
  starting transfers between devices: 27.3 us -> 25.9 us
    mul x6 -> x0, other arithmetic: 7.51 us -> none  [the longest x2 5.12 us: screen(): return (jnp.cos(theta), sign * jnp.sin(theta))]
    ppermute x1, waiting for transfers between devices: 5.58 us -> 12.2 us  [shards(): lax.ppermute(slowness[0], both, [(flat(0, r), flat(0, r ^ radix)) for r i...]
    all_to_all x2, waiting for transfers between devices: 8.05 us -> 12.5 us  [exchange(): return lax.all_to_all(x, 'row', split_axis=0, concat_axis=0, tiled=True)]
    ppermute x6, waiting for transfers between devices: 7.85 us -> 11.4 us  [inner(): lax.ppermute(arrays[step], 'row', [(r, r ^ step) for r in range(ranks)])]
    pallas_call x5 -> x6, Pallas kernels: 5.51 us -> 8.36 us  [call(): pl.pallas_call(kernel, in_specs=[smem] * len(scalars) + [vmem] * len(args...]
    cos x1 -> x0, other arithmetic: 2.22 us -> none  [screen(): return (jnp.cos(theta), sign * jnp.sin(theta))]
    all_to_all x2, starting transfers between devices: 12.7 us -> 11.1 us  [exchange(): return lax.all_to_all(x, 'row', split_axis=0, concat_axis=0, tiled=True)]
    slice x2 -> x0, local copies, waits for them, and re-layouts: 1.31 us -> none  [the longest x1 0.66 us: shards(): omegas[f]]
  transfers between devices with their start and end apart: 14 -> 14, of which waited for: 9 -> 10; matrix products, arithmetic and copies ran while one was open for 14% -> 0% of each run, Pallas kernels for 2% -> 4%
where the time goes in v5:
time: 82.3 us; the launch traced here: 81.9 us
  waiting for transfers between devices  44.4 us (54%)
  starting transfers between devices  25.9 us (31%)
  Pallas kernels  10.7 us (13%)
    all_to_all x2, waiting for transfers between devices, exchange(): return lax.all_to_all(x, 'row', split_axis=0, concat_axis=0, tiled=True)  12.5 us
    ppermute x1, waiting for transfers between devices, shards(): lax.ppermute(slowness[0], both, [(flat(0, r), flat(0, r ^ radix)) for r i...  12.2 us
    ppermute x6, waiting for transfers between devices, inner(): lax.ppermute(arrays[step], 'row', [(r, r ^ step) for r in range(ranks)])  11.4 us
    all_to_all x2, starting transfers between devices, exchange(): return lax.all_to_all(x, 'row', split_axis=0, concat_axis=0, tiled=True)  11.1 us
    pallas_call x6, Pallas kernels, call(): pl.pallas_call(kernel, in_specs=[smem] * len(scalars) + [vmem] * len(args...  8.36 us
    ppermute x1, waiting for transfers between devices, shards(): lax.ppermute(share, both, [(flat(1, r), flat(0, r ^ radix)) for r in rang...  7.29 us
    ppermute x6, starting transfers between devices, inner(): lax.ppermute(arrays[step], 'row', [(r, r ^ step) for r in range(ranks)])  7.11 us
    ppermute x1, starting transfers between devices, shards(): lax.ppermute(slowness[0], both, [(flat(0, r), flat(0, r ^ radix)) for r i...  4.94 us
  transfers between devices with their start and end apart: 14, of which 10 were waited for; matrix products, arithmetic and copies ran while one was open for 0% of the time, Pallas kernels for 4%

profile of v5, /device:TPU:0, one launch (start us, length us, event | category | flops | bytes accessed | tf_op | source)
XLA Modules:
  0.0 81.9 jit_solution(8198487312713776991)
XLA Ops:
  0.6 2.4 %shard_map.113 = f32[8,2,64,128]{3,2,1,0:T(8,128)} custom-call(s32[1]{0:T(128)} %bitcast.core_ref, f32[2,4,64,512]{3,2,1,0:T(8,128)} %planes_ref.1, f32[4,2,128]{2,1,0:T(2,128)} %constant.14.clone.tw.tw_ref, bf16[2,256,256]{2,1,0:T(8,128)(2,1)} %constant.15.clone.table.inverse.refs_10_.refs_8_), custom_call_target="tpu_custom_call" | custom-call | tf_op jit(solution)/shard_map/pallas_call | solution.py:466
  3.0 7.5 %all-to-all-start = ((f32[8,2,64,128]{3,2,1,0:T(8,128)}), f32[8,2,64,128]{3,2,1,0:T(8,128)S(1)}, u32[]{:S(2)}, u32[]{:S(2)}) async-start(f32[8,2,64,128]{3,2,1,0:T(8,128)} %shard_map.113), calls=%async_computation | async-start | bytes 1048576 | tf_op jit(solution)/shard_map/all_to_all | solution.py:458
  10.5 4.9 %collective-permute-start.1 = (f32[64,512]{1,0:T(8,128)S(1)}, f32[64,512]{1,0:T(8,128)S(1)}, u32[]{:S(2)}, u32[]{:S(2)}) collective-permute-start(f32[64,512]{1,0:T(8,128)S(1)} %bitcast.4), channel_id=1, source_target_pairs={{0,4},{1,5},{2,6},{3,7},{4,0},{5,1},{6,2},{7,3},{16,20},{17,21},{1... | collective-permute-start | bytes 393224 | tf_op jit(solution)/shard_map/ppermute | solution.py:460
  15.5 12.2 %collective-permute-done.1.far_ref = f32[64,512]{1,0:T(8,128)S(1)} collective-permute-done((f32[64,512]{1,0:T(8,128)S(1)}, f32[64,512]{1,0:T(8,128)S(1)}, u32[]{:S(2)}, u32[]{:S(2)}) %collective-permute-start.1) | collective-permute-done | bytes 131104 | tf_op jit(solution)/shard_map/ppermute | solution.py:460
  27.7 1.3 %collective-permute-start.2 = (f32[64,512]{1,0:T(8,128)S(1)}, f32[64,512]{1,0:T(8,128)S(1)}, u32[]{:S(2)}, u32[]{:S(2)}) collective-permute-start(f32[64,512]{1,0:T(8,128)S(1)} %collective-permute-done.1.far_ref), channel_id=1, source_target_pairs={{0,8},{1,9},{2,10},{3,11},{4,12},{5,13},{6,14},{7,15},{16,24},{17,... | collective-permute-start | bytes 393224 | tf_op jit(solution)/shard_map/ppermute | solution.py:481
  29.0 1.0 %collective-permute-done.2.sent_ref = f32[64,512]{1,0:T(8,128)S(1)} collective-permute-done((f32[64,512]{1,0:T(8,128)S(1)}, f32[64,512]{1,0:T(8,128)S(1)}, u32[]{:S(2)}, u32[]{:S(2)}) %collective-permute-start.2) | collective-permute-done | bytes 131104 | tf_op jit(solution)/shard_map/ppermute | solution.py:481
  30.0 2.8 %shard_map.114 = (f32[4,2,128]{2,1,0:T(2,128)S(1)}, f32[4,128,128]{2,1,0:T(8,128)S(1)}, f32[4,128,128]{2,1,0:T(8,128)S(1)}, f32[4,128,128]{2,1,0:T(8,128)S(1)}, ...) custom-call(s32[2]{0:T(128)S(1)} %copy-done.5, ...), custom_call_target="tpu_custom_call" | custom-call | tf_op jit(solution)/shard_map/pallas_call | solution.py:423
  32.9 1.1 %shard_map.115 = (f32[2,128,128]{2,1,0:T(8,128)S(1)}, f32[2,128,128]{2,1,0:T(8,128)S(1)}, f32[2,128,128]{2,1,0:T(8,128)S(1)}, f32[2,128,128]{2,1,0:T(8,128)S(1)}) custom-call(f32[8,2,64,128]{3,2,1,0:T(8,128)S(1)} %all-to-all-done.in_ref, f32[4,128,128]{2,1,0:T(8,128)S(1)} %get-tuple-element.25.hre, f32[4,128,128]{2,1,0:T(8,128)S(1)} %get-tuple-element.26.him, ...), custom_call_target="tpu_custom_call" | custom-call | tf_op jit(solution)/shard_map/pallas_call | solution.py:423
  34.0 1.5 %collective-permute-start.3 = (f32[2,128,128]{2,1,0:T(8,128)S(1)}, f32[2,128,128]{2,1,0:T(8,128)S(1)}, u32[]{:S(2)}, u32[]{:S(2)}) collective-permute-start(f32[2,128,128]{2,1,0:T(8,128)S(1)} %get-tuple-element.28), channel_id=1, source_target_pairs={{0,1},{1,0},{2,3},{3,2},{4,5},{5,4},{6,7},{7,6},{8,9},{9,8},{10,11... | collective-permute-start | bytes 393224 | tf_op jit(solution)/shard_map/ppermute | solution.py:454
  35.5 2.0 %collective-permute-start.5 = (f32[2,128,128]{2,1,0:T(8,128)S(1)}, f32[2,128,128]{2,1,0:T(8,128)S(1)}, u32[]{:S(2)}, u32[]{:S(2)}) collective-permute-start(f32[2,128,128]{2,1,0:T(8,128)S(1)} %get-tuple-element.30), channel_id=1, source_target_pairs={{0,3},{1,2},{2,1},{3,0},{4,7},{5,6},{6,5},{7,4},{8,11},{9,10},{10,... | collective-permute-start | bytes 393224 | tf_op jit(solution)/shard_map/ppermute | solution.py:454
  37.5 2.3 %collective-permute-done.3.refs_1_ = f32[2,128,128]{2,1,0:T(8,128)S(1)} collective-permute-done((f32[2,128,128]{2,1,0:T(8,128)S(1)}, f32[2,128,128]{2,1,0:T(8,128)S(1)}, u32[]{:S(2)}, u32[]{:S(2)}) %collective-permute-start.3) | collective-permute-done | bytes 131104 | tf_op jit(solution)/shard_map/ppermute | solution.py:454
  39.8 2.1 %collective-permute-done.4.refs_2_ = f32[2,128,128]{2,1,0:T(8,128)S(1)} collective-permute-done((f32[2,128,128]{2,1,0:T(8,128)S(1)}, f32[2,128,128]{2,1,0:T(8,128)S(1)}, u32[]{:S(2)}, u32[]{:S(2)}) %collective-permute-start.4) | collective-permute-done | bytes 131104 | tf_op jit(solution)/shard_map/ppermute | solution.py:454
  41.9 1.9 %collective-permute-done.5.refs_3_ = f32[2,128,128]{2,1,0:T(8,128)S(1)} collective-permute-done((f32[2,128,128]{2,1,0:T(8,128)S(1)}, f32[2,128,128]{2,1,0:T(8,128)S(1)}, u32[]{:S(2)}, u32[]{:S(2)}) %collective-permute-start.5) | collective-permute-done | bytes 131104 | tf_op jit(solution)/shard_map/ppermute | solution.py:454
  43.8 1.3 %shard_map.116 = (f32[2,128,128]{2,1,0:T(8,128)S(1)}, f32[2,128,128]{2,1,0:T(8,128)S(1)}, f32[2,128,128]{2,1,0:T(8,128)S(1)}, f32[2,128,128]{2,1,0:T(8,128)S(1)}...) custom-call(f32[2,128,128]{2,1,0:T(8,128)S(1)} %get-tuple-element.27.refs_0_, ...), custom_call_target="tpu_custom_call" | custom-call | tf_op jit(solution)/shard_map/pallas_call | solution.py:423
  45.1 1.5 %collective-permute-start.6 = (f32[2,128,128]{2,1,0:T(8,128)S(1)}, f32[2,128,128]{2,1,0:T(8,128)S(1)}, u32[]{:S(2)}, u32[]{:S(2)}) collective-permute-start(f32[2,128,128]{2,1,0:T(8,128)S(1)} %get-tuple-element.37), channel_id=1, source_target_pairs={{0,1},{1,0},{2,3},{3,2},{4,5},{5,4},{6,7},{7,6},{8,9},{9,8},{10,11... | collective-permute-start | bytes 393224 | tf_op jit(solution)/shard_map/ppermute | solution.py:454
  46.9 1.7 %collective-permute-start.8 = (f32[2,128,128]{2,1,0:T(8,128)S(1)}, f32[2,128,128]{2,1,0:T(8,128)S(1)}, u32[]{:S(2)}, u32[]{:S(2)}) collective-permute-start(f32[2,128,128]{2,1,0:T(8,128)S(1)} %get-tuple-element.39), channel_id=1, source_target_pairs={{0,3},{1,2},{2,1},{3,0},{4,7},{5,6},{6,5},{7,4},{8,11},{9,10},{10,... | collective-permute-start | bytes 393224 | tf_op jit(solution)/shard_map/ppermute | solution.py:454
  48.6 2.6 %collective-permute-done.6.refs_1_ = f32[2,128,128]{2,1,0:T(8,128)S(1)} collective-permute-done((f32[2,128,128]{2,1,0:T(8,128)S(1)}, f32[2,128,128]{2,1,0:T(8,128)S(1)}, u32[]{:S(2)}, u32[]{:S(2)}) %collective-permute-start.6) | collective-permute-done | bytes 131104 | tf_op jit(solution)/shard_map/ppermute | solution.py:454
  51.3 1.1 %collective-permute-done.7.refs_2_ = f32[2,128,128]{2,1,0:T(8,128)S(1)} collective-permute-done((f32[2,128,128]{2,1,0:T(8,128)S(1)}, f32[2,128,128]{2,1,0:T(8,128)S(1)}, u32[]{:S(2)}, u32[]{:S(2)}) %collective-permute-start.7) | collective-permute-done | bytes 131104 | tf_op jit(solution)/shard_map/ppermute | solution.py:454
  52.4 1.4 %collective-permute-done.8.refs_3_ = f32[2,128,128]{2,1,0:T(8,128)S(1)} collective-permute-done((f32[2,128,128]{2,1,0:T(8,128)S(1)}, f32[2,128,128]{2,1,0:T(8,128)S(1)}, u32[]{:S(2)}, u32[]{:S(2)}) %collective-permute-start.8) | collective-permute-done | bytes 131104 | tf_op jit(solution)/shard_map/ppermute | solution.py:454
  53.8 1.9 %shard_map.117 = f32[8,2,64,128]{3,2,1,0:T(8,128)} custom-call(f32[2,128,128]{2,1,0:T(8,128)S(1)} %get-tuple-element.36.refs_0_, f32[2,128,128]{2,1,0:T(8,128)S(1)} %collective-permute-done.6.refs_1_, f32[2,128,128]{2,1,0:T(8,128)S(1)} %collective-permute-done.7.refs_2_, f32[2,128,128]{2,1,0:T(8,128)S(1)} %collective-permute-done.8.refs_3_, ...), custom_call_target="tpu_custom_call" | custom-call | tf_op jit(solution)/shard_map/pallas_call | solution.py:423
  55.6 3.7 %all-to-all-start.1 = ((f32[8,2,64,128]{3,2,1,0:T(8,128)}), f32[8,2,64,128]{3,2,1,0:T(8,128)S(1)}, u32[]{:S(2)}, u32[]{:S(2)}) async-start(f32[8,2,64,128]{3,2,1,0:T(8,128)} %shard_map.117), calls=%async_computation.1 | async-start | bytes 1048576 | tf_op jit(solution)/shard_map/all_to_all | solution.py:458
  59.3 12.5 %all-to-all-done.1.in_ref = f32[8,2,64,128]{3,2,1,0:T(8,128)S(1)} async-done(((f32[8,2,64,128]{3,2,1,0:T(8,128)}), f32[8,2,64,128]{3,2,1,0:T(8,128)S(1)}, u32[]{:S(2)}, u32[]{:S(2)}) %all-to-all-start.1) | async-done | bytes 524320 | tf_op jit(solution)/shard_map/all_to_all | solution.py:458
  72.4 1.3 %collective-permute-start.11 = (f32[64,512]{1,0:T(8,128)S(1)}, f32[64,512]{1,0:T(8,128)S(1)}, u32[]{:S(2)}, u32[]{:S(2)}) collective-permute-start(f32[64,512]{1,0:T(8,128)S(1)} %fusion.1.share_ref), channel_id=1, source_target_pairs={{8,4},{9,5},{10,6},{11,7},{12,0},{13,1},{14,2},{15,3},{24,20},{25,... | collective-permute-start | bytes 393224 | tf_op jit(solution)/shard_map/ppermute | solution.py:510
  73.7 7.3 %collective-permute-done.11.more_ref = f32[64,512]{1,0:T(8,128)S(1)} collective-permute-done((f32[64,512]{1,0:T(8,128)S(1)}, f32[64,512]{1,0:T(8,128)S(1)}, u32[]{:S(2)}, u32[]{:S(2)}) %collective-permute-start.11) | collective-permute-done | bytes 131104 | tf_op jit(solution)/shard_map/ppermute | solution.py:510
  (26 shorter events, 1.8 us)
Async XLA Ops:
  3.0 7.5 %copy-start.3 = (f32[1,64,512]{2,1,0:T(8,128)S(1)}, f32[1,64,512]{2,1,0:T(8,128)}, u32[]{:S(2)}) copy-start(f32[1,64,512]{2,1,0:T(8,128)} %slow_ref.1) | copy-start | bytes 393220
  3.0 27.0 %copy-start.4 = (f32[4,2,128]{2,1,0:T(2,128)S(1)}, f32[4,2,128]{2,1,0:T(2,128)}, u32[]{:S(2)}) copy-start(f32[4,2,128]{2,1,0:T(2,128)} %constant.14.clone.tw.tw_ref) | copy-start | bytes 12292
  3.0 29.9 %copy-start.2 = (f32[128,8]{1,0:T(8,128)S(1)}, f32[128,8]{1,0:T(8,128)}, u32[]{:S(2)}) copy-start(f32[128,8]{1,0:T(8,128)} %constant.16.clone.tw.refs_6_) | copy-start | bytes 12292
  3.0 29.8 %all-to-all-start = ((f32[8,2,64,128]{3,2,1,0:T(8,128)}), f32[8,2,64,128]{3,2,1,0:T(8,128)S(1)}, u32[]{:S(2)}, u32[]{:S(2)}) async-start(f32[8,2,64,128]{3,2,1,0:T(8,128)} %shard_map.113), calls=%async_computation | async-start | bytes 1048576 | tf_op jit(solution)/shard_map/all_to_all | solution.py:458
  10.5 19.5 %copy-start.5 = (s32[2]{0:T(128)S(1)}, s32[2]{0:T(128)}, u32[]{:S(2)}) copy-start(s32[2]{0:T(128)} %freq_ref.1) | copy-start | bytes 28
  10.5 19.5 %copy-start.6 = (f32[2]{0:T(128)S(1)}, f32[2]{0:T(128)}, u32[]{:S(2)}) copy-start(f32[2]{0:T(128)} %ref_ref.1) | copy-start | bytes 28
  10.5 22.4 %copy-start = (bf16[2,256,256]{2,1,0:T(8,128)(2,1)S(1)}, bf16[2,256,256]{2,1,0:T(8,128)(2,1)}, u32[]{:S(2)}) copy-start(bf16[2,256,256]{2,1,0:T(8,128)(2,1)} %constant.17.clone.forward.refs_9_.refs_7_.refs_5_) | copy-start | bytes 786436
  10.5 22.4 %copy-start.1 = (bf16[2,256,256]{2,1,0:T(8,128)(2,1)S(1)}, bf16[2,256,256]{2,1,0:T(8,128)(2,1)}, u32[]{:S(2)}) copy-start(bf16[2,256,256]{2,1,0:T(8,128)(2,1)} %constant.15.clone.table.inverse.refs_10_.refs_8_) | copy-start | bytes 786436
  10.5 17.2 %collective-permute-start.1 = (f32[64,512]{1,0:T(8,128)S(1)}, f32[64,512]{1,0:T(8,128)S(1)}, u32[]{:S(2)}, u32[]{:S(2)}) collective-permute-start(f32[64,512]{1,0:T(8,128)S(1)} %bitcast.4), channel_id=1, source_target_pairs={{0,4},{1,5},{2,6},{3,7},{4,0},{5,1},{6,2},{7,3},{16,20},{17,21},{1... | collective-permute-start | bytes 393224 | tf_op jit(solution)/shard_map/ppermute | solution.py:460
  15.5 13.6 %collective-permute-start = (f32[1,64,512]{2,1,0:T(8,128)S(1)}, f32[1,64,512]{2,1,0:T(8,128)S(1)}, u32[]{:S(2)}, u32[]{:S(2)}) collective-permute-start(f32[1,64,512]{2,1,0:T(8,128)S(1)} %copy-done.3), channel_id=1, source_target_pairs={{0,8},{8,0},{1,9},{9,1},{2,10},{10,2},{3,11},{11,3},{4,12},{12,4},... | collective-permute-start | bytes 393224 | tf_op jit(solution)/shard_map/ppermute | solution.py:461
  27.7 2.3 %collective-permute-start.2 = (f32[64,512]{1,0:T(8,128)S(1)}, f32[64,512]{1,0:T(8,128)S(1)}, u32[]{:S(2)}, u32[]{:S(2)}) collective-permute-start(f32[64,512]{1,0:T(8,128)S(1)} %collective-permute-done.1.far_ref), channel_id=1, source_target_pairs={{0,8},{1,9},{2,10},{3,11},{4,12},{5,13},{6,14},{7,15},{16,24},{17,... | collective-permute-start | bytes 393224 | tf_op jit(solution)/shard_map/ppermute | solution.py:481
  34.0 5.8 %collective-permute-start.3 = (f32[2,128,128]{2,1,0:T(8,128)S(1)}, f32[2,128,128]{2,1,0:T(8,128)S(1)}, u32[]{:S(2)}, u32[]{:S(2)}) collective-permute-start(f32[2,128,128]{2,1,0:T(8,128)S(1)} %get-tuple-element.28), channel_id=1, source_target_pairs={{0,1},{1,0},{2,3},{3,2},{4,5},{5,4},{6,7},{7,6},{8,9},{9,8},{10,11... | collective-permute-start | bytes 393224 | tf_op jit(solution)/shard_map/ppermute | solution.py:454
  35.5 6.4 %collective-permute-start.4 = (f32[2,128,128]{2,1,0:T(8,128)S(1)}, f32[2,128,128]{2,1,0:T(8,128)S(1)}, u32[]{:S(2)}, u32[]{:S(2)}) collective-permute-start(f32[2,128,128]{2,1,0:T(8,128)S(1)} %get-tuple-element.29), channel_id=1, source_target_pairs={{0,2},{1,3},{2,0},{3,1},{4,6},{5,7},{6,4},{7,5},{8,10},{9,11},{10,... | collective-permute-start | bytes 393224 | tf_op jit(solution)/shard_map/ppermute | solution.py:454
  35.5 8.3 %collective-permute-start.5 = (f32[2,128,128]{2,1,0:T(8,128)S(1)}, f32[2,128,128]{2,1,0:T(8,128)S(1)}, u32[]{:S(2)}, u32[]{:S(2)}) collective-permute-start(f32[2,128,128]{2,1,0:T(8,128)S(1)} %get-tuple-element.30), channel_id=1, source_target_pairs={{0,3},{1,2},{2,1},{3,0},{4,7},{5,6},{6,5},{7,4},{8,11},{9,10},{10,... | collective-permute-start | bytes 393224 | tf_op jit(solution)/shard_map/ppermute | solution.py:454
  45.1 6.2 %collective-permute-start.6 = (f32[2,128,128]{2,1,0:T(8,128)S(1)}, f32[2,128,128]{2,1,0:T(8,128)S(1)}, u32[]{:S(2)}, u32[]{:S(2)}) collective-permute-start(f32[2,128,128]{2,1,0:T(8,128)S(1)} %get-tuple-element.37), channel_id=1, source_target_pairs={{0,1},{1,0},{2,3},{3,2},{4,5},{5,4},{6,7},{7,6},{8,9},{9,8},{10,11... | collective-permute-start | bytes 393224 | tf_op jit(solution)/shard_map/ppermute | solution.py:454
  46.6 5.8 %collective-permute-start.7 = (f32[2,128,128]{2,1,0:T(8,128)S(1)}, f32[2,128,128]{2,1,0:T(8,128)S(1)}, u32[]{:S(2)}, u32[]{:S(2)}) collective-permute-start(f32[2,128,128]{2,1,0:T(8,128)S(1)} %get-tuple-element.38), channel_id=1, source_target_pairs={{0,2},{1,3},{2,0},{3,1},{4,6},{5,7},{6,4},{7,5},{8,10},{9,11},{10,... | collective-permute-start | bytes 393224 | tf_op jit(solution)/shard_map/ppermute | solution.py:454
  46.9 6.9 %collective-permute-start.8 = (f32[2,128,128]{2,1,0:T(8,128)S(1)}, f32[2,128,128]{2,1,0:T(8,128)S(1)}, u32[]{:S(2)}, u32[]{:S(2)}) collective-permute-start(f32[2,128,128]{2,1,0:T(8,128)S(1)} %get-tuple-element.39), channel_id=1, source_target_pairs={{0,3},{1,2},{2,1},{3,0},{4,7},{5,6},{6,5},{7,4},{8,11},{9,10},{10,... | collective-permute-start | bytes 393224 | tf_op jit(solution)/shard_map/ppermute | solution.py:454
  55.6 16.2 %all-to-all-start.1 = ((f32[8,2,64,128]{3,2,1,0:T(8,128)}), f32[8,2,64,128]{3,2,1,0:T(8,128)S(1)}, u32[]{:S(2)}, u32[]{:S(2)}) async-start(f32[8,2,64,128]{3,2,1,0:T(8,128)} %shard_map.117), calls=%async_computation.1 | async-start | bytes 1048576 | tf_op jit(solution)/shard_map/all_to_all | solution.py:458
  59.3 13.0 %collective-permute-start.10 = (f32[2,64,512]{2,1,0:T(8,128)S(1)}, f32[2,64,512]{2,1,0:T(8,128)S(1)}, u32[]{:S(2)}, u32[]{:S(2)}) collective-permute-start(f32[2,64,512]{2,1,0:T(8,128)S(1)} %get-tuple-element.47), channel_id=1, source_target_pairs={{0,8},{8,0},{1,9},{9,1},{2,10},{10,2},{3,11},{11,3},{4,12},{12,4},... | collective-permute-start | bytes 786440 | tf_op jit(solution)/shard_map/ppermute | solution.py:508
  72.3 8.7 %collective-permute-start.9 = (f32[2,2,64,512]{3,2,1,0:T(8,128)S(1)}, f32[2,2,64,512]{3,2,1,0:T(8,128)S(1)}, u32[]{:S(2)}, u32[]{:S(2)}) collective-permute-start(f32[2,2,64,512]{3,2,1,0:T(8,128)S(1)} %shard_map.118.own_ref), channel_id=1, source_target_pairs={{0,8},{8,0},{1,9},{9,1},{2,10},{10,2},{3,11},{11,3},{4,12},{12,4},... | collective-permute-start | bytes 1572872 | tf_op jit(solution)/shard_map/ppermute | solution.py:524
  72.4 8.6 %collective-permute-start.11 = (f32[64,512]{1,0:T(8,128)S(1)}, f32[64,512]{1,0:T(8,128)S(1)}, u32[]{:S(2)}, u32[]{:S(2)}) collective-permute-start(f32[64,512]{1,0:T(8,128)S(1)} %fusion.1.share_ref), channel_id=1, source_target_pairs={{8,4},{9,5},{10,6},{11,7},{12,0},{13,1},{14,2},{15,3},{24,20},{25,... | collective-permute-start | bytes 393224 | tf_op jit(solution)/shard_map/ppermute | solution.py:510

commit v6 on v5

--- a/solution.py
+++ b/solution.py
@@ -133,13 +133,27 @@
     out_ref[:, 1] = value[:, points:].reshape(count, rows, points)
 
 
-def first_kernel(radix, core_ref, planes_ref, tw, table, out_ref):
-    count, _, rows, points = out_ref.shape
-    parts = [
-        tuple(planes_ref[0, i, :, m * points : (m + 1) * points] for i in range(2)) for m in range(radix)
+def first_kernel(radix, planes_ref, tw, table, *rest):
+    out_refs, (loaded, held, sems) = rest[:-3], rest[-3:]
+    freqs, _, rows, length = loaded.shape
+    points = length // radix
+    core = lax.axis_index("depth")
+    copies = [
+        pltpu.make_async_copy(planes_ref.at[f, pl.ds(2 * core, 2)], loaded.at[f], sems.at[f])
+        for f in range(freqs)
     ]
-    value = row_forward([parts], tw, table)
-    store_blocks(out_ref, value, count, rows, points)
+    for copy in copies:
+        copy.start()
+    for f, copy in enumerate(copies):
+        copy.wait()
+        parts = [
+            tuple(loaded[f, i, :, m * points : (m + 1) * points] for i in range(2)) for m in range(radix)
+        ]
+        value = row_forward([parts], tw, table)
+        at = slice(f * radix, (f + 1) * radix)
+        held[at, 0] = value[:, :points].reshape(radix, rows, points)
+        held[at, 1] = value[:, points:].reshape(radix, rows, points)
+    spread(held, out_refs, lax.axis_index("row"))
 
 
 def residue_of():
@@ -150,14 +164,12 @@
     return lax.axis_index("row") // (lax.axis_size("row") // 2)
 
 
-def spread(held, out_refs):
-    own = residue_of()
+def spread(held, out_refs, own):
     for step, ref in enumerate(out_refs):
         ref[...] = held[own ^ step]
 
 
-def collect(in_refs, held):
-    own = residue_of()
+def collect(in_refs, held, own):
     for step, ref in enumerate(in_refs):
         held[own ^ step] = ref[...]
 
@@ -180,48 +192,24 @@
         return quarter, part, slice(half * self.rows, (half + 1) * self.rows)
 
 
-def columns_to_quarters(col_radix, in_ref, hre, him, tw, forward, inverse, *rest):
-    out_refs, held = rest[:-1], rest[-1]
-    ranks, rows = in_ref.shape[0], in_ref.shape[2]
-    source, target = Blocks(in_ref, ranks, rows), Quarters(held, ranks, rows)
+def columns_to_quarters(col_radix, ranks, *refs):
+    in_refs, (hre, him, tw, forward, inverse), rest = refs[:ranks], refs[ranks : ranks + 5], refs[ranks + 5 :]
+    out_refs, (blocks, quarters) = rest[:-2], rest[-2:]
+    rows = blocks.shape[2]
+    collect(in_refs, blocks, lax.axis_index("row"))
+    source, target = Blocks(blocks, ranks, rows), Quarters(quarters, ranks, rows)
     column_kernel(col_radix, source, hre, him, tw, forward, inverse, target)
-    spread(held, out_refs)
+    spread(quarters, out_refs, residue_of())
 
 
 def quarters_to_columns(col_radix, radix, *refs):
-    in_refs, (hre, him, tw, forward, inverse, out_ref, held) = refs[:radix], refs[radix:]
-    ranks, rows = out_ref.shape[0], out_ref.shape[2]
-    collect(in_refs, held)
-    source, target = Quarters(held, ranks, rows), Blocks(out_ref, ranks, rows)
+    in_refs, (hre, him, tw, forward, inverse), rest = refs[:radix], refs[radix : radix + 5], refs[radix + 5 :]
+    out_refs, (blocks, quarters) = rest[:-2], rest[-2:]
+    ranks, rows = blocks.shape[0], blocks.shape[2]
+    collect(in_refs, quarters, residue_of())
+    source, target = Quarters(quarters, ranks, rows), Blocks(blocks, ranks, rows)
     column_kernel(col_radix, source, hre, him, tw, forward, inverse, target)
-
-
-def middle_kernel(radix, *refs):
-    in_refs, refs = refs[:radix], refs[radix:]
-    (own_cos, own_sin, far_cos, far_sin, tw, inverse, forward), refs = refs[:7], refs[7:]
-    out_refs, (keep_ref, send_ref, held, field, screen) = refs[:radix], refs[radix:]
-    rows, points = held.shape[2], held.shape[3]
-    mine = frequency_of()
-    for half, pair_refs in ((mine, (own_cos, own_sin)), (1 - mine, (far_cos, far_sin))):
-        for i, ref in enumerate(pair_refs):
-            screen[i, half] = ref[...]
-    collect(in_refs, held)
-    (cells,) = row_inverse(held, tw, inverse, radix, 1)
-    turned = []
-    for m in range(radix):
-        at = slice(m * points, (m + 1) * points)
-        factor = [screen[i, :, :, at].reshape(rows, points) for i in range(2)]
-        part = turn(cells[m], factor, False)
-        for half in range(2):
-            for i in range(2):
-                field[half, i, :, at] = part[i][half * rows // 2 : (half + 1) * rows // 2]
-        turned.append(part)
-    kept = mine ^ lax.axis_index("depth")
-    keep_ref[...] = field[kept]
-    send_ref[...] = field[1 - kept]
-    value = row_forward([turned], tw, forward)
-    store_blocks(held, value, radix, rows, points)
-    spread(held, out_refs)
+    spread(blocks, out_refs, lax.axis_index("row"))
 
 
 def column_kernel(radix, source, hre, him, tw, forward, inverse, target):
@@ -271,7 +259,7 @@
     for half, pair_refs in ((mine, (own_cos, own_sin)), (1 - mine, (far_cos, far_sin))):
         for i, ref in enumerate(pair_refs):
             screen[i, half] = ref[...]
-    collect(in_refs, held)
+    collect(in_refs, held, residue_of())
     (cells,) = row_inverse(held, tw, inverse, radix, 1)
     turned = []
     for m in range(radix):
@@ -287,7 +275,7 @@
     send_ref[...] = field[1 - kept]
     value = row_forward([turned], tw, forward)
     store_blocks(held, value, radix, rows, points)
-    spread(held, out_refs)
+    spread(held, out_refs, residue_of())
 
 
 def column_kernel(radix, source, hre, him, tw, forward, inverse, target):
@@ -328,10 +316,11 @@
             target.ref[target.at(m * per + i, 1)] = im[at]
 
 
-def last_kernel(radix, in_ref, *refs):
-    screens, (tw, inverse, out_ref) = refs[:4], refs[4:]
-    points = in_ref.shape[3]
-    for f, parts in enumerate(row_inverse(in_ref, tw, inverse, radix, 2)):
+def last_kernel(radix, ranks, *refs):
+    in_refs, screens, (tw, inverse, out_ref, held) = refs[:ranks], refs[ranks : ranks + 4], refs[ranks + 4 :]
+    points = held.shape[3]
+    collect(in_refs, held, lax.axis_index("row"))
+    for f, parts in enumerate(row_inverse(held, tw, inverse, radix, 2)):
         for m, part in enumerate(parts):
             at = slice(m * points, (m + 1) * points)
             factor = (screens[2 * f][:, at], screens[2 * f + 1][:, at])
@@ -436,7 +425,6 @@
     radix = ranks // 2
     points = length // radix
     col_radix = length // lanes
-    core = lax.axis_index("depth")
 
     row_forward_table, row_inverse_table = real_form(points)
     col_inverse_table, col_forward_table = real_form(lanes)
@@ -448,36 +436,35 @@
     def flat(c, r):
         return c * ranks + r
 
-    def inner(arrays):
-        got = [arrays[0]]
-        for step in range(1, radix):
-            got.append(lax.ppermute(arrays[step], "row", [(r, r ^ step) for r in range(ranks)]))
+    def hop(array, step):
+        return lax.ppermute(array, "row", [(r, r ^ step) for r in range(ranks)])
+
+    def exchange(arrays, steps):
+        got = list(arrays)
+        for step in steps:
+            got[step] = hop(arrays[step], step)
         return got
 
-    def exchange(x):
-        return lax.all_to_all(x, "row", split_axis=0, concat_axis=0, tiled=True)
+    inner_steps = list(range(radix - 1, 0, -1))
+    outer_steps = list(range(radix, ranks)) + list(range(1, radix))
 
     far = lax.ppermute(slowness[0], both, [(flat(0, r), flat(0, r ^ radix)) for r in range(ranks)])
     other = lax.ppermute(slowness, "depth", swap)
     blocks = (ranks, 2, rows, points)
     quarter = (2, 2 * rows, points)
     half_field = (2, rows, length)
-    per_freq = (ranks // freqs,) + blocks[1:]
+    vmem, hbm = (pl.BlockSpec(memory_space=space) for space in (pltpu.VMEM, pl.ANY))
     spectra = pl.pallas_call(
         functools.partial(first_kernel, radix),
-        grid_spec=pltpu.PrefetchScalarGridSpec(
-            num_scalar_prefetch=1,
-            grid=(freqs,),
-            in_specs=[
-                pl.BlockSpec((1, 2, rows, length), lambda f, c: (f, c[0], 0, 0)),
-                pl.BlockSpec(row_tw.shape, lambda f, c: (0, 0, 0)),
-                pl.BlockSpec(row_forward_table.shape, lambda f, c: (0, 0, 0)),
-            ],
-            out_specs=pl.BlockSpec(per_freq, lambda f, c: (f, 0, 0, 0)),
-        ),
-        out_shape=jax.ShapeDtypeStruct(blocks, jnp.float32),
-    )(core.astype(jnp.int32).reshape(1), planes, row_tw, row_forward_table)
-
+        in_specs=[hbm, vmem, vmem],
+        out_specs=[vmem] * ranks,
+        out_shape=[pltpu.VMEM(blocks[1:], jnp.float32)] * ranks,
+        scratch_shapes=[
+            pltpu.VMEM((freqs,) + half_field, jnp.float32),
+            pltpu.VMEM(blocks, jnp.float32),
+            pltpu.SemaphoreType.DMA((freqs,)),
+        ],
+    )(planes, row_tw, row_forward_table)
     sent = lax.ppermute(far, "depth", [(0, 1)])
     plane = (rows, length)
     factor = (col_radix, lanes, points)
@@ -490,36 +477,36 @@
     )
     propagator_a, propagator_b = factors[:2], factors[2:4]
     screens_a, screens_b = factors[4:8], factors[8:12]
-    columns = exchange(spectra)
+    columns = exchange(spectra, outer_steps)
     quarters = call(
-        functools.partial(columns_to_quarters, col_radix),
+        functools.partial(columns_to_quarters, col_radix, ranks),
         [quarter] * radix,
-        [(radix,) + quarter],
-        (columns, *propagator_a, col_tw, col_forward_table, col_inverse_table),
-    )
-    quarters = inner(quarters)
+        [blocks, (radix,) + quarter],
+        (*columns, *propagator_a, col_tw, col_forward_table, col_inverse_table),
+    )
+    quarters = exchange(quarters, inner_steps)
     *quarters, keep, send = call(
         functools.partial(middle_kernel, radix),
         [quarter] * radix + [half_field] * 2,
         [(radix,) + quarter, (2,) + half_field, (2,) + half_field],
         (*quarters, *screens_a, held_tw, row_inverse_table, row_forward_table),
     )
-    quarters = inner(quarters)
+    quarters = exchange(quarters, inner_steps)
     got = lax.ppermute(send, "depth", swap)
     share = keep[0] * got[0] + keep[1] * got[1]
     more = lax.ppermute(share, both, [(flat(1, r), flat(0, r ^ radix)) for r in range(ranks)])
-    (columns,) = call(
+    columns = call(
         functools.partial(quarters_to_columns, col_radix, radix),
+        [blocks[1:]] * ranks,
+        [blocks, (radix,) + quarter],
+        (*quarters, *propagator_b, col_tw, col_forward_table, col_inverse_table),
+    )
+    cells = exchange(columns, outer_steps)
+    (fields,) = call(
+        functools.partial(last_kernel, radix, ranks),
+        [(freqs,) + half_field],
         [blocks],
-        [(radix,) + quarter],
-        (*quarters, *propagator_b, col_tw, col_forward_table, col_inverse_table),
-    )
-    cells = exchange(columns)
-    (fields,) = call(
-        functools.partial(last_kernel, radix),
-        [(freqs,) + half_field],
-        [],
-        (cells, *screens_b, held_tw, row_inverse_table),
+        (*cells, *screens_b, held_tw, row_inverse_table),
     )
     swapped = lax.ppermute(fields, "depth", swap)
     image, leaving = call(

time: 82.3 us -> 81.4 us (0.989)
  waiting for transfers between devices: 44.4 us -> 28.7 us
  starting transfers between devices: 25.9 us -> 41.1 us
    ppermute x6 -> x20, starting transfers between devices: 7.11 us -> 32.2 us  [hop(): return lax.ppermute(array, 'row', [(r, r ^ step) for r in range(ranks)])]
    all_to_all x2 -> x0, waiting for transfers between devices: 12.5 us -> none  [exchange(): return lax.all_to_all(x, 'row', split_axis=0, concat_axis=0, tiled=True)]
    all_to_all x2 -> x0, starting transfers between devices: 11.1 us -> none  [exchange(): return lax.all_to_all(x, 'row', split_axis=0, concat_axis=0, tiled=True)]
    ppermute x1, waiting for transfers between devices: 12.2 us -> 3.07 us  [shards(): lax.ppermute(slowness[0], both, [(flat(0, r), flat(0, r ^ radix)) for r i...]
    ppermute x6 -> x20, waiting for transfers between devices: 11.4 us -> 19.7 us  [hop(): return lax.ppermute(array, 'row', [(r, r ^ step) for r in range(ranks)])]
    ppermute x1, waiting for transfers between devices: 7.29 us -> 5.89 us  [shards(): lax.ppermute(share, both, [(flat(1, r), flat(0, r ^ radix)) for r in rang...]
    ppermute x1, starting transfers between devices: 4.94 us -> 6.1 us  [shards(): lax.ppermute(slowness[0], both, [(flat(0, r), flat(0, r ^ radix)) for r i...]
    ppermute x1, waiting for transfers between devices: 0.95 us -> 0.01 us  [shards(): sent = lax.ppermute(far, 'depth', [(0, 1)])]
  transfers between devices with their start and end apart: 14 -> 26, of which waited for: 10 -> 13; matrix products, arithmetic and copies ran while one was open for 0% -> 0% of each run, Pallas kernels for 4% -> 7%
where the time goes in v6:
time: 81.4 us; the launch traced here: 80.9 us
  starting transfers between devices  41.1 us (50%)
  waiting for transfers between devices  28.7 us (35%)
  Pallas kernels  10.3 us (13%)
    ppermute x20, starting transfers between devices, hop(): return lax.ppermute(array, 'row', [(r, r ^ step) for r in range(ranks)])  32.2 us
    ppermute x20, waiting for transfers between devices, hop(): return lax.ppermute(array, 'row', [(r, r ^ step) for r in range(ranks)])  19.7 us
    pallas_call x6, Pallas kernels, call(): pl.pallas_call(kernel, in_specs=[smem] * len(scalars) + [vmem] * len(args...  7.56 us
    ppermute x1, starting transfers between devices, shards(): lax.ppermute(slowness[0], both, [(flat(0, r), flat(0, r ^ radix)) for r i...  6.1 us
    ppermute x1, waiting for transfers between devices, shards(): lax.ppermute(share, both, [(flat(1, r), flat(0, r ^ radix)) for r in rang...  5.89 us
    ppermute x1, waiting for transfers between devices, shards(): lax.ppermute(slowness[0], both, [(flat(0, r), flat(0, r ^ radix)) for r i...  3.07 us
    pallas_call x1, Pallas kernels, shards(): pl.pallas_call(functools.partial(first_kernel, radix), in_specs=[hbm, vme...  2.71 us
  transfers between devices with their start and end apart: 26, of which 13 were waited for; matrix products, arithmetic and copies ran while one was open for 0% of the time, Pallas kernels for 7%

profile of v6, /device:TPU:0, one launch (start us, length us, event | category | flops | bytes accessed | tf_op | source)
XLA Modules:
  0.0 80.9 jit_solution(18084921904615497078)
XLA Ops:
  0.6 6.1 %collective-permute-start.8 = (f32[64,512]{1,0:T(8,128)}, f32[64,512]{1,0:T(8,128)S(1)}, u32[]{:S(2)}, u32[]{:S(2)}) collective-permute-start(f32[64,512]{1,0:T(8,128)} %bitcast.3), channel_id=1, source_target_pairs={{0,4},{1,5},{2,6},{3,7},{4,0},{5,1},{6,2},{7,3},{16,20},{17,21},{1... | collective-permute-start | bytes 393224 | tf_op jit(solution)/shard_map/ppermute | solution.py:451
  6.8 3.1 %collective-permute-done.8.far_ref = f32[64,512]{1,0:T(8,128)S(1)} collective-permute-done((f32[64,512]{1,0:T(8,128)}, f32[64,512]{1,0:T(8,128)S(1)}, u32[]{:S(2)}, u32[]{:S(2)}) %collective-permute-start.8) | collective-permute-done | bytes 131104 | tf_op jit(solution)/shard_map/ppermute | solution.py:451
  9.9 1.3 %collective-permute-start.9 = (f32[64,512]{1,0:T(8,128)S(1)}, f32[64,512]{1,0:T(8,128)S(1)}, u32[]{:S(2)}, u32[]{:S(2)}) collective-permute-start(f32[64,512]{1,0:T(8,128)S(1)} %collective-permute-done.8.far_ref), channel_id=1, source_target_pairs={{0,8},{1,9},{2,10},{3,11},{4,12},{5,13},{6,14},{7,15},{16,24},{17,... | collective-permute-start | bytes 393224 | tf_op jit(solution)/shard_map/ppermute | solution.py:468
  11.2 2.7 %shard_map.113 = (f32[2,64,128]{2,1,0:T(8,128)S(1)}, f32[2,64,128]{2,1,0:T(8,128)S(1)}, f32[2,64,128]{2,1,0:T(8,128)S(1)}, f32[2,64,128]{2,1,0:T(8,128)S(1)}, f3...) custom-call(f32[2,4,64,512]{3,2,1,0:T(8,128)} %planes_ref.1, ...), custom_call_target="tpu_custom_call" | custom-call | tf_op jit(solution)/shard_map/pallas_call | solution.py:457
  13.9 3.3 %collective-permute-start = (f32[2,64,128]{2,1,0:T(8,128)S(1)}, f32[2,64,128]{2,1,0:T(8,128)S(1)}, u32[]{:S(2)}, u32[]{:S(2)}) collective-permute-start(f32[2,64,128]{2,1,0:T(8,128)S(1)} %get-tuple-element.42), channel_id=1, source_target_pairs={{0,1},{1,0},{2,3},{3,2},{4,5},{5,4},{6,7},{7,6},{8,9},{9,8},{10,11... | collective-permute-start | bytes 196616 | tf_op jit(solution)/shard_map/ppermute | solution.py:440
  19.5 1.8 %collective-permute-start.3 = (f32[2,64,128]{2,1,0:T(8,128)S(1)}, f32[2,64,128]{2,1,0:T(8,128)S(1)}, u32[]{:S(2)}, u32[]{:S(2)}) collective-permute-start(f32[2,64,128]{2,1,0:T(8,128)S(1)} %get-tuple-element.45), channel_id=1, source_target_pairs={{0,4},{1,5},{2,6},{3,7},{4,0},{5,1},{6,2},{7,3},{8,12},{9,13},{10,... | collective-permute-start | bytes 196616 | tf_op jit(solution)/shard_map/ppermute | solution.py:440
  21.7 2.6 %collective-permute-start.4 = (f32[2,64,128]{2,1,0:T(8,128)S(1)}, f32[2,64,128]{2,1,0:T(8,128)S(1)}, u32[]{:S(2)}, u32[]{:S(2)}) collective-permute-start(f32[2,64,128]{2,1,0:T(8,128)S(1)} %get-tuple-element.46), channel_id=1, source_target_pairs={{0,5},{1,4},{2,7},{3,6},{4,1},{5,0},{6,3},{7,2},{8,13},{9,12},{10,... | collective-permute-start | bytes 196616 | tf_op jit(solution)/shard_map/ppermute | solution.py:440
  24.3 3.7 %collective-permute-start.5 = (f32[2,64,128]{2,1,0:T(8,128)S(1)}, f32[2,64,128]{2,1,0:T(8,128)S(1)}, u32[]{:S(2)}, u32[]{:S(2)}) collective-permute-start(f32[2,64,128]{2,1,0:T(8,128)S(1)} %get-tuple-element.47), channel_id=1, source_target_pairs={{0,6},{1,7},{2,4},{3,5},{4,2},{5,3},{6,0},{7,1},{8,14},{9,15},{10,... | collective-permute-start | bytes 196616 | tf_op jit(solution)/shard_map/ppermute | solution.py:440
  29.0 2.8 %shard_map.114 = (f32[4,2,128]{2,1,0:T(2,128)S(1)}, f32[4,128,128]{2,1,0:T(8,128)S(1)}, f32[4,128,128]{2,1,0:T(8,128)S(1)}, f32[4,128,128]{2,1,0:T(8,128)S(1)}, ...) custom-call(s32[2]{0:T(128)S(1)} %copy-done.5, ...), custom_call_target="tpu_custom_call" | custom-call | tf_op jit(solution)/shard_map/pallas_call | solution.py:412
  31.9 3.2 %collective-permute-done.6.refs_7_ = f32[2,64,128]{2,1,0:T(8,128)S(1)} collective-permute-done((f32[2,64,128]{2,1,0:T(8,128)S(1)}, f32[2,64,128]{2,1,0:T(8,128)S(1)}, u32[]{:S(2)}, u32[]{:S(2)}) %collective-permute-start.6) | collective-permute-done | bytes 65568 | tf_op jit(solution)/shard_map/ppermute | solution.py:440
  37.2 2.4 %collective-permute-start.12 = (f32[2,128,128]{2,1,0:T(8,128)S(1)}, f32[2,128,128]{2,1,0:T(8,128)S(1)}, u32[]{:S(2)}, u32[]{:S(2)}) collective-permute-start(f32[2,128,128]{2,1,0:T(8,128)S(1)} %get-tuple-element.54), channel_id=1, source_target_pairs={{0,3},{1,2},{2,1},{3,0},{4,7},{5,6},{6,5},{7,4},{8,11},{9,10},{10,... | collective-permute-start | bytes 393224 | tf_op jit(solution)/shard_map/ppermute | solution.py:440
  39.7 2.3 %collective-permute-done.10.refs_1_ = f32[2,128,128]{2,1,0:T(8,128)S(1)} collective-permute-done((f32[2,128,128]{2,1,0:T(8,128)S(1)}, f32[2,128,128]{2,1,0:T(8,128)S(1)}, u32[]{:S(2)}, u32[]{:S(2)}) %collective-permute-start.10) | collective-permute-done | bytes 131104 | tf_op jit(solution)/shard_map/ppermute | solution.py:440
  42.0 1.6 %collective-permute-done.11.refs_2_ = f32[2,128,128]{2,1,0:T(8,128)S(1)} collective-permute-done((f32[2,128,128]{2,1,0:T(8,128)S(1)}, f32[2,128,128]{2,1,0:T(8,128)S(1)}, u32[]{:S(2)}, u32[]{:S(2)}) %collective-permute-start.11) | collective-permute-done | bytes 131104 | tf_op jit(solution)/shard_map/ppermute | solution.py:440
  43.6 1.4 %collective-permute-done.12.refs_3_ = f32[2,128,128]{2,1,0:T(8,128)S(1)} collective-permute-done((f32[2,128,128]{2,1,0:T(8,128)S(1)}, f32[2,128,128]{2,1,0:T(8,128)S(1)}, u32[]{:S(2)}, u32[]{:S(2)}) %collective-permute-start.12) | collective-permute-done | bytes 131104 | tf_op jit(solution)/shard_map/ppermute | solution.py:440
  46.2 1.7 %collective-permute-start.13 = (f32[2,128,128]{2,1,0:T(8,128)S(1)}, f32[2,128,128]{2,1,0:T(8,128)S(1)}, u32[]{:S(2)}, u32[]{:S(2)}) collective-permute-start(f32[2,128,128]{2,1,0:T(8,128)S(1)} %get-tuple-element.61), channel_id=1, source_target_pairs={{0,1},{1,0},{2,3},{3,2},{4,5},{5,4},{6,7},{7,6},{8,9},{9,8},{10,11... | collective-permute-start | bytes 393224 | tf_op jit(solution)/shard_map/ppermute | solution.py:440
  48.3 1.5 %collective-permute-start.15 = (f32[2,128,128]{2,1,0:T(8,128)S(1)}, f32[2,128,128]{2,1,0:T(8,128)S(1)}, u32[]{:S(2)}, u32[]{:S(2)}) collective-permute-start(f32[2,128,128]{2,1,0:T(8,128)S(1)} %get-tuple-element.63), channel_id=1, source_target_pairs={{0,3},{1,2},{2,1},{3,0},{4,7},{5,6},{6,5},{7,4},{8,11},{9,10},{10,... | collective-permute-start | bytes 393224 | tf_op jit(solution)/shard_map/ppermute | solution.py:440
  49.8 2.2 %collective-permute-done.13.refs_1_ = f32[2,128,128]{2,1,0:T(8,128)S(1)} collective-permute-done((f32[2,128,128]{2,1,0:T(8,128)S(1)}, f32[2,128,128]{2,1,0:T(8,128)S(1)}, u32[]{:S(2)}, u32[]{:S(2)}) %collective-permute-start.13) | collective-permute-done | bytes 131104 | tf_op jit(solution)/shard_map/ppermute | solution.py:440
  55.2 1.7 %collective-permute-start.16 = (f32[2,64,128]{2,1,0:T(8,128)S(1)}, f32[2,64,128]{2,1,0:T(8,128)S(1)}, u32[]{:S(2)}, u32[]{:S(2)}) collective-permute-start(f32[2,64,128]{2,1,0:T(8,128)S(1)} %get-tuple-element.67), channel_id=1, source_target_pairs={{0,1},{1,0},{2,3},{3,2},{4,5},{5,4},{6,7},{7,6},{8,9},{9,8},{10,11... | collective-permute-start | bytes 196616 | tf_op jit(solution)/shard_map/ppermute | solution.py:440
  57.4 1.4 %collective-permute-start.18 = (f32[2,64,128]{2,1,0:T(8,128)S(1)}, f32[2,64,128]{2,1,0:T(8,128)S(1)}, u32[]{:S(2)}, u32[]{:S(2)}) collective-permute-start(f32[2,64,128]{2,1,0:T(8,128)S(1)} %get-tuple-element.69), channel_id=1, source_target_pairs={{0,3},{1,2},{2,1},{3,0},{4,7},{5,6},{6,5},{7,4},{8,11},{9,10},{10,... | collective-permute-start | bytes 196616 | tf_op jit(solution)/shard_map/ppermute | solution.py:440
  59.7 3.1 %collective-permute-start.20 = (f32[2,64,128]{2,1,0:T(8,128)S(1)}, f32[2,64,128]{2,1,0:T(8,128)S(1)}, u32[]{:S(2)}, u32[]{:S(2)}) collective-permute-start(f32[2,64,128]{2,1,0:T(8,128)S(1)} %get-tuple-element.71), channel_id=1, source_target_pairs={{0,5},{1,4},{2,7},{3,6},{4,1},{5,0},{6,3},{7,2},{8,13},{9,12},{10,... | collective-permute-start | bytes 196616 | tf_op jit(solution)/shard_map/ppermute | solution.py:440
  63.5 3.0 %collective-permute-start.22 = (f32[2,64,128]{2,1,0:T(8,128)S(1)}, f32[2,64,128]{2,1,0:T(8,128)S(1)}, u32[]{:S(2)}, u32[]{:S(2)}) collective-permute-start(f32[2,64,128]{2,1,0:T(8,128)S(1)} %get-tuple-element.73), channel_id=1, source_target_pairs={{0,7},{1,6},{2,5},{3,4},{4,3},{5,2},{6,1},{7,0},{8,15},{9,14},{10,... | collective-permute-start | bytes 196616 | tf_op jit(solution)/shard_map/ppermute | solution.py:440
  67.1 5.1 %collective-permute-done.20.refs_5_ = f32[2,64,128]{2,1,0:T(8,128)S(1)} collective-permute-done((f32[2,64,128]{2,1,0:T(8,128)S(1)}, f32[2,64,128]{2,1,0:T(8,128)S(1)}, u32[]{:S(2)}, u32[]{:S(2)}) %collective-permute-start.20) | collective-permute-done | bytes 65568 | tf_op jit(solution)/shard_map/ppermute | solution.py:440
  72.8 1.3 %collective-permute-start.25 = (f32[64,512]{1,0:T(8,128)S(1)}, f32[64,512]{1,0:T(8,128)S(1)}, u32[]{:S(2)}, u32[]{:S(2)}) collective-permute-start(f32[64,512]{1,0:T(8,128)S(1)} %fusion.1.share_ref), channel_id=1, source_target_pairs={{8,4},{9,5},{10,6},{11,7},{12,0},{13,1},{14,2},{15,3},{24,20},{25,... | collective-permute-start | bytes 393224 | tf_op jit(solution)/shard_map/ppermute | solution.py:497
  74.1 5.9 %collective-permute-done.25.more_ref = f32[64,512]{1,0:T(8,128)S(1)} collective-permute-done((f32[64,512]{1,0:T(8,128)S(1)}, f32[64,512]{1,0:T(8,128)S(1)}, u32[]{:S(2)}, u32[]{:S(2)}) %collective-permute-start.25) | collective-permute-done | bytes 131104 | tf_op jit(solution)/shard_map/ppermute | solution.py:497
  (50 shorter events, 14.7 us)
Async XLA Ops:
  0.6 9.3 %collective-permute-start.8 = (f32[64,512]{1,0:T(8,128)}, f32[64,512]{1,0:T(8,128)S(1)}, u32[]{:S(2)}, u32[]{:S(2)}) collective-permute-start(f32[64,512]{1,0:T(8,128)} %bitcast.3), channel_id=1, source_target_pairs={{0,4},{1,5},{2,6},{3,7},{4,0},{5,1},{6,2},{7,3},{16,20},{17,21},{1... | collective-permute-start | bytes 393224 | tf_op jit(solution)/shard_map/ppermute | solution.py:451
  6.8 17.6 %collective-permute-start.7 = (f32[1,64,512]{2,1,0:T(8,128)}, f32[1,64,512]{2,1,0:T(8,128)S(1)}, u32[]{:S(2)}, u32[]{:S(2)}) collective-permute-start(f32[1,64,512]{2,1,0:T(8,128)} %slow_ref.1), channel_id=1, source_target_pairs={{0,8},{8,0},{1,9},{9,1},{2,10},{10,2},{3,11},{11,3},{4,12},{12,4},... | collective-permute-start | bytes 393224 | tf_op jit(solution)/shard_map/ppermute | solution.py:452
  9.9 18.1 %collective-permute-start.9 = (f32[64,512]{1,0:T(8,128)S(1)}, f32[64,512]{1,0:T(8,128)S(1)}, u32[]{:S(2)}, u32[]{:S(2)}) collective-permute-start(f32[64,512]{1,0:T(8,128)S(1)} %collective-permute-done.8.far_ref), channel_id=1, source_target_pairs={{0,8},{1,9},{2,10},{3,11},{4,12},{5,13},{6,14},{7,15},{16,24},{17,... | collective-permute-start | bytes 393224 | tf_op jit(solution)/shard_map/ppermute | solution.py:468
  13.9 5.6 %collective-permute-start = (f32[2,64,128]{2,1,0:T(8,128)S(1)}, f32[2,64,128]{2,1,0:T(8,128)S(1)}, u32[]{:S(2)}, u32[]{:S(2)}) collective-permute-start(f32[2,64,128]{2,1,0:T(8,128)S(1)} %get-tuple-element.42), channel_id=1, source_target_pairs={{0,1},{1,0},{2,3},{3,2},{4,5},{5,4},{6,7},{7,6},{8,9},{9,8},{10,11... | collective-permute-start | bytes 196616 | tf_op jit(solution)/shard_map/ppermute | solution.py:440
  18.0 13.8 %collective-permute-start.2 = (f32[2,64,128]{2,1,0:T(8,128)S(1)}, f32[2,64,128]{2,1,0:T(8,128)S(1)}, u32[]{:S(2)}, u32[]{:S(2)}) collective-permute-start(f32[2,64,128]{2,1,0:T(8,128)S(1)} %get-tuple-element.44), channel_id=1, source_target_pairs={{0,3},{1,2},{2,1},{3,0},{4,7},{5,6},{6,5},{7,4},{8,11},{9,10},{10,... | collective-permute-start | bytes 196616 | tf_op jit(solution)/shard_map/ppermute | solution.py:440
  19.5 12.3 %collective-permute-start.3 = (f32[2,64,128]{2,1,0:T(8,128)S(1)}, f32[2,64,128]{2,1,0:T(8,128)S(1)}, u32[]{:S(2)}, u32[]{:S(2)}) collective-permute-start(f32[2,64,128]{2,1,0:T(8,128)S(1)} %get-tuple-element.45), channel_id=1, source_target_pairs={{0,4},{1,5},{2,6},{3,7},{4,0},{5,1},{6,2},{7,3},{8,12},{9,13},{10,... | collective-permute-start | bytes 196616 | tf_op jit(solution)/shard_map/ppermute | solution.py:440
  21.7 10.1 %collective-permute-start.4 = (f32[2,64,128]{2,1,0:T(8,128)S(1)}, f32[2,64,128]{2,1,0:T(8,128)S(1)}, u32[]{:S(2)}, u32[]{:S(2)}) collective-permute-start(f32[2,64,128]{2,1,0:T(8,128)S(1)} %get-tuple-element.46), channel_id=1, source_target_pairs={{0,5},{1,4},{2,7},{3,6},{4,1},{5,0},{6,3},{7,2},{8,13},{9,12},{10,... | collective-permute-start | bytes 196616 | tf_op jit(solution)/shard_map/ppermute | solution.py:440
  24.3 7.5 %collective-permute-start.5 = (f32[2,64,128]{2,1,0:T(8,128)S(1)}, f32[2,64,128]{2,1,0:T(8,128)S(1)}, u32[]{:S(2)}, u32[]{:S(2)}) collective-permute-start(f32[2,64,128]{2,1,0:T(8,128)S(1)} %get-tuple-element.47), channel_id=1, source_target_pairs={{0,6},{1,7},{2,4},{3,5},{4,2},{5,3},{6,0},{7,1},{8,14},{9,15},{10,... | collective-permute-start | bytes 196616 | tf_op jit(solution)/shard_map/ppermute | solution.py:440
  28.1 7.0 %collective-permute-start.6 = (f32[2,64,128]{2,1,0:T(8,128)S(1)}, f32[2,64,128]{2,1,0:T(8,128)S(1)}, u32[]{:S(2)}, u32[]{:S(2)}) collective-permute-start(f32[2,64,128]{2,1,0:T(8,128)S(1)} %get-tuple-element.48), channel_id=1, source_target_pairs={{0,7},{1,6},{2,5},{3,4},{4,3},{5,2},{6,1},{7,0},{8,15},{9,14},{10,... | collective-permute-start | bytes 196616 | tf_op jit(solution)/shard_map/ppermute | solution.py:440
  36.1 5.8 %collective-permute-start.10 = (f32[2,128,128]{2,1,0:T(8,128)S(1)}, f32[2,128,128]{2,1,0:T(8,128)S(1)}, u32[]{:S(2)}, u32[]{:S(2)}) collective-permute-start(f32[2,128,128]{2,1,0:T(8,128)S(1)} %get-tuple-element.52), channel_id=1, source_target_pairs={{0,1},{1,0},{2,3},{3,2},{4,5},{5,4},{6,7},{7,6},{8,9},{9,8},{10,11... | collective-permute-start | bytes 393224 | tf_op jit(solution)/shard_map/ppermute | solution.py:440
  37.2 6.4 %collective-permute-start.11 = (f32[2,128,128]{2,1,0:T(8,128)S(1)}, f32[2,128,128]{2,1,0:T(8,128)S(1)}, u32[]{:S(2)}, u32[]{:S(2)}) collective-permute-start(f32[2,128,128]{2,1,0:T(8,128)S(1)} %get-tuple-element.53), channel_id=1, source_target_pairs={{0,2},{1,3},{2,0},{3,1},{4,6},{5,7},{6,4},{7,5},{8,10},{9,11},{10,... | collective-permute-start | bytes 393224 | tf_op jit(solution)/shard_map/ppermute | solution.py:440
  37.2 7.8 %collective-permute-start.12 = (f32[2,128,128]{2,1,0:T(8,128)S(1)}, f32[2,128,128]{2,1,0:T(8,128)S(1)}, u32[]{:S(2)}, u32[]{:S(2)}) collective-permute-start(f32[2,128,128]{2,1,0:T(8,128)S(1)} %get-tuple-element.54), channel_id=1, source_target_pairs={{0,3},{1,2},{2,1},{3,0},{4,7},{5,6},{6,5},{7,4},{8,11},{9,10},{10,... | collective-permute-start | bytes 393224 | tf_op jit(solution)/shard_map/ppermute | solution.py:440
  46.2 5.7 %collective-permute-start.13 = (f32[2,128,128]{2,1,0:T(8,128)S(1)}, f32[2,128,128]{2,1,0:T(8,128)S(1)}, u32[]{:S(2)}, u32[]{:S(2)}) collective-permute-start(f32[2,128,128]{2,1,0:T(8,128)S(1)} %get-tuple-element.61), channel_id=1, source_target_pairs={{0,1},{1,0},{2,3},{3,2},{4,5},{5,4},{6,7},{7,6},{8,9},{9,8},{10,11... | collective-permute-start | bytes 393224 | tf_op jit(solution)/shard_map/ppermute | solution.py:440
  48.0 5.0 %collective-permute-start.14 = (f32[2,128,128]{2,1,0:T(8,128)S(1)}, f32[2,128,128]{2,1,0:T(8,128)S(1)}, u32[]{:S(2)}, u32[]{:S(2)}) collective-permute-start(f32[2,128,128]{2,1,0:T(8,128)S(1)} %get-tuple-element.62), channel_id=1, source_target_pairs={{0,2},{1,3},{2,0},{3,1},{4,6},{5,7},{6,4},{7,5},{8,10},{9,11},{10,... | collective-permute-start | bytes 393224 | tf_op jit(solution)/shard_map/ppermute | solution.py:440
  48.3 5.9 %collective-permute-start.15 = (f32[2,128,128]{2,1,0:T(8,128)S(1)}, f32[2,128,128]{2,1,0:T(8,128)S(1)}, u32[]{:S(2)}, u32[]{:S(2)}) collective-permute-start(f32[2,128,128]{2,1,0:T(8,128)S(1)} %get-tuple-element.63), channel_id=1, source_target_pairs={{0,3},{1,2},{2,1},{3,0},{4,7},{5,6},{6,5},{7,4},{8,11},{9,10},{10,... | collective-permute-start | bytes 393224 | tf_op jit(solution)/shard_map/ppermute | solution.py:440
  57.0 5.9 %collective-permute-start.17 = (f32[2,64,128]{2,1,0:T(8,128)S(1)}, f32[2,64,128]{2,1,0:T(8,128)S(1)}, u32[]{:S(2)}, u32[]{:S(2)}) collective-permute-start(f32[2,64,128]{2,1,0:T(8,128)S(1)} %get-tuple-element.68), channel_id=1, source_target_pairs={{0,2},{1,3},{2,0},{3,1},{4,6},{5,7},{6,4},{7,5},{8,10},{9,11},{10,... | collective-permute-start | bytes 196616 | tf_op jit(solution)/shard_map/ppermute | solution.py:440
  57.4 6.1 %collective-permute-start.18 = (f32[2,64,128]{2,1,0:T(8,128)S(1)}, f32[2,64,128]{2,1,0:T(8,128)S(1)}, u32[]{:S(2)}, u32[]{:S(2)}) collective-permute-start(f32[2,64,128]{2,1,0:T(8,128)S(1)} %get-tuple-element.69), channel_id=1, source_target_pairs={{0,3},{1,2},{2,1},{3,0},{4,7},{5,6},{6,5},{7,4},{8,11},{9,10},{10,... | collective-permute-start | bytes 196616 | tf_op jit(solution)/shard_map/ppermute | solution.py:440
  58.8 14.0 %collective-permute-start.24 = (f32[2,64,512]{2,1,0:T(8,128)S(1)}, f32[2,64,512]{2,1,0:T(8,128)S(1)}, u32[]{:S(2)}, u32[]{:S(2)}) collective-permute-start(f32[2,64,512]{2,1,0:T(8,128)S(1)} %get-tuple-element.79), channel_id=1, source_target_pairs={{0,8},{8,0},{1,9},{9,1},{2,10},{10,2},{3,11},{11,3},{4,12},{12,4},... | collective-permute-start | bytes 786440 | tf_op jit(solution)/shard_map/ppermute | solution.py:495
  58.8 8.4 %collective-permute-start.19 = (f32[2,64,128]{2,1,0:T(8,128)S(1)}, f32[2,64,128]{2,1,0:T(8,128)S(1)}, u32[]{:S(2)}, u32[]{:S(2)}) collective-permute-start(f32[2,64,128]{2,1,0:T(8,128)S(1)} %get-tuple-element.70), channel_id=1, source_target_pairs={{0,4},{1,5},{2,6},{3,7},{4,0},{5,1},{6,2},{7,3},{8,12},{9,13},{10,... | collective-permute-start | bytes 196616 | tf_op jit(solution)/shard_map/ppermute | solution.py:440
  59.7 12.5 %collective-permute-start.20 = (f32[2,64,128]{2,1,0:T(8,128)S(1)}, f32[2,64,128]{2,1,0:T(8,128)S(1)}, u32[]{:S(2)}, u32[]{:S(2)}) collective-permute-start(f32[2,64,128]{2,1,0:T(8,128)S(1)} %get-tuple-element.71), channel_id=1, source_target_pairs={{0,5},{1,4},{2,7},{3,6},{4,1},{5,0},{6,3},{7,2},{8,13},{9,12},{10,... | collective-permute-start | bytes 196616 | tf_op jit(solution)/shard_map/ppermute | solution.py:440
  62.8 9.4 %collective-permute-start.21 = (f32[2,64,128]{2,1,0:T(8,128)S(1)}, f32[2,64,128]{2,1,0:T(8,128)S(1)}, u32[]{:S(2)}, u32[]{:S(2)}) collective-permute-start(f32[2,64,128]{2,1,0:T(8,128)S(1)} %get-tuple-element.72), channel_id=1, source_target_pairs={{0,6},{1,7},{2,4},{3,5},{4,2},{5,3},{6,0},{7,1},{8,14},{9,15},{10,... | collective-permute-start | bytes 196616 | tf_op jit(solution)/shard_map/ppermute | solution.py:440
  63.5 8.8 %collective-permute-start.22 = (f32[2,64,128]{2,1,0:T(8,128)S(1)}, f32[2,64,128]{2,1,0:T(8,128)S(1)}, u32[]{:S(2)}, u32[]{:S(2)}) collective-permute-start(f32[2,64,128]{2,1,0:T(8,128)S(1)} %get-tuple-element.73), channel_id=1, source_target_pairs={{0,7},{1,6},{2,5},{3,4},{4,3},{5,2},{6,1},{7,0},{8,15},{9,14},{10,... | collective-permute-start | bytes 196616 | tf_op jit(solution)/shard_map/ppermute | solution.py:440
  72.7 7.3 %collective-permute-start.23 = (f32[2,2,64,512]{3,2,1,0:T(8,128)S(1)}, f32[2,2,64,512]{3,2,1,0:T(8,128)S(1)}, u32[]{:S(2)}, u32[]{:S(2)}) collective-permute-start(f32[2,2,64,512]{3,2,1,0:T(8,128)S(1)} %shard_map.118.own_ref), channel_id=1, source_target_pairs={{0,8},{8,0},{1,9},{9,1},{2,10},{10,2},{3,11},{11,3},{4,12},{12,4},... | collective-permute-start | bytes 1572872 | tf_op jit(solution)/shard_map/ppermute | solution.py:511
  72.8 7.2 %collective-permute-start.25 = (f32[64,512]{1,0:T(8,128)S(1)}, f32[64,512]{1,0:T(8,128)S(1)}, u32[]{:S(2)}, u32[]{:S(2)}) collective-permute-start(f32[64,512]{1,0:T(8,128)S(1)} %fusion.1.share_ref), channel_id=1, source_target_pairs={{8,4},{9,5},{10,6},{11,7},{12,0},{13,1},{14,2},{15,3},{24,20},{25,... | collective-permute-start | bytes 393224 | tf_op jit(solution)/shard_map/ppermute | solution.py:497
  (9 other events, 95.3 us)

commit v7 on v6

--- a/solution.py
+++ b/solution.py
@@ -133,8 +133,8 @@
     out_ref[:, 1] = value[:, points:].reshape(count, rows, points)
 
 
-def first_kernel(radix, planes_ref, tw, table, *rest):
-    out_refs, (loaded, held, sems) = rest[:-3], rest[-3:]
+def first_kernel(radix, planes_ref, tw_ref, table_ref, *rest):
+    out_refs, (loaded, tw, table, held, sems) = rest[:-5], rest[-5:]
     freqs, _, rows, length = loaded.shape
     points = length // radix
     core = lax.axis_index("depth")
@@ -142,8 +142,14 @@
         pltpu.make_async_copy(planes_ref.at[f, pl.ds(2 * core, 2)], loaded.at[f], sems.at[f])
         for f in range(freqs)
     ]
-    for copy in copies:
+    constants = [
+        pltpu.make_async_copy(table_ref, table, sems.at[freqs]),
+        pltpu.make_async_copy(tw_ref, tw, sems.at[freqs + 1]),
+    ]
+    for copy in copies + constants:
         copy.start()
+    for copy in constants:
+        copy.wait()
     for f, copy in enumerate(copies):
         copy.wait()
         parts = [
@@ -370,39 +376,55 @@
     return new_cos, new_sin
 
 
-def factor_kernel(radix, freq_ref, ref_ref, slow_ref, other_ref, far_ref, sent_ref, tw_ref, *outs):
-    (tw_out, hre_a, him_a, hre_b, him_b), outs = outs[:5], outs[5:]
-    tw_out[...] = tw_ref[...]
-    col_radix, points, width = hre_a.shape
+def omegas_of(freq_ref):
+    omegas = [omega_step * freq_ref[f].astype(jnp.float32) for f in range(2)]
+    return omegas, jnp.where(frequency_of() == 0, omegas[0], omegas[1])
+
+
+def core_sign():
+    return jnp.where(lax.axis_index("depth") == 0, -1.0, 1.0)
+
+
+def propagator(radix, level, freq_ref, ref_ref, hre, him):
+    col_radix, points, width = hre.shape
     length = col_radix * points
-    core = lax.axis_index("depth")
-    first = core == 0
-    sign = jnp.where(first, -1.0, 1.0)
-    omegas = [omega_step * freq_ref[f].astype(jnp.float32) for f in range(2)]
-    omega = jnp.where(frequency_of() == 0, omegas[0], omegas[1])
+    _, omega = omegas_of(freq_ref)
     scale = 1.0 / (length * length)
     row_at = lax.broadcasted_iota(jnp.int32, (1, width), 1) * radix + residue_of()
     row_square = signed_wave(row_at, length) ** 2
     for r in range(col_radix):
         col_at = lax.broadcasted_iota(jnp.int32, (points, width), 0) * col_radix + r
-        plane_waves = signed_wave(col_at, length) ** 2 + row_square
-        for level, (hre, him) in enumerate(((hre_a, him_a), (hre_b, him_b))):
-            radicand = (omega * ref_ref[level]) ** 2 - plane_waves
-            vertical = jnp.sqrt(jnp.maximum(radicand, 0.0)) * depth_step
-            damping = scale * jnp.exp(-jnp.sqrt(jnp.maximum(-radicand, 0.0)) * depth_step)
-            cosine, sine = cos_sin(vertical)
-            hre[r], him[r] = damping * cosine, sign * damping * sine
-
-    def screen(slow, level, frequency, at):
-        cosine, sine = cos_sin(frequency * (slow - ref_ref[level]) * depth_step)
-        outs[at][...], outs[at + 1][...] = cosine, sign * sine
-
-    own, other = slow_ref[0], other_ref[0]
-    screen(jnp.where(first, own, other), 0, omega, 0)
-    screen(jnp.where(first, far_ref[...], sent_ref[...]), 0, omega, 2)
-    last = jnp.where(first, other, own)
+        radicand = (omega * ref_ref[level]) ** 2 - (signed_wave(col_at, length) ** 2 + row_square)
+        vertical = jnp.sqrt(jnp.maximum(radicand, 0.0)) * depth_step
+        damping = scale * jnp.exp(-jnp.sqrt(jnp.maximum(-radicand, 0.0)) * depth_step)
+        cosine, sine = cos_sin(vertical)
+        hre[r], him[r] = damping * cosine, core_sign() * damping * sine
+
+
+def screen(slow, slow_ref, omega, cos_ref, sin_ref):
+    cosine, sine = cos_sin(omega * (slow - slow_ref) * depth_step)
+    cos_ref[...], sin_ref[...] = cosine, core_sign() * sine
+
+
+def factors_a(radix, freq_ref, ref_ref, tw_ref, tw_out, hre, him):
+    tw_out[...] = tw_ref[...]
+    propagator(radix, 0, freq_ref, ref_ref, hre, him)
+
+
+def factors_b(radix, freq_ref, ref_ref, slow_ref, other_ref, far_ref, sent_ref, hre, him, *outs):
+    first = lax.axis_index("depth") == 0
+    _, omega = omegas_of(freq_ref)
+    propagator(radix, 1, freq_ref, ref_ref, hre, him)
+    screen(jnp.where(first, slow_ref[0], other_ref[0]), ref_ref[0], omega, *outs[:2])
+    screen(jnp.where(first, far_ref[...], sent_ref[...]), ref_ref[0], omega, *outs[2:])
+
+
+def factors_c(freq_ref, ref_ref, slow_ref, other_ref, keep_ref, got_ref, share_ref, *outs):
+    last = jnp.where(lax.axis_index("depth") == 0, other_ref[0], slow_ref[0])
+    omegas, _ = omegas_of(freq_ref)
+    share_ref[...] = keep_ref[0] * got_ref[0] + keep_ref[1] * got_ref[1]
     for f in range(2):
-        screen(last, 1, omegas[f], 4 + 2 * f)
+        screen(last, ref_ref[1], omegas[f], *outs[2 * f : 2 * f + 2])
 
 
 def call(kernel, out_shapes, scratch, args, held=True, scalars=()):
@@ -445,38 +467,47 @@
             got[step] = hop(arrays[step], step)
         return got
 
-    inner_steps = list(range(radix - 1, 0, -1))
+    inner_steps = list(range(1, radix))
     outer_steps = list(range(radix, ranks)) + list(range(1, radix))
 
-    far = lax.ppermute(slowness[0], both, [(flat(0, r), flat(0, r ^ radix)) for r in range(ranks)])
-    other = lax.ppermute(slowness, "depth", swap)
     blocks = (ranks, 2, rows, points)
     quarter = (2, 2 * rows, points)
     half_field = (2, rows, length)
     vmem, hbm = (pl.BlockSpec(memory_space=space) for space in (pltpu.VMEM, pl.ANY))
     spectra = pl.pallas_call(
         functools.partial(first_kernel, radix),
-        in_specs=[hbm, vmem, vmem],
+        in_specs=[hbm] * 3,
         out_specs=[vmem] * ranks,
         out_shape=[pltpu.VMEM(blocks[1:], jnp.float32)] * ranks,
         scratch_shapes=[
             pltpu.VMEM((freqs,) + half_field, jnp.float32),
+            pltpu.VMEM(row_tw.shape, jnp.float32),
+            pltpu.VMEM(row_forward_table.shape, jnp.bfloat16),
             pltpu.VMEM(blocks, jnp.float32),
-            pltpu.SemaphoreType.DMA((freqs,)),
+            pltpu.SemaphoreType.DMA((freqs + 2,)),
         ],
     )(planes, row_tw, row_forward_table)
-    sent = lax.ppermute(far, "depth", [(0, 1)])
     plane = (rows, length)
     factor = (col_radix, lanes, points)
-    held_tw, *factors = call(
-        functools.partial(factor_kernel, radix),
-        [row_tw.shape] + [factor] * 4 + [plane] * 8,
+    scalars = (freq_index, ref_slowness)
+    held_tw, *propagator_a = call(
+        functools.partial(factors_a, radix),
+        [row_tw.shape] + [factor] * 2,
         [],
-        (slowness, other, far, sent, row_tw),
-        scalars=(freq_index, ref_slowness),
-    )
-    propagator_a, propagator_b = factors[:2], factors[2:4]
-    screens_a, screens_b = factors[4:8], factors[8:12]
+        (row_tw,),
+        scalars=scalars,
+    )
+    far = lax.ppermute(slowness[0], both, [(flat(0, r), flat(0, r ^ radix)) for r in range(ranks)])
+    other = lax.ppermute(slowness, "depth", swap)
+    sent = lax.ppermute(far, "depth", [(0, 1)])
+    factors = call(
+        functools.partial(factors_b, radix),
+        [factor] * 2 + [plane] * 4,
+        [],
+        (slowness, other, far, sent),
+        scalars=scalars,
+    )
+    propagator_b, screens_a = factors[:2], factors[2:]
     columns = exchange(spectra, outer_steps)
     quarters = call(
         functools.partial(columns_to_quarters, col_radix, ranks),
@@ -493,7 +524,9 @@
     )
     quarters = exchange(quarters, inner_steps)
     got = lax.ppermute(send, "depth", swap)
-    share = keep[0] * got[0] + keep[1] * got[1]
+    share, *screens_b = call(
+        factors_c, [plane] * 5, [], (slowness, other, keep, got), scalars=scalars
+    )
     more = lax.ppermute(share, both, [(flat(1, r), flat(0, r ^ radix)) for r in range(ranks)])
     columns = call(
         functools.partial(quarters_to_columns, col_radix, radix),

time: 81.4 us -> 74.7 us (0.918)
  waiting for transfers between devices: 28.7 us -> 24.4 us
  starting transfers between devices: 41.1 us -> 38.5 us
    ppermute x1, waiting for transfers between devices: 3.07 us -> 0.01 us  [shards(): lax.ppermute(slowness[0], both, [(flat(0, r), flat(0, r ^ radix)) for r i...]
    ppermute x20, starting transfers between devices: 32.2 us -> 30.7 us  [hop(): return lax.ppermute(array, 'row', [(r, r ^ step) for r in range(ranks)])]
    pallas_call x6 -> x8, Pallas kernels: 7.56 us -> 8.76 us  [call(): pl.pallas_call(kernel, in_specs=[smem] * len(scalars) + [vmem] * len(args...]
    ppermute x20, waiting for transfers between devices: 19.7 us -> 18.5 us  [hop(): return lax.ppermute(array, 'row', [(r, r ^ step) for r in range(ranks)])]
    ppermute x1, starting transfers between devices: 6.1 us -> 5.01 us  [shards(): lax.ppermute(slowness[0], both, [(flat(0, r), flat(0, r ^ radix)) for r i...]
  transfers between devices with their start and end apart: 26 -> 26, of which waited for: 13 -> 11; matrix products, arithmetic and copies ran while one was open for 0% -> 0% of each run, Pallas kernels for 7% -> 8%
where the time goes in v7:
time: 74.7 us; the launch traced here: 74.5 us
  starting transfers between devices  38.5 us (52%)
  waiting for transfers between devices  24.4 us (33%)
  Pallas kernels  10.7 us (14%)
  between operations  0.83 us (1%)
    ppermute x20, starting transfers between devices, hop(): return lax.ppermute(array, 'row', [(r, r ^ step) for r in range(ranks)])  30.7 us
    ppermute x20, waiting for transfers between devices, hop(): return lax.ppermute(array, 'row', [(r, r ^ step) for r in range(ranks)])  18.5 us
    pallas_call x8, Pallas kernels, call(): pl.pallas_call(kernel, in_specs=[smem] * len(scalars) + [vmem] * len(args...  8.76 us
    ppermute x1, waiting for transfers between devices, shards(): lax.ppermute(share, both, [(flat(1, r), flat(0, r ^ radix)) for r in rang...  5.89 us
    ppermute x1, starting transfers between devices, shards(): lax.ppermute(slowness[0], both, [(flat(0, r), flat(0, r ^ radix)) for r i...  5.01 us
    pallas_call x1, Pallas kernels, shards(): pl.pallas_call(functools.partial(first_kernel, radix), in_specs=[hbm] * 3...  1.98 us
  transfers between devices with their start and end apart: 26, of which 11 were waited for; matrix products, arithmetic and copies ran while one was open for 0% of the time, Pallas kernels for 8%

profile of v7, /device:TPU:0, one launch (start us, length us, event | category | flops | bytes accessed | tf_op | source)
XLA Modules:
  0.0 74.5 jit_solution(6149127475888889933)
XLA Ops:
  0.7 2.0 %shard_map.113 = (f32[2,64,128]{2,1,0:T(8,128)S(1)}, f32[2,64,128]{2,1,0:T(8,128)S(1)}, f32[2,64,128]{2,1,0:T(8,128)S(1)}, f32[2,64,128]{2,1,0:T(8,128)S(1)}, f3...) custom-call(f32[2,4,64,512]{3,2,1,0:T(8,128)} %planes_ref.1, ...), custom_call_target="tpu_custom_call" | custom-call | tf_op jit(solution)/shard_map/pallas_call | solution.py:477
  2.7 3.1 %collective-permute-start = (f32[2,64,128]{2,1,0:T(8,128)S(1)}, f32[2,64,128]{2,1,0:T(8,128)S(1)}, u32[]{:S(2)}, u32[]{:S(2)}) collective-permute-start(f32[2,64,128]{2,1,0:T(8,128)S(1)} %get-tuple-element.43), channel_id=1, source_target_pairs={{0,1},{1,0},{2,3},{3,2},{4,5},{5,4},{6,7},{7,6},{8,9},{9,8},{10,11... | collective-permute-start | bytes 196616 | tf_op jit(solution)/shard_map/ppermute | solution.py:462
  5.7 1.6 %collective-permute-start.1 = (f32[2,64,128]{2,1,0:T(8,128)S(1)}, f32[2,64,128]{2,1,0:T(8,128)S(1)}, u32[]{:S(2)}, u32[]{:S(2)}) collective-permute-start(f32[2,64,128]{2,1,0:T(8,128)S(1)} %get-tuple-element.44), channel_id=1, source_target_pairs={{0,2},{1,3},{2,0},{3,1},{4,6},{5,7},{6,4},{7,5},{8,10},{9,11},{10,... | collective-permute-start | bytes 196616 | tf_op jit(solution)/shard_map/ppermute | solution.py:462
  7.3 5.0 %collective-permute-start.11 = (f32[64,512]{1,0:T(8,128)S(1)}, f32[64,512]{1,0:T(8,128)S(1)}, u32[]{:S(2)}, u32[]{:S(2)}) collective-permute-start(f32[64,512]{1,0:T(8,128)S(1)} %bitcast.1), channel_id=1, source_target_pairs={{0,4},{1,5},{2,6},{3,7},{4,0},{5,1},{6,2},{7,3},{16,20},{17,21},{1... | collective-permute-start | bytes 393224 | tf_op jit(solution)/shard_map/ppermute | solution.py:500
  12.4 3.9 %collective-permute-start.4 = (f32[2,64,128]{2,1,0:T(8,128)S(1)}, f32[2,64,128]{2,1,0:T(8,128)S(1)}, u32[]{:S(2)}, u32[]{:S(2)}) collective-permute-start(f32[2,64,128]{2,1,0:T(8,128)S(1)} %get-tuple-element.47), channel_id=1, source_target_pairs={{0,5},{1,4},{2,7},{3,6},{4,1},{5,0},{6,3},{7,2},{8,13},{9,12},{10,... | collective-permute-start | bytes 196616 | tf_op jit(solution)/shard_map/ppermute | solution.py:462
  16.3 1.3 %collective-permute-start.5 = (f32[2,64,128]{2,1,0:T(8,128)S(1)}, f32[2,64,128]{2,1,0:T(8,128)S(1)}, u32[]{:S(2)}, u32[]{:S(2)}) collective-permute-start(f32[2,64,128]{2,1,0:T(8,128)S(1)} %get-tuple-element.48), channel_id=1, source_target_pairs={{0,6},{1,7},{2,4},{3,5},{4,2},{5,3},{6,0},{7,1},{8,14},{9,15},{10,... | collective-permute-start | bytes 196616 | tf_op jit(solution)/shard_map/ppermute | solution.py:462
  17.6 2.4 %collective-permute-start.6 = (f32[2,64,128]{2,1,0:T(8,128)S(1)}, f32[2,64,128]{2,1,0:T(8,128)S(1)}, u32[]{:S(2)}, u32[]{:S(2)}) collective-permute-start(f32[2,64,128]{2,1,0:T(8,128)S(1)} %get-tuple-element.49), channel_id=1, source_target_pairs={{0,7},{1,6},{2,5},{3,4},{4,3},{5,2},{6,1},{7,0},{8,15},{9,14},{10,... | collective-permute-start | bytes 196616 | tf_op jit(solution)/shard_map/ppermute | solution.py:462
  21.3 2.6 %collective-permute-done.3.refs_4_ = f32[2,64,128]{2,1,0:T(8,128)S(1)} collective-permute-done((f32[2,64,128]{2,1,0:T(8,128)S(1)}, f32[2,64,128]{2,1,0:T(8,128)S(1)}, u32[]{:S(2)}, u32[]{:S(2)}) %collective-permute-start.3) | collective-permute-done | bytes 65568 | tf_op jit(solution)/shard_map/ppermute | solution.py:462
  23.9 1.6 %collective-permute-done.4.refs_5_ = f32[2,64,128]{2,1,0:T(8,128)S(1)} collective-permute-done((f32[2,64,128]{2,1,0:T(8,128)S(1)}, f32[2,64,128]{2,1,0:T(8,128)S(1)}, u32[]{:S(2)}, u32[]{:S(2)}) %collective-permute-start.4) | collective-permute-done | bytes 65568 | tf_op jit(solution)/shard_map/ppermute | solution.py:462
  29.1 2.0 %collective-permute-start.8 = (f32[2,128,128]{2,1,0:T(8,128)S(1)}, f32[2,128,128]{2,1,0:T(8,128)S(1)}, u32[]{:S(2)}, u32[]{:S(2)}) collective-permute-start(f32[2,128,128]{2,1,0:T(8,128)S(1)} %get-tuple-element.54), channel_id=1, source_target_pairs={{0,2},{1,3},{2,0},{3,1},{4,6},{5,7},{6,4},{7,5},{8,10},{9,11},{10,... | collective-permute-start | bytes 393224 | tf_op jit(solution)/shard_map/ppermute | solution.py:462
  31.6 1.7 %shard_map.116 = (f32[4,128,128]{2,1,0:T(8,128)S(1)}, f32[4,128,128]{2,1,0:T(8,128)S(1)}, f32[64,512]{1,0:T(8,128)S(1)}, f32[64,512]{1,0:T(8,128)S(1)}, f32[64,512]{1,0:T(8,128)S(1)}, /*index=5*/f32[64,512]{1,0:T(8,128)S(1)}) custom-call(s32[2]{0:T(128)S(1)} %copy-done.5, f32[2]{0:T(128)S(1)} %copy-done.6, f32[1,64,512]{2,1,0:T(8,128)S(1)} %copy-done.2, ...), custom_call_target="tpu_custom_call" | custom-call | tf_op jit(solution)/shard_map/pallas_call | solution.py:434
  33.3 1.7 %collective-permute-done.8.refs_2_ = f32[2,128,128]{2,1,0:T(8,128)S(1)} collective-permute-done((f32[2,128,128]{2,1,0:T(8,128)S(1)}, f32[2,128,128]{2,1,0:T(8,128)S(1)}, u32[]{:S(2)}, u32[]{:S(2)}) %collective-permute-start.8) | collective-permute-done | bytes 131104 | tf_op jit(solution)/shard_map/ppermute | solution.py:462
  35.0 2.0 %collective-permute-done.9.refs_3_ = f32[2,128,128]{2,1,0:T(8,128)S(1)} collective-permute-done((f32[2,128,128]{2,1,0:T(8,128)S(1)}, f32[2,128,128]{2,1,0:T(8,128)S(1)}, u32[]{:S(2)}, u32[]{:S(2)}) %collective-permute-start.9) | collective-permute-done | bytes 131104 | tf_op jit(solution)/shard_map/ppermute | solution.py:462
  40.3 1.5 %collective-permute-start.15 = (f32[2,128,128]{2,1,0:T(8,128)S(1)}, f32[2,128,128]{2,1,0:T(8,128)S(1)}, u32[]{:S(2)}, u32[]{:S(2)}) collective-permute-start(f32[2,128,128]{2,1,0:T(8,128)S(1)} %get-tuple-element.64), channel_id=1, source_target_pairs={{0,3},{1,2},{2,1},{3,0},{4,7},{5,6},{6,5},{7,4},{8,11},{9,10},{10,... | collective-permute-start | bytes 393224 | tf_op jit(solution)/shard_map/ppermute | solution.py:462
  41.8 2.3 %collective-permute-done.13.refs_1_ = f32[2,128,128]{2,1,0:T(8,128)S(1)} collective-permute-done((f32[2,128,128]{2,1,0:T(8,128)S(1)}, f32[2,128,128]{2,1,0:T(8,128)S(1)}, u32[]{:S(2)}, u32[]{:S(2)}) %collective-permute-start.13) | collective-permute-done | bytes 131104 | tf_op jit(solution)/shard_map/ppermute | solution.py:462
  44.2 1.5 %collective-permute-done.14.refs_2_ = f32[2,128,128]{2,1,0:T(8,128)S(1)} collective-permute-done((f32[2,128,128]{2,1,0:T(8,128)S(1)}, f32[2,128,128]{2,1,0:T(8,128)S(1)}, u32[]{:S(2)}, u32[]{:S(2)}) %collective-permute-start.14) | collective-permute-done | bytes 131104 | tf_op jit(solution)/shard_map/ppermute | solution.py:462
  45.7 2.5 %collective-permute-done.15.refs_3_ = f32[2,128,128]{2,1,0:T(8,128)S(1)} collective-permute-done((f32[2,128,128]{2,1,0:T(8,128)S(1)}, f32[2,128,128]{2,1,0:T(8,128)S(1)}, u32[]{:S(2)}, u32[]{:S(2)}) %collective-permute-start.15) | collective-permute-done | bytes 131104 | tf_op jit(solution)/shard_map/ppermute | solution.py:462
  51.3 1.5 %collective-permute-start.18 = (f32[2,64,128]{2,1,0:T(8,128)S(1)}, f32[2,64,128]{2,1,0:T(8,128)S(1)}, u32[]{:S(2)}, u32[]{:S(2)}) collective-permute-start(f32[2,64,128]{2,1,0:T(8,128)S(1)} %get-tuple-element.70), channel_id=1, source_target_pairs={{0,3},{1,2},{2,1},{3,0},{4,7},{5,6},{6,5},{7,4},{8,11},{9,10},{10,... | collective-permute-start | bytes 196616 | tf_op jit(solution)/shard_map/ppermute | solution.py:462
  52.8 2.1 %collective-permute-start.19 = (f32[2,64,128]{2,1,0:T(8,128)S(1)}, f32[2,64,128]{2,1,0:T(8,128)S(1)}, u32[]{:S(2)}, u32[]{:S(2)}) collective-permute-start(f32[2,64,128]{2,1,0:T(8,128)S(1)} %get-tuple-element.71), channel_id=1, source_target_pairs={{0,4},{1,5},{2,6},{3,7},{4,0},{5,1},{6,2},{7,3},{8,12},{9,13},{10,... | collective-permute-start | bytes 196616 | tf_op jit(solution)/shard_map/ppermute | solution.py:462
  56.1 2.7 %collective-permute-start.21 = (f32[2,64,128]{2,1,0:T(8,128)S(1)}, f32[2,64,128]{2,1,0:T(8,128)S(1)}, u32[]{:S(2)}, u32[]{:S(2)}) collective-permute-start(f32[2,64,128]{2,1,0:T(8,128)S(1)} %get-tuple-element.73), channel_id=1, source_target_pairs={{0,6},{1,7},{2,4},{3,5},{4,2},{5,3},{6,0},{7,1},{8,14},{9,15},{10,... | collective-permute-start | bytes 196616 | tf_op jit(solution)/shard_map/ppermute | solution.py:462
  58.8 1.6 %collective-permute-start.22 = (f32[2,64,128]{2,1,0:T(8,128)S(1)}, f32[2,64,128]{2,1,0:T(8,128)S(1)}, u32[]{:S(2)}, u32[]{:S(2)}) collective-permute-start(f32[2,64,128]{2,1,0:T(8,128)S(1)} %get-tuple-element.74), channel_id=1, source_target_pairs={{0,7},{1,6},{2,5},{3,4},{4,3},{5,2},{6,1},{7,0},{8,15},{9,14},{10,... | collective-permute-start | bytes 196616 | tf_op jit(solution)/shard_map/ppermute | solution.py:462
  61.5 1.4 %collective-permute-done.19.refs_4_ = f32[2,64,128]{2,1,0:T(8,128)S(1)} collective-permute-done((f32[2,64,128]{2,1,0:T(8,128)S(1)}, f32[2,64,128]{2,1,0:T(8,128)S(1)}, u32[]{:S(2)}, u32[]{:S(2)}) %collective-permute-start.19) | collective-permute-done | bytes 65568 | tf_op jit(solution)/shard_map/ppermute | solution.py:462
  62.9 1.7 %collective-permute-done.20.refs_5_ = f32[2,64,128]{2,1,0:T(8,128)S(1)} collective-permute-done((f32[2,64,128]{2,1,0:T(8,128)S(1)}, f32[2,64,128]{2,1,0:T(8,128)S(1)}, u32[]{:S(2)}, u32[]{:S(2)}) %collective-permute-start.20) | collective-permute-done | bytes 65568 | tf_op jit(solution)/shard_map/ppermute | solution.py:462
  67.7 5.9 %collective-permute-done.25.more_ref = f32[64,512]{1,0:T(8,128)S(1)} collective-permute-done((f32[64,512]{1,0:T(8,128)S(1)}, f32[64,512]{1,0:T(8,128)S(1)}, u32[]{:S(2)}, u32[]{:S(2)}) %collective-permute-start.25) | collective-permute-done | bytes 131104 | tf_op jit(solution)/shard_map/ppermute | solution.py:530
  (51 shorter events, 18.1 us)
Async XLA Ops:
  2.7 9.7 %collective-permute-start = (f32[2,64,128]{2,1,0:T(8,128)S(1)}, f32[2,64,128]{2,1,0:T(8,128)S(1)}, u32[]{:S(2)}, u32[]{:S(2)}) collective-permute-start(f32[2,64,128]{2,1,0:T(8,128)S(1)} %get-tuple-element.43), channel_id=1, source_target_pairs={{0,1},{1,0},{2,3},{3,2},{4,5},{5,4},{6,7},{7,6},{8,9},{9,8},{10,11... | collective-permute-start | bytes 196616 | tf_op jit(solution)/shard_map/ppermute | solution.py:462
  5.7 10.6 %collective-permute-start.1 = (f32[2,64,128]{2,1,0:T(8,128)S(1)}, f32[2,64,128]{2,1,0:T(8,128)S(1)}, u32[]{:S(2)}, u32[]{:S(2)}) collective-permute-start(f32[2,64,128]{2,1,0:T(8,128)S(1)} %get-tuple-element.44), channel_id=1, source_target_pairs={{0,2},{1,3},{2,0},{3,1},{4,6},{5,7},{6,4},{7,5},{8,10},{9,11},{10,... | collective-permute-start | bytes 196616 | tf_op jit(solution)/shard_map/ppermute | solution.py:462
  7.3 10.3 %collective-permute-start.2 = (f32[2,64,128]{2,1,0:T(8,128)S(1)}, f32[2,64,128]{2,1,0:T(8,128)S(1)}, u32[]{:S(2)}, u32[]{:S(2)}) collective-permute-start(f32[2,64,128]{2,1,0:T(8,128)S(1)} %get-tuple-element.45), channel_id=1, source_target_pairs={{0,3},{1,2},{2,1},{3,0},{4,7},{5,6},{6,5},{7,4},{8,11},{9,10},{10,... | collective-permute-start | bytes 196616 | tf_op jit(solution)/shard_map/ppermute | solution.py:462
  7.3 20.4 %collective-permute-start.11 = (f32[64,512]{1,0:T(8,128)S(1)}, f32[64,512]{1,0:T(8,128)S(1)}, u32[]{:S(2)}, u32[]{:S(2)}) collective-permute-start(f32[64,512]{1,0:T(8,128)S(1)} %bitcast.1), channel_id=1, source_target_pairs={{0,4},{1,5},{2,6},{3,7},{4,0},{5,1},{6,2},{7,3},{16,20},{17,21},{1... | collective-permute-start | bytes 393224 | tf_op jit(solution)/shard_map/ppermute | solution.py:500
  12.3 11.6 %collective-permute-start.3 = (f32[2,64,128]{2,1,0:T(8,128)S(1)}, f32[2,64,128]{2,1,0:T(8,128)S(1)}, u32[]{:S(2)}, u32[]{:S(2)}) collective-permute-start(f32[2,64,128]{2,1,0:T(8,128)S(1)} %get-tuple-element.46), channel_id=1, source_target_pairs={{0,4},{1,5},{2,6},{3,7},{4,0},{5,1},{6,2},{7,3},{8,12},{9,13},{10,... | collective-permute-start | bytes 196616 | tf_op jit(solution)/shard_map/ppermute | solution.py:462
  12.4 13.1 %collective-permute-start.4 = (f32[2,64,128]{2,1,0:T(8,128)S(1)}, f32[2,64,128]{2,1,0:T(8,128)S(1)}, u32[]{:S(2)}, u32[]{:S(2)}) collective-permute-start(f32[2,64,128]{2,1,0:T(8,128)S(1)} %get-tuple-element.47), channel_id=1, source_target_pairs={{0,5},{1,4},{2,7},{3,6},{4,1},{5,0},{6,3},{7,2},{8,13},{9,12},{10,... | collective-permute-start | bytes 196616 | tf_op jit(solution)/shard_map/ppermute | solution.py:462
  16.3 9.2 %collective-permute-start.5 = (f32[2,64,128]{2,1,0:T(8,128)S(1)}, f32[2,64,128]{2,1,0:T(8,128)S(1)}, u32[]{:S(2)}, u32[]{:S(2)}) collective-permute-start(f32[2,64,128]{2,1,0:T(8,128)S(1)} %get-tuple-element.48), channel_id=1, source_target_pairs={{0,6},{1,7},{2,4},{3,5},{4,2},{5,3},{6,0},{7,1},{8,14},{9,15},{10,... | collective-permute-start | bytes 196616 | tf_op jit(solution)/shard_map/ppermute | solution.py:462
  17.6 7.9 %collective-permute-start.6 = (f32[2,64,128]{2,1,0:T(8,128)S(1)}, f32[2,64,128]{2,1,0:T(8,128)S(1)}, u32[]{:S(2)}, u32[]{:S(2)}) collective-permute-start(f32[2,64,128]{2,1,0:T(8,128)S(1)} %get-tuple-element.49), channel_id=1, source_target_pairs={{0,7},{1,6},{2,5},{3,4},{4,3},{5,2},{6,1},{7,0},{8,15},{9,14},{10,... | collective-permute-start | bytes 196616 | tf_op jit(solution)/shard_map/ppermute | solution.py:462
  23.9 7.6 %collective-permute-start.10 = (f32[1,64,512]{2,1,0:T(8,128)S(1)}, f32[1,64,512]{2,1,0:T(8,128)S(1)}, u32[]{:S(2)}, u32[]{:S(2)}) collective-permute-start(f32[1,64,512]{2,1,0:T(8,128)S(1)} %copy-done.2), channel_id=1, source_target_pairs={{0,8},{8,0},{1,9},{9,1},{2,10},{10,2},{3,11},{11,3},{4,12},{12,4},... | collective-permute-start | bytes 393224 | tf_op jit(solution)/shard_map/ppermute | solution.py:501
  26.6 6.7 %collective-permute-start.7 = (f32[2,128,128]{2,1,0:T(8,128)S(1)}, f32[2,128,128]{2,1,0:T(8,128)S(1)}, u32[]{:S(2)}, u32[]{:S(2)}) collective-permute-start(f32[2,128,128]{2,1,0:T(8,128)S(1)} %get-tuple-element.53), channel_id=1, source_target_pairs={{0,1},{1,0},{2,3},{3,2},{4,5},{5,4},{6,7},{7,6},{8,9},{9,8},{10,11... | collective-permute-start | bytes 393224 | tf_op jit(solution)/shard_map/ppermute | solution.py:462
  29.1 5.9 %collective-permute-start.8 = (f32[2,128,128]{2,1,0:T(8,128)S(1)}, f32[2,128,128]{2,1,0:T(8,128)S(1)}, u32[]{:S(2)}, u32[]{:S(2)}) collective-permute-start(f32[2,128,128]{2,1,0:T(8,128)S(1)} %get-tuple-element.54), channel_id=1, source_target_pairs={{0,2},{1,3},{2,0},{3,1},{4,6},{5,7},{6,4},{7,5},{8,10},{9,11},{10,... | collective-permute-start | bytes 393224 | tf_op jit(solution)/shard_map/ppermute | solution.py:462
  31.1 5.9 %collective-permute-start.9 = (f32[2,128,128]{2,1,0:T(8,128)S(1)}, f32[2,128,128]{2,1,0:T(8,128)S(1)}, u32[]{:S(2)}, u32[]{:S(2)}) collective-permute-start(f32[2,128,128]{2,1,0:T(8,128)S(1)} %get-tuple-element.55), channel_id=1, source_target_pairs={{0,3},{1,2},{2,1},{3,0},{4,7},{5,6},{6,5},{7,4},{8,11},{9,10},{10,... | collective-permute-start | bytes 393224 | tf_op jit(solution)/shard_map/ppermute | solution.py:462
  38.2 20.6 %collective-permute-start.23 = (f32[2,64,512]{2,1,0:T(8,128)S(1)}, f32[2,64,512]{2,1,0:T(8,128)S(1)}, u32[]{:S(2)}, u32[]{:S(2)}) collective-permute-start(f32[2,64,512]{2,1,0:T(8,128)S(1)} %get-tuple-element.76), channel_id=1, source_target_pairs={{0,8},{8,0},{1,9},{9,1},{2,10},{10,2},{3,11},{11,3},{4,12},{12,4},... | collective-permute-start | bytes 786440 | tf_op jit(solution)/shard_map/ppermute | solution.py:526
  38.3 5.9 %collective-permute-start.13 = (f32[2,128,128]{2,1,0:T(8,128)S(1)}, f32[2,128,128]{2,1,0:T(8,128)S(1)}, u32[]{:S(2)}, u32[]{:S(2)}) collective-permute-start(f32[2,128,128]{2,1,0:T(8,128)S(1)} %get-tuple-element.62), channel_id=1, source_target_pairs={{0,1},{1,0},{2,3},{3,2},{4,5},{5,4},{6,7},{7,6},{8,9},{9,8},{10,11... | collective-permute-start | bytes 393224 | tf_op jit(solution)/shard_map/ppermute | solution.py:462
  39.3 6.4 %collective-permute-start.14 = (f32[2,128,128]{2,1,0:T(8,128)S(1)}, f32[2,128,128]{2,1,0:T(8,128)S(1)}, u32[]{:S(2)}, u32[]{:S(2)}) collective-permute-start(f32[2,128,128]{2,1,0:T(8,128)S(1)} %get-tuple-element.63), channel_id=1, source_target_pairs={{0,2},{1,3},{2,0},{3,1},{4,6},{5,7},{6,4},{7,5},{8,10},{9,11},{10,... | collective-permute-start | bytes 393224 | tf_op jit(solution)/shard_map/ppermute | solution.py:462
  40.3 7.8 %collective-permute-start.15 = (f32[2,128,128]{2,1,0:T(8,128)S(1)}, f32[2,128,128]{2,1,0:T(8,128)S(1)}, u32[]{:S(2)}, u32[]{:S(2)}) collective-permute-start(f32[2,128,128]{2,1,0:T(8,128)S(1)} %get-tuple-element.64), channel_id=1, source_target_pairs={{0,3},{1,2},{2,1},{3,0},{4,7},{5,6},{6,5},{7,4},{8,11},{9,10},{10,... | collective-permute-start | bytes 393224 | tf_op jit(solution)/shard_map/ppermute | solution.py:462
  50.3 5.9 %collective-permute-start.17 = (f32[2,64,128]{2,1,0:T(8,128)S(1)}, f32[2,64,128]{2,1,0:T(8,128)S(1)}, u32[]{:S(2)}, u32[]{:S(2)}) collective-permute-start(f32[2,64,128]{2,1,0:T(8,128)S(1)} %get-tuple-element.69), channel_id=1, source_target_pairs={{0,2},{1,3},{2,0},{3,1},{4,6},{5,7},{6,4},{7,5},{8,10},{9,11},{10,... | collective-permute-start | bytes 196616 | tf_op jit(solution)/shard_map/ppermute | solution.py:462
  51.3 10.2 %collective-permute-start.18 = (f32[2,64,128]{2,1,0:T(8,128)S(1)}, f32[2,64,128]{2,1,0:T(8,128)S(1)}, u32[]{:S(2)}, u32[]{:S(2)}) collective-permute-start(f32[2,64,128]{2,1,0:T(8,128)S(1)} %get-tuple-element.70), channel_id=1, source_target_pairs={{0,3},{1,2},{2,1},{3,0},{4,7},{5,6},{6,5},{7,4},{8,11},{9,10},{10,... | collective-permute-start | bytes 196616 | tf_op jit(solution)/shard_map/ppermute | solution.py:462
  52.8 10.1 %collective-permute-start.19 = (f32[2,64,128]{2,1,0:T(8,128)S(1)}, f32[2,64,128]{2,1,0:T(8,128)S(1)}, u32[]{:S(2)}, u32[]{:S(2)}) collective-permute-start(f32[2,64,128]{2,1,0:T(8,128)S(1)} %get-tuple-element.71), channel_id=1, source_target_pairs={{0,4},{1,5},{2,6},{3,7},{4,0},{5,1},{6,2},{7,3},{8,12},{9,13},{10,... | collective-permute-start | bytes 196616 | tf_op jit(solution)/shard_map/ppermute | solution.py:462
  54.9 9.7 %collective-permute-start.20 = (f32[2,64,128]{2,1,0:T(8,128)S(1)}, f32[2,64,128]{2,1,0:T(8,128)S(1)}, u32[]{:S(2)}, u32[]{:S(2)}) collective-permute-start(f32[2,64,128]{2,1,0:T(8,128)S(1)} %get-tuple-element.72), channel_id=1, source_target_pairs={{0,5},{1,4},{2,7},{3,6},{4,1},{5,0},{6,3},{7,2},{8,13},{9,12},{10,... | collective-permute-start | bytes 196616 | tf_op jit(solution)/shard_map/ppermute | solution.py:462
  56.1 8.5 %collective-permute-start.21 = (f32[2,64,128]{2,1,0:T(8,128)S(1)}, f32[2,64,128]{2,1,0:T(8,128)S(1)}, u32[]{:S(2)}, u32[]{:S(2)}) collective-permute-start(f32[2,64,128]{2,1,0:T(8,128)S(1)} %get-tuple-element.73), channel_id=1, source_target_pairs={{0,6},{1,7},{2,4},{3,5},{4,2},{5,3},{6,0},{7,1},{8,14},{9,15},{10,... | collective-permute-start | bytes 196616 | tf_op jit(solution)/shard_map/ppermute | solution.py:462
  58.8 7.1 %collective-permute-start.22 = (f32[2,64,128]{2,1,0:T(8,128)S(1)}, f32[2,64,128]{2,1,0:T(8,128)S(1)}, u32[]{:S(2)}, u32[]{:S(2)}) collective-permute-start(f32[2,64,128]{2,1,0:T(8,128)S(1)} %get-tuple-element.74), channel_id=1, source_target_pairs={{0,7},{1,6},{2,5},{3,4},{4,3},{5,2},{6,1},{7,0},{8,15},{9,14},{10,... | collective-permute-start | bytes 196616 | tf_op jit(solution)/shard_map/ppermute | solution.py:462
  66.3 7.3 %collective-permute-start.24 = (f32[2,2,64,512]{3,2,1,0:T(8,128)S(1)}, f32[2,2,64,512]{3,2,1,0:T(8,128)S(1)}, u32[]{:S(2)}, u32[]{:S(2)}) collective-permute-start(f32[2,2,64,512]{3,2,1,0:T(8,128)S(1)} %shard_map.120.own_ref), channel_id=1, source_target_pairs={{0,8},{8,0},{1,9},{9,1},{2,10},{10,2},{3,11},{11,3},{4,12},{12,4},... | collective-permute-start | bytes 1572872 | tf_op jit(solution)/shard_map/ppermute | solution.py:544
  66.4 7.2 %collective-permute-start.25 = (f32[64,512]{1,0:T(8,128)S(1)}, f32[64,512]{1,0:T(8,128)S(1)}, u32[]{:S(2)}, u32[]{:S(2)}) collective-permute-start(f32[64,512]{1,0:T(8,128)S(1)} %get-tuple-element.81.share_ref), channel_id=1, source_target_pairs={{8,4},{9,5},{10,6},{11,7},{12,0},{13,1},{14,2},{15,3},{24,20},{25,... | collective-permute-start | bytes 393224 | tf_op jit(solution)/shard_map/ppermute | solution.py:530
  (9 other events, 111.1 us)

commit v8 on v7

--- a/solution.py
+++ b/solution.py
@@ -276,7 +276,7 @@
             for i in range(2):
                 field[half, i, :, at] = part[i][half * rows // 2 : (half + 1) * rows // 2]
         turned.append(part)
-    kept = mine ^ lax.axis_index("depth")
+    kept = mine ^ lax.axis_index("depth") ^ 1
     keep_ref[...] = field[kept]
     send_ref[...] = field[1 - kept]
     value = row_forward([turned], tw, forward)
@@ -323,29 +323,31 @@
 
 
 def last_kernel(radix, ranks, *refs):
-    in_refs, screens, (tw, inverse, out_ref, held) = refs[:ranks], refs[ranks : ranks + 4], refs[ranks + 4 :]
+    in_refs, screens, refs = refs[:ranks], refs[ranks : ranks + 4], refs[ranks + 4 :]
+    share_ref, tw, inverse, out_ref, held = refs
     points = held.shape[3]
+    out_ref[4] = share_ref[...]
     collect(in_refs, held, lax.axis_index("row"))
     for f, parts in enumerate(row_inverse(held, tw, inverse, radix, 2)):
         for m, part in enumerate(parts):
             at = slice(m * points, (m + 1) * points)
             factor = (screens[2 * f][:, at], screens[2 * f + 1][:, at])
             re, im = turn(part, factor, False)
-            out_ref[f, 0, :, at] = re
-            out_ref[f, 1, :, at] = im
-
-
-def output_kernel(own_ref, got_ref, share_ref, more_ref, image_ref, leaving_ref):
+            out_ref[2 * f, :, at] = re
+            out_ref[2 * f + 1, :, at] = im
+
+
+def output_kernel(own_ref, got_ref, more_ref, image_ref, leaving_ref):
     for core, (source, receiver) in enumerate(((own_ref, got_ref), (got_ref, own_ref))):
 
         @pl.when(lax.axis_index("depth") == core)
         def _():
-            leaving_ref[0, 0:2] = source[core]
-            leaving_ref[0, 2:4] = receiver[core]
+            leaving_ref[0, 0:2] = source[2 * core : 2 * core + 2]
+            leaving_ref[0, 2:4] = receiver[2 * core : 2 * core + 2]
             if core == 0:
-                image_ref[0] = share_ref[...] + more_ref[...]
+                image_ref[0] = got_ref[4] + more_ref[...]
             else:
-                terms = [source[f, i] * receiver[f, i] for f in range(2) for i in range(2)]
+                terms = [source[i] * receiver[i] for i in range(4)]
                 image_ref[0] = (terms[0] + terms[1]) + (terms[2] + terms[3])
 
 
@@ -411,15 +413,15 @@
     propagator(radix, 0, freq_ref, ref_ref, hre, him)
 
 
-def factors_b(radix, freq_ref, ref_ref, slow_ref, other_ref, far_ref, sent_ref, hre, him, *outs):
+def factors_b(freq_ref, ref_ref, slow_ref, other_ref, far_ref, sent_ref, *outs):
     first = lax.axis_index("depth") == 0
     _, omega = omegas_of(freq_ref)
-    propagator(radix, 1, freq_ref, ref_ref, hre, him)
     screen(jnp.where(first, slow_ref[0], other_ref[0]), ref_ref[0], omega, *outs[:2])
     screen(jnp.where(first, far_ref[...], sent_ref[...]), ref_ref[0], omega, *outs[2:])
 
 
-def factors_c(freq_ref, ref_ref, slow_ref, other_ref, keep_ref, got_ref, share_ref, *outs):
+def factors_c(radix, freq_ref, ref_ref, slow_ref, other_ref, keep_ref, got_ref, hre, him, share_ref, *outs):
+    propagator(radix, 1, freq_ref, ref_ref, hre, him)
     last = jnp.where(lax.axis_index("depth") == 0, other_ref[0], slow_ref[0])
     omegas, _ = omegas_of(freq_ref)
     share_ref[...] = keep_ref[0] * got_ref[0] + keep_ref[1] * got_ref[1]
@@ -500,14 +502,7 @@
     far = lax.ppermute(slowness[0], both, [(flat(0, r), flat(0, r ^ radix)) for r in range(ranks)])
     other = lax.ppermute(slowness, "depth", swap)
     sent = lax.ppermute(far, "depth", [(0, 1)])
-    factors = call(
-        functools.partial(factors_b, radix),
-        [factor] * 2 + [plane] * 4,
-        [],
-        (slowness, other, far, sent),
-        scalars=scalars,
-    )
-    propagator_b, screens_a = factors[:2], factors[2:]
+    screens_a = call(factors_b, [plane] * 4, [], (slowness, other, far, sent), scalars=scalars)
     columns = exchange(spectra, outer_steps)
     quarters = call(
         functools.partial(columns_to_quarters, col_radix, ranks),
@@ -524,10 +519,15 @@
     )
     quarters = exchange(quarters, inner_steps)
     got = lax.ppermute(send, "depth", swap)
-    share, *screens_b = call(
-        factors_c, [plane] * 5, [], (slowness, other, keep, got), scalars=scalars
-    )
-    more = lax.ppermute(share, both, [(flat(1, r), flat(0, r ^ radix)) for r in range(ranks)])
+    factors = call(
+        functools.partial(factors_c, radix),
+        [factor] * 2 + [plane] * 5,
+        [],
+        (slowness, other, keep, got),
+        scalars=scalars,
+    )
+    propagator_b, share, screens_b = factors[:2], factors[2], factors[3:]
+    more = lax.ppermute(share, both, [(flat(0, r), flat(0, r ^ radix)) for r in range(ranks)])
     columns = call(
         functools.partial(quarters_to_columns, col_radix, radix),
         [blocks[1:]] * ranks,
@@ -537,16 +537,16 @@
     cells = exchange(columns, outer_steps)
     (fields,) = call(
         functools.partial(last_kernel, radix, ranks),
-        [(freqs,) + half_field],
+        [(2 * freqs + 1,) + plane],
         [blocks],
-        (*cells, *screens_b, held_tw, row_inverse_table),
+        (*cells, *screens_b, share, held_tw, row_inverse_table),
     )
     swapped = lax.ppermute(fields, "depth", swap)
     image, leaving = call(
         output_kernel,
         [(1, rows, length), (1,) + planes.shape[1:]],
         [],
-        (fields, swapped, share, more),
+        (fields, swapped, more),
         held=False,
     )
     return image, leaving

time: 74.7 us -> 75.3 us (level)
  starting transfers between devices: 38.5 us -> 41.3 us
  waiting for transfers between devices: 24.4 us -> 22.2 us
    ppermute x1, starting transfers between devices: 1.29 us -> 4.1 us  [shards(): lax.ppermute(share, both, [(flat(0, r), flat(0, r ^ radix)) for r in rang...]
    ppermute x1, waiting for transfers between devices: 5.89 us -> 3.65 us  [shards(): lax.ppermute(share, both, [(flat(0, r), flat(0, r ^ radix)) for r in rang...]
  transfers between devices with their start and end apart: 26 -> 26, of which waited for: 11 -> 11; matrix products, arithmetic and copies ran while one was open for 0% -> 0% of each run, Pallas kernels for 8% -> 7%
where the time goes in v8:
time: 75.3 us; the launch traced here: 75.1 us
  starting transfers between devices  41.3 us (55%)
  waiting for transfers between devices  22.2 us (29%)
  Pallas kernels  10.8 us (14%)
  between operations  0.82 us (1%)
    ppermute x20, starting transfers between devices, hop(): return lax.ppermute(array, 'row', [(r, r ^ step) for r in range(ranks)])  30.7 us
    ppermute x20, waiting for transfers between devices, hop(): return lax.ppermute(array, 'row', [(r, r ^ step) for r in range(ranks)])  18.5 us
    pallas_call x8, Pallas kernels, call(): pl.pallas_call(kernel, in_specs=[smem] * len(scalars) + [vmem] * len(args...  8.77 us
    ppermute x1, starting transfers between devices, shards(): lax.ppermute(slowness[0], both, [(flat(0, r), flat(0, r ^ radix)) for r i...  5.01 us
    ppermute x1, starting transfers between devices, shards(): lax.ppermute(share, both, [(flat(0, r), flat(0, r ^ radix)) for r in rang...  4.1 us
    ppermute x1, waiting for transfers between devices, shards(): lax.ppermute(share, both, [(flat(0, r), flat(0, r ^ radix)) for r in rang...  3.65 us
    pallas_call x1, Pallas kernels, shards(): pl.pallas_call(functools.partial(first_kernel, radix), in_specs=[hbm] * 3...  1.98 us
  transfers between devices with their start and end apart: 26, of which 11 were waited for; matrix products, arithmetic and copies ran while one was open for 0% of the time, Pallas kernels for 7%

profile of v8, /device:TPU:0, one launch (start us, length us, event | category | flops | bytes accessed | tf_op | source)
XLA Modules:
  0.0 75.1 jit_solution(16711443001056824442)
XLA Ops:
  0.7 2.0 %shard_map.113 = (f32[2,64,128]{2,1,0:T(8,128)S(1)}, f32[2,64,128]{2,1,0:T(8,128)S(1)}, f32[2,64,128]{2,1,0:T(8,128)S(1)}, f32[2,64,128]{2,1,0:T(8,128)S(1)}, f3...) custom-call(f32[2,4,64,512]{3,2,1,0:T(8,128)} %planes_ref.1, ...), custom_call_target="tpu_custom_call" | custom-call | tf_op jit(solution)/shard_map/pallas_call | solution.py:479
  2.7 3.1 %collective-permute-start = (f32[2,64,128]{2,1,0:T(8,128)S(1)}, f32[2,64,128]{2,1,0:T(8,128)S(1)}, u32[]{:S(2)}, u32[]{:S(2)}) collective-permute-start(f32[2,64,128]{2,1,0:T(8,128)S(1)} %get-tuple-element.43), channel_id=1, source_target_pairs={{0,1},{1,0},{2,3},{3,2},{4,5},{5,4},{6,7},{7,6},{8,9},{9,8},{10,11... | collective-permute-start | bytes 196616 | tf_op jit(solution)/shard_map/ppermute | solution.py:464
  5.7 1.6 %collective-permute-start.1 = (f32[2,64,128]{2,1,0:T(8,128)S(1)}, f32[2,64,128]{2,1,0:T(8,128)S(1)}, u32[]{:S(2)}, u32[]{:S(2)}) collective-permute-start(f32[2,64,128]{2,1,0:T(8,128)S(1)} %get-tuple-element.44), channel_id=1, source_target_pairs={{0,2},{1,3},{2,0},{3,1},{4,6},{5,7},{6,4},{7,5},{8,10},{9,11},{10,... | collective-permute-start | bytes 196616 | tf_op jit(solution)/shard_map/ppermute | solution.py:464
  7.3 5.0 %collective-permute-start.11 = (f32[64,512]{1,0:T(8,128)S(1)}, f32[64,512]{1,0:T(8,128)S(1)}, u32[]{:S(2)}, u32[]{:S(2)}) collective-permute-start(f32[64,512]{1,0:T(8,128)S(1)} %bitcast.1), channel_id=1, source_target_pairs={{0,4},{1,5},{2,6},{3,7},{4,0},{5,1},{6,2},{7,3},{16,20},{17,21},{1... | collective-permute-start | bytes 393224 | tf_op jit(solution)/shard_map/ppermute | solution.py:502
  12.4 3.9 %collective-permute-start.4 = (f32[2,64,128]{2,1,0:T(8,128)S(1)}, f32[2,64,128]{2,1,0:T(8,128)S(1)}, u32[]{:S(2)}, u32[]{:S(2)}) collective-permute-start(f32[2,64,128]{2,1,0:T(8,128)S(1)} %get-tuple-element.47), channel_id=1, source_target_pairs={{0,5},{1,4},{2,7},{3,6},{4,1},{5,0},{6,3},{7,2},{8,13},{9,12},{10,... | collective-permute-start | bytes 196616 | tf_op jit(solution)/shard_map/ppermute | solution.py:464
  16.3 1.3 %collective-permute-start.5 = (f32[2,64,128]{2,1,0:T(8,128)S(1)}, f32[2,64,128]{2,1,0:T(8,128)S(1)}, u32[]{:S(2)}, u32[]{:S(2)}) collective-permute-start(f32[2,64,128]{2,1,0:T(8,128)S(1)} %get-tuple-element.48), channel_id=1, source_target_pairs={{0,6},{1,7},{2,4},{3,5},{4,2},{5,3},{6,0},{7,1},{8,14},{9,15},{10,... | collective-permute-start | bytes 196616 | tf_op jit(solution)/shard_map/ppermute | solution.py:464
  17.6 2.4 %collective-permute-start.6 = (f32[2,64,128]{2,1,0:T(8,128)S(1)}, f32[2,64,128]{2,1,0:T(8,128)S(1)}, u32[]{:S(2)}, u32[]{:S(2)}) collective-permute-start(f32[2,64,128]{2,1,0:T(8,128)S(1)} %get-tuple-element.49), channel_id=1, source_target_pairs={{0,7},{1,6},{2,5},{3,4},{4,3},{5,2},{6,1},{7,0},{8,15},{9,14},{10,... | collective-permute-start | bytes 196616 | tf_op jit(solution)/shard_map/ppermute | solution.py:464
  21.3 2.6 %collective-permute-done.3.refs_4_ = f32[2,64,128]{2,1,0:T(8,128)S(1)} collective-permute-done((f32[2,64,128]{2,1,0:T(8,128)S(1)}, f32[2,64,128]{2,1,0:T(8,128)S(1)}, u32[]{:S(2)}, u32[]{:S(2)}) %collective-permute-start.3) | collective-permute-done | bytes 65568 | tf_op jit(solution)/shard_map/ppermute | solution.py:464
  23.9 1.6 %collective-permute-done.4.refs_5_ = f32[2,64,128]{2,1,0:T(8,128)S(1)} collective-permute-done((f32[2,64,128]{2,1,0:T(8,128)S(1)}, f32[2,64,128]{2,1,0:T(8,128)S(1)}, u32[]{:S(2)}, u32[]{:S(2)}) %collective-permute-start.4) | collective-permute-done | bytes 65568 | tf_op jit(solution)/shard_map/ppermute | solution.py:464
  29.1 2.0 %collective-permute-start.8 = (f32[2,128,128]{2,1,0:T(8,128)S(1)}, f32[2,128,128]{2,1,0:T(8,128)S(1)}, u32[]{:S(2)}, u32[]{:S(2)}) collective-permute-start(f32[2,128,128]{2,1,0:T(8,128)S(1)} %get-tuple-element.54), channel_id=1, source_target_pairs={{0,2},{1,3},{2,0},{3,1},{4,6},{5,7},{6,4},{7,5},{8,10},{9,11},{10,... | collective-permute-start | bytes 393224 | tf_op jit(solution)/shard_map/ppermute | solution.py:464
  32.6 2.4 %collective-permute-done.8.refs_2_ = f32[2,128,128]{2,1,0:T(8,128)S(1)} collective-permute-done((f32[2,128,128]{2,1,0:T(8,128)S(1)}, f32[2,128,128]{2,1,0:T(8,128)S(1)}, u32[]{:S(2)}, u32[]{:S(2)}) %collective-permute-start.8) | collective-permute-done | bytes 131104 | tf_op jit(solution)/shard_map/ppermute | solution.py:464
  35.0 2.0 %collective-permute-done.9.refs_3_ = f32[2,128,128]{2,1,0:T(8,128)S(1)} collective-permute-done((f32[2,128,128]{2,1,0:T(8,128)S(1)}, f32[2,128,128]{2,1,0:T(8,128)S(1)}, u32[]{:S(2)}, u32[]{:S(2)}) %collective-permute-start.9) | collective-permute-done | bytes 131104 | tf_op jit(solution)/shard_map/ppermute | solution.py:464
  40.3 1.5 %collective-permute-start.15 = (f32[2,128,128]{2,1,0:T(8,128)S(1)}, f32[2,128,128]{2,1,0:T(8,128)S(1)}, u32[]{:S(2)}, u32[]{:S(2)}) collective-permute-start(f32[2,128,128]{2,1,0:T(8,128)S(1)} %get-tuple-element.64), channel_id=1, source_target_pairs={{0,3},{1,2},{2,1},{3,0},{4,7},{5,6},{6,5},{7,4},{8,11},{9,10},{10,... | collective-permute-start | bytes 393224 | tf_op jit(solution)/shard_map/ppermute | solution.py:464
  41.8 1.8 %shard_map.118 = (f32[4,128,128]{2,1,0:T(8,128)S(1)}, f32[4,128,128]{2,1,0:T(8,128)S(1)}, f32[64,512]{1,0:T(8,128)S(1)}, f32[64,512]{1,0:T(8,128)S(1)}, f32[64,5...) custom-call(s32[2]{0:T(128)S(1)} %copy-done.5, f32[2]{0:T(128)S(1)} %copy-done.6, ...), custom_call_target="tpu_custom_call" | custom-call | tf_op jit(solution)/shard_map/pallas_call | solution.py:436
  44.2 1.5 %collective-permute-done.14.refs_2_ = f32[2,128,128]{2,1,0:T(8,128)S(1)} collective-permute-done((f32[2,128,128]{2,1,0:T(8,128)S(1)}, f32[2,128,128]{2,1,0:T(8,128)S(1)}, u32[]{:S(2)}, u32[]{:S(2)}) %collective-permute-start.14) | collective-permute-done | bytes 131104 | tf_op jit(solution)/shard_map/ppermute | solution.py:464
  45.7 2.5 %collective-permute-done.15.refs_3_ = f32[2,128,128]{2,1,0:T(8,128)S(1)} collective-permute-done((f32[2,128,128]{2,1,0:T(8,128)S(1)}, f32[2,128,128]{2,1,0:T(8,128)S(1)}, u32[]{:S(2)}, u32[]{:S(2)}) %collective-permute-start.15) | collective-permute-done | bytes 131104 | tf_op jit(solution)/shard_map/ppermute | solution.py:464
  51.3 1.5 %collective-permute-start.19 = (f32[2,64,128]{2,1,0:T(8,128)S(1)}, f32[2,64,128]{2,1,0:T(8,128)S(1)}, u32[]{:S(2)}, u32[]{:S(2)}) collective-permute-start(f32[2,64,128]{2,1,0:T(8,128)S(1)} %get-tuple-element.72), channel_id=1, source_target_pairs={{0,3},{1,2},{2,1},{3,0},{4,7},{5,6},{6,5},{7,4},{8,11},{9,10},{10,... | collective-permute-start | bytes 196616 | tf_op jit(solution)/shard_map/ppermute | solution.py:464
  52.8 2.1 %collective-permute-start.20 = (f32[2,64,128]{2,1,0:T(8,128)S(1)}, f32[2,64,128]{2,1,0:T(8,128)S(1)}, u32[]{:S(2)}, u32[]{:S(2)}) collective-permute-start(f32[2,64,128]{2,1,0:T(8,128)S(1)} %get-tuple-element.73), channel_id=1, source_target_pairs={{0,4},{1,5},{2,6},{3,7},{4,0},{5,1},{6,2},{7,3},{8,12},{9,13},{10,... | collective-permute-start | bytes 196616 | tf_op jit(solution)/shard_map/ppermute | solution.py:464
  56.1 2.7 %collective-permute-start.22 = (f32[2,64,128]{2,1,0:T(8,128)S(1)}, f32[2,64,128]{2,1,0:T(8,128)S(1)}, u32[]{:S(2)}, u32[]{:S(2)}) collective-permute-start(f32[2,64,128]{2,1,0:T(8,128)S(1)} %get-tuple-element.75), channel_id=1, source_target_pairs={{0,6},{1,7},{2,4},{3,5},{4,2},{5,3},{6,0},{7,1},{8,14},{9,15},{10,... | collective-permute-start | bytes 196616 | tf_op jit(solution)/shard_map/ppermute | solution.py:464
  58.8 1.6 %collective-permute-start.23 = (f32[2,64,128]{2,1,0:T(8,128)S(1)}, f32[2,64,128]{2,1,0:T(8,128)S(1)}, u32[]{:S(2)}, u32[]{:S(2)}) collective-permute-start(f32[2,64,128]{2,1,0:T(8,128)S(1)} %get-tuple-element.76), channel_id=1, source_target_pairs={{0,7},{1,6},{2,5},{3,4},{4,3},{5,2},{6,1},{7,0},{8,15},{9,14},{10,... | collective-permute-start | bytes 196616 | tf_op jit(solution)/shard_map/ppermute | solution.py:464
  60.4 2.4 %collective-permute-done.20.refs_4_ = f32[2,64,128]{2,1,0:T(8,128)S(1)} collective-permute-done((f32[2,64,128]{2,1,0:T(8,128)S(1)}, f32[2,64,128]{2,1,0:T(8,128)S(1)}, u32[]{:S(2)}, u32[]{:S(2)}) %collective-permute-start.20) | collective-permute-done | bytes 65568 | tf_op jit(solution)/shard_map/ppermute | solution.py:464
  62.9 1.7 %collective-permute-done.21.refs_5_ = f32[2,64,128]{2,1,0:T(8,128)S(1)} collective-permute-done((f32[2,64,128]{2,1,0:T(8,128)S(1)}, f32[2,64,128]{2,1,0:T(8,128)S(1)}, u32[]{:S(2)}, u32[]{:S(2)}) %collective-permute-start.21) | collective-permute-done | bytes 65568 | tf_op jit(solution)/shard_map/ppermute | solution.py:464
  66.4 4.1 %collective-permute-start.25 = (f32[64,512]{1,0:T(8,128)S(1)}, f32[64,512]{1,0:T(8,128)S(1)}, u32[]{:S(2)}, u32[]{:S(2)}) collective-permute-start(f32[64,512]{1,0:T(8,128)S(1)} %get-tuple-element.81.refs_12_), channel_id=1, source_target_pairs={{0,4},{1,5},{2,6},{3,7},{4,0},{5,1},{6,2},{7,3},{16,20},{17,21},{1... | collective-permute-start | bytes 393224 | tf_op jit(solution)/shard_map/ppermute | solution.py:530
  70.5 3.7 %collective-permute-done.25.more_ref = f32[64,512]{1,0:T(8,128)S(1)} collective-permute-done((f32[64,512]{1,0:T(8,128)S(1)}, f32[64,512]{1,0:T(8,128)S(1)}, u32[]{:S(2)}, u32[]{:S(2)}) %collective-permute-start.25) | collective-permute-done | bytes 131104 | tf_op jit(solution)/shard_map/ppermute | solution.py:530
  (51 shorter events, 17.4 us)
Async XLA Ops:
  2.7 9.7 %collective-permute-start = (f32[2,64,128]{2,1,0:T(8,128)S(1)}, f32[2,64,128]{2,1,0:T(8,128)S(1)}, u32[]{:S(2)}, u32[]{:S(2)}) collective-permute-start(f32[2,64,128]{2,1,0:T(8,128)S(1)} %get-tuple-element.43), channel_id=1, source_target_pairs={{0,1},{1,0},{2,3},{3,2},{4,5},{5,4},{6,7},{7,6},{8,9},{9,8},{10,11... | collective-permute-start | bytes 196616 | tf_op jit(solution)/shard_map/ppermute | solution.py:464
  5.7 10.6 %collective-permute-start.1 = (f32[2,64,128]{2,1,0:T(8,128)S(1)}, f32[2,64,128]{2,1,0:T(8,128)S(1)}, u32[]{:S(2)}, u32[]{:S(2)}) collective-permute-start(f32[2,64,128]{2,1,0:T(8,128)S(1)} %get-tuple-element.44), channel_id=1, source_target_pairs={{0,2},{1,3},{2,0},{3,1},{4,6},{5,7},{6,4},{7,5},{8,10},{9,11},{10,... | collective-permute-start | bytes 196616 | tf_op jit(solution)/shard_map/ppermute | solution.py:464
  7.3 10.3 %collective-permute-start.2 = (f32[2,64,128]{2,1,0:T(8,128)S(1)}, f32[2,64,128]{2,1,0:T(8,128)S(1)}, u32[]{:S(2)}, u32[]{:S(2)}) collective-permute-start(f32[2,64,128]{2,1,0:T(8,128)S(1)} %get-tuple-element.45), channel_id=1, source_target_pairs={{0,3},{1,2},{2,1},{3,0},{4,7},{5,6},{6,5},{7,4},{8,11},{9,10},{10,... | collective-permute-start | bytes 196616 | tf_op jit(solution)/shard_map/ppermute | solution.py:464
  7.3 20.4 %collective-permute-start.11 = (f32[64,512]{1,0:T(8,128)S(1)}, f32[64,512]{1,0:T(8,128)S(1)}, u32[]{:S(2)}, u32[]{:S(2)}) collective-permute-start(f32[64,512]{1,0:T(8,128)S(1)} %bitcast.1), channel_id=1, source_target_pairs={{0,4},{1,5},{2,6},{3,7},{4,0},{5,1},{6,2},{7,3},{16,20},{17,21},{1... | collective-permute-start | bytes 393224 | tf_op jit(solution)/shard_map/ppermute | solution.py:502
  12.3 11.6 %collective-permute-start.3 = (f32[2,64,128]{2,1,0:T(8,128)S(1)}, f32[2,64,128]{2,1,0:T(8,128)S(1)}, u32[]{:S(2)}, u32[]{:S(2)}) collective-permute-start(f32[2,64,128]{2,1,0:T(8,128)S(1)} %get-tuple-element.46), channel_id=1, source_target_pairs={{0,4},{1,5},{2,6},{3,7},{4,0},{5,1},{6,2},{7,3},{8,12},{9,13},{10,... | collective-permute-start | bytes 196616 | tf_op jit(solution)/shard_map/ppermute | solution.py:464
  12.4 13.1 %collective-permute-start.4 = (f32[2,64,128]{2,1,0:T(8,128)S(1)}, f32[2,64,128]{2,1,0:T(8,128)S(1)}, u32[]{:S(2)}, u32[]{:S(2)}) collective-permute-start(f32[2,64,128]{2,1,0:T(8,128)S(1)} %get-tuple-element.47), channel_id=1, source_target_pairs={{0,5},{1,4},{2,7},{3,6},{4,1},{5,0},{6,3},{7,2},{8,13},{9,12},{10,... | collective-permute-start | bytes 196616 | tf_op jit(solution)/shard_map/ppermute | solution.py:464
  16.3 9.2 %collective-permute-start.5 = (f32[2,64,128]{2,1,0:T(8,128)S(1)}, f32[2,64,128]{2,1,0:T(8,128)S(1)}, u32[]{:S(2)}, u32[]{:S(2)}) collective-permute-start(f32[2,64,128]{2,1,0:T(8,128)S(1)} %get-tuple-element.48), channel_id=1, source_target_pairs={{0,6},{1,7},{2,4},{3,5},{4,2},{5,3},{6,0},{7,1},{8,14},{9,15},{10,... | collective-permute-start | bytes 196616 | tf_op jit(solution)/shard_map/ppermute | solution.py:464
  17.6 7.9 %collective-permute-start.6 = (f32[2,64,128]{2,1,0:T(8,128)S(1)}, f32[2,64,128]{2,1,0:T(8,128)S(1)}, u32[]{:S(2)}, u32[]{:S(2)}) collective-permute-start(f32[2,64,128]{2,1,0:T(8,128)S(1)} %get-tuple-element.49), channel_id=1, source_target_pairs={{0,7},{1,6},{2,5},{3,4},{4,3},{5,2},{6,1},{7,0},{8,15},{9,14},{10,... | collective-permute-start | bytes 196616 | tf_op jit(solution)/shard_map/ppermute | solution.py:464
  23.9 7.6 %collective-permute-start.10 = (f32[1,64,512]{2,1,0:T(8,128)S(1)}, f32[1,64,512]{2,1,0:T(8,128)S(1)}, u32[]{:S(2)}, u32[]{:S(2)}) collective-permute-start(f32[1,64,512]{2,1,0:T(8,128)S(1)} %copy-done.2), channel_id=1, source_target_pairs={{0,8},{8,0},{1,9},{9,1},{2,10},{10,2},{3,11},{11,3},{4,12},{12,4},... | collective-permute-start | bytes 393224 | tf_op jit(solution)/shard_map/ppermute | solution.py:503
  26.6 6.0 %collective-permute-start.7 = (f32[2,128,128]{2,1,0:T(8,128)S(1)}, f32[2,128,128]{2,1,0:T(8,128)S(1)}, u32[]{:S(2)}, u32[]{:S(2)}) collective-permute-start(f32[2,128,128]{2,1,0:T(8,128)S(1)} %get-tuple-element.53), channel_id=1, source_target_pairs={{0,1},{1,0},{2,3},{3,2},{4,5},{5,4},{6,7},{7,6},{8,9},{9,8},{10,11... | collective-permute-start | bytes 393224 | tf_op jit(solution)/shard_map/ppermute | solution.py:464
  29.1 5.9 %collective-permute-start.8 = (f32[2,128,128]{2,1,0:T(8,128)S(1)}, f32[2,128,128]{2,1,0:T(8,128)S(1)}, u32[]{:S(2)}, u32[]{:S(2)}) collective-permute-start(f32[2,128,128]{2,1,0:T(8,128)S(1)} %get-tuple-element.54), channel_id=1, source_target_pairs={{0,2},{1,3},{2,0},{3,1},{4,6},{5,7},{6,4},{7,5},{8,10},{9,11},{10,... | collective-permute-start | bytes 393224 | tf_op jit(solution)/shard_map/ppermute | solution.py:464
  31.1 5.9 %collective-permute-start.9 = (f32[2,128,128]{2,1,0:T(8,128)S(1)}, f32[2,128,128]{2,1,0:T(8,128)S(1)}, u32[]{:S(2)}, u32[]{:S(2)}) collective-permute-start(f32[2,128,128]{2,1,0:T(8,128)S(1)} %get-tuple-element.55), channel_id=1, source_target_pairs={{0,3},{1,2},{2,1},{3,0},{4,7},{5,6},{6,5},{7,4},{8,11},{9,10},{10,... | collective-permute-start | bytes 393224 | tf_op jit(solution)/shard_map/ppermute | solution.py:464
  38.3 5.9 %collective-permute-start.13 = (f32[2,128,128]{2,1,0:T(8,128)S(1)}, f32[2,128,128]{2,1,0:T(8,128)S(1)}, u32[]{:S(2)}, u32[]{:S(2)}) collective-permute-start(f32[2,128,128]{2,1,0:T(8,128)S(1)} %get-tuple-element.62), channel_id=1, source_target_pairs={{0,1},{1,0},{2,3},{3,2},{4,5},{5,4},{6,7},{7,6},{8,9},{9,8},{10,11... | collective-permute-start | bytes 393224 | tf_op jit(solution)/shard_map/ppermute | solution.py:464
  39.3 6.4 %collective-permute-start.14 = (f32[2,128,128]{2,1,0:T(8,128)S(1)}, f32[2,128,128]{2,1,0:T(8,128)S(1)}, u32[]{:S(2)}, u32[]{:S(2)}) collective-permute-start(f32[2,128,128]{2,1,0:T(8,128)S(1)} %get-tuple-element.63), channel_id=1, source_target_pairs={{0,2},{1,3},{2,0},{3,1},{4,6},{5,7},{6,4},{7,5},{8,10},{9,11},{10,... | collective-permute-start | bytes 393224 | tf_op jit(solution)/shard_map/ppermute | solution.py:464
  40.3 7.8 %collective-permute-start.15 = (f32[2,128,128]{2,1,0:T(8,128)S(1)}, f32[2,128,128]{2,1,0:T(8,128)S(1)}, u32[]{:S(2)}, u32[]{:S(2)}) collective-permute-start(f32[2,128,128]{2,1,0:T(8,128)S(1)} %get-tuple-element.64), channel_id=1, source_target_pairs={{0,3},{1,2},{2,1},{3,0},{4,7},{5,6},{6,5},{7,4},{8,11},{9,10},{10,... | collective-permute-start | bytes 393224 | tf_op jit(solution)/shard_map/ppermute | solution.py:464
  49.2 6.9 %collective-permute-start.17 = (f32[2,64,128]{2,1,0:T(8,128)S(1)}, f32[2,64,128]{2,1,0:T(8,128)S(1)}, u32[]{:S(2)}, u32[]{:S(2)}) collective-permute-start(f32[2,64,128]{2,1,0:T(8,128)S(1)} %get-tuple-element.70), channel_id=1, source_target_pairs={{0,1},{1,0},{2,3},{3,2},{4,5},{5,4},{6,7},{7,6},{8,9},{9,8},{10,11... | collective-permute-start | bytes 196616 | tf_op jit(solution)/shard_map/ppermute | solution.py:464
  50.3 8.5 %collective-permute-start.18 = (f32[2,64,128]{2,1,0:T(8,128)S(1)}, f32[2,64,128]{2,1,0:T(8,128)S(1)}, u32[]{:S(2)}, u32[]{:S(2)}) collective-permute-start(f32[2,64,128]{2,1,0:T(8,128)S(1)} %get-tuple-element.71), channel_id=1, source_target_pairs={{0,2},{1,3},{2,0},{3,1},{4,6},{5,7},{6,4},{7,5},{8,10},{9,11},{10,... | collective-permute-start | bytes 196616 | tf_op jit(solution)/shard_map/ppermute | solution.py:464
  51.3 9.2 %collective-permute-start.19 = (f32[2,64,128]{2,1,0:T(8,128)S(1)}, f32[2,64,128]{2,1,0:T(8,128)S(1)}, u32[]{:S(2)}, u32[]{:S(2)}) collective-permute-start(f32[2,64,128]{2,1,0:T(8,128)S(1)} %get-tuple-element.72), channel_id=1, source_target_pairs={{0,3},{1,2},{2,1},{3,0},{4,7},{5,6},{6,5},{7,4},{8,11},{9,10},{10,... | collective-permute-start | bytes 196616 | tf_op jit(solution)/shard_map/ppermute | solution.py:464
  52.8 10.1 %collective-permute-start.20 = (f32[2,64,128]{2,1,0:T(8,128)S(1)}, f32[2,64,128]{2,1,0:T(8,128)S(1)}, u32[]{:S(2)}, u32[]{:S(2)}) collective-permute-start(f32[2,64,128]{2,1,0:T(8,128)S(1)} %get-tuple-element.73), channel_id=1, source_target_pairs={{0,4},{1,5},{2,6},{3,7},{4,0},{5,1},{6,2},{7,3},{8,12},{9,13},{10,... | collective-permute-start | bytes 196616 | tf_op jit(solution)/shard_map/ppermute | solution.py:464
  54.9 9.7 %collective-permute-start.21 = (f32[2,64,128]{2,1,0:T(8,128)S(1)}, f32[2,64,128]{2,1,0:T(8,128)S(1)}, u32[]{:S(2)}, u32[]{:S(2)}) collective-permute-start(f32[2,64,128]{2,1,0:T(8,128)S(1)} %get-tuple-element.74), channel_id=1, source_target_pairs={{0,5},{1,4},{2,7},{3,6},{4,1},{5,0},{6,3},{7,2},{8,13},{9,12},{10,... | collective-permute-start | bytes 196616 | tf_op jit(solution)/shard_map/ppermute | solution.py:464
  56.1 8.5 %collective-permute-start.22 = (f32[2,64,128]{2,1,0:T(8,128)S(1)}, f32[2,64,128]{2,1,0:T(8,128)S(1)}, u32[]{:S(2)}, u32[]{:S(2)}) collective-permute-start(f32[2,64,128]{2,1,0:T(8,128)S(1)} %get-tuple-element.75), channel_id=1, source_target_pairs={{0,6},{1,7},{2,4},{3,5},{4,2},{5,3},{6,0},{7,1},{8,14},{9,15},{10,... | collective-permute-start | bytes 196616 | tf_op jit(solution)/shard_map/ppermute | solution.py:464
  58.8 7.1 %collective-permute-start.23 = (f32[2,64,128]{2,1,0:T(8,128)S(1)}, f32[2,64,128]{2,1,0:T(8,128)S(1)}, u32[]{:S(2)}, u32[]{:S(2)}) collective-permute-start(f32[2,64,128]{2,1,0:T(8,128)S(1)} %get-tuple-element.76), channel_id=1, source_target_pairs={{0,7},{1,6},{2,5},{3,4},{4,3},{5,2},{6,1},{7,0},{8,15},{9,14},{10,... | collective-permute-start | bytes 196616 | tf_op jit(solution)/shard_map/ppermute | solution.py:464
  66.3 7.8 %collective-permute-start.24 = (f32[5,64,512]{2,1,0:T(8,128)S(1)}, f32[5,64,512]{2,1,0:T(8,128)S(1)}, u32[]{:S(2)}, u32[]{:S(2)}) collective-permute-start(f32[5,64,512]{2,1,0:T(8,128)S(1)} %shard_map.120.own_ref), channel_id=1, source_target_pairs={{0,8},{8,0},{1,9},{9,1},{2,10},{10,2},{3,11},{11,3},{4,12},{12,4},... | collective-permute-start | bytes 1966088 | tf_op jit(solution)/shard_map/ppermute | solution.py:544
  66.4 7.8 %collective-permute-start.25 = (f32[64,512]{1,0:T(8,128)S(1)}, f32[64,512]{1,0:T(8,128)S(1)}, u32[]{:S(2)}, u32[]{:S(2)}) collective-permute-start(f32[64,512]{1,0:T(8,128)S(1)} %get-tuple-element.81.refs_12_), channel_id=1, source_target_pairs={{0,4},{1,5},{2,6},{3,7},{4,0},{5,1},{6,2},{7,3},{16,20},{17,21},{1... | collective-permute-start | bytes 393224 | tf_op jit(solution)/shard_map/ppermute | solution.py:530
  (9 other events, 109.0 us)

commit v9 on v7

--- a/solution.py
+++ b/solution.py
@@ -411,15 +411,15 @@
     propagator(radix, 0, freq_ref, ref_ref, hre, him)
 
 
-def factors_b(radix, freq_ref, ref_ref, slow_ref, other_ref, far_ref, sent_ref, hre, him, *outs):
+def factors_b(freq_ref, ref_ref, slow_ref, other_ref, far_ref, sent_ref, *outs):
     first = lax.axis_index("depth") == 0
     _, omega = omegas_of(freq_ref)
-    propagator(radix, 1, freq_ref, ref_ref, hre, him)
     screen(jnp.where(first, slow_ref[0], other_ref[0]), ref_ref[0], omega, *outs[:2])
     screen(jnp.where(first, far_ref[...], sent_ref[...]), ref_ref[0], omega, *outs[2:])
 
 
-def factors_c(freq_ref, ref_ref, slow_ref, other_ref, keep_ref, got_ref, share_ref, *outs):
+def factors_c(radix, freq_ref, ref_ref, slow_ref, other_ref, keep_ref, got_ref, hre, him, share_ref, *outs):
+    propagator(radix, 1, freq_ref, ref_ref, hre, him)
     last = jnp.where(lax.axis_index("depth") == 0, other_ref[0], slow_ref[0])
     omegas, _ = omegas_of(freq_ref)
     share_ref[...] = keep_ref[0] * got_ref[0] + keep_ref[1] * got_ref[1]
@@ -500,14 +500,7 @@
     far = lax.ppermute(slowness[0], both, [(flat(0, r), flat(0, r ^ radix)) for r in range(ranks)])
     other = lax.ppermute(slowness, "depth", swap)
     sent = lax.ppermute(far, "depth", [(0, 1)])
-    factors = call(
-        functools.partial(factors_b, radix),
-        [factor] * 2 + [plane] * 4,
-        [],
-        (slowness, other, far, sent),
-        scalars=scalars,
-    )
-    propagator_b, screens_a = factors[:2], factors[2:]
+    screens_a = call(factors_b, [plane] * 4, [], (slowness, other, far, sent), scalars=scalars)
     columns = exchange(spectra, outer_steps)
     quarters = call(
         functools.partial(columns_to_quarters, col_radix, ranks),
@@ -524,9 +517,14 @@
     )
     quarters = exchange(quarters, inner_steps)
     got = lax.ppermute(send, "depth", swap)
-    share, *screens_b = call(
-        factors_c, [plane] * 5, [], (slowness, other, keep, got), scalars=scalars
-    )
+    factors = call(
+        functools.partial(factors_c, radix),
+        [factor] * 2 + [plane] * 5,
+        [],
+        (slowness, other, keep, got),
+        scalars=scalars,
+    )
+    propagator_b, share, screens_b = factors[:2], factors[2], factors[3:]
     more = lax.ppermute(share, both, [(flat(1, r), flat(0, r ^ radix)) for r in range(ranks)])
     columns = call(
         functools.partial(quarters_to_columns, col_radix, radix),

time: 74.7 us -> 74.7 us (level)
  transfers between devices with their start and end apart: 26 -> 26, of which waited for: 11 -> 11; matrix products, arithmetic and copies ran while one was open for 0% -> 0% of each run, Pallas kernels for 8% -> 7%
where the time goes in v9:
time: 74.7 us; the launch traced here: 74.5 us
  starting transfers between devices  38.4 us (51%)
  waiting for transfers between devices  24.4 us (33%)
  Pallas kernels  10.8 us (14%)
  between operations  0.82 us (1%)
    ppermute x20, starting transfers between devices, hop(): return lax.ppermute(array, 'row', [(r, r ^ step) for r in range(ranks)])  30.7 us
    ppermute x20, waiting for transfers between devices, hop(): return lax.ppermute(array, 'row', [(r, r ^ step) for r in range(ranks)])  18.5 us
    pallas_call x8, Pallas kernels, call(): pl.pallas_call(kernel, in_specs=[smem] * len(scalars) + [vmem] * len(args...  8.77 us
    ppermute x1, waiting for transfers between devices, shards(): lax.ppermute(share, both, [(flat(1, r), flat(0, r ^ radix)) for r in rang...  5.89 us
    ppermute x1, starting transfers between devices, shards(): lax.ppermute(slowness[0], both, [(flat(0, r), flat(0, r ^ radix)) for r i...  5.01 us
    pallas_call x1, Pallas kernels, shards(): pl.pallas_call(functools.partial(first_kernel, radix), in_specs=[hbm] * 3...  1.98 us
  transfers between devices with their start and end apart: 26, of which 11 were waited for; matrix products, arithmetic and copies ran while one was open for 0% of the time, Pallas kernels for 7%

profile of v9, /device:TPU:0, one launch (start us, length us, event | category | flops | bytes accessed | tf_op | source)
XLA Modules:
  0.0 74.5 jit_solution(2133890180875482299)
XLA Ops:
  0.7 2.0 %shard_map.113 = (f32[2,64,128]{2,1,0:T(8,128)S(1)}, f32[2,64,128]{2,1,0:T(8,128)S(1)}, f32[2,64,128]{2,1,0:T(8,128)S(1)}, f32[2,64,128]{2,1,0:T(8,128)S(1)}, f3...) custom-call(f32[2,4,64,512]{3,2,1,0:T(8,128)} %planes_ref.1, ...), custom_call_target="tpu_custom_call" | custom-call | tf_op jit(solution)/shard_map/pallas_call | solution.py:477
  2.7 3.1 %collective-permute-start = (f32[2,64,128]{2,1,0:T(8,128)S(1)}, f32[2,64,128]{2,1,0:T(8,128)S(1)}, u32[]{:S(2)}, u32[]{:S(2)}) collective-permute-start(f32[2,64,128]{2,1,0:T(8,128)S(1)} %get-tuple-element.43), channel_id=1, source_target_pairs={{0,1},{1,0},{2,3},{3,2},{4,5},{5,4},{6,7},{7,6},{8,9},{9,8},{10,11... | collective-permute-start | bytes 196616 | tf_op jit(solution)/shard_map/ppermute | solution.py:462
  5.7 1.6 %collective-permute-start.1 = (f32[2,64,128]{2,1,0:T(8,128)S(1)}, f32[2,64,128]{2,1,0:T(8,128)S(1)}, u32[]{:S(2)}, u32[]{:S(2)}) collective-permute-start(f32[2,64,128]{2,1,0:T(8,128)S(1)} %get-tuple-element.44), channel_id=1, source_target_pairs={{0,2},{1,3},{2,0},{3,1},{4,6},{5,7},{6,4},{7,5},{8,10},{9,11},{10,... | collective-permute-start | bytes 196616 | tf_op jit(solution)/shard_map/ppermute | solution.py:462
  7.3 5.0 %collective-permute-start.11 = (f32[64,512]{1,0:T(8,128)S(1)}, f32[64,512]{1,0:T(8,128)S(1)}, u32[]{:S(2)}, u32[]{:S(2)}) collective-permute-start(f32[64,512]{1,0:T(8,128)S(1)} %bitcast.1), channel_id=1, source_target_pairs={{0,4},{1,5},{2,6},{3,7},{4,0},{5,1},{6,2},{7,3},{16,20},{17,21},{1... | collective-permute-start | bytes 393224 | tf_op jit(solution)/shard_map/ppermute | solution.py:500
  12.4 3.9 %collective-permute-start.4 = (f32[2,64,128]{2,1,0:T(8,128)S(1)}, f32[2,64,128]{2,1,0:T(8,128)S(1)}, u32[]{:S(2)}, u32[]{:S(2)}) collective-permute-start(f32[2,64,128]{2,1,0:T(8,128)S(1)} %get-tuple-element.47), channel_id=1, source_target_pairs={{0,5},{1,4},{2,7},{3,6},{4,1},{5,0},{6,3},{7,2},{8,13},{9,12},{10,... | collective-permute-start | bytes 196616 | tf_op jit(solution)/shard_map/ppermute | solution.py:462
  16.3 1.3 %collective-permute-start.5 = (f32[2,64,128]{2,1,0:T(8,128)S(1)}, f32[2,64,128]{2,1,0:T(8,128)S(1)}, u32[]{:S(2)}, u32[]{:S(2)}) collective-permute-start(f32[2,64,128]{2,1,0:T(8,128)S(1)} %get-tuple-element.48), channel_id=1, source_target_pairs={{0,6},{1,7},{2,4},{3,5},{4,2},{5,3},{6,0},{7,1},{8,14},{9,15},{10,... | collective-permute-start | bytes 196616 | tf_op jit(solution)/shard_map/ppermute | solution.py:462
  17.6 2.4 %collective-permute-start.6 = (f32[2,64,128]{2,1,0:T(8,128)S(1)}, f32[2,64,128]{2,1,0:T(8,128)S(1)}, u32[]{:S(2)}, u32[]{:S(2)}) collective-permute-start(f32[2,64,128]{2,1,0:T(8,128)S(1)} %get-tuple-element.49), channel_id=1, source_target_pairs={{0,7},{1,6},{2,5},{3,4},{4,3},{5,2},{6,1},{7,0},{8,15},{9,14},{10,... | collective-permute-start | bytes 196616 | tf_op jit(solution)/shard_map/ppermute | solution.py:462
  21.3 2.6 %collective-permute-done.3.refs_4_ = f32[2,64,128]{2,1,0:T(8,128)S(1)} collective-permute-done((f32[2,64,128]{2,1,0:T(8,128)S(1)}, f32[2,64,128]{2,1,0:T(8,128)S(1)}, u32[]{:S(2)}, u32[]{:S(2)}) %collective-permute-start.3) | collective-permute-done | bytes 65568 | tf_op jit(solution)/shard_map/ppermute | solution.py:462
  23.9 1.6 %collective-permute-done.4.refs_5_ = f32[2,64,128]{2,1,0:T(8,128)S(1)} collective-permute-done((f32[2,64,128]{2,1,0:T(8,128)S(1)}, f32[2,64,128]{2,1,0:T(8,128)S(1)}, u32[]{:S(2)}, u32[]{:S(2)}) %collective-permute-start.4) | collective-permute-done | bytes 65568 | tf_op jit(solution)/shard_map/ppermute | solution.py:462
  29.1 2.0 %collective-permute-start.8 = (f32[2,128,128]{2,1,0:T(8,128)S(1)}, f32[2,128,128]{2,1,0:T(8,128)S(1)}, u32[]{:S(2)}, u32[]{:S(2)}) collective-permute-start(f32[2,128,128]{2,1,0:T(8,128)S(1)} %get-tuple-element.54), channel_id=1, source_target_pairs={{0,2},{1,3},{2,0},{3,1},{4,6},{5,7},{6,4},{7,5},{8,10},{9,11},{10,... | collective-permute-start | bytes 393224 | tf_op jit(solution)/shard_map/ppermute | solution.py:462
  32.6 2.4 %collective-permute-done.8.refs_2_ = f32[2,128,128]{2,1,0:T(8,128)S(1)} collective-permute-done((f32[2,128,128]{2,1,0:T(8,128)S(1)}, f32[2,128,128]{2,1,0:T(8,128)S(1)}, u32[]{:S(2)}, u32[]{:S(2)}) %collective-permute-start.8) | collective-permute-done | bytes 131104 | tf_op jit(solution)/shard_map/ppermute | solution.py:462
  35.0 2.0 %collective-permute-done.9.refs_3_ = f32[2,128,128]{2,1,0:T(8,128)S(1)} collective-permute-done((f32[2,128,128]{2,1,0:T(8,128)S(1)}, f32[2,128,128]{2,1,0:T(8,128)S(1)}, u32[]{:S(2)}, u32[]{:S(2)}) %collective-permute-start.9) | collective-permute-done | bytes 131104 | tf_op jit(solution)/shard_map/ppermute | solution.py:462
  40.3 1.5 %collective-permute-start.15 = (f32[2,128,128]{2,1,0:T(8,128)S(1)}, f32[2,128,128]{2,1,0:T(8,128)S(1)}, u32[]{:S(2)}, u32[]{:S(2)}) collective-permute-start(f32[2,128,128]{2,1,0:T(8,128)S(1)} %get-tuple-element.64), channel_id=1, source_target_pairs={{0,3},{1,2},{2,1},{3,0},{4,7},{5,6},{6,5},{7,4},{8,11},{9,10},{10,... | collective-permute-start | bytes 393224 | tf_op jit(solution)/shard_map/ppermute | solution.py:462
  41.8 1.8 %shard_map.118 = (f32[4,128,128]{2,1,0:T(8,128)S(1)}, f32[4,128,128]{2,1,0:T(8,128)S(1)}, f32[64,512]{1,0:T(8,128)S(1)}, f32[64,512]{1,0:T(8,128)S(1)}, f32[64,5...) custom-call(s32[2]{0:T(128)S(1)} %copy-done.5, f32[2]{0:T(128)S(1)} %copy-done.6, ...), custom_call_target="tpu_custom_call" | custom-call | tf_op jit(solution)/shard_map/pallas_call | solution.py:434
  44.2 1.5 %collective-permute-done.14.refs_2_ = f32[2,128,128]{2,1,0:T(8,128)S(1)} collective-permute-done((f32[2,128,128]{2,1,0:T(8,128)S(1)}, f32[2,128,128]{2,1,0:T(8,128)S(1)}, u32[]{:S(2)}, u32[]{:S(2)}) %collective-permute-start.14) | collective-permute-done | bytes 131104 | tf_op jit(solution)/shard_map/ppermute | solution.py:462
  45.7 2.5 %collective-permute-done.15.refs_3_ = f32[2,128,128]{2,1,0:T(8,128)S(1)} collective-permute-done((f32[2,128,128]{2,1,0:T(8,128)S(1)}, f32[2,128,128]{2,1,0:T(8,128)S(1)}, u32[]{:S(2)}, u32[]{:S(2)}) %collective-permute-start.15) | collective-permute-done | bytes 131104 | tf_op jit(solution)/shard_map/ppermute | solution.py:462
  51.3 1.5 %collective-permute-start.19 = (f32[2,64,128]{2,1,0:T(8,128)S(1)}, f32[2,64,128]{2,1,0:T(8,128)S(1)}, u32[]{:S(2)}, u32[]{:S(2)}) collective-permute-start(f32[2,64,128]{2,1,0:T(8,128)S(1)} %get-tuple-element.72), channel_id=1, source_target_pairs={{0,3},{1,2},{2,1},{3,0},{4,7},{5,6},{6,5},{7,4},{8,11},{9,10},{10,... | collective-permute-start | bytes 196616 | tf_op jit(solution)/shard_map/ppermute | solution.py:462
  52.8 2.1 %collective-permute-start.20 = (f32[2,64,128]{2,1,0:T(8,128)S(1)}, f32[2,64,128]{2,1,0:T(8,128)S(1)}, u32[]{:S(2)}, u32[]{:S(2)}) collective-permute-start(f32[2,64,128]{2,1,0:T(8,128)S(1)} %get-tuple-element.73), channel_id=1, source_target_pairs={{0,4},{1,5},{2,6},{3,7},{4,0},{5,1},{6,2},{7,3},{8,12},{9,13},{10,... | collective-permute-start | bytes 196616 | tf_op jit(solution)/shard_map/ppermute | solution.py:462
  56.1 2.7 %collective-permute-start.22 = (f32[2,64,128]{2,1,0:T(8,128)S(1)}, f32[2,64,128]{2,1,0:T(8,128)S(1)}, u32[]{:S(2)}, u32[]{:S(2)}) collective-permute-start(f32[2,64,128]{2,1,0:T(8,128)S(1)} %get-tuple-element.75), channel_id=1, source_target_pairs={{0,6},{1,7},{2,4},{3,5},{4,2},{5,3},{6,0},{7,1},{8,14},{9,15},{10,... | collective-permute-start | bytes 196616 | tf_op jit(solution)/shard_map/ppermute | solution.py:462
  58.8 1.6 %collective-permute-start.23 = (f32[2,64,128]{2,1,0:T(8,128)S(1)}, f32[2,64,128]{2,1,0:T(8,128)S(1)}, u32[]{:S(2)}, u32[]{:S(2)}) collective-permute-start(f32[2,64,128]{2,1,0:T(8,128)S(1)} %get-tuple-element.76), channel_id=1, source_target_pairs={{0,7},{1,6},{2,5},{3,4},{4,3},{5,2},{6,1},{7,0},{8,15},{9,14},{10,... | collective-permute-start | bytes 196616 | tf_op jit(solution)/shard_map/ppermute | solution.py:462
  60.4 2.4 %collective-permute-done.20.refs_4_ = f32[2,64,128]{2,1,0:T(8,128)S(1)} collective-permute-done((f32[2,64,128]{2,1,0:T(8,128)S(1)}, f32[2,64,128]{2,1,0:T(8,128)S(1)}, u32[]{:S(2)}, u32[]{:S(2)}) %collective-permute-start.20) | collective-permute-done | bytes 65568 | tf_op jit(solution)/shard_map/ppermute | solution.py:462
  62.9 1.7 %collective-permute-done.21.refs_5_ = f32[2,64,128]{2,1,0:T(8,128)S(1)} collective-permute-done((f32[2,64,128]{2,1,0:T(8,128)S(1)}, f32[2,64,128]{2,1,0:T(8,128)S(1)}, u32[]{:S(2)}, u32[]{:S(2)}) %collective-permute-start.21) | collective-permute-done | bytes 65568 | tf_op jit(solution)/shard_map/ppermute | solution.py:462
  66.4 1.3 %collective-permute-start.25 = (f32[64,512]{1,0:T(8,128)S(1)}, f32[64,512]{1,0:T(8,128)S(1)}, u32[]{:S(2)}, u32[]{:S(2)}) collective-permute-start(f32[64,512]{1,0:T(8,128)S(1)} %get-tuple-element.81.share_ref), channel_id=1, source_target_pairs={{8,4},{9,5},{10,6},{11,7},{12,0},{13,1},{14,2},{15,3},{24,20},{25,... | collective-permute-start | bytes 393224 | tf_op jit(solution)/shard_map/ppermute | solution.py:528
  67.7 5.9 %collective-permute-done.25.more_ref = f32[64,512]{1,0:T(8,128)S(1)} collective-permute-done((f32[64,512]{1,0:T(8,128)S(1)}, f32[64,512]{1,0:T(8,128)S(1)}, u32[]{:S(2)}, u32[]{:S(2)}) %collective-permute-start.25) | collective-permute-done | bytes 131104 | tf_op jit(solution)/shard_map/ppermute | solution.py:528
  (51 shorter events, 17.4 us)
Async XLA Ops:
  2.7 9.7 %collective-permute-start = (f32[2,64,128]{2,1,0:T(8,128)S(1)}, f32[2,64,128]{2,1,0:T(8,128)S(1)}, u32[]{:S(2)}, u32[]{:S(2)}) collective-permute-start(f32[2,64,128]{2,1,0:T(8,128)S(1)} %get-tuple-element.43), channel_id=1, source_target_pairs={{0,1},{1,0},{2,3},{3,2},{4,5},{5,4},{6,7},{7,6},{8,9},{9,8},{10,11... | collective-permute-start | bytes 196616 | tf_op jit(solution)/shard_map/ppermute | solution.py:462
  5.7 10.6 %collective-permute-start.1 = (f32[2,64,128]{2,1,0:T(8,128)S(1)}, f32[2,64,128]{2,1,0:T(8,128)S(1)}, u32[]{:S(2)}, u32[]{:S(2)}) collective-permute-start(f32[2,64,128]{2,1,0:T(8,128)S(1)} %get-tuple-element.44), channel_id=1, source_target_pairs={{0,2},{1,3},{2,0},{3,1},{4,6},{5,7},{6,4},{7,5},{8,10},{9,11},{10,... | collective-permute-start | bytes 196616 | tf_op jit(solution)/shard_map/ppermute | solution.py:462
  7.3 10.3 %collective-permute-start.2 = (f32[2,64,128]{2,1,0:T(8,128)S(1)}, f32[2,64,128]{2,1,0:T(8,128)S(1)}, u32[]{:S(2)}, u32[]{:S(2)}) collective-permute-start(f32[2,64,128]{2,1,0:T(8,128)S(1)} %get-tuple-element.45), channel_id=1, source_target_pairs={{0,3},{1,2},{2,1},{3,0},{4,7},{5,6},{6,5},{7,4},{8,11},{9,10},{10,... | collective-permute-start | bytes 196616 | tf_op jit(solution)/shard_map/ppermute | solution.py:462
  7.3 20.4 %collective-permute-start.11 = (f32[64,512]{1,0:T(8,128)S(1)}, f32[64,512]{1,0:T(8,128)S(1)}, u32[]{:S(2)}, u32[]{:S(2)}) collective-permute-start(f32[64,512]{1,0:T(8,128)S(1)} %bitcast.1), channel_id=1, source_target_pairs={{0,4},{1,5},{2,6},{3,7},{4,0},{5,1},{6,2},{7,3},{16,20},{17,21},{1... | collective-permute-start | bytes 393224 | tf_op jit(solution)/shard_map/ppermute | solution.py:500
  12.3 11.6 %collective-permute-start.3 = (f32[2,64,128]{2,1,0:T(8,128)S(1)}, f32[2,64,128]{2,1,0:T(8,128)S(1)}, u32[]{:S(2)}, u32[]{:S(2)}) collective-permute-start(f32[2,64,128]{2,1,0:T(8,128)S(1)} %get-tuple-element.46), channel_id=1, source_target_pairs={{0,4},{1,5},{2,6},{3,7},{4,0},{5,1},{6,2},{7,3},{8,12},{9,13},{10,... | collective-permute-start | bytes 196616 | tf_op jit(solution)/shard_map/ppermute | solution.py:462
  12.4 13.1 %collective-permute-start.4 = (f32[2,64,128]{2,1,0:T(8,128)S(1)}, f32[2,64,128]{2,1,0:T(8,128)S(1)}, u32[]{:S(2)}, u32[]{:S(2)}) collective-permute-start(f32[2,64,128]{2,1,0:T(8,128)S(1)} %get-tuple-element.47), channel_id=1, source_target_pairs={{0,5},{1,4},{2,7},{3,6},{4,1},{5,0},{6,3},{7,2},{8,13},{9,12},{10,... | collective-permute-start | bytes 196616 | tf_op jit(solution)/shard_map/ppermute | solution.py:462
  16.3 9.2 %collective-permute-start.5 = (f32[2,64,128]{2,1,0:T(8,128)S(1)}, f32[2,64,128]{2,1,0:T(8,128)S(1)}, u32[]{:S(2)}, u32[]{:S(2)}) collective-permute-start(f32[2,64,128]{2,1,0:T(8,128)S(1)} %get-tuple-element.48), channel_id=1, source_target_pairs={{0,6},{1,7},{2,4},{3,5},{4,2},{5,3},{6,0},{7,1},{8,14},{9,15},{10,... | collective-permute-start | bytes 196616 | tf_op jit(solution)/shard_map/ppermute | solution.py:462
  17.6 7.9 %collective-permute-start.6 = (f32[2,64,128]{2,1,0:T(8,128)S(1)}, f32[2,64,128]{2,1,0:T(8,128)S(1)}, u32[]{:S(2)}, u32[]{:S(2)}) collective-permute-start(f32[2,64,128]{2,1,0:T(8,128)S(1)} %get-tuple-element.49), channel_id=1, source_target_pairs={{0,7},{1,6},{2,5},{3,4},{4,3},{5,2},{6,1},{7,0},{8,15},{9,14},{10,... | collective-permute-start | bytes 196616 | tf_op jit(solution)/shard_map/ppermute | solution.py:462
  23.9 7.6 %collective-permute-start.10 = (f32[1,64,512]{2,1,0:T(8,128)S(1)}, f32[1,64,512]{2,1,0:T(8,128)S(1)}, u32[]{:S(2)}, u32[]{:S(2)}) collective-permute-start(f32[1,64,512]{2,1,0:T(8,128)S(1)} %copy-done.2), channel_id=1, source_target_pairs={{0,8},{8,0},{1,9},{9,1},{2,10},{10,2},{3,11},{11,3},{4,12},{12,4},... | collective-permute-start | bytes 393224 | tf_op jit(solution)/shard_map/ppermute | solution.py:501
  26.6 6.0 %collective-permute-start.7 = (f32[2,128,128]{2,1,0:T(8,128)S(1)}, f32[2,128,128]{2,1,0:T(8,128)S(1)}, u32[]{:S(2)}, u32[]{:S(2)}) collective-permute-start(f32[2,128,128]{2,1,0:T(8,128)S(1)} %get-tuple-element.53), channel_id=1, source_target_pairs={{0,1},{1,0},{2,3},{3,2},{4,5},{5,4},{6,7},{7,6},{8,9},{9,8},{10,11... | collective-permute-start | bytes 393224 | tf_op jit(solution)/shard_map/ppermute | solution.py:462
  29.1 5.9 %collective-permute-start.8 = (f32[2,128,128]{2,1,0:T(8,128)S(1)}, f32[2,128,128]{2,1,0:T(8,128)S(1)}, u32[]{:S(2)}, u32[]{:S(2)}) collective-permute-start(f32[2,128,128]{2,1,0:T(8,128)S(1)} %get-tuple-element.54), channel_id=1, source_target_pairs={{0,2},{1,3},{2,0},{3,1},{4,6},{5,7},{6,4},{7,5},{8,10},{9,11},{10,... | collective-permute-start | bytes 393224 | tf_op jit(solution)/shard_map/ppermute | solution.py:462
  31.1 5.9 %collective-permute-start.9 = (f32[2,128,128]{2,1,0:T(8,128)S(1)}, f32[2,128,128]{2,1,0:T(8,128)S(1)}, u32[]{:S(2)}, u32[]{:S(2)}) collective-permute-start(f32[2,128,128]{2,1,0:T(8,128)S(1)} %get-tuple-element.55), channel_id=1, source_target_pairs={{0,3},{1,2},{2,1},{3,0},{4,7},{5,6},{6,5},{7,4},{8,11},{9,10},{10,... | collective-permute-start | bytes 393224 | tf_op jit(solution)/shard_map/ppermute | solution.py:462
  38.3 5.9 %collective-permute-start.13 = (f32[2,128,128]{2,1,0:T(8,128)S(1)}, f32[2,128,128]{2,1,0:T(8,128)S(1)}, u32[]{:S(2)}, u32[]{:S(2)}) collective-permute-start(f32[2,128,128]{2,1,0:T(8,128)S(1)} %get-tuple-element.62), channel_id=1, source_target_pairs={{0,1},{1,0},{2,3},{3,2},{4,5},{5,4},{6,7},{7,6},{8,9},{9,8},{10,11... | collective-permute-start | bytes 393224 | tf_op jit(solution)/shard_map/ppermute | solution.py:462
  39.3 6.4 %collective-permute-start.14 = (f32[2,128,128]{2,1,0:T(8,128)S(1)}, f32[2,128,128]{2,1,0:T(8,128)S(1)}, u32[]{:S(2)}, u32[]{:S(2)}) collective-permute-start(f32[2,128,128]{2,1,0:T(8,128)S(1)} %get-tuple-element.63), channel_id=1, source_target_pairs={{0,2},{1,3},{2,0},{3,1},{4,6},{5,7},{6,4},{7,5},{8,10},{9,11},{10,... | collective-permute-start | bytes 393224 | tf_op jit(solution)/shard_map/ppermute | solution.py:462
  40.3 7.8 %collective-permute-start.15 = (f32[2,128,128]{2,1,0:T(8,128)S(1)}, f32[2,128,128]{2,1,0:T(8,128)S(1)}, u32[]{:S(2)}, u32[]{:S(2)}) collective-permute-start(f32[2,128,128]{2,1,0:T(8,128)S(1)} %get-tuple-element.64), channel_id=1, source_target_pairs={{0,3},{1,2},{2,1},{3,0},{4,7},{5,6},{6,5},{7,4},{8,11},{9,10},{10,... | collective-permute-start | bytes 393224 | tf_op jit(solution)/shard_map/ppermute | solution.py:462
  49.2 6.9 %collective-permute-start.17 = (f32[2,64,128]{2,1,0:T(8,128)S(1)}, f32[2,64,128]{2,1,0:T(8,128)S(1)}, u32[]{:S(2)}, u32[]{:S(2)}) collective-permute-start(f32[2,64,128]{2,1,0:T(8,128)S(1)} %get-tuple-element.70), channel_id=1, source_target_pairs={{0,1},{1,0},{2,3},{3,2},{4,5},{5,4},{6,7},{7,6},{8,9},{9,8},{10,11... | collective-permute-start | bytes 196616 | tf_op jit(solution)/shard_map/ppermute | solution.py:462
  50.3 8.5 %collective-permute-start.18 = (f32[2,64,128]{2,1,0:T(8,128)S(1)}, f32[2,64,128]{2,1,0:T(8,128)S(1)}, u32[]{:S(2)}, u32[]{:S(2)}) collective-permute-start(f32[2,64,128]{2,1,0:T(8,128)S(1)} %get-tuple-element.71), channel_id=1, source_target_pairs={{0,2},{1,3},{2,0},{3,1},{4,6},{5,7},{6,4},{7,5},{8,10},{9,11},{10,... | collective-permute-start | bytes 196616 | tf_op jit(solution)/shard_map/ppermute | solution.py:462
  51.3 9.2 %collective-permute-start.19 = (f32[2,64,128]{2,1,0:T(8,128)S(1)}, f32[2,64,128]{2,1,0:T(8,128)S(1)}, u32[]{:S(2)}, u32[]{:S(2)}) collective-permute-start(f32[2,64,128]{2,1,0:T(8,128)S(1)} %get-tuple-element.72), channel_id=1, source_target_pairs={{0,3},{1,2},{2,1},{3,0},{4,7},{5,6},{6,5},{7,4},{8,11},{9,10},{10,... | collective-permute-start | bytes 196616 | tf_op jit(solution)/shard_map/ppermute | solution.py:462
  52.8 10.1 %collective-permute-start.20 = (f32[2,64,128]{2,1,0:T(8,128)S(1)}, f32[2,64,128]{2,1,0:T(8,128)S(1)}, u32[]{:S(2)}, u32[]{:S(2)}) collective-permute-start(f32[2,64,128]{2,1,0:T(8,128)S(1)} %get-tuple-element.73), channel_id=1, source_target_pairs={{0,4},{1,5},{2,6},{3,7},{4,0},{5,1},{6,2},{7,3},{8,12},{9,13},{10,... | collective-permute-start | bytes 196616 | tf_op jit(solution)/shard_map/ppermute | solution.py:462
  54.9 9.7 %collective-permute-start.21 = (f32[2,64,128]{2,1,0:T(8,128)S(1)}, f32[2,64,128]{2,1,0:T(8,128)S(1)}, u32[]{:S(2)}, u32[]{:S(2)}) collective-permute-start(f32[2,64,128]{2,1,0:T(8,128)S(1)} %get-tuple-element.74), channel_id=1, source_target_pairs={{0,5},{1,4},{2,7},{3,6},{4,1},{5,0},{6,3},{7,2},{8,13},{9,12},{10,... | collective-permute-start | bytes 196616 | tf_op jit(solution)/shard_map/ppermute | solution.py:462
  56.1 8.5 %collective-permute-start.22 = (f32[2,64,128]{2,1,0:T(8,128)S(1)}, f32[2,64,128]{2,1,0:T(8,128)S(1)}, u32[]{:S(2)}, u32[]{:S(2)}) collective-permute-start(f32[2,64,128]{2,1,0:T(8,128)S(1)} %get-tuple-element.75), channel_id=1, source_target_pairs={{0,6},{1,7},{2,4},{3,5},{4,2},{5,3},{6,0},{7,1},{8,14},{9,15},{10,... | collective-permute-start | bytes 196616 | tf_op jit(solution)/shard_map/ppermute | solution.py:462
  58.8 7.1 %collective-permute-start.23 = (f32[2,64,128]{2,1,0:T(8,128)S(1)}, f32[2,64,128]{2,1,0:T(8,128)S(1)}, u32[]{:S(2)}, u32[]{:S(2)}) collective-permute-start(f32[2,64,128]{2,1,0:T(8,128)S(1)} %get-tuple-element.76), channel_id=1, source_target_pairs={{0,7},{1,6},{2,5},{3,4},{4,3},{5,2},{6,1},{7,0},{8,15},{9,14},{10,... | collective-permute-start | bytes 196616 | tf_op jit(solution)/shard_map/ppermute | solution.py:462
  66.3 7.3 %collective-permute-start.24 = (f32[2,2,64,512]{3,2,1,0:T(8,128)S(1)}, f32[2,2,64,512]{3,2,1,0:T(8,128)S(1)}, u32[]{:S(2)}, u32[]{:S(2)}) collective-permute-start(f32[2,2,64,512]{3,2,1,0:T(8,128)S(1)} %shard_map.120.own_ref), channel_id=1, source_target_pairs={{0,8},{8,0},{1,9},{9,1},{2,10},{10,2},{3,11},{11,3},{4,12},{12,4},... | collective-permute-start | bytes 1572872 | tf_op jit(solution)/shard_map/ppermute | solution.py:542
  66.4 7.2 %collective-permute-start.25 = (f32[64,512]{1,0:T(8,128)S(1)}, f32[64,512]{1,0:T(8,128)S(1)}, u32[]{:S(2)}, u32[]{:S(2)}) collective-permute-start(f32[64,512]{1,0:T(8,128)S(1)} %get-tuple-element.81.share_ref), channel_id=1, source_target_pairs={{8,4},{9,5},{10,6},{11,7},{12,0},{13,1},{14,2},{15,3},{24,20},{25,... | collective-permute-start | bytes 393224 | tf_op jit(solution)/shard_map/ppermute | solution.py:528
  (9 other events, 109.0 us)

commit v10 on v8

--- a/solution.py
+++ b/solution.py
@@ -172,12 +172,12 @@
 
 def spread(held, out_refs, own):
     for step, ref in enumerate(out_refs):
-        ref[...] = held[own ^ step]
+        ref[0:2] = held[own ^ step]
 
 
 def collect(in_refs, held, own):
     for step, ref in enumerate(in_refs):
-        held[own ^ step] = ref[...]
+        held[own ^ step] = ref[0:2]
 
 
 def quarter_place(block, ranks):
@@ -209,10 +209,13 @@
 
 
 def quarters_to_columns(col_radix, radix, *refs):
-    in_refs, (hre, him, tw, forward, inverse), rest = refs[:radix], refs[radix : radix + 5], refs[radix + 5 :]
+    in_refs, (share_ref, hre, him, tw, forward, inverse), rest = refs[:radix], refs[radix : radix + 6], refs[radix + 6 :]
     out_refs, (blocks, quarters) = rest[:-2], rest[-2:]
-    ranks, rows = blocks.shape[0], blocks.shape[2]
+    ranks, rows, width = blocks.shape[0], blocks.shape[2], blocks.shape[3]
     collect(in_refs, quarters, residue_of())
+    for k in range(radix):
+        at = slice(k % 2 * rows // 2, (k % 2 + 1) * rows // 2)
+        out_refs[radix][2 + k // 2, at] = share_ref[rows // 2 :, k * width : (k + 1) * width]
     source, target = Quarters(quarters, ranks, rows), Blocks(blocks, ranks, rows)
     column_kernel(col_radix, source, hre, him, tw, forward, inverse, target)
     spread(blocks, out_refs, lax.axis_index("row"))
@@ -276,9 +279,11 @@
             for i in range(2):
                 field[half, i, :, at] = part[i][half * rows // 2 : (half + 1) * rows // 2]
         turned.append(part)
-    kept = mine ^ lax.axis_index("depth") ^ 1
-    keep_ref[...] = field[kept]
-    send_ref[...] = field[1 - kept]
+    core, part_rows = lax.axis_index("depth"), rows // 4
+    for ref, sub in ((keep_ref, core), (send_ref, 1 - core)):
+        at = pl.ds(pl.multiple_of(sub * part_rows, 8), part_rows)
+        for place, block in enumerate((mine, 1 - mine)):
+            ref[:, place * part_rows : (place + 1) * part_rows] = field[block, :, at]
     value = row_forward([turned], tw, forward)
     store_blocks(held, value, radix, rows, points)
     spread(held, out_refs, residue_of())
@@ -325,8 +330,10 @@
 def last_kernel(radix, ranks, *refs):
     in_refs, screens, refs = refs[:ranks], refs[ranks : ranks + 4], refs[ranks + 4 :]
     share_ref, tw, inverse, out_ref, held = refs
-    points = held.shape[3]
-    out_ref[4] = share_ref[...]
+    rows, points = held.shape[2], held.shape[3]
+    for k in range(radix):
+        at, columns = slice(k % 2 * rows // 2, (k % 2 + 1) * rows // 2), slice(k * points, (k + 1) * points)
+        out_ref[4, : rows // 2, columns] = share_ref[: rows // 2, columns] + in_refs[radix][2 + k // 2, at]
     collect(in_refs, held, lax.axis_index("row"))
     for f, parts in enumerate(row_inverse(held, tw, inverse, radix, 2)):
         for m, part in enumerate(parts):
@@ -337,7 +344,8 @@
             out_ref[2 * f + 1, :, at] = im
 
 
-def output_kernel(own_ref, got_ref, more_ref, image_ref, leaving_ref):
+def output_kernel(own_ref, got_ref, image_ref, leaving_ref):
+    half = own_ref.shape[1] // 2
     for core, (source, receiver) in enumerate(((own_ref, got_ref), (got_ref, own_ref))):
 
         @pl.when(lax.axis_index("depth") == core)
@@ -345,7 +353,8 @@
             leaving_ref[0, 0:2] = source[2 * core : 2 * core + 2]
             leaving_ref[0, 2:4] = receiver[2 * core : 2 * core + 2]
             if core == 0:
-                image_ref[0] = got_ref[4] + more_ref[...]
+                image_ref[0, :half] = own_ref[4, :half]
+                image_ref[0, half:] = got_ref[4, :half]
             else:
                 terms = [source[i] * receiver[i] for i in range(4)]
                 image_ref[0] = (terms[0] + terms[1]) + (terms[2] + terms[3])
@@ -527,12 +536,11 @@
         scalars=scalars,
     )
     propagator_b, share, screens_b = factors[:2], factors[2], factors[3:]
-    more = lax.ppermute(share, both, [(flat(0, r), flat(0, r ^ radix)) for r in range(ranks)])
     columns = call(
         functools.partial(quarters_to_columns, col_radix, radix),
-        [blocks[1:]] * ranks,
+        [(2 + radix // 2 if step == radix else 2,) + blocks[2:] for step in range(ranks)],
         [blocks, (radix,) + quarter],
-        (*quarters, *propagator_b, col_tw, col_forward_table, col_inverse_table),
+        (*quarters, share, *propagator_b, col_tw, col_forward_table, col_inverse_table),
     )
     cells = exchange(columns, outer_steps)
     (fields,) = call(
@@ -546,7 +554,7 @@
         output_kernel,
         [(1, rows, length), (1,) + planes.shape[1:]],
         [],
-        (fields, swapped, more),
+        (fields, swapped),
         held=False,
     )
     return image, leaving

time: 75.3 us -> 69.7 us (0.926)
  starting transfers between devices: 41.3 us -> 37.2 us
  waiting for transfers between devices: 22.2 us -> 20.6 us
    ppermute x1 -> x0, starting transfers between devices: 4.1 us -> none  [shards(): lax.ppermute(share, both, [(flat(0, r), flat(0, r ^ radix)) for r in rang...]
    ppermute x1 -> x0, waiting for transfers between devices: 3.65 us -> none  [shards(): lax.ppermute(share, both, [(flat(0, r), flat(0, r ^ radix)) for r in rang...]
    ppermute x1, waiting for transfers between devices: 0.01 us -> 2.08 us  [shards(): swapped = lax.ppermute(fields, 'depth', swap)]
  transfers between devices with their start and end apart: 26 -> 25, of which waited for: 11 -> 10; matrix products, arithmetic and copies ran while one was open for 0% -> 0% of each run, Pallas kernels for 7% -> 7%
where the time goes in v10:
time: 69.7 us; the launch traced here: 69.4 us
  starting transfers between devices  37.2 us (53%)
  waiting for transfers between devices  20.6 us (30%)
  Pallas kernels  10.8 us (15%)
  between operations  0.81 us (1%)
    ppermute x20, starting transfers between devices, hop(): return lax.ppermute(array, 'row', [(r, r ^ step) for r in range(ranks)])  30.7 us
    ppermute x20, waiting for transfers between devices, hop(): return lax.ppermute(array, 'row', [(r, r ^ step) for r in range(ranks)])  18.5 us
    pallas_call x8, Pallas kernels, call(): pl.pallas_call(kernel, in_specs=[smem] * len(scalars) + [vmem] * len(args...  8.78 us
    ppermute x1, starting transfers between devices, shards(): lax.ppermute(slowness[0], both, [(flat(0, r), flat(0, r ^ radix)) for r i...  5.01 us
    ppermute x1, waiting for transfers between devices, shards(): swapped = lax.ppermute(fields, 'depth', swap)  2.08 us
    pallas_call x1, Pallas kernels, shards(): pl.pallas_call(functools.partial(first_kernel, radix), in_specs=[hbm] * 3...  1.98 us
  transfers between devices with their start and end apart: 25, of which 10 were waited for; matrix products, arithmetic and copies ran while one was open for 0% of the time, Pallas kernels for 7%

profile of v10, /device:TPU:0, one launch (start us, length us, event | category | flops | bytes accessed | tf_op | source)
XLA Modules:
  0.0 69.4 jit_solution(5821799505361466106)
XLA Ops:
  0.7 2.0 %shard_map.113 = (f32[2,64,128]{2,1,0:T(8,128)S(1)}, f32[2,64,128]{2,1,0:T(8,128)S(1)}, f32[2,64,128]{2,1,0:T(8,128)S(1)}, f32[2,64,128]{2,1,0:T(8,128)S(1)}, f3...) custom-call(f32[2,4,64,512]{3,2,1,0:T(8,128)} %planes_ref.1, ...), custom_call_target="tpu_custom_call" | custom-call | tf_op jit(solution)/shard_map/pallas_call | solution.py:488
  2.7 3.1 %collective-permute-start = (f32[2,64,128]{2,1,0:T(8,128)S(1)}, f32[2,64,128]{2,1,0:T(8,128)S(1)}, u32[]{:S(2)}, u32[]{:S(2)}) collective-permute-start(f32[2,64,128]{2,1,0:T(8,128)S(1)} %get-tuple-element.43), channel_id=1, source_target_pairs={{0,1},{1,0},{2,3},{3,2},{4,5},{5,4},{6,7},{7,6},{8,9},{9,8},{10,11... | collective-permute-start | bytes 196616 | tf_op jit(solution)/shard_map/ppermute | solution.py:473
  5.7 1.6 %collective-permute-start.1 = (f32[2,64,128]{2,1,0:T(8,128)S(1)}, f32[2,64,128]{2,1,0:T(8,128)S(1)}, u32[]{:S(2)}, u32[]{:S(2)}) collective-permute-start(f32[2,64,128]{2,1,0:T(8,128)S(1)} %get-tuple-element.44), channel_id=1, source_target_pairs={{0,2},{1,3},{2,0},{3,1},{4,6},{5,7},{6,4},{7,5},{8,10},{9,11},{10,... | collective-permute-start | bytes 196616 | tf_op jit(solution)/shard_map/ppermute | solution.py:473
  7.3 5.0 %collective-permute-start.11 = (f32[64,512]{1,0:T(8,128)S(1)}, f32[64,512]{1,0:T(8,128)S(1)}, u32[]{:S(2)}, u32[]{:S(2)}) collective-permute-start(f32[64,512]{1,0:T(8,128)S(1)} %bitcast.1), channel_id=1, source_target_pairs={{0,4},{1,5},{2,6},{3,7},{4,0},{5,1},{6,2},{7,3},{16,20},{17,21},{1... | collective-permute-start | bytes 393224 | tf_op jit(solution)/shard_map/ppermute | solution.py:511
  12.4 3.9 %collective-permute-start.4 = (f32[2,64,128]{2,1,0:T(8,128)S(1)}, f32[2,64,128]{2,1,0:T(8,128)S(1)}, u32[]{:S(2)}, u32[]{:S(2)}) collective-permute-start(f32[2,64,128]{2,1,0:T(8,128)S(1)} %get-tuple-element.47), channel_id=1, source_target_pairs={{0,5},{1,4},{2,7},{3,6},{4,1},{5,0},{6,3},{7,2},{8,13},{9,12},{10,... | collective-permute-start | bytes 196616 | tf_op jit(solution)/shard_map/ppermute | solution.py:473
  16.3 1.3 %collective-permute-start.5 = (f32[2,64,128]{2,1,0:T(8,128)S(1)}, f32[2,64,128]{2,1,0:T(8,128)S(1)}, u32[]{:S(2)}, u32[]{:S(2)}) collective-permute-start(f32[2,64,128]{2,1,0:T(8,128)S(1)} %get-tuple-element.48), channel_id=1, source_target_pairs={{0,6},{1,7},{2,4},{3,5},{4,2},{5,3},{6,0},{7,1},{8,14},{9,15},{10,... | collective-permute-start | bytes 196616 | tf_op jit(solution)/shard_map/ppermute | solution.py:473
  17.6 2.4 %collective-permute-start.6 = (f32[2,64,128]{2,1,0:T(8,128)S(1)}, f32[2,64,128]{2,1,0:T(8,128)S(1)}, u32[]{:S(2)}, u32[]{:S(2)}) collective-permute-start(f32[2,64,128]{2,1,0:T(8,128)S(1)} %get-tuple-element.49), channel_id=1, source_target_pairs={{0,7},{1,6},{2,5},{3,4},{4,3},{5,2},{6,1},{7,0},{8,15},{9,14},{10,... | collective-permute-start | bytes 196616 | tf_op jit(solution)/shard_map/ppermute | solution.py:473
  20.1 1.3 %shard_map.114 = (f32[4,2,128]{2,1,0:T(2,128)S(1)}, f32[4,128,128]{2,1,0:T(8,128)S(1)}, f32[4,128,128]{2,1,0:T(8,128)S(1)}) custom-call(s32[2]{0:T(128)S(1)} %copy-done.5, f32[2]{0:T(128)S(1)} %copy-done.6, f32[4,2,128]{2,1,0:T(2,128)S(1)} %copy-done.4), custom_call_target="tpu_custom_call" | custom-call | tf_op jit(solution)/shard_map/pallas_call | solution.py:445
  21.3 2.6 %collective-permute-done.3.refs_4_ = f32[2,64,128]{2,1,0:T(8,128)S(1)} collective-permute-done((f32[2,64,128]{2,1,0:T(8,128)S(1)}, f32[2,64,128]{2,1,0:T(8,128)S(1)}, u32[]{:S(2)}, u32[]{:S(2)}) %collective-permute-start.3) | collective-permute-done | bytes 65568 | tf_op jit(solution)/shard_map/ppermute | solution.py:473
  23.9 1.6 %collective-permute-done.4.refs_5_ = f32[2,64,128]{2,1,0:T(8,128)S(1)} collective-permute-done((f32[2,64,128]{2,1,0:T(8,128)S(1)}, f32[2,64,128]{2,1,0:T(8,128)S(1)}, u32[]{:S(2)}, u32[]{:S(2)}) %collective-permute-start.4) | collective-permute-done | bytes 65568 | tf_op jit(solution)/shard_map/ppermute | solution.py:473
  27.8 1.3 %collective-permute-start.12 = (f32[64,512]{1,0:T(8,128)S(1)}, f32[64,512]{1,0:T(8,128)S(1)}, u32[]{:S(2)}, u32[]{:S(2)}) collective-permute-start(f32[64,512]{1,0:T(8,128)S(1)} %collective-permute-done.11.far_ref), channel_id=1, source_target_pairs={{0,8},{1,9},{2,10},{3,11},{4,12},{5,13},{6,14},{7,15},{16,24},{17,... | collective-permute-start | bytes 393224 | tf_op jit(solution)/shard_map/ppermute | solution.py:513
  29.1 2.0 %collective-permute-start.8 = (f32[2,128,128]{2,1,0:T(8,128)S(1)}, f32[2,128,128]{2,1,0:T(8,128)S(1)}, u32[]{:S(2)}, u32[]{:S(2)}) collective-permute-start(f32[2,128,128]{2,1,0:T(8,128)S(1)} %get-tuple-element.54), channel_id=1, source_target_pairs={{0,2},{1,3},{2,0},{3,1},{4,6},{5,7},{6,4},{7,5},{8,10},{9,11},{10,... | collective-permute-start | bytes 393224 | tf_op jit(solution)/shard_map/ppermute | solution.py:473
  32.6 2.4 %collective-permute-done.8.refs_2_ = f32[2,128,128]{2,1,0:T(8,128)S(1)} collective-permute-done((f32[2,128,128]{2,1,0:T(8,128)S(1)}, f32[2,128,128]{2,1,0:T(8,128)S(1)}, u32[]{:S(2)}, u32[]{:S(2)}) %collective-permute-start.8) | collective-permute-done | bytes 131104 | tf_op jit(solution)/shard_map/ppermute | solution.py:473
  35.0 2.0 %collective-permute-done.9.refs_3_ = f32[2,128,128]{2,1,0:T(8,128)S(1)} collective-permute-done((f32[2,128,128]{2,1,0:T(8,128)S(1)}, f32[2,128,128]{2,1,0:T(8,128)S(1)}, u32[]{:S(2)}, u32[]{:S(2)}) %collective-permute-start.9) | collective-permute-done | bytes 131104 | tf_op jit(solution)/shard_map/ppermute | solution.py:473
  40.3 1.5 %collective-permute-start.15 = (f32[2,128,128]{2,1,0:T(8,128)S(1)}, f32[2,128,128]{2,1,0:T(8,128)S(1)}, u32[]{:S(2)}, u32[]{:S(2)}) collective-permute-start(f32[2,128,128]{2,1,0:T(8,128)S(1)} %get-tuple-element.64), channel_id=1, source_target_pairs={{0,3},{1,2},{2,1},{3,0},{4,7},{5,6},{6,5},{7,4},{8,11},{9,10},{10,... | collective-permute-start | bytes 393224 | tf_op jit(solution)/shard_map/ppermute | solution.py:473
  41.8 1.8 %shard_map.118 = (f32[4,128,128]{2,1,0:T(8,128)S(1)}, f32[4,128,128]{2,1,0:T(8,128)S(1)}, f32[64,512]{1,0:T(8,128)S(1)}, f32[64,512]{1,0:T(8,128)S(1)}, f32[64,5...) custom-call(s32[2]{0:T(128)S(1)} %copy-done.5, f32[2]{0:T(128)S(1)} %copy-done.6, ...), custom_call_target="tpu_custom_call" | custom-call | tf_op jit(solution)/shard_map/pallas_call | solution.py:445
  44.2 1.5 %collective-permute-done.14.refs_2_ = f32[2,128,128]{2,1,0:T(8,128)S(1)} collective-permute-done((f32[2,128,128]{2,1,0:T(8,128)S(1)}, f32[2,128,128]{2,1,0:T(8,128)S(1)}, u32[]{:S(2)}, u32[]{:S(2)}) %collective-permute-start.14) | collective-permute-done | bytes 131104 | tf_op jit(solution)/shard_map/ppermute | solution.py:473
  45.7 2.5 %collective-permute-done.15.refs_3_ = f32[2,128,128]{2,1,0:T(8,128)S(1)} collective-permute-done((f32[2,128,128]{2,1,0:T(8,128)S(1)}, f32[2,128,128]{2,1,0:T(8,128)S(1)}, u32[]{:S(2)}, u32[]{:S(2)}) %collective-permute-start.15) | collective-permute-done | bytes 131104 | tf_op jit(solution)/shard_map/ppermute | solution.py:473
  51.3 2.2 %collective-permute-start.20 = (f32[4,64,128]{2,1,0:T(8,128)S(1)}, f32[4,64,128]{2,1,0:T(8,128)S(1)}, u32[]{:S(2)}, u32[]{:S(2)}) collective-permute-start(f32[4,64,128]{2,1,0:T(8,128)S(1)} %get-tuple-element.74), channel_id=1, source_target_pairs={{0,4},{1,5},{2,6},{3,7},{4,0},{5,1},{6,2},{7,3},{8,12},{9,13},{10,... | collective-permute-start | bytes 393224 | tf_op jit(solution)/shard_map/ppermute | solution.py:473
  53.5 1.4 %collective-permute-start.19 = (f32[2,64,128]{2,1,0:T(8,128)S(1)}, f32[2,64,128]{2,1,0:T(8,128)S(1)}, u32[]{:S(2)}, u32[]{:S(2)}) collective-permute-start(f32[2,64,128]{2,1,0:T(8,128)S(1)} %get-tuple-element.73), channel_id=1, source_target_pairs={{0,3},{1,2},{2,1},{3,0},{4,7},{5,6},{6,5},{7,4},{8,11},{9,10},{10,... | collective-permute-start | bytes 196616 | tf_op jit(solution)/shard_map/ppermute | solution.py:473
  56.1 2.7 %collective-permute-start.22 = (f32[2,64,128]{2,1,0:T(8,128)S(1)}, f32[2,64,128]{2,1,0:T(8,128)S(1)}, u32[]{:S(2)}, u32[]{:S(2)}) collective-permute-start(f32[2,64,128]{2,1,0:T(8,128)S(1)} %get-tuple-element.76), channel_id=1, source_target_pairs={{0,6},{1,7},{2,4},{3,5},{4,2},{5,3},{6,0},{7,1},{8,14},{9,15},{10,... | collective-permute-start | bytes 196616 | tf_op jit(solution)/shard_map/ppermute | solution.py:473
  58.8 1.6 %collective-permute-start.23 = (f32[2,64,128]{2,1,0:T(8,128)S(1)}, f32[2,64,128]{2,1,0:T(8,128)S(1)}, u32[]{:S(2)}, u32[]{:S(2)}) collective-permute-start(f32[2,64,128]{2,1,0:T(8,128)S(1)} %get-tuple-element.77), channel_id=1, source_target_pairs={{0,7},{1,6},{2,5},{3,4},{4,3},{5,2},{6,1},{7,0},{8,15},{9,14},{10,... | collective-permute-start | bytes 196616 | tf_op jit(solution)/shard_map/ppermute | solution.py:473
  60.5 4.7 %collective-permute-done.21.refs_5_ = f32[2,64,128]{2,1,0:T(8,128)S(1)} collective-permute-done((f32[2,64,128]{2,1,0:T(8,128)S(1)}, f32[2,64,128]{2,1,0:T(8,128)S(1)}, u32[]{:S(2)}, u32[]{:S(2)}) %collective-permute-start.21) | collective-permute-done | bytes 65568 | tf_op jit(solution)/shard_map/ppermute | solution.py:473
  66.4 2.1 %collective-permute-done.24.got_ref = f32[5,64,512]{2,1,0:T(8,128)S(1)} collective-permute-done((f32[5,64,512]{2,1,0:T(8,128)S(1)}, f32[5,64,512]{2,1,0:T(8,128)S(1)}, u32[]{:S(2)}, u32[]{:S(2)}) %collective-permute-start.24) | collective-permute-done | bytes 655392 | tf_op jit(solution)/shard_map/ppermute | solution.py:552
  (49 shorter events, 14.3 us)
Async XLA Ops:
  2.7 9.7 %collective-permute-start = (f32[2,64,128]{2,1,0:T(8,128)S(1)}, f32[2,64,128]{2,1,0:T(8,128)S(1)}, u32[]{:S(2)}, u32[]{:S(2)}) collective-permute-start(f32[2,64,128]{2,1,0:T(8,128)S(1)} %get-tuple-element.43), channel_id=1, source_target_pairs={{0,1},{1,0},{2,3},{3,2},{4,5},{5,4},{6,7},{7,6},{8,9},{9,8},{10,11... | collective-permute-start | bytes 196616 | tf_op jit(solution)/shard_map/ppermute | solution.py:473
  5.7 10.6 %collective-permute-start.1 = (f32[2,64,128]{2,1,0:T(8,128)S(1)}, f32[2,64,128]{2,1,0:T(8,128)S(1)}, u32[]{:S(2)}, u32[]{:S(2)}) collective-permute-start(f32[2,64,128]{2,1,0:T(8,128)S(1)} %get-tuple-element.44), channel_id=1, source_target_pairs={{0,2},{1,3},{2,0},{3,1},{4,6},{5,7},{6,4},{7,5},{8,10},{9,11},{10,... | collective-permute-start | bytes 196616 | tf_op jit(solution)/shard_map/ppermute | solution.py:473
  7.3 10.3 %collective-permute-start.2 = (f32[2,64,128]{2,1,0:T(8,128)S(1)}, f32[2,64,128]{2,1,0:T(8,128)S(1)}, u32[]{:S(2)}, u32[]{:S(2)}) collective-permute-start(f32[2,64,128]{2,1,0:T(8,128)S(1)} %get-tuple-element.45), channel_id=1, source_target_pairs={{0,3},{1,2},{2,1},{3,0},{4,7},{5,6},{6,5},{7,4},{8,11},{9,10},{10,... | collective-permute-start | bytes 196616 | tf_op jit(solution)/shard_map/ppermute | solution.py:473
  7.3 20.4 %collective-permute-start.11 = (f32[64,512]{1,0:T(8,128)S(1)}, f32[64,512]{1,0:T(8,128)S(1)}, u32[]{:S(2)}, u32[]{:S(2)}) collective-permute-start(f32[64,512]{1,0:T(8,128)S(1)} %bitcast.1), channel_id=1, source_target_pairs={{0,4},{1,5},{2,6},{3,7},{4,0},{5,1},{6,2},{7,3},{16,20},{17,21},{1... | collective-permute-start | bytes 393224 | tf_op jit(solution)/shard_map/ppermute | solution.py:511
  12.3 11.6 %collective-permute-start.3 = (f32[2,64,128]{2,1,0:T(8,128)S(1)}, f32[2,64,128]{2,1,0:T(8,128)S(1)}, u32[]{:S(2)}, u32[]{:S(2)}) collective-permute-start(f32[2,64,128]{2,1,0:T(8,128)S(1)} %get-tuple-element.46), channel_id=1, source_target_pairs={{0,4},{1,5},{2,6},{3,7},{4,0},{5,1},{6,2},{7,3},{8,12},{9,13},{10,... | collective-permute-start | bytes 196616 | tf_op jit(solution)/shard_map/ppermute | solution.py:473
  12.4 13.1 %collective-permute-start.4 = (f32[2,64,128]{2,1,0:T(8,128)S(1)}, f32[2,64,128]{2,1,0:T(8,128)S(1)}, u32[]{:S(2)}, u32[]{:S(2)}) collective-permute-start(f32[2,64,128]{2,1,0:T(8,128)S(1)} %get-tuple-element.47), channel_id=1, source_target_pairs={{0,5},{1,4},{2,7},{3,6},{4,1},{5,0},{6,3},{7,2},{8,13},{9,12},{10,... | collective-permute-start | bytes 196616 | tf_op jit(solution)/shard_map/ppermute | solution.py:473
  16.3 9.2 %collective-permute-start.5 = (f32[2,64,128]{2,1,0:T(8,128)S(1)}, f32[2,64,128]{2,1,0:T(8,128)S(1)}, u32[]{:S(2)}, u32[]{:S(2)}) collective-permute-start(f32[2,64,128]{2,1,0:T(8,128)S(1)} %get-tuple-element.48), channel_id=1, source_target_pairs={{0,6},{1,7},{2,4},{3,5},{4,2},{5,3},{6,0},{7,1},{8,14},{9,15},{10,... | collective-permute-start | bytes 196616 | tf_op jit(solution)/shard_map/ppermute | solution.py:473
  17.6 7.9 %collective-permute-start.6 = (f32[2,64,128]{2,1,0:T(8,128)S(1)}, f32[2,64,128]{2,1,0:T(8,128)S(1)}, u32[]{:S(2)}, u32[]{:S(2)}) collective-permute-start(f32[2,64,128]{2,1,0:T(8,128)S(1)} %get-tuple-element.49), channel_id=1, source_target_pairs={{0,7},{1,6},{2,5},{3,4},{4,3},{5,2},{6,1},{7,0},{8,15},{9,14},{10,... | collective-permute-start | bytes 196616 | tf_op jit(solution)/shard_map/ppermute | solution.py:473
  23.9 7.6 %collective-permute-start.10 = (f32[1,64,512]{2,1,0:T(8,128)S(1)}, f32[1,64,512]{2,1,0:T(8,128)S(1)}, u32[]{:S(2)}, u32[]{:S(2)}) collective-permute-start(f32[1,64,512]{2,1,0:T(8,128)S(1)} %copy-done.2), channel_id=1, source_target_pairs={{0,8},{8,0},{1,9},{9,1},{2,10},{10,2},{3,11},{11,3},{4,12},{12,4},... | collective-permute-start | bytes 393224 | tf_op jit(solution)/shard_map/ppermute | solution.py:512
  26.6 6.0 %collective-permute-start.7 = (f32[2,128,128]{2,1,0:T(8,128)S(1)}, f32[2,128,128]{2,1,0:T(8,128)S(1)}, u32[]{:S(2)}, u32[]{:S(2)}) collective-permute-start(f32[2,128,128]{2,1,0:T(8,128)S(1)} %get-tuple-element.53), channel_id=1, source_target_pairs={{0,1},{1,0},{2,3},{3,2},{4,5},{5,4},{6,7},{7,6},{8,9},{9,8},{10,11... | collective-permute-start | bytes 393224 | tf_op jit(solution)/shard_map/ppermute | solution.py:473
  27.8 3.8 %collective-permute-start.12 = (f32[64,512]{1,0:T(8,128)S(1)}, f32[64,512]{1,0:T(8,128)S(1)}, u32[]{:S(2)}, u32[]{:S(2)}) collective-permute-start(f32[64,512]{1,0:T(8,128)S(1)} %collective-permute-done.11.far_ref), channel_id=1, source_target_pairs={{0,8},{1,9},{2,10},{3,11},{4,12},{5,13},{6,14},{7,15},{16,24},{17,... | collective-permute-start | bytes 393224 | tf_op jit(solution)/shard_map/ppermute | solution.py:513
  29.1 5.9 %collective-permute-start.8 = (f32[2,128,128]{2,1,0:T(8,128)S(1)}, f32[2,128,128]{2,1,0:T(8,128)S(1)}, u32[]{:S(2)}, u32[]{:S(2)}) collective-permute-start(f32[2,128,128]{2,1,0:T(8,128)S(1)} %get-tuple-element.54), channel_id=1, source_target_pairs={{0,2},{1,3},{2,0},{3,1},{4,6},{5,7},{6,4},{7,5},{8,10},{9,11},{10,... | collective-permute-start | bytes 393224 | tf_op jit(solution)/shard_map/ppermute | solution.py:473
  31.1 5.9 %collective-permute-start.9 = (f32[2,128,128]{2,1,0:T(8,128)S(1)}, f32[2,128,128]{2,1,0:T(8,128)S(1)}, u32[]{:S(2)}, u32[]{:S(2)}) collective-permute-start(f32[2,128,128]{2,1,0:T(8,128)S(1)} %get-tuple-element.55), channel_id=1, source_target_pairs={{0,3},{1,2},{2,1},{3,0},{4,7},{5,6},{6,5},{7,4},{8,11},{9,10},{10,... | collective-permute-start | bytes 393224 | tf_op jit(solution)/shard_map/ppermute | solution.py:473
  38.2 3.6 %collective-permute-start.16 = (f32[2,64,512]{2,1,0:T(8,128)S(1)}, f32[2,64,512]{2,1,0:T(8,128)S(1)}, u32[]{:S(2)}, u32[]{:S(2)}) collective-permute-start(f32[2,64,512]{2,1,0:T(8,128)S(1)} %get-tuple-element.66), channel_id=1, source_target_pairs={{0,8},{8,0},{1,9},{9,1},{2,10},{10,2},{3,11},{11,3},{4,12},{12,4},... | collective-permute-start | bytes 786440 | tf_op jit(solution)/shard_map/ppermute | solution.py:530
  38.3 5.9 %collective-permute-start.13 = (f32[2,128,128]{2,1,0:T(8,128)S(1)}, f32[2,128,128]{2,1,0:T(8,128)S(1)}, u32[]{:S(2)}, u32[]{:S(2)}) collective-permute-start(f32[2,128,128]{2,1,0:T(8,128)S(1)} %get-tuple-element.62), channel_id=1, source_target_pairs={{0,1},{1,0},{2,3},{3,2},{4,5},{5,4},{6,7},{7,6},{8,9},{9,8},{10,11... | collective-permute-start | bytes 393224 | tf_op jit(solution)/shard_map/ppermute | solution.py:473
  39.3 6.4 %collective-permute-start.14 = (f32[2,128,128]{2,1,0:T(8,128)S(1)}, f32[2,128,128]{2,1,0:T(8,128)S(1)}, u32[]{:S(2)}, u32[]{:S(2)}) collective-permute-start(f32[2,128,128]{2,1,0:T(8,128)S(1)} %get-tuple-element.63), channel_id=1, source_target_pairs={{0,2},{1,3},{2,0},{3,1},{4,6},{5,7},{6,4},{7,5},{8,10},{9,11},{10,... | collective-permute-start | bytes 393224 | tf_op jit(solution)/shard_map/ppermute | solution.py:473
  40.3 7.8 %collective-permute-start.15 = (f32[2,128,128]{2,1,0:T(8,128)S(1)}, f32[2,128,128]{2,1,0:T(8,128)S(1)}, u32[]{:S(2)}, u32[]{:S(2)}) collective-permute-start(f32[2,128,128]{2,1,0:T(8,128)S(1)} %get-tuple-element.64), channel_id=1, source_target_pairs={{0,3},{1,2},{2,1},{3,0},{4,7},{5,6},{6,5},{7,4},{8,11},{9,10},{10,... | collective-permute-start | bytes 393224 | tf_op jit(solution)/shard_map/ppermute | solution.py:473
  49.2 6.9 %collective-permute-start.17 = (f32[2,64,128]{2,1,0:T(8,128)S(1)}, f32[2,64,128]{2,1,0:T(8,128)S(1)}, u32[]{:S(2)}, u32[]{:S(2)}) collective-permute-start(f32[2,64,128]{2,1,0:T(8,128)S(1)} %get-tuple-element.71), channel_id=1, source_target_pairs={{0,1},{1,0},{2,3},{3,2},{4,5},{5,4},{6,7},{7,6},{8,9},{9,8},{10,11... | collective-permute-start | bytes 196616 | tf_op jit(solution)/shard_map/ppermute | solution.py:473
  50.3 8.5 %collective-permute-start.18 = (f32[2,64,128]{2,1,0:T(8,128)S(1)}, f32[2,64,128]{2,1,0:T(8,128)S(1)}, u32[]{:S(2)}, u32[]{:S(2)}) collective-permute-start(f32[2,64,128]{2,1,0:T(8,128)S(1)} %get-tuple-element.72), channel_id=1, source_target_pairs={{0,2},{1,3},{2,0},{3,1},{4,6},{5,7},{6,4},{7,5},{8,10},{9,11},{10,... | collective-permute-start | bytes 196616 | tf_op jit(solution)/shard_map/ppermute | solution.py:473
  51.3 14.6 %collective-permute-start.20 = (f32[4,64,128]{2,1,0:T(8,128)S(1)}, f32[4,64,128]{2,1,0:T(8,128)S(1)}, u32[]{:S(2)}, u32[]{:S(2)}) collective-permute-start(f32[4,64,128]{2,1,0:T(8,128)S(1)} %get-tuple-element.74), channel_id=1, source_target_pairs={{0,4},{1,5},{2,6},{3,7},{4,0},{5,1},{6,2},{7,3},{8,12},{9,13},{10,... | collective-permute-start | bytes 393224 | tf_op jit(solution)/shard_map/ppermute | solution.py:473
  53.5 6.9 %collective-permute-start.19 = (f32[2,64,128]{2,1,0:T(8,128)S(1)}, f32[2,64,128]{2,1,0:T(8,128)S(1)}, u32[]{:S(2)}, u32[]{:S(2)}) collective-permute-start(f32[2,64,128]{2,1,0:T(8,128)S(1)} %get-tuple-element.73), channel_id=1, source_target_pairs={{0,3},{1,2},{2,1},{3,0},{4,7},{5,6},{6,5},{7,4},{8,11},{9,10},{10,... | collective-permute-start | bytes 196616 | tf_op jit(solution)/shard_map/ppermute | solution.py:473
  54.9 10.3 %collective-permute-start.21 = (f32[2,64,128]{2,1,0:T(8,128)S(1)}, f32[2,64,128]{2,1,0:T(8,128)S(1)}, u32[]{:S(2)}, u32[]{:S(2)}) collective-permute-start(f32[2,64,128]{2,1,0:T(8,128)S(1)} %get-tuple-element.75), channel_id=1, source_target_pairs={{0,5},{1,4},{2,7},{3,6},{4,1},{5,0},{6,3},{7,2},{8,13},{9,12},{10,... | collective-permute-start | bytes 196616 | tf_op jit(solution)/shard_map/ppermute | solution.py:473
  56.1 9.1 %collective-permute-start.22 = (f32[2,64,128]{2,1,0:T(8,128)S(1)}, f32[2,64,128]{2,1,0:T(8,128)S(1)}, u32[]{:S(2)}, u32[]{:S(2)}) collective-permute-start(f32[2,64,128]{2,1,0:T(8,128)S(1)} %get-tuple-element.76), channel_id=1, source_target_pairs={{0,6},{1,7},{2,4},{3,5},{4,2},{5,3},{6,0},{7,1},{8,14},{9,15},{10,... | collective-permute-start | bytes 196616 | tf_op jit(solution)/shard_map/ppermute | solution.py:473
  58.8 7.1 %collective-permute-start.23 = (f32[2,64,128]{2,1,0:T(8,128)S(1)}, f32[2,64,128]{2,1,0:T(8,128)S(1)}, u32[]{:S(2)}, u32[]{:S(2)}) collective-permute-start(f32[2,64,128]{2,1,0:T(8,128)S(1)} %get-tuple-element.77), channel_id=1, source_target_pairs={{0,7},{1,6},{2,5},{3,4},{4,3},{5,2},{6,1},{7,0},{8,15},{9,14},{10,... | collective-permute-start | bytes 196616 | tf_op jit(solution)/shard_map/ppermute | solution.py:473
  (8 other events, 103.7 us)
